TPU v7x, 32 devices: a whole 2x2x4 slice. The times are simulated.
32 devices in a mesh: gx: 4 (over y, x), gy: 4 (over z), gz: 2 (over core).
Axes of the slice: x: 2, y: 2, z: 4, core: 2. Of those that a mesh axis runs over, the one named last changes fastest.
Arguments:
- force: float32 [3, 128, 64, 256], P(None, 'gx', 'gy', 'gz'), may hold values from -6 to 6
- phase: int32 [128, 64, 256], P('gx', 'gy', 'gz'), may hold values from 0 to 7
- viscosity_table: float32 [8], replicated, may hold values from 0.1 to 10
- boundary_flags: int32 [6], replicated, may hold values from 0 to 1
Outputs:
- pressure: float32 [128, 64, 256], P('gx', 'gy', 'gz')
- residual: float32 [128, 64, 256], P('gx', 'gy', 'gz')
- res_norms: float32 [3], replicated
Inputs may be any that keep to these rules, and one draw needn't show every extreme that they name: phase ids index viscosity_table. `boundary_flags`: 0 marks a no-slip face, 1 a free-slip face.
All inputs are finite; a program needn't handle non-finite values.
Results may differ from a plain program's by a relative error of at most 0.0003.
Values sent between devices are 32-bit elements; how exact they have to be, the bound alone decides.
No kernel may reach another device: no remote copies, remote signals or barrier semaphores. Data moves between devices by JAX's collectives and lax.ppermute only.
A program may use at most 192 MiB of HBM per device.

v0:
```python
import jax
import jax.numpy as jnp
from jax import lax
from jax.sharding import PartitionSpec as P

ITERS = 3
SWEEPS = 4


OMEGA = 0.8


def passed_along(value, axis, by):
    devices = lax.axis_size(axis)
    pairs = [(i, i + by) for i in range(devices) if 0 <= i + by < devices]
    return lax.ppermute(value, axis, pairs)


def extended(cells, sides, width):
    for axis, dim in sides:
        count = lax.axis_size(axis)
        ends = count - 1
        head = lax.slice_in_dim(cells, 0, width, axis=dim)
        tail = lax.slice_in_dim(cells, cells.shape[dim] - width, cells.shape[dim], axis=dim)
        cells = jnp.concatenate(
            [
                lax.ppermute(tail, axis, [(i, (i + 1) % count) for i in range(ends)]),
                cells,
                lax.ppermute(head, axis, [((i + 1) % count, i) for i in range(ends)]),
            ],
            axis=dim,
        )
    return cells


def lookup(phase, table):
    eta = jnp.zeros(phase.shape, jnp.float32)
    for level in range(table.shape[0]):
        eta = eta + jnp.where(phase == level, table[level], jnp.float32(0.0))
    return eta


def trim(array, keep):
    for dim in range(3):
        if dim != keep:
            array = lax.slice_in_dim(array, 1, array.shape[dim] - 1, axis=dim)
    return array


def coefficients(eta_wide, flags, starts, totals):
    walls = (flags == 0).astype(jnp.float32)
    inner = eta_wide[1:-1, 1:-1, 1:-1]
    faces = []
    diag = [jnp.zeros_like(inner) for comp in range(3)]
    for axis in range(3):
        length = eta_wide.shape[axis]
        spots = starts[axis] + jnp.arange(length, dtype=jnp.int32)
        inside = (spots >= 0) & (spots < totals[axis])
        shape = [1, 1, 1]
        shape[axis] = length - 2
        upper_in = inside[2:].reshape(shape)
        lower_in = inside[:-2].reshape(shape)
        sides = trim(eta_wide, axis)
        middle = lax.slice_in_dim(sides, 1, length - 1, axis=axis)
        upper = 0.5 * (middle + lax.slice_in_dim(sides, 2, length, axis=axis))
        lower = 0.5 * (middle + lax.slice_in_dim(sides, 0, length - 2, axis=axis))
        faces.append((jnp.where(upper_in, upper, 0.0), jnp.where(lower_in, lower, 0.0)))
        for comp in range(3):
            normal = 1.0 if comp == axis else 0.0
            wall_low = jnp.maximum(walls[2 * axis], normal)
            wall_high = jnp.maximum(walls[2 * axis + 1], normal)
            diag[comp] = (
                diag[comp]
                + jnp.where(upper_in, upper, wall_high * inner)
                + jnp.where(lower_in, lower, wall_low * inner)
            )
    return (faces, jnp.stack(diag))


def viscous(wide, faces, diag):
    result = diag * wide[:, 1:-1, 1:-1, 1:-1]
    for axis in range(3):
        dim = axis + 1
        sides = wide
        for other in range(1, 4):
            if other != dim:
                sides = lax.slice_in_dim(sides, 1, sides.shape[other] - 1, axis=other)
        length = wide.shape[dim]
        result = result - faces[axis][0] * lax.slice_in_dim(sides, 2, length, axis=dim)
        result = result - faces[axis][1] * lax.slice_in_dim(sides, 0, length - 2, axis=dim)
    return result


def gradient(field):
    upper_x = passed_along(field[0:1], "gx", -1)
    upper_y = passed_along(field[:, 0:1], "gy", -1)
    upper_z = passed_along(field[:, :, 0:1], "gz", -1)
    along_x = jnp.concatenate([field[1:], upper_x], 0) - field
    along_y = jnp.concatenate([field[:, 1:], upper_y], 1) - field
    along_z = jnp.concatenate([field[:, :, 1:], upper_z], 2) - field
    return jnp.stack([along_x, along_y, along_z])


def divergence(velocity):
    lower_x = passed_along(velocity[0][-1:], "gx", 1)
    lower_y = passed_along(velocity[1][:, -1:], "gy", 1)
    lower_z = passed_along(velocity[2][:, :, -1:], "gz", 1)
    total = jnp.concatenate([lower_x, velocity[0][:-1]], 0) - velocity[0]
    total = total + jnp.concatenate([lower_y, velocity[1][:, :-1]], 1) - velocity[1]
    total = total + jnp.concatenate([lower_z, velocity[2][:, :, :-1]], 2) - velocity[2]
    return total


def per_device(force, phase, viscosity_table, boundary_flags):
    rows = phase.shape
    totals = (
        rows[0] * lax.axis_size("gx"),
        rows[1] * lax.axis_size("gy"),
        rows[2] * lax.axis_size("gz"),
    )
    indices = (lax.axis_index("gx"), lax.axis_index("gy"), lax.axis_index("gz"))
    cells = float(totals[0] * totals[1] * totals[2])
    phase_wide = extended(phase, (("gx", 0), ("gy", 1), ("gz", 2)), 1)
    starts = tuple((indices[dim] * rows[dim] - 1 for dim in range(3)))
    eta_wide = lookup(phase_wide, viscosity_table)
    faces, diag = coefficients(eta_wide, boundary_flags, starts, totals)
    eta = eta_wide[1:-1, 1:-1, 1:-1]
    inverse = 1.0 / diag

    def sweeps(source, state, count):
        for sweep in range(count):
            wide = extended(state, (("gx", 1), ("gy", 2), ("gz", 3)), 1)
            state = state + OMEGA * inverse * (source - viscous(wide, faces, diag))
        return state

    def schur(field):
        source = gradient(field)
        return divergence(sweeps(source, OMEGA * inverse * source, SWEEPS - 1))

    rhs = divergence(sweeps(force, OMEGA * inverse * force, SWEEPS - 1))
    pressure = jnp.zeros_like(rhs)
    residual = rhs
    norms = []
    scaled = eta * residual
    applied = schur(scaled)
    for step in range(ITERS):
        last = step + 1 == ITERS
        gamma, delta, squares = lax.psum(
            (jnp.sum(residual * scaled), jnp.sum(applied * scaled), jnp.sum(residual * residual)),
            ("gx", "gy", "gz"),
        )
        norms.append(squares / cells)
        if not last:
            mass_applied = eta * applied
            twice_applied = schur(mass_applied)
        if step == 0:
            alpha = gamma / delta
            search = scaled
            search_image = applied
            scaled_image = mass_applied
            applied_image = twice_applied
        else:
            beta = gamma / gamma_old
            alpha = gamma / (delta - beta * gamma / alpha_old)
            search = scaled + beta * search
            search_image = applied + beta * search_image
            if not last:
                scaled_image = mass_applied + beta * scaled_image
                applied_image = twice_applied + beta * applied_image
        pressure = pressure + alpha * search
        residual = residual - alpha * search_image
        if not last:
            scaled = scaled - alpha * scaled_image
            applied = applied - alpha * applied_image
        gamma_old = gamma
        alpha_old = alpha
    return (pressure, residual, jnp.stack(norms))


def solution(mesh):
    placed = (P(None, "gx", "gy", "gz"), P("gx", "gy", "gz"), P(), P())
    return jax.shard_map(
        per_device,
        mesh=mesh,
        in_specs=placed,
        out_specs=(P("gx", "gy", "gz"), P("gx", "gy", "gz"), P()),
        check_vma=False,
    )
```

profile of v0, /device:TPU:0, one launch (start us, length us, event | category | flops | bytes accessed | tf_op | source)
XLA Modules:
  0.0 704.8 jit_solution(14778603171935534211)
XLA Ops:
  31.7 5.9 select_add_fusion
  68.1 5.2 fusion.169
  74.6 5.4 collective-permute-start.13
  102.9 5.2 fusion.154
  109.4 6.4 collective-permute-start.19
  138.1 5.2 fusion.139
  149.2 5.1 collective-permute-start.24
  166.3 5.7 collective-permute-start.31
  175.0 5.2 collective-permute-start.33
  199.0 5.3 fusion.124
  205.7 5.4 collective-permute-start.37
  237.4 5.3 fusion.109
  244.0 5.7 collective-permute-start.43
  275.8 5.3 fusion.94
  286.9 5.1 collective-permute-start.48
  304.1 5.7 collective-permute-start.55
  312.8 5.2 collective-permute-start.57
  336.8 5.4 fusion.79
  343.5 5.4 collective-permute-start.61
  351.9 5.1 collective-permute-start.63
  375.0 5.4 fusion.64
  381.7 5.7 collective-permute-start.67
  408.7 44.9 %all-reduce.2 = (f32[]{:T(128)}, f32[]{:T(128)}) all-reduce(f32[]{:T(128)} %get-tuple-element.14, f32[]{:T(128)} %get-tuple-element.13), channel_id=1, replica_groups=mesh['gx'=4,'gy'=4,'gz'=2] {'gx','gy','gz'}, use_global_device_ids=true, to_apply=%region_1.2 | all-reduce | flops 2 | bytes 16 | tf_op jit(solution)/shard_map/psum | solution.py:148
  459.7 5.4 fusion.49
  486.2 5.4 collective-permute-start.79
  494.6 5.2 collective-permute-start.81
  515.6 5.4 fusion.34
  522.4 5.4 collective-permute-start.85
  551.3 5.4 fusion.19
  558.0 5.7 collective-permute-start.91
  585.6 44.9 %all-reduce.1 = (f32[]{:T(128)}, f32[]{:T(128)}) all-reduce(f32[]{:T(128)} %get-tuple-element.9, f32[]{:T(128)} %get-tuple-element.8), channel_id=1, replica_groups=mesh['gx'=4,'gy'=4,'gz'=2] {'gx','gy','gz'}, use_global_device_ids=true, to_apply=%region_5.6 | all-reduce | flops 2 | bytes 16 | tf_op jit(solution)/shard_map/psum | solution.py:148
  655.9 41.0 %all-reduce = (f32[]{:T(128)}, f32[]{:T(128)}, f32[]{:T(128)}, f32[]{:T(128)}, f32[]{:T(128)}) all-reduce(f32[]{:T(128)} %get-tuple-element.7, f32[]{:T(128)} %get-tuple-element.12, f32[]{:T(128)} %get-tuple-element.6, f32[]{:T(128)} %get-tuple-element.10, f32[]{:T(128)} %get-tuple-element.11), channel_id=1, replica_groups=mesh['gx'=4,'gy'=4,'gz'=2] {'gx','gy','gz'}, use_global_device_ids=true, to_apply=%region_9.10 | all-reduce | flops 5 | bytes 40 | tf_op jit(solution)/shard_map/psum | solution.py:148
  (448 shorter events, 394.2 us)
Async XLA Ops:
  1.4 7.1 %collective-permute-start = (s32[1,16,128]{2,1,0:T(8,128)S(1)}, s32[1,16,128]{2,1,0:T(8,128)S(1)}, u32[]{:S(2)}, u32[]{:S(2)}) collective-permute-start(s32[1,16,128]{2,1,0:T(8,128)S(1)} %get-tuple-element.130), channel_id=1, source_target_pairs={{0,8},{8,16},{16,24},{1,9},{9,17},{17,25},{2,10},{10,18},{18,26},{... | collective-permute-start | bytes 24584 | tf_op jit(solution)/shard_map/ppermute | solution.py:27
  21.2 10.5 %collective-permute-start.4 = (s32[34,18,1]{2,1,0:T(8,128)S(1)}, s32[34,18,1]{2,1,0:T(8,128)S(1)}, u32[]{:S(2)}, u32[]{:S(2)}) collective-permute-start(s32[34,18,1]{2,1,0:T(8,128)S(1)} %get-tuple-element.116), channel_id=1, source_target_pairs={{0,1},{2,3},{4,5},{6,7},{8,9},{10,11},{12,13},{14,15},{16,17},{18,... | collective-permute-start | bytes 7352 | tf_op jit(solution)/shard_map/ppermute | solution.py:27
  22.5 9.2 %collective-permute-start.5 = (s32[34,18,1]{2,1,0:T(8,128)S(1)}, s32[34,18,1]{2,1,0:T(8,128)S(1)}, u32[]{:S(2)}, u32[]{:S(2)}) collective-permute-start(s32[34,18,1]{2,1,0:T(8,128)S(1)} %get-tuple-element.117), channel_id=1, source_target_pairs={{1,0},{3,2},{5,4},{7,6},{9,8},{11,10},{13,12},{15,14},{17,16},{19,... | collective-permute-start | bytes 7352 | tf_op jit(solution)/shard_map/ppermute | solution.py:29
  108.1 7.7 %collective-permute-start.18 = (f32[3,1,16,128]{3,2,1,0:T(8,128)S(1)}, f32[3,1,16,128]{3,2,1,0:T(8,128)S(1)}, u32[]{:S(2)}, u32[]{:S(2)}) collective-permute-start(f32[3,1,16,128]{3,2,1,0:T(8,128)S(1)} %get-tuple-element.111), channel_id=1, source_target_pairs={{8,0},{16,8},{24,16},{9,1},{17,9},{25,17},{10,2},{18,10},{26,18},{... | collective-permute-start | bytes 73736 | tf_op jit(solution)/shard_map/ppermute | solution.py:29
  109.4 7.4 %collective-permute-start.19 = (f32[3,1,16,128]{3,2,1,0:T(8,128)S(1)}, f32[3,1,16,128]{3,2,1,0:T(8,128)S(1)}, u32[]{:S(2)}, u32[]{:S(2)}) collective-permute-start(f32[3,1,16,128]{3,2,1,0:T(8,128)S(1)} %get-tuple-element.110), channel_id=1, source_target_pairs={{0,8},{8,16},{16,24},{1,9},{9,17},{17,25},{2,10},{10,18},{18,26},{... | collective-permute-start | bytes 73736 | tf_op jit(solution)/shard_map/ppermute | solution.py:27
  143.5 10.9 %collective-permute-start.26 = (f32[32,16,1]{2,1,0:T(8,128)S(1)}, f32[32,16,1]{2,1,0:T(8,128)S(1)}, u32[]{:S(2)}, u32[]{:S(2)}) collective-permute-start(f32[32,16,1]{2,1,0:T(8,128)S(1)} %slice.1376), channel_id=1, source_target_pairs={{0,1},{2,3},{4,5},{6,7},{8,9},{10,11},{12,13},{14,15},{16,17},{18,... | collective-permute-start | bytes 6152 | tf_op jit(solution)/shard_map/ppermute | solution.py:16
  145.0 10.7 %collective-permute-start.25 = (f32[32,1,128]{2,1,0:T(1,128)S(1)}, f32[32,1,128]{2,1,0:T(1,128)S(1)}, u32[]{:S(2)}, u32[]{:S(2)}) collective-permute-start(f32[32,1,128]{2,1,0:T(1,128)S(1)} %slice.1373), channel_id=1, source_target_pairs={{0,2},{2,4},{4,6},{1,3},{3,5},{5,7},{8,10},{10,12},{12,14},{9,11},... | collective-permute-start | bytes 49160 | tf_op jit(solution)/shard_map/ppermute | solution.py:16
  156.7 8.1 %collective-permute-start.28 = (f32[32,1,128]{2,1,0:T(1,128)S(1)}, f32[32,1,128]{2,1,0:T(1,128)S(1)}, u32[]{:S(2)}, u32[]{:S(2)}) collective-permute-start(f32[32,1,128]{2,1,0:T(1,128)S(1)} %slice.1381), channel_id=1, source_target_pairs={{2,0},{4,2},{6,4},{3,1},{5,3},{7,5},{10,8},{12,10},{14,12},{11,9},... | collective-permute-start | bytes 49160 | tf_op jit(solution)/shard_map/ppermute | solution.py:16
  166.3 7.2 %collective-permute-start.31 = (f32[3,1,16,128]{3,2,1,0:T(8,128)S(1)}, f32[3,1,16,128]{3,2,1,0:T(8,128)S(1)}, u32[]{:S(2)}, u32[]{:S(2)}) collective-permute-start(f32[3,1,16,128]{3,2,1,0:T(8,128)S(1)} %get-tuple-element.106), channel_id=1, source_target_pairs={{0,8},{8,16},{16,24},{1,9},{9,17},{17,25},{2,10},{10,18},{18,26},{... | collective-permute-start | bytes 73736 | tf_op jit(solution)/shard_map/ppermute | solution.py:27
  186.4 7.9 %collective-permute-start.34 = (f32[3,34,18,1]{1,3,2,0:T(1,128)S(1)}, f32[3,34,18,1]{1,3,2,0:T(1,128)}, u32[]{:S(2)}, u32[]{:S(2)}) collective-permute-start(f32[3,34,18,1]{1,3,2,0:T(1,128)S(1)} %copy.32), channel_id=1, source_target_pairs={{1,0},{3,2},{5,4},{7,6},{9,8},{11,10},{13,12},{15,14},{17,16},{19,... | collective-permute-start | bytes 22040 | tf_op jit(solution)/shard_map/ppermute | solution.py:29
  224.5 8.0 %collective-permute-start.40 = (f32[3,34,18,1]{1,3,2,0:T(1,128)S(1)}, f32[3,34,18,1]{1,3,2,0:T(1,128)}, u32[]{:S(2)}, u32[]{:S(2)}) collective-permute-start(f32[3,34,18,1]{1,3,2,0:T(1,128)S(1)} %copy.36), channel_id=1, source_target_pairs={{1,0},{3,2},{5,4},{7,6},{9,8},{11,10},{13,12},{15,14},{17,16},{19,... | collective-permute-start | bytes 22040 | tf_op jit(solution)/shard_map/ppermute | solution.py:29
  242.7 7.0 %collective-permute-start.42 = (f32[3,1,16,128]{3,2,1,0:T(8,128)S(1)}, f32[3,1,16,128]{3,2,1,0:T(8,128)S(1)}, u32[]{:S(2)}, u32[]{:S(2)}) collective-permute-start(f32[3,1,16,128]{3,2,1,0:T(8,128)S(1)} %get-tuple-element.103), channel_id=1, source_target_pairs={{8,0},{16,8},{24,16},{9,1},{17,9},{25,17},{10,2},{18,10},{26,18},{... | collective-permute-start | bytes 73736 | tf_op jit(solution)/shard_map/ppermute | solution.py:29
  244.0 7.2 %collective-permute-start.43 = (f32[3,1,16,128]{3,2,1,0:T(8,128)S(1)}, f32[3,1,16,128]{3,2,1,0:T(8,128)S(1)}, u32[]{:S(2)}, u32[]{:S(2)}) collective-permute-start(f32[3,1,16,128]{3,2,1,0:T(8,128)S(1)} %get-tuple-element.102), channel_id=1, source_target_pairs={{0,8},{8,16},{16,24},{1,9},{9,17},{17,25},{2,10},{10,18},{18,26},{... | collective-permute-start | bytes 73736 | tf_op jit(solution)/shard_map/ppermute | solution.py:27
  263.1 7.9 %collective-permute-start.46 = (f32[3,34,18,1]{1,3,2,0:T(1,128)S(1)}, f32[3,34,18,1]{1,3,2,0:T(1,128)}, u32[]{:S(2)}, u32[]{:S(2)}) collective-permute-start(f32[3,34,18,1]{1,3,2,0:T(1,128)S(1)} %copy.40), channel_id=1, source_target_pairs={{1,0},{3,2},{5,4},{7,6},{9,8},{11,10},{13,12},{15,14},{17,16},{19,... | collective-permute-start | bytes 22040 | tf_op jit(solution)/shard_map/ppermute | solution.py:29
  281.3 10.7 %collective-permute-start.50 = (f32[32,16,1]{2,1,0:T(8,128)S(1)}, f32[32,16,1]{2,1,0:T(8,128)S(1)}, u32[]{:S(2)}, u32[]{:S(2)}) collective-permute-start(f32[32,16,1]{2,1,0:T(8,128)S(1)} %slice.1403), channel_id=1, source_target_pairs={{0,1},{2,3},{4,5},{6,7},{8,9},{10,11},{12,13},{14,15},{16,17},{18,... | collective-permute-start | bytes 6152 | tf_op jit(solution)/shard_map/ppermute | solution.py:16
  282.7 10.7 %collective-permute-start.49 = (f32[32,1,128]{2,1,0:T(1,128)S(1)}, f32[32,1,128]{2,1,0:T(1,128)S(1)}, u32[]{:S(2)}, u32[]{:S(2)}) collective-permute-start(f32[32,1,128]{2,1,0:T(1,128)S(1)} %slice.1400), channel_id=1, source_target_pairs={{0,2},{2,4},{4,6},{1,3},{3,5},{5,7},{8,10},{10,12},{12,14},{9,11},... | collective-permute-start | bytes 49160 | tf_op jit(solution)/shard_map/ppermute | solution.py:16
  294.4 8.1 %collective-permute-start.52 = (f32[32,1,128]{2,1,0:T(1,128)S(1)}, f32[32,1,128]{2,1,0:T(1,128)S(1)}, u32[]{:S(2)}, u32[]{:S(2)}) collective-permute-start(f32[32,1,128]{2,1,0:T(1,128)S(1)} %slice.1408), channel_id=1, source_target_pairs={{2,0},{4,2},{6,4},{3,1},{5,3},{7,5},{10,8},{12,10},{14,12},{11,9},... | collective-permute-start | bytes 49160 | tf_op jit(solution)/shard_map/ppermute | solution.py:16
  304.1 7.2 %collective-permute-start.55 = (f32[3,1,16,128]{3,2,1,0:T(8,128)S(1)}, f32[3,1,16,128]{3,2,1,0:T(8,128)S(1)}, u32[]{:S(2)}, u32[]{:S(2)}) collective-permute-start(f32[3,1,16,128]{3,2,1,0:T(8,128)S(1)} %get-tuple-element.98), channel_id=1, source_target_pairs={{0,8},{8,16},{16,24},{1,9},{9,17},{17,25},{2,10},{10,18},{18,26},{... | collective-permute-start | bytes 73736 | tf_op jit(solution)/shard_map/ppermute | solution.py:27
  324.2 7.9 %collective-permute-start.58 = (f32[3,34,18,1]{1,3,2,0:T(1,128)S(1)}, f32[3,34,18,1]{1,3,2,0:T(1,128)}, u32[]{:S(2)}, u32[]{:S(2)}) collective-permute-start(f32[3,34,18,1]{1,3,2,0:T(1,128)S(1)} %copy.44), channel_id=1, source_target_pairs={{1,0},{3,2},{5,4},{7,6},{9,8},{11,10},{13,12},{15,14},{17,16},{19,... | collective-permute-start | bytes 22040 | tf_op jit(solution)/shard_map/ppermute | solution.py:29
  362.3 7.9 %collective-permute-start.64 = (f32[3,34,18,1]{1,3,2,0:T(1,128)S(1)}, f32[3,34,18,1]{1,3,2,0:T(1,128)}, u32[]{:S(2)}, u32[]{:S(2)}) collective-permute-start(f32[3,34,18,1]{1,3,2,0:T(1,128)S(1)} %copy.48), channel_id=1, source_target_pairs={{1,0},{3,2},{5,4},{7,6},{9,8},{11,10},{13,12},{15,14},{17,16},{19,... | collective-permute-start | bytes 22040 | tf_op jit(solution)/shard_map/ppermute | solution.py:29
  380.4 7.0 %collective-permute-start.66 = (f32[3,1,16,128]{3,2,1,0:T(8,128)S(1)}, f32[3,1,16,128]{3,2,1,0:T(8,128)S(1)}, u32[]{:S(2)}, u32[]{:S(2)}) collective-permute-start(f32[3,1,16,128]{3,2,1,0:T(8,128)S(1)} %get-tuple-element.95), channel_id=1, source_target_pairs={{8,0},{16,8},{24,16},{9,1},{17,9},{25,17},{10,2},{18,10},{26,18},{... | collective-permute-start | bytes 73736 | tf_op jit(solution)/shard_map/ppermute | solution.py:29
  381.7 7.2 %collective-permute-start.67 = (f32[3,1,16,128]{3,2,1,0:T(8,128)S(1)}, f32[3,1,16,128]{3,2,1,0:T(8,128)S(1)}, u32[]{:S(2)}, u32[]{:S(2)}) collective-permute-start(f32[3,1,16,128]{3,2,1,0:T(8,128)S(1)} %get-tuple-element.94), channel_id=1, source_target_pairs={{0,8},{8,16},{16,24},{1,9},{9,17},{17,25},{2,10},{10,18},{18,26},{... | collective-permute-start | bytes 73736 | tf_op jit(solution)/shard_map/ppermute | solution.py:27
  400.8 54.1 %collective-permute-start.70 = (f32[3,34,18,1]{1,3,2,0:T(1,128)S(1)}, f32[3,34,18,1]{1,3,2,0:T(1,128)}, u32[]{:S(2)}, u32[]{:S(2)}) collective-permute-start(f32[3,34,18,1]{1,3,2,0:T(1,128)S(1)} %copy.52), channel_id=1, source_target_pairs={{1,0},{3,2},{5,4},{7,6},{9,8},{11,10},{13,12},{15,14},{17,16},{19,... | collective-permute-start | bytes 22040 | tf_op jit(solution)/shard_map/ppermute | solution.py:29
  404.5 52.8 %collective-permute-start.71 = (f32[3,34,18,1]{1,3,2,0:T(1,128)}, f32[3,34,18,1]{1,3,2,0:T(1,128)}, u32[]{:S(2)}, u32[]{:S(2)}) collective-permute-start(f32[3,34,18,1]{1,3,2,0:T(1,128)} %copy.54), channel_id=1, source_target_pairs={{0,1},{2,3},{4,5},{6,7},{8,9},{10,11},{12,13},{14,15},{16,17},{18,... | collective-permute-start | bytes 22040 | tf_op jit(solution)/shard_map/ppermute | solution.py:27
  465.3 9.6 %collective-permute-start.74 = (f32[32,16,1]{2,1,0:T(8,128)S(1)}, f32[32,16,1]{2,1,0:T(8,128)S(1)}, u32[]{:S(2)}, u32[]{:S(2)}) collective-permute-start(f32[32,16,1]{2,1,0:T(8,128)S(1)} %slice.1430), channel_id=1, source_target_pairs={{0,1},{2,3},{4,5},{6,7},{8,9},{10,11},{12,13},{14,15},{16,17},{18,... | collective-permute-start | bytes 6152 | tf_op jit(solution)/shard_map/ppermute | solution.py:16
  466.8 9.5 %collective-permute-start.73 = (f32[32,1,128]{2,1,0:T(1,128)S(1)}, f32[32,1,128]{2,1,0:T(1,128)S(1)}, u32[]{:S(2)}, u32[]{:S(2)}) collective-permute-start(f32[32,1,128]{2,1,0:T(1,128)S(1)} %slice.1427), channel_id=1, source_target_pairs={{0,2},{2,4},{4,6},{1,3},{3,5},{5,7},{8,10},{10,12},{12,14},{9,11},... | collective-permute-start | bytes 49160 | tf_op jit(solution)/shard_map/ppermute | solution.py:16
  477.4 7.1 %collective-permute-start.76 = (f32[32,1,128]{2,1,0:T(1,128)S(1)}, f32[32,1,128]{2,1,0:T(1,128)S(1)}, u32[]{:S(2)}, u32[]{:S(2)}) collective-permute-start(f32[32,1,128]{2,1,0:T(1,128)S(1)} %slice.1435), channel_id=1, source_target_pairs={{2,0},{4,2},{6,4},{3,1},{5,3},{7,5},{10,8},{12,10},{14,12},{11,9},... | collective-permute-start | bytes 49160 | tf_op jit(solution)/shard_map/ppermute | solution.py:16
  558.0 7.2 %collective-permute-start.91 = (f32[3,1,16,128]{3,2,1,0:T(8,128)S(1)}, f32[3,1,16,128]{3,2,1,0:T(8,128)S(1)}, u32[]{:S(2)}, u32[]{:S(2)}) collective-permute-start(f32[3,1,16,128]{3,2,1,0:T(8,128)S(1)} %get-tuple-element.86), channel_id=1, source_target_pairs={{0,8},{8,16},{16,24},{1,9},{9,17},{17,25},{2,10},{10,18},{18,26},{... | collective-permute-start | bytes 73736 | tf_op jit(solution)/shard_map/ppermute | solution.py:27
  577.7 57.4 %collective-permute-start.94 = (f32[3,34,18,1]{1,3,2,0:T(1,128)S(1)}, f32[3,34,18,1]{1,3,2,0:T(1,128)}, u32[]{:S(2)}, u32[]{:S(2)}) collective-permute-start(f32[3,34,18,1]{1,3,2,0:T(1,128)S(1)} %copy.64), channel_id=1, source_target_pairs={{1,0},{3,2},{5,4},{7,6},{9,8},{11,10},{13,12},{15,14},{17,16},{19,... | collective-permute-start | bytes 22040 | tf_op jit(solution)/shard_map/ppermute | solution.py:29
  581.4 56.1 %collective-permute-start.95 = (f32[3,34,18,1]{1,3,2,0:T(1,128)}, f32[3,34,18,1]{1,3,2,0:T(1,128)}, u32[]{:S(2)}, u32[]{:S(2)}) collective-permute-start(f32[3,34,18,1]{1,3,2,0:T(1,128)} %copy.66), channel_id=1, source_target_pairs={{0,1},{2,3},{4,5},{6,7},{8,9},{10,11},{12,13},{14,15},{16,17},{18,... | collective-permute-start | bytes 22040 | tf_op jit(solution)/shard_map/ppermute | solution.py:27
  643.9 9.6 %collective-permute-start.98 = (f32[32,16,1]{2,1,0:T(8,128)S(1)}, f32[32,16,1]{2,1,0:T(8,128)S(1)}, u32[]{:S(2)}, u32[]{:S(2)}) collective-permute-start(f32[32,16,1]{2,1,0:T(8,128)S(1)} %slice.1457), channel_id=1, source_target_pairs={{0,1},{2,3},{4,5},{6,7},{8,9},{10,11},{12,13},{14,15},{16,17},{18,... | collective-permute-start | bytes 6152 | tf_op jit(solution)/shard_map/ppermute | solution.py:16
  645.4 9.5 %collective-permute-start.97 = (f32[32,1,128]{2,1,0:T(1,128)S(1)}, f32[32,1,128]{2,1,0:T(1,128)S(1)}, u32[]{:S(2)}, u32[]{:S(2)}) collective-permute-start(f32[32,1,128]{2,1,0:T(1,128)S(1)} %slice.1454), channel_id=1, source_target_pairs={{0,2},{2,4},{4,6},{1,3},{3,5},{5,7},{8,10},{10,12},{12,14},{9,11},... | collective-permute-start | bytes 49160 | tf_op jit(solution)/shard_map/ppermute | solution.py:16
  (117 other events, 843.9 us)
where the time goes:
time: 718 us; the launch traced here: 705 us
  starting transfers between devices  284 us (40%)
  blocking collectives  131 us (18%)
  local copies, waits for them, and re-layouts  127 us (18%)
  other arithmetic  81 us (11%)
  waiting for transfers between devices  59.7 us (8%)
  between operations  22.3 us (3%)
    ppermute x39, starting transfers between devices, extended(): lax.ppermute(tail, axis, [(i, (i + 1) % count) for i in range(ends)])  181 us
    psum x3, blocking collectives, per_device(): lax.psum((jnp.sum(residual * scaled), jnp.sum(applied * scaled), jnp.sum(...  131 us
    add x12, other arithmetic, sweeps(): state = state + OMEGA * inverse * (source - viscous(wide, faces, diag))  62.4 us
    ppermute x21, starting transfers between devices, passed_along(): return lax.ppermute(value, axis, pairs)  52.2 us
    ppermute x39, starting transfers between devices, extended(): lax.ppermute(head, axis, [((i + 1) % count, i) for i in range(ends)])  50.3 us
    slice x25, local copies, waits for them, and re-layouts, extended(): head = lax.slice_in_dim(cells, 0, width, axis=dim)  44.3 us
    ppermute x39, waiting for transfers between devices, extended(): lax.ppermute(tail, axis, [(i, (i + 1) % count) for i in range(ends)])  36.6 us
    ppermute x12, local copies, waits for them, and re-layouts, extended(): lax.ppermute(head, axis, [((i + 1) % count, i) for i in range(ends)])  25.1 us
  transfers between devices with their start and end apart: 99, of which 47 were waited for; matrix products, arithmetic and copies ran while one was open for 8% of the time, Pallas kernels for 0%

commit v1 on v0

v1 whole, which is shorter than its diff:
```python
import functools

import jax
import jax.numpy as jnp
from jax import lax
from jax.experimental import pallas as pl
from jax.experimental.pallas import tpu as pltpu
from jax.sharding import PartitionSpec as P

ITERS = 3
SWEEPS = 4
OMEGA = 0.8
HALO = 4
LANES = 128
F32 = jnp.float32

VMEM = pl.BlockSpec(memory_space=pltpu.VMEM)
SMEM = pl.BlockSpec(memory_space=pltpu.SMEM)


def sds(*shape):
    return jax.ShapeDtypeStruct(shape, F32)


def call(kernel, outs, ins, specs=None, scratch=(), flops=10**6, name=None):
    return pl.pallas_call(
        kernel,
        out_shape=outs,
        in_specs=specs or [VMEM] * len(ins),
        out_specs=jax.tree.map(lambda _: VMEM, outs),
        scratch_shapes=list(scratch),
        compiler_params=pltpu.CompilerParams(vmem_limit_bytes=24 * 2**20),
        cost_estimate=pl.CostEstimate(flops=flops, bytes_accessed=2**20, transcendentals=0),
        name=name,
    )(*ins)


def pick(items, index):
    value = items[0]
    for k in range(1, len(items)):
        value = jnp.where(index == k, items[k], value)
    return value


def split_z(value, core, n):
    blocks = [value[..., t * LANES : (t + 1) * LANES] for t in range(n)]
    return [pick(blocks, lax.rem(core + j, n)) for j in range(n)]


def join_own(parts, core):
    n = len(parts)
    return jnp.concatenate([pick(parts, lax.rem(t - core + n, n)) for t in range(n)], -1)


def join_received(parts, core):
    n = len(parts)
    return jnp.concatenate([pick(parts, lax.rem(core - t + n, n)) for t in range(n)], -1)


def up_y(row):
    return pltpu.roll(row, row.shape[0] - 1, 0)


def down_y(row):
    return pltpu.roll(row, 1, 0)


def up_z(row):
    return pltpu.roll(row, row.shape[1] - 1, 1)


def down_z(row):
    return pltpu.roll(row, 1, 1)


def rows_loop(start, stop, body, step=3):
    count = stop - start
    whole = count // step

    def chunk(i, carry):
        for k in range(step):
            body(start + i * step + k)
        return carry

    if whole > 1:
        lax.fori_loop(0, whole, chunk, 0)
        rest = start + whole * step
    else:
        rest = start
    for r in range(rest, stop):
        body(r)


def pair_perm(n, first):
    pairs = []
    for i in range(first, n - 1, 2):
        pairs += [(i, i + 1), (i + 1, i)]
    return pairs


def exchange(axis, n, a, b):
    return (
        lax.ppermute(a, axis, pair_perm(n, 0)),
        lax.ppermute(b, axis, pair_perm(n, 1)),
    )


def core_shift(value, n, j):
    return lax.ppermute(value, "gz", [(i, (i + j) % n) for i in range(n)])


def prep_kernel(n, force, phase, table, *outs):
    core = lax.axis_index("gz")
    rows = outs[0].shape[1]
    eta_out = outs[n]
    levels = table.shape[0]

    def one(r):
        ids = phase[r]
        eta = jnp.zeros(ids.shape, F32)
        for level in range(levels):
            eta = jnp.where(ids == level, table[level], eta)
        eta_out[r] = eta

    rows_loop(0, phase.shape[0], one, 4)
    for j in range(n):
        base = lax.rem(core + j, n) * rows

        def two(r, j=j, base=base):
            for c in range(3):
                outs[j][c, r] = force[c, base + r]
            outs[j][3, r] = eta_out[base + r]

        rows_loop(0, rows, two, 4)


def gather_kernel(n, *refs):
    parts = refs[:n]
    full, send_a, send_b = refs[n:]
    core = lax.axis_index("gz")
    odd = lax.rem(lax.axis_index("gy"), 2) == 1
    fields, rows, ys, _ = full.shape
    h = HALO

    for c in range(fields):

        def one(r, c=c):
            row = join_received([p[c, r] for p in parts], core)
            full[c, r] = row
            low, high = row[:h], row[ys - h :]
            send_a[c * rows + r] = jnp.where(odd, low, high)
            send_b[c * rows + r] = jnp.where(odd, high, low)

        rows_loop(0, rows, one, 4)
    for r in range(rows):
        line = full[3, r, ys - h - 1 : ys - h, :]
        send_a[fields * rows + r // 4, r % 4 : r % 4 + 1, :] = line
        send_b[fields * rows + r // 4, r % 4 : r % 4 + 1, :] = line


def force_edges_kernel(full, got_a, got_b, send_a, send_b):
    odd_y = lax.rem(lax.axis_index("gy"), 2) == 1
    place = lax.axis_index("gx") * lax.axis_size("gz") + lax.axis_index("gz")
    odd_x = lax.rem(place, 2) == 1
    fields, rows, ys, _ = full.shape
    h = HALO
    for send, first in ((send_a, odd_x), (send_b, jnp.logical_not(odd_x))):
        start = jnp.where(first, 0, rows - h)
        for c in range(fields):
            for k in range(h):
                r = start + k
                t = 3 * (c * h + k)
                row = full[c, r]
                a, b = got_a[c * rows + r], got_b[c * rows + r]
                send[t] = row[:8]
                send[t + 1] = row[8:]
                send[t + 2, :4, :] = jnp.where(odd_y, b, a)
                send[t + 2, 4:, :] = jnp.where(odd_y, a, b)
        t = 3 * fields * h
        r = jnp.where(first, h, rows - h - 1)
        row = full[3, r]
        a, b = got_a[3 * rows + r], got_b[3 * rows + r]
        send[t] = row[:8]
        send[t + 1] = row[8:]
        send[t + 2, :4, :] = jnp.where(odd_y, b, a)
        send[t + 2, 4:, :] = jnp.where(odd_y, a, b)
        line = fields * rows + start // 4
        send[t + 3, :4, :] = jnp.where(odd_y, got_a[line], got_b[line])
        send[t + 3, 4:, :] = jnp.zeros_like(send[t + 3, 4:, :])


def edges_kernel(p, got_a, got_b, send_a, send_b):
    odd_y = lax.rem(lax.axis_index("gy"), 2) == 1
    place = lax.axis_index("gx") * lax.axis_size("gz") + lax.axis_index("gz")
    odd_x = lax.rem(place, 2) == 1
    rows, ys, _ = p.shape
    h = HALO
    for send, first in ((send_a, odd_x), (send_b, jnp.logical_not(odd_x))):
        start = jnp.where(first, 0, rows - h)
        for k in range(h):
            r = start + k
            a, b = got_a[r], got_b[r]
            send[k, :ys, :] = p[r]
            send[k, ys : ys + h, :] = jnp.where(odd_y, b, a)
            send[k, ys + h :, :] = jnp.where(odd_y, a, b)


def sweep(source, target, b, w, kx, ky, kz, start, stop):
    keep = 1.0 - OMEGA

    def one(r):
        here_x, past_x, here_y, here_z = kx[r], kx[r - 1], ky[r], kz[r]
        for c in range(3):
            u = source[c, r]
            near = here_x * source[c, r + 1] + past_x * source[c, r - 1]
            near = near + here_y * up_y(u) + down_y(here_y * u)
            near = near + here_z * up_z(u) + down_z(here_z * u)
            target[c, r] = keep * u + (b[c, r] + w[c, r] * near)

    rows_loop(start, stop, one)


def solve_and_diverge(b, one_buf, two_buf, w, kx, ky, kz, emit):
    total = b.shape[1]
    source, target = b, one_buf
    for s in range(1, SWEEPS):
        sweep(source, target, b, w, kx, ky, kz, s, total - 1 - s)
        source, target = target, (two_buf if s % 2 == 1 else one_buf)
    v = source
    h = SWEEPS

    def one(r):
        vy, vz = v[1, r], v[2, r]
        lane = lax.broadcasted_iota(jnp.int32, vz.shape, 1)
        out = v[0, r - 1] - v[0, r]
        out = out + (down_y(vy) - vy)
        out = out + (jnp.where(lane == 0, 0.0, down_z(vz)) - vz)
        emit(r - h, out)

    rows_loop(h, total - h, one, 2)


def emit_result(v_own, v_others, p_out, send_a, send_b, eta_at, sums):
    n = 1 + len(v_others)
    core = lax.axis_index("gz")
    odd = lax.rem(lax.axis_index("gy"), 2) == 1
    h = HALO

    def emit(r, out):
        ys = v_own.shape[1]
        out = out[:ys]
        parts = split_z(out, core, n)
        v_own[r] = parts[0]
        for ref, part in zip(v_others, parts[1:]):
            ref[r] = part
        p = eta_at(r) * out
        if p_out is not None:
            p_out[r] = p
            low, high = p[:h], p[ys - h :]
            send_a[r] = jnp.where(odd, low, high)
            send_b[r] = jnp.where(odd, high, low)
        sums(r, out, p)

    return emit


def fold(acc, moment, index):
    value = acc[index]
    total = value[:8]
    for k in range(1, value.shape[0] // 8):
        total = total + value[8 * k : 8 * k + 8]
    lanes = total[:, :LANES]
    for t in range(1, total.shape[1] // LANES):
        lanes = lanes + total[:, t * LANES : (t + 1) * LANES]
    moment[index] = lanes


def first_kernel(n, sizes, *refs):
    full, ya, yb, xa, xb, flags = refs[:6]
    v_own, *rest = refs[6:]
    v_others, rest = rest[: n - 1], rest[n - 1 :]
    p_out, send_a, send_b, moment, kx, ky, kz, w = rest[:8]
    force, eta, line, b, one_buf, two_buf, acc = rest[8:]
    fields, rows, ys, lanes = full.shape
    h = HALO
    odd_y = lax.rem(lax.axis_index("gy"), 2) == 1
    place = lax.axis_index("gx") * lax.axis_size("gz") + lax.axis_index("gz")
    odd_x = lax.rem(place, 2) == 1
    slots = ys + 2 * h
    total = rows + 2 * h

    def set_row(ref, index, row, a, b_):
        ref[(*index, slice(0, ys), slice(None))] = row
        ref[(*index, slice(ys, ys + h), slice(None))] = jnp.where(odd_y, b_, a)
        ref[(*index, slice(ys + h, slots), slice(None))] = jnp.where(odd_y, a, b_)

    for c in range(fields):

        def one(r, c=c):
            row, a, b_ = full[c, r], ya[c * rows + r], yb[c * rows + r]
            if c < 3:
                set_row(force, (c, r + h), row, a, b_)
            else:
                set_row(eta, (r + h + 1,), row, a, b_)

        rows_loop(0, rows, one, 4)
        for k in range(h):
            t = 3 * (c * h + k)
            for q in range(3):
                a, b_ = xa[t + q], xb[t + q]
                lower, upper = jnp.where(odd_x, a, b_), jnp.where(odd_x, b_, a)
                where = slice(8 * q, 8 * q + 8)
                if c < 3:
                    force[c, k, where, :] = lower
                    force[c, h + rows + k, where, :] = upper
                else:
                    eta[1 + k, where, :] = lower
                    eta[1 + h + rows + k, where, :] = upper
    t = 3 * fields * h
    for q in range(3):
        eta[0, 8 * q : 8 * q + 8, :] = jnp.where(odd_x, xa[t + q], xb[t + q])
    lower = jnp.where(odd_x, xa[t + 3], xb[t + 3])
    upper = jnp.where(odd_x, xb[t + 3], xa[t + 3])
    for k in range(h):
        line[k] = lower[k : k + 1]
        line[h + rows + k] = upper[k : k + 1]
    for q in range(rows // 4):
        block = jnp.where(odd_y, ya[fields * rows + q], yb[fields * rows + q])
        for k in range(4):
            line[h + 4 * q + k] = block[k : k + 1]

    first_x = place * rows - h
    first_y = lax.axis_index("gy") * ys
    slot = lax.broadcasted_iota(jnp.int32, (slots, lanes), 0)
    at_y = first_y + slot - jnp.where(slot >= ys + h, slots, 0)
    at_z = lax.broadcasted_iota(jnp.int32, (slots, lanes), 1)
    in_y = (at_y >= 0) & (at_y < sizes[1])
    y_up, y_low = at_y + 1 < sizes[1], at_y >= 1
    z_up, z_low = at_z + 1 < sizes[2], at_z >= 1
    wall = [jnp.where(flags[k] == 0, 1.0, 0.0).astype(F32) for k in range(6)]

    def coefs(r):
        mid, before, after = eta[r + 1], eta[r], eta[jnp.minimum(r + 2, total)]
        at_x = first_x + r
        x_up = jnp.full(mid.shape, at_x + 1, jnp.int32) < sizes[0]
        x_low = jnp.full(mid.shape, at_x, jnp.int32) >= 1
        inside = in_y & jnp.broadcast_to((at_x >= 0) & (at_x < sizes[0]), mid.shape)
        y_before = jnp.where(slot == ys + h, line[r], down_y(mid))
        sides = (
            (x_up, after, x_low, before),
            (y_up, up_y(mid), y_low, y_before),
            (z_up, up_z(mid), z_low, down_z(mid)),
        )
        diag = [jnp.zeros_like(mid) for _ in range(3)]
        for axis, (up_in, up, low_in, low) in enumerate(sides):
            up, low = 0.5 * (mid + up), 0.5 * (mid + low)
            (kx, ky, kz)[axis][r] = jnp.where(up_in, up, 0.0)
            for c in range(3):
                low_wall = 1.0 if c == axis else wall[2 * axis]
                up_wall = 1.0 if c == axis else wall[2 * axis + 1]
                diag[c] = diag[c] + jnp.where(up_in, up, up_wall * mid)
                diag[c] = diag[c] + jnp.where(low_in, low, low_wall * mid)
        for c in range(3):
            weight = jnp.where(inside, OMEGA / diag[c], 0.0)
            w[c, r] = weight
            b[c, r] = weight * force[c, r]

    rows_loop(0, total, coefs, 1)
    acc[...] = jnp.zeros_like(acc)

    def sums(r, v, p):
        acc[0] = acc[0] + v * p
        acc[1] = acc[1] + v * v

    emit = emit_result(v_own, v_others, p_out, send_a, send_b, lambda r: full[3, r], sums)
    solve_and_diverge(b, one_buf, two_buf, w, kx, ky, kz, emit)
    for k in range(2):
        fold(acc, moment, k)


def next_kernel(n, step, *refs):
    p_in, ya, yb, xa, xb, full, kx, ky, kz, w = refs[:10]
    refs = refs[10:]
    earlier = [refs[k * n : (k + 1) * n] for k in range(step if step < ITERS else 0)]
    refs = refs[len(earlier) * n :]
    v_own, v_others, refs = refs[0], refs[1:n], refs[n:]
    if step < ITERS:
        p_out, send_a, send_b, refs = refs[0], refs[1], refs[2], refs[3:]
    else:
        p_out = send_a = send_b = None
    moment, p, b, one_buf, two_buf, acc = refs
    rows, ys, lanes = p_in.shape
    h = HALO
    core = lax.axis_index("gz")
    odd_y = lax.rem(lax.axis_index("gy"), 2) == 1
    place = lax.axis_index("gx") * lax.axis_size("gz") + lax.axis_index("gz")
    odd_x = lax.rem(place, 2) == 1
    total = rows + 2 * h
    slots = ys + 2 * h

    def fill(r):
        a, b_ = ya[r], yb[r]
        p[r + h, :ys, :] = p_in[r]
        p[r + h, ys : ys + h, :] = jnp.where(odd_y, b_, a)
        p[r + h, ys + h :, :] = jnp.where(odd_y, a, b_)

    rows_loop(0, rows, fill, 4)
    for k in range(h):
        a, b_ = xa[k], xb[k]
        p[k] = jnp.where(odd_x, a, b_)
        p[h + rows + k] = jnp.where(odd_x, b_, a)

    def grads(r):
        mid = p[r]
        lane = lax.broadcasted_iota(jnp.int32, mid.shape, 1)
        b[0, r] = w[0, r] * (p[r + 1] - mid)
        b[1, r] = w[1, r] * (up_y(mid) - mid)
        b[2, r] = w[2, r] * (jnp.where(lane == lanes - 1, 0.0, up_z(mid)) - mid)

    rows_loop(0, total - 1, grads, 2)
    acc[...] = jnp.zeros_like(acc)

    def sums(r, v, pv):
        acc[0] = acc[0] + v * p_in[r]
        if step < ITERS:
            acc[1] = acc[1] + v * pv
            acc[2] = acc[2] + v * v
            for k, parts in enumerate(earlier):
                acc[3 + k] = acc[3 + k] + v * join_own([q[r] for q in parts], core)

    emit = emit_result(v_own, v_others, p_out, send_a, send_b, lambda r: full[3, r], sums)
    solve_and_diverge(b, one_buf, two_buf, w, kx, ky, kz, emit)
    for k in range(acc.shape[0]):
        fold(acc, moment, k)


def two_sum(a, b):
    s = a + b
    t = s - a
    return s, (a - (s - t)) + (b - t)


def quick(a, b):
    s = a + b
    return s, b - (s - a)


def halves(a):
    t = 4097.0 * a
    high = t - (t - a)
    return high, a - high


def two_prod(a, b):
    p = a * b
    ah, al = halves(a)
    bh, bl = halves(b)
    return p, ((ah * bh - p) + ah * bl + al * bh) + al * bl


def add(a, b):
    s, e = two_sum(a[0], b[0])
    return quick(s, e + (a[1] + b[1]))


def mul(a, b):
    p, e = two_prod(a[0], b[0])
    return quick(p, e + (a[0] * b[1] + a[1] * b[0]))


def neg(a):
    return -a[0], -a[1]


def div(a, b):
    q = a[0] / b[0]
    r = add(a, neg(mul((q, jnp.zeros_like(q)), b)))
    q2 = r[0] / b[0]
    return quick(q, q2)


def twice(a):
    return 2.0 * a[0], 2.0 * a[1]


def last_kernel(n, cells, sums, eta, *refs):
    own = refs[: 4 * n]
    pressure, residual, norms = refs[4 * n :]
    core = lax.axis_index("gz")
    pair = (sums[0], sums[1])
    for shift in (64, 32, 16, 8, 4, 2, 1):
        pair = add(pair, tuple(pltpu.roll(x, shift, 1) for x in pair))
    item = [(pair[0][k : k + 1], pair[1][k : k + 1]) for k in range(12)]
    m0, n00, m1, m2, n11, n01, m3, m4, n22, n02, n12, m5 = item
    one = (jnp.ones_like(m0[0]), jnp.zeros_like(m0[0]))
    a0 = div(m0, m1)
    c11 = neg(a0)
    g1 = mul(c11, add(m1, mul(c11, m2)))
    b0 = div(g1, m0)
    d10, d11 = add(one, b0), c11
    a1 = div(g1, mul(d11, add(mul(d10, m2), mul(d11, m3))))
    c21 = add(c11, neg(mul(a1, d10)))
    c22 = neg(mul(a1, d11))
    g2 = mul(c22, add(m2, add(mul(c21, m3), mul(c22, m4))))
    b1 = div(g2, g1)
    d20 = add(one, mul(b1, d10))
    d21 = add(c21, mul(b1, d11))
    d22 = c22
    a2 = div(g2, mul(d22, add(mul(d20, m3), add(mul(d21, m4), mul(d22, m5)))))
    p0 = add(a0, add(mul(a1, d10), mul(a2, d20)))[0]
    p1 = add(mul(a1, d11), mul(a2, d21))[0]
    p2 = mul(a2, d22)[0]
    r1 = add(c21, neg(mul(a2, d20)))[0]
    r2 = add(c22, neg(mul(a2, d21)))[0]
    r3 = -p2
    norm1 = add(n00, mul(c11, add(twice(n01), mul(c11, n11))))
    norm2 = add(n00, mul(c21, add(twice(n01), mul(c21, n11))))
    norm2 = add(norm2, mul(c22, add(twice(n02), add(mul(twice(c21), n12), mul(c22, n22)))))
    row = lax.broadcasted_iota(jnp.int32, norms.shape, 0)
    value = jnp.where(row == 0, n00[0], jnp.where(row == 1, norm1[0], norm2[0]))
    norms[...] = value / cells
    rows = own[0].shape[0]
    for j in range(n):
        base = lax.rem(core - j + n, n) * rows
        v0, v1, v2, v3 = (own[k * n + j] for k in range(4))

        def one_row(r, base=base, v0=v0, v1=v1, v2=v2, v3=v3):
            x0, x1, x2, x3 = v0[r], v1[r], v2[r], v3[r]
            pressure[base + r] = eta[base + r] * (p0 * x0 + p1 * x1 + p2 * x2)
            residual[base + r] = (x0 + r1 * x1) + (r2 * x2 + r3 * x3)

        rows_loop(0, rows, one_row, 4)


def sums_kernel(m0, m1, m2, m3, out):
    at = 0
    for ref in (m0, m1, m2, m3):
        for k in range(ref.shape[0]):
            out[at : at + 1, :] = jnp.sum(ref[k], 0, keepdims=True)
            at += 1
    out[at:, :] = jnp.zeros_like(out[at:, :])


def reduce_all(value, counts):
    pair = jnp.stack([value, jnp.zeros_like(value)])
    for axis, n in counts:
        step = 1
        while step < n:
            other = lax.ppermute(pair, axis, [(i, i ^ step) for i in range(n)])
            s, e = two_sum(pair[0], other[0])
            pair = jnp.stack([s, e + (pair[1] + other[1])])
            step *= 2
    return pair


def per_device(nx, ny, nz, force, phase, table, flags):
    h = HALO
    wide, ys, lanes = phase.shape
    rows = wide // nz
    zs = lanes * nz
    sizes = (wide * nx, ys * ny, zs)
    slots, total = ys + 2 * h, rows + 2 * h
    cells = float(sizes[0] * sizes[1] * sizes[2])
    chain = nx * nz

    parts = call(
        functools.partial(prep_kernel, nz),
        [sds(4, rows, ys, lanes)] * nz + [sds(*phase.shape)],
        (force, phase, table),
        [VMEM, VMEM, SMEM],
        name="prep",
    )
    eta = parts[-1]
    parts = [parts[0]] + [core_shift(parts[j], nz, j) for j in range(1, nz)]
    edge = sds(4 * rows + rows // 4, h, zs)
    full, ya, yb = call(
        functools.partial(gather_kernel, nz),
        [sds(4, rows, ys, zs), edge, edge],
        parts,
        name="gather",
    )
    ya, yb = exchange("gy", ny, ya, yb)
    edge = sds(3 * 4 * h + 4, 8, zs)
    xa, xb = call(force_edges_kernel, [edge, edge], (full, ya, yb), name="force_edges")
    xa, xb = exchange(("gx", "gz"), chain, xa, xb)

    v_shape = [sds(rows, ys, lanes)] * nz
    sent = [sds(rows, ys, zs), sds(rows, h, zs), sds(rows, h, zs)]
    field = pltpu.VMEM((3, total, slots, zs), F32)
    coefs = [sds(total, slots, zs)] * 3 + [sds(3, total, slots, zs)]
    outs = call(
        functools.partial(first_kernel, nz, sizes),
        v_shape + sent + [sds(2, 8, LANES)] + coefs,
        (full, ya, yb, xa, xb, flags),
        [VMEM] * 5 + [SMEM],
        [
            field,
            pltpu.VMEM((total + 1, slots, zs), F32),
            pltpu.VMEM((total, 1, zs), F32),
            field,
            field,
            field,
            pltpu.VMEM((2, ys, zs), F32),
        ],
        name="first",
    )
    vs = [list(outs[:nz])]
    p, ya, yb, moment = outs[nz : nz + 4]
    coefs = outs[nz + 4 :]
    moments = [moment]
    for step in range(1, ITERS + 1):
        ya, yb = exchange("gy", ny, ya, yb)
        edge = sds(h, slots, zs)
        xa, xb = call(edges_kernel, [edge, edge], (p, ya, yb), name="edges")
        xa, xb = exchange(("gx", "gz"), chain, xa, xb)
        more = step < ITERS
        earlier = [q for v in vs for q in v] if more else []
        count = 3 + step if more else 1
        outs = call(
            functools.partial(next_kernel, nz, step),
            v_shape + (sent if more else []) + [sds(count, 8, LANES)],
            (p, ya, yb, xa, xb, full, *coefs, *earlier),
            None,
            [
                pltpu.VMEM((total, slots, zs), F32),
                field,
                field,
                field,
                pltpu.VMEM((count, ys, zs), F32),
            ],
            name="next",
        )
        vs.append(list(outs[:nz]))
        if more:
            p, ya, yb = outs[nz : nz + 3]
        moments.append(outs[-1])

    placed = [[v[0]] + [core_shift(v[j], nz, j) for j in range(1, nz)] for v in vs]
    flat = call(sums_kernel, sds(16, LANES), moments, name="sums")
    pair = reduce_all(flat, (("gz", nz), ("gx", nx), ("gy", ny)))
    pressure, residual, norms = call(
        functools.partial(last_kernel, nz, cells),
        [sds(*phase.shape), sds(*phase.shape), sds(8, LANES)],
        (pair, eta, *[q for v in placed for q in v]),
        name="last",
    )
    return pressure, residual, norms[:ITERS, 0]


def solution(mesh):
    placed = (P(None, "gx", "gy", "gz"), P("gx", "gy", "gz"), P(), P())
    return jax.shard_map(
        functools.partial(per_device, mesh.shape["gx"], mesh.shape["gy"], mesh.shape["gz"]),
        mesh=mesh,
        in_specs=placed,
        out_specs=(P("gx", "gy", "gz"), P("gx", "gy", "gz"), P()),
        check_vma=False,
    )
```

time: 718 us -> 121 us (0.17); the launches traced: 705 us -> 121 us
  starting transfers between devices: 284 us -> 64.2 us
  blocking collectives: 131 us -> 0 us
  local copies, waits for them, and re-layouts: 127 us -> 3.36 us
  other arithmetic: 81 us -> 0.07 us
  waiting for transfers between devices: 59.7 us -> 23.3 us
  Pallas kernels: 0 us -> 29.1 us
  between operations: 22.3 us -> 0.85 us
    ppermute x99 -> x26, starting transfers between devices: 284 us -> 64.2 us  [the longest x8 38.2 us: exchange(): lax.ppermute(a, axis, pair_perm(n, 0))]
    psum x3 -> x0, blocking collectives: 131 us -> none  [per_device(): lax.psum((jnp.sum(residual * scaled), jnp.sum(applied * scaled), jnp.sum(...]
    slice x87 -> x1, local copies, waits for them, and re-layouts: 72.4 us -> 0.63 us  [per_device(): return (pressure, residual, norms[:ITERS, 0])]
    add x13 -> x1, other arithmetic: 68.3 us -> 0.01 us  [reduce_all(): pair = jnp.stack([s, e + (pair[1] + other[1])])]
    ppermute x24 -> x0, local copies, waits for them, and re-layouts: 50.1 us -> none  [the longest x12 25.1 us: extended(): lax.ppermute(head, axis, [((i + 1) % count, i) for i in range(ends)])]
    ppermute x99 -> x26, waiting for transfers between devices: 59.7 us -> 23.3 us  [the longest x8 13.9 us: exchange(): lax.ppermute(a, axis, pair_perm(n, 0))]
    pallas_call x0 -> x12, Pallas kernels: none -> 29.1 us  [call(): pl.pallas_call(kernel, out_shape=outs, in_specs=specs or [VMEM] * len(ins...]
  transfers between devices with their start and end apart: 99 -> 26, of which waited for: 47 -> 14; matrix products, arithmetic and copies ran while one was open for 8% -> 0% of each run, Pallas kernels for 0% -> 0%
where the time goes in v1:
time: 121 us
  starting transfers between devices  64.2 us (53%)
  Pallas kernels  29.1 us (24%)
  waiting for transfers between devices  23.3 us (19%)
  local copies, waits for them, and re-layouts  3.36 us (3%)
    ppermute x8, starting transfers between devices, exchange(): lax.ppermute(a, axis, pair_perm(n, 0))  38.2 us
    pallas_call x12, Pallas kernels, call(): pl.pallas_call(kernel, out_shape=outs, in_specs=specs or [VMEM] * len(ins...  29.1 us
    ppermute x5, starting transfers between devices, reduce_all(): other = lax.ppermute(pair, axis, [(i, i ^ step) for i in range(n)])  19.1 us
    ppermute x8, waiting for transfers between devices, exchange(): lax.ppermute(a, axis, pair_perm(n, 0))  13.9 us
    ppermute x5, waiting for transfers between devices, reduce_all(): other = lax.ppermute(pair, axis, [(i, i ^ step) for i in range(n)])  7.86 us
    ppermute x8, starting transfers between devices, exchange(): lax.ppermute(b, axis, pair_perm(n, 1))  5.29 us
    unnamed x8, local copies, waits for them, and re-layouts  2.73 us
  transfers between devices with their start and end apart: 26, of which 14 were waited for; matrix products, arithmetic and copies ran while one was open for 0% of the time, Pallas kernels for 0%

profile of v1, /device:TPU:0, one launch (start us, length us, event | category | flops | bytes accessed | tf_op | source)
XLA Modules:
  0.0 120.8 jit_solution(4471413226286862834)
XLA Ops:
  0.6 1.1 copy-done
  1.8 0.9 copy-done.1
  3.4 0.8 prep.1
  4.8 1.5 %collective-permute-done.refs_1_ = f32[4,16,16,128]{3,2,1,0:T(8,128)S(1)} collective-permute-done((f32[4,16,16,128]{3,2,1,0:T(8,128)S(1)}, f32[4,16,16,128]{3,2,1,0:T(8,128)S(1)}, u32[]{:S(2)}, u32[]{:S(2)}) %collective-permute-start) | collective-permute-done | bytes 524320 | tf_op jit(solution)/shard_map/ppermute | solution.py:109
  6.5 3.0 %collective-permute-start.1 = (f32[68,4,256]{2,1,0:T(4,128)S(1)}, f32[68,4,256]{2,1,0:T(4,128)S(1)}, u32[]{:S(2)}, u32[]{:S(2)}) collective-permute-start(f32[68,4,256]{2,1,0:T(4,128)S(1)} %get-tuple-element.48), channel_id=1, source_target_pairs={{0,2},{2,0},{4,6},{6,4},{1,3},{3,1},{5,7},{7,5},{8,10},{10,8},{12,... | collective-permute-start | bytes 835592 | tf_op jit(solution)/shard_map/ppermute | solution.py:103
  10.2 6.3 %collective-permute-done.1.got_a.refs_1_ = f32[68,4,256]{2,1,0:T(4,128)S(1)} collective-permute-done((f32[68,4,256]{2,1,0:T(4,128)S(1)}, f32[68,4,256]{2,1,0:T(4,128)S(1)}, u32[]{:S(2)}, u32[]{:S(2)}) %collective-permute-start.1) | collective-permute-done | bytes 278560 | tf_op jit(solution)/shard_map/ppermute | solution.py:103
  16.6 0.7 collective-permute-start.4
  17.3 1.1 collective-permute-done.3.refs_3_
  18.4 8.1 %first.1 = (f32[16,16,128]{2,1,0:T(8,128)S(1)}, f32[16,16,128]{2,1,0:T(8,128)S(1)}, f32[16,16,256]{2,1,0:T(8,128)S(1)}, f32[16,4,256]{2,1,0:T(4,128)S(1)}, f32[1...) custom-call(f32[4,16,16,256]{3,2,1,0:T(8,128)S(1)} %get-tuple-elemen, ...), custom_call_target="tpu_custom_call" | custom-call | flops 1000000 | bytes 1048576 | tf_op jit(solution)/shard_map/first/pallas_call | solution.py:26
  26.5 4.8 %collective-permute-start.5 = (f32[16,4,256]{2,1,0:T(4,128)S(1)}, f32[16,4,256]{2,1,0:T(4,128)S(1)}, u32[]{:S(2)}, u32[]{:S(2)}) collective-permute-start(f32[16,4,256]{2,1,0:T(4,128)S(1)} %get-tuple-element.54), channel_id=1, source_target_pairs={{0,2},{2,0},{4,6},{6,4},{1,3},{3,1},{5,7},{7,5},{8,10},{10,8},{12,... | collective-permute-start | bytes 196616 | tf_op jit(solution)/shard_map/ppermute | solution.py:103
  32.0 1.6 %collective-permute-done.5.got_a.refs_1_ = f32[16,4,256]{2,1,0:T(4,128)S(1)} collective-permute-done((f32[16,4,256]{2,1,0:T(4,128)S(1)}, f32[16,4,256]{2,1,0:T(4,128)S(1)}, u32[]{:S(2)}, u32[]{:S(2)}) %collective-permute-start.5) | collective-permute-done | bytes 65568 | tf_op jit(solution)/shard_map/ppermute | solution.py:103
  33.6 11.7 %collective-permute-start.7 = (f32[4,24,256]{2,1,0:T(8,128)S(1)}, f32[4,24,256]{2,1,0:T(8,128)S(1)}, u32[]{:S(2)}, u32[]{:S(2)}) collective-permute-start(f32[4,24,256]{2,1,0:T(8,128)S(1)} %get-tuple-element.56), channel_id=1, source_target_pairs={{0,1},{1,0},{8,9},{9,8},{16,17},{17,16},{24,25},{25,24},{2,3},{3,2... | collective-permute-start | bytes 294920 | tf_op jit(solution)/shard_map/ppermute | solution.py:103
  46.2 6.0 %next.3 = (f32[16,16,128]{2,1,0:T(8,128)S(1)}, f32[16,16,128]{2,1,0:T(8,128)S(1)}, f32[16,16,256]{2,1,0:T(8,128)S(1)}, f32[16,4,256]{2,1,0:T(4,128)S(1)}, f32[16...) custom-call(f32[16,16,256]{2,1,0:T(8,128)S(1)} %get-tuple-element.53.p.refs_0_, ...), custom_call_target="tpu_custom_call" | custom-call | flops 1000000 | bytes 1048576 | tf_op jit(solution)/shard_map/next/pallas_call | solution.py:26
  52.9 6.7 %collective-permute-start.9 = (f32[16,4,256]{2,1,0:T(4,128)S(1)}, f32[16,4,256]{2,1,0:T(4,128)S(1)}, u32[]{:S(2)}, u32[]{:S(2)}) collective-permute-start(f32[16,4,256]{2,1,0:T(4,128)S(1)} %get-tuple-element.66), channel_id=1, source_target_pairs={{0,2},{2,0},{4,6},{6,4},{1,3},{3,1},{5,7},{7,5},{8,10},{10,8},{12,... | collective-permute-start | bytes 196616 | tf_op jit(solution)/shard_map/ppermute | solution.py:103
  59.6 2.2 %collective-permute-done.9.got_a.refs_1_ = f32[16,4,256]{2,1,0:T(4,128)S(1)} collective-permute-done((f32[16,4,256]{2,1,0:T(4,128)S(1)}, f32[16,4,256]{2,1,0:T(4,128)S(1)}, u32[]{:S(2)}, u32[]{:S(2)}) %collective-permute-start.9) | collective-permute-done | bytes 65568 | tf_op jit(solution)/shard_map/ppermute | solution.py:103
  61.9 4.3 %collective-permute-start.11 = (f32[4,24,256]{2,1,0:T(8,128)S(1)}, f32[4,24,256]{2,1,0:T(8,128)S(1)}, u32[]{:S(2)}, u32[]{:S(2)}) collective-permute-start(f32[4,24,256]{2,1,0:T(8,128)S(1)} %get-tuple-element.68), channel_id=1, source_target_pairs={{0,1},{1,0},{8,9},{9,8},{16,17},{17,16},{24,25},{25,24},{2,3},{3,2... | collective-permute-start | bytes 294920 | tf_op jit(solution)/shard_map/ppermute | solution.py:103
  67.1 6.0 %next.4 = (f32[16,16,128]{2,1,0:T(8,128)S(1)}, f32[16,16,128]{2,1,0:T(8,128)S(1)}, f32[16,16,256]{2,1,0:T(8,128)S(1)}, f32[16,4,256]{2,1,0:T(4,128)S(1)}, f32[16...) custom-call(f32[16,16,256]{2,1,0:T(8,128)S(1)} %get-tuple-element.65.p.refs_0_, ...), custom_call_target="tpu_custom_call" | custom-call | flops 1000000 | bytes 1048576 | tf_op jit(solution)/shard_map/next/pallas_call | solution.py:26
  73.1 1.8 %collective-permute-start.13 = (f32[16,4,256]{2,1,0:T(4,128)S(1)}, f32[16,4,256]{2,1,0:T(4,128)S(1)}, u32[]{:S(2)}, u32[]{:S(2)}) collective-permute-start(f32[16,4,256]{2,1,0:T(4,128)S(1)} %get-tuple-element.74), channel_id=1, source_target_pairs={{0,2},{2,0},{4,6},{6,4},{1,3},{3,1},{5,7},{7,5},{8,10},{10,8},{12,... | collective-permute-start | bytes 196616 | tf_op jit(solution)/shard_map/ppermute | solution.py:103
  75.6 1.9 %collective-permute-done.13.got_a.refs_1_ = f32[16,4,256]{2,1,0:T(4,128)S(1)} collective-permute-done((f32[16,4,256]{2,1,0:T(4,128)S(1)}, f32[16,4,256]{2,1,0:T(4,128)S(1)}, u32[]{:S(2)}, u32[]{:S(2)}) %collective-permute-start.13) | collective-permute-done | bytes 65568 | tf_op jit(solution)/shard_map/ppermute | solution.py:103
  77.5 5.8 %collective-permute-start.15 = (f32[4,24,256]{2,1,0:T(8,128)S(1)}, f32[4,24,256]{2,1,0:T(8,128)S(1)}, u32[]{:S(2)}, u32[]{:S(2)}) collective-permute-start(f32[4,24,256]{2,1,0:T(8,128)S(1)} %get-tuple-element.76), channel_id=1, source_target_pairs={{0,1},{1,0},{8,9},{9,8},{16,17},{17,16},{24,25},{25,24},{2,3},{3,2... | collective-permute-start | bytes 294920 | tf_op jit(solution)/shard_map/ppermute | solution.py:103
  84.2 5.9 %next.5 = (f32[16,16,128]{2,1,0:T(8,128)S(1)}, f32[16,16,128]{2,1,0:T(8,128)S(1)}, f32[1,8,128]{2,1,0:T(8,128)S(1)}) custom-call(f32[16,16,256]{2,1,0:T(8,128)S(1)} %get-tuple-element.73.p.refs_0_, f32[16,4,256]{2,1,0:T(4,128)S(1)} %collective-permute-done.13.got_a.refs_1_, f32[16,4,256]{2,1,0:T(4,128)S(1)} %collective-permute-done.14.got_b.refs_2_, ...), custom_call_target="tpu_custom_call" | custom-call | flops 1000000 | bytes 1048576 | tf_op jit(solution)/shard_map/next/pallas_call | solution.py:26
  90.2 7.2 %collective-permute-start.17 = (f32[2,16,128]{2,1,0:T(8,128)S(1)}, f32[2,16,128]{2,1,0:T(8,128)S(1)}, u32[]{:S(2)}, u32[]{:S(2)}) collective-permute-start(f32[2,16,128]{2,1,0:T(8,128)S(1)} %stack.52), channel_id=1, source_target_pairs={{0,1},{1,0},{2,3},{3,2},{4,5},{5,4},{6,7},{7,6},{8,9},{9,8},{10,11... | collective-permute-start | bytes 49160 | tf_op jit(solution)/shard_map/ppermute | solution.py:549
  97.4 0.8 collective-permute-done.17
  98.2 3.5 %collective-permute-start.18 = (f32[2,16,128]{2,1,0:T(8,128)S(1)}, f32[2,16,128]{2,1,0:T(8,128)S(1)}, u32[]{:S(2)}, u32[]{:S(2)}) collective-permute-start(f32[2,16,128]{2,1,0:T(8,128)S(1)} %pad_maximum_fusion), channel_id=1, source_target_pairs={{0,8},{8,0},{16,24},{24,16},{1,9},{9,1},{17,25},{25,17},{2,10},{10... | collective-permute-start | bytes 49160 | tf_op jit(solution)/shard_map/ppermute | solution.py:549
  101.7 1.7 %collective-permute-done.18 = f32[2,16,128]{2,1,0:T(8,128)S(1)} collective-permute-done((f32[2,16,128]{2,1,0:T(8,128)S(1)}, f32[2,16,128]{2,1,0:T(8,128)S(1)}, u32[]{:S(2)}, u32[]{:S(2)}) %collective-permute-start.18) | collective-permute-done | bytes 16416 | tf_op jit(solution)/shard_map/ppermute | solution.py:549
  103.4 2.6 %collective-permute-start.19 = (f32[2,16,128]{2,1,0:T(8,128)S(1)}, f32[2,16,128]{2,1,0:T(8,128)S(1)}, u32[]{:S(2)}, u32[]{:S(2)}) collective-permute-start(f32[2,16,128]{2,1,0:T(8,128)S(1)} %pad_maximum_fusion.1), channel_id=1, source_target_pairs={{0,16},{8,24},{16,0},{24,8},{1,17},{9,25},{17,1},{25,9},{2,18},{10... | collective-permute-start | bytes 49160 | tf_op jit(solution)/shard_map/ppermute | solution.py:549
  106.1 1.7 %collective-permute-done.19 = f32[2,16,128]{2,1,0:T(8,128)S(1)} collective-permute-done((f32[2,16,128]{2,1,0:T(8,128)S(1)}, f32[2,16,128]{2,1,0:T(8,128)S(1)}, u32[]{:S(2)}, u32[]{:S(2)}) %collective-permute-start.19) | collective-permute-done | bytes 16416 | tf_op jit(solution)/shard_map/ppermute | solution.py:549
  107.8 4.0 %collective-permute-start.20 = (f32[2,16,128]{2,1,0:T(8,128)S(1)}, f32[2,16,128]{2,1,0:T(8,128)S(1)}, u32[]{:S(2)}, u32[]{:S(2)}) collective-permute-start(f32[2,16,128]{2,1,0:T(8,128)S(1)} %pad_maximum_fusion.2), channel_id=1, source_target_pairs={{0,2},{2,0},{4,6},{6,4},{1,3},{3,1},{5,7},{7,5},{8,10},{10,8},{12,... | collective-permute-start | bytes 49160 | tf_op jit(solution)/shard_map/ppermute | solution.py:549
  111.8 1.7 %collective-permute-done.20 = f32[2,16,128]{2,1,0:T(8,128)S(1)} collective-permute-done((f32[2,16,128]{2,1,0:T(8,128)S(1)}, f32[2,16,128]{2,1,0:T(8,128)S(1)}, u32[]{:S(2)}, u32[]{:S(2)}) %collective-permute-start.20) | collective-permute-done | bytes 16416 | tf_op jit(solution)/shard_map/ppermute | solution.py:549
  113.5 1.8 %collective-permute-start.21 = (f32[2,16,128]{2,1,0:T(8,128)S(1)}, f32[2,16,128]{2,1,0:T(8,128)S(1)}, u32[]{:S(2)}, u32[]{:S(2)}) collective-permute-start(f32[2,16,128]{2,1,0:T(8,128)S(1)} %pad_maximum_fusion.3), channel_id=1, source_target_pairs={{0,4},{2,6},{4,0},{6,2},{1,5},{3,7},{5,1},{7,3},{8,12},{10,14},{12... | collective-permute-start | bytes 49160 | tf_op jit(solution)/shard_map/ppermute | solution.py:549
  116.4 1.9 %collective-permute-done.21 = f32[2,16,128]{2,1,0:T(8,128)S(1)} collective-permute-done((f32[2,16,128]{2,1,0:T(8,128)S(1)}, f32[2,16,128]{2,1,0:T(8,128)S(1)}, u32[]{:S(2)}, u32[]{:S(2)}) %collective-permute-start.21) | collective-permute-done | bytes 16416 | tf_op jit(solution)/shard_map/ppermute | solution.py:549
  118.3 1.9 %last.1 = (f32[32,16,128]{2,1,0:T(8,128)}, f32[32,16,128]{2,1,0:T(8,128)}, f32[8,128]{1,0:T(8,128)S(1)}) custom-call(f32[2,16,128]{2,1,0:T(8,128)S(1)} %pad_maximum_fusion.4.sums, f32[32,16,128]{2,1,0:T(8,128)S(1)} %get-tuple-element.79.eta, f32[16,16,128]{2,1,0:T(8,128)S(1)} %get-tuple-element.62.refs_10_.refs_0_, ...), custom_call_target="tpu_custom_call" | custom-call | flops 1000000 | bytes 1048576 | tf_op jit(solution)/shard_map/last/pallas_call | solution.py:26
  (52 shorter events, 8.9 us)
Async XLA Ops:
  0.6 1.1 copy-start
  1.8 0.9 copy-start.1
  2.7 0.7 copy-start.2
  3.4 15.0 %copy-start.3 = (s32[6]{0:T(128)S(1)}, s32[6]{0:T(128)}, u32[]{:S(2)}) copy-start(s32[6]{0:T(128)} %refs_5_.1) | copy-start | bytes 76
  4.2 2.1 %collective-permute-start = (f32[4,16,16,128]{3,2,1,0:T(8,128)S(1)}, f32[4,16,16,128]{3,2,1,0:T(8,128)S(1)}, u32[]{:S(2)}, u32[]{:S(2)}) collective-permute-start(f32[4,16,16,128]{3,2,1,0:T(8,128)S(1)} %get-tuple-element.46), channel_id=1, source_target_pairs={{0,1},{1,0},{2,3},{3,2},{4,5},{5,4},{6,7},{7,6},{8,9},{9,8},{10,11... | collective-permute-start | bytes 1572872 | tf_op jit(solution)/shard_map/ppermute | solution.py:109
  6.5 10.0 %collective-permute-start.1 = (f32[68,4,256]{2,1,0:T(4,128)S(1)}, f32[68,4,256]{2,1,0:T(4,128)S(1)}, u32[]{:S(2)}, u32[]{:S(2)}) collective-permute-start(f32[68,4,256]{2,1,0:T(4,128)S(1)} %get-tuple-element.48), channel_id=1, source_target_pairs={{0,2},{2,0},{4,6},{6,4},{1,3},{3,1},{5,7},{7,5},{8,10},{10,8},{12,... | collective-permute-start | bytes 835592 | tf_op jit(solution)/shard_map/ppermute | solution.py:103
  9.5 7.0 %collective-permute-start.2 = (f32[68,4,256]{2,1,0:T(4,128)S(1)}, f32[68,4,256]{2,1,0:T(4,128)S(1)}, u32[]{:S(2)}, u32[]{:S(2)}) collective-permute-start(f32[68,4,256]{2,1,0:T(4,128)S(1)} %get-tuple-element.49), channel_id=1, source_target_pairs={{2,4},{4,2},{3,5},{5,3},{10,12},{12,10},{11,13},{13,11},{18,20},{2... | collective-permute-start | bytes 835592 | tf_op jit(solution)/shard_map/ppermute | solution.py:104
  16.6 1.8 %collective-permute-start.3 = (f32[52,8,256]{2,1,0:T(8,128)S(1)}, f32[52,8,256]{2,1,0:T(8,128)S(1)}, u32[]{:S(2)}, u32[]{:S(2)}) collective-permute-start(f32[52,8,256]{2,1,0:T(8,128)S(1)} %get-tuple-element.50), channel_id=1, source_target_pairs={{0,1},{1,0},{8,9},{9,8},{16,17},{17,16},{24,25},{25,24},{2,3},{3,2... | collective-permute-start | bytes 1277960 | tf_op jit(solution)/shard_map/ppermute | solution.py:103
  16.6 1.8 %collective-permute-start.4 = (f32[52,8,256]{2,1,0:T(8,128)S(1)}, f32[52,8,256]{2,1,0:T(8,128)S(1)}, u32[]{:S(2)}, u32[]{:S(2)}) collective-permute-start(f32[52,8,256]{2,1,0:T(8,128)S(1)} %get-tuple-element.51), channel_id=1, source_target_pairs={{1,8},{8,1},{9,16},{16,9},{17,24},{24,17},{3,10},{10,3},{11,18},{1... | collective-permute-start | bytes 1277960 | tf_op jit(solution)/shard_map/ppermute | solution.py:104
  26.5 7.1 %collective-permute-start.5 = (f32[16,4,256]{2,1,0:T(4,128)S(1)}, f32[16,4,256]{2,1,0:T(4,128)S(1)}, u32[]{:S(2)}, u32[]{:S(2)}) collective-permute-start(f32[16,4,256]{2,1,0:T(4,128)S(1)} %get-tuple-element.54), channel_id=1, source_target_pairs={{0,2},{2,0},{4,6},{6,4},{1,3},{3,1},{5,7},{7,5},{8,10},{10,8},{12,... | collective-permute-start | bytes 196616 | tf_op jit(solution)/shard_map/ppermute | solution.py:103
  31.3 2.2 %collective-permute-start.6 = (f32[16,4,256]{2,1,0:T(4,128)S(1)}, f32[16,4,256]{2,1,0:T(4,128)S(1)}, u32[]{:S(2)}, u32[]{:S(2)}) collective-permute-start(f32[16,4,256]{2,1,0:T(4,128)S(1)} %get-tuple-element.55), channel_id=1, source_target_pairs={{2,4},{4,2},{3,5},{5,3},{10,12},{12,10},{11,13},{13,11},{18,20},{2... | collective-permute-start | bytes 196616 | tf_op jit(solution)/shard_map/ppermute | solution.py:104
  33.6 12.7 %collective-permute-start.7 = (f32[4,24,256]{2,1,0:T(8,128)S(1)}, f32[4,24,256]{2,1,0:T(8,128)S(1)}, u32[]{:S(2)}, u32[]{:S(2)}) collective-permute-start(f32[4,24,256]{2,1,0:T(8,128)S(1)} %get-tuple-element.56), channel_id=1, source_target_pairs={{0,1},{1,0},{8,9},{9,8},{16,17},{17,16},{24,25},{25,24},{2,3},{3,2... | collective-permute-start | bytes 294920 | tf_op jit(solution)/shard_map/ppermute | solution.py:103
  45.3 0.9 collective-permute-start.8
  52.2 7.4 %collective-permute-start.10 = (f32[16,4,256]{2,1,0:T(4,128)S(1)}, f32[16,4,256]{2,1,0:T(4,128)S(1)}, u32[]{:S(2)}, u32[]{:S(2)}) collective-permute-start(f32[16,4,256]{2,1,0:T(4,128)S(1)} %get-tuple-element.67), channel_id=1, source_target_pairs={{2,4},{4,2},{3,5},{5,3},{10,12},{12,10},{11,13},{13,11},{18,20},{2... | collective-permute-start | bytes 196616 | tf_op jit(solution)/shard_map/ppermute | solution.py:104
  52.9 8.9 %collective-permute-start.9 = (f32[16,4,256]{2,1,0:T(4,128)S(1)}, f32[16,4,256]{2,1,0:T(4,128)S(1)}, u32[]{:S(2)}, u32[]{:S(2)}) collective-permute-start(f32[16,4,256]{2,1,0:T(4,128)S(1)} %get-tuple-element.66), channel_id=1, source_target_pairs={{0,2},{2,0},{4,6},{6,4},{1,3},{3,1},{5,7},{7,5},{8,10},{10,8},{12,... | collective-permute-start | bytes 196616 | tf_op jit(solution)/shard_map/ppermute | solution.py:103
  61.9 5.2 %collective-permute-start.11 = (f32[4,24,256]{2,1,0:T(8,128)S(1)}, f32[4,24,256]{2,1,0:T(8,128)S(1)}, u32[]{:S(2)}, u32[]{:S(2)}) collective-permute-start(f32[4,24,256]{2,1,0:T(8,128)S(1)} %get-tuple-element.68), channel_id=1, source_target_pairs={{0,1},{1,0},{8,9},{9,8},{16,17},{17,16},{24,25},{25,24},{2,3},{3,2... | collective-permute-start | bytes 294920 | tf_op jit(solution)/shard_map/ppermute | solution.py:103
  66.1 0.9 collective-permute-start.12
  73.1 4.3 %collective-permute-start.13 = (f32[16,4,256]{2,1,0:T(4,128)S(1)}, f32[16,4,256]{2,1,0:T(4,128)S(1)}, u32[]{:S(2)}, u32[]{:S(2)}) collective-permute-start(f32[16,4,256]{2,1,0:T(4,128)S(1)} %get-tuple-element.74), channel_id=1, source_target_pairs={{0,2},{2,0},{4,6},{6,4},{1,3},{3,1},{5,7},{7,5},{8,10},{10,8},{12,... | collective-permute-start | bytes 196616 | tf_op jit(solution)/shard_map/ppermute | solution.py:103
  74.9 2.5 %collective-permute-start.14 = (f32[16,4,256]{2,1,0:T(4,128)S(1)}, f32[16,4,256]{2,1,0:T(4,128)S(1)}, u32[]{:S(2)}, u32[]{:S(2)}) collective-permute-start(f32[16,4,256]{2,1,0:T(4,128)S(1)} %get-tuple-element.75), channel_id=1, source_target_pairs={{2,4},{4,2},{3,5},{5,3},{10,12},{12,10},{11,13},{13,11},{18,20},{2... | collective-permute-start | bytes 196616 | tf_op jit(solution)/shard_map/ppermute | solution.py:104
  77.5 6.8 %collective-permute-start.15 = (f32[4,24,256]{2,1,0:T(8,128)S(1)}, f32[4,24,256]{2,1,0:T(8,128)S(1)}, u32[]{:S(2)}, u32[]{:S(2)}) collective-permute-start(f32[4,24,256]{2,1,0:T(8,128)S(1)} %get-tuple-element.76), channel_id=1, source_target_pairs={{0,1},{1,0},{8,9},{9,8},{16,17},{17,16},{24,25},{25,24},{2,3},{3,2... | collective-permute-start | bytes 294920 | tf_op jit(solution)/shard_map/ppermute | solution.py:103
  83.3 0.9 collective-permute-start.16
  90.2 8.0 %collective-permute-start.17 = (f32[2,16,128]{2,1,0:T(8,128)S(1)}, f32[2,16,128]{2,1,0:T(8,128)S(1)}, u32[]{:S(2)}, u32[]{:S(2)}) collective-permute-start(f32[2,16,128]{2,1,0:T(8,128)S(1)} %stack.52), channel_id=1, source_target_pairs={{0,1},{1,0},{2,3},{3,2},{4,5},{5,4},{6,7},{7,6},{8,9},{9,8},{10,11... | collective-permute-start | bytes 49160 | tf_op jit(solution)/shard_map/ppermute | solution.py:549
  98.2 5.2 %collective-permute-start.18 = (f32[2,16,128]{2,1,0:T(8,128)S(1)}, f32[2,16,128]{2,1,0:T(8,128)S(1)}, u32[]{:S(2)}, u32[]{:S(2)}) collective-permute-start(f32[2,16,128]{2,1,0:T(8,128)S(1)} %pad_maximum_fusion), channel_id=1, source_target_pairs={{0,8},{8,0},{16,24},{24,16},{1,9},{9,1},{17,25},{25,17},{2,10},{10... | collective-permute-start | bytes 49160 | tf_op jit(solution)/shard_map/ppermute | solution.py:549
  103.4 4.4 %collective-permute-start.19 = (f32[2,16,128]{2,1,0:T(8,128)S(1)}, f32[2,16,128]{2,1,0:T(8,128)S(1)}, u32[]{:S(2)}, u32[]{:S(2)}) collective-permute-start(f32[2,16,128]{2,1,0:T(8,128)S(1)} %pad_maximum_fusion.1), channel_id=1, source_target_pairs={{0,16},{8,24},{16,0},{24,8},{1,17},{9,25},{17,1},{25,9},{2,18},{10... | collective-permute-start | bytes 49160 | tf_op jit(solution)/shard_map/ppermute | solution.py:549
  107.8 5.7 %collective-permute-start.20 = (f32[2,16,128]{2,1,0:T(8,128)S(1)}, f32[2,16,128]{2,1,0:T(8,128)S(1)}, u32[]{:S(2)}, u32[]{:S(2)}) collective-permute-start(f32[2,16,128]{2,1,0:T(8,128)S(1)} %pad_maximum_fusion.2), channel_id=1, source_target_pairs={{0,2},{2,0},{4,6},{6,4},{1,3},{3,1},{5,7},{7,5},{8,10},{10,8},{12,... | collective-permute-start | bytes 49160 | tf_op jit(solution)/shard_map/ppermute | solution.py:549
  113.5 4.7 %collective-permute-start.21 = (f32[2,16,128]{2,1,0:T(8,128)S(1)}, f32[2,16,128]{2,1,0:T(8,128)S(1)}, u32[]{:S(2)}, u32[]{:S(2)}) collective-permute-start(f32[2,16,128]{2,1,0:T(8,128)S(1)} %pad_maximum_fusion.3), channel_id=1, source_target_pairs={{0,4},{2,6},{4,0},{6,2},{1,5},{3,7},{5,1},{7,3},{8,12},{10,14},{12... | collective-permute-start | bytes 49160 | tf_op jit(solution)/shard_map/ppermute | solution.py:549
  115.3 2.9 %collective-permute-start.22 = (f32[16,16,128]{2,1,0:T(8,128)S(1)}, f32[16,16,128]{2,1,0:T(8,128)S(1)}, u32[]{:S(2)}, u32[]{:S(2)}) collective-permute-start(f32[16,16,128]{2,1,0:T(8,128)S(1)} %get-tuple-element.63.refs_11_), channel_id=1, source_target_pairs={{0,1},{1,0},{2,3},{3,2},{4,5},{5,4},{6,7},{7,6},{8,9},{9,8},{10,11... | collective-permute-start | bytes 393224 | tf_op jit(solution)/shard_map/ppermute | solution.py:109
  115.3 2.9 %collective-permute-start.23 = (f32[16,16,128]{2,1,0:T(8,128)S(1)}, f32[16,16,128]{2,1,0:T(8,128)S(1)}, u32[]{:S(2)}, u32[]{:S(2)}) collective-permute-start(f32[16,16,128]{2,1,0:T(8,128)S(1)} %get-tuple-element.71.refs_13_), channel_id=1, source_target_pairs={{0,1},{1,0},{2,3},{3,2},{4,5},{5,4},{6,7},{7,6},{8,9},{9,8},{10,11... | collective-permute-start | bytes 393224 | tf_op jit(solution)/shard_map/ppermute | solution.py:109
  115.8 2.4 %collective-permute-start.24 = (f32[16,16,128]{2,1,0:T(8,128)S(1)}, f32[16,16,128]{2,1,0:T(8,128)S(1)}, u32[]{:S(2)}, u32[]{:S(2)}) collective-permute-start(f32[16,16,128]{2,1,0:T(8,128)S(1)} %get-tuple-element.81), channel_id=1, source_target_pairs={{0,1},{1,0},{2,3},{3,2},{4,5},{5,4},{6,7},{7,6},{8,9},{9,8},{10,11... | collective-permute-start | bytes 393224 | tf_op jit(solution)/shard_map/ppermute | solution.py:109
  115.8 2.4 %collective-permute-start.25 = (f32[16,16,128]{2,1,0:T(8,128)S(1)}, f32[16,16,128]{2,1,0:T(8,128)S(1)}, u32[]{:S(2)}, u32[]{:S(2)}) collective-permute-start(f32[16,16,128]{2,1,0:T(8,128)S(1)} %get-tuple-element.83), channel_id=1, source_target_pairs={{0,1},{1,0},{2,3},{3,2},{4,5},{5,4},{6,7},{7,6},{8,9},{9,8},{10,11... | collective-permute-start | bytes 393224 | tf_op jit(solution)/shard_map/ppermute | solution.py:109

commit v2 on v1

--- a/solution.py
+++ b/solution.py
@@ -205,42 +205,75 @@
             send[k, ys + h :, :] = jnp.where(odd_y, a, b)
 
 
-def sweep(source, target, b, w, kx, ky, kz, start, stop):
+class Rows:
+    def __init__(self, early, late, first, end):
+        self.early, self.late, self.first, self.end = early, late, first, end
+
+    def __getitem__(self, index):
+        r = index[-1] if isinstance(index, tuple) else index
+        mine = not isinstance(r, int) or not self.first <= r < self.end
+        return (self.late if mine else self.early)[index]
+
+
+def spans(lo, hi, total):
+    full = [(s, total - 1 - s) for s in range(SWEEPS)] + [(HALO, total - HALO)]
+    inner = [(lo + s, hi - s) for s in range(SWEEPS)] + [(lo + SWEEPS, hi - SWEEPS + 1)]
+    inner = [i if i[0] < i[1] else (f[0], f[0]) for f, i in zip(full, inner)]
+    return full, inner
+
+
+def outside(full, inner):
+    return list(range(full[0], inner[0])) + list(range(inner[1], full[1]))
+
+
+def update(source, b, w, kx, ky, kz, target, r):
     keep = 1.0 - OMEGA
-
-    def one(r):
-        here_x, past_x, here_y, here_z = kx[r], kx[r - 1], ky[r], kz[r]
-        for c in range(3):
-            u = source[c, r]
-            near = here_x * source[c, r + 1] + past_x * source[c, r - 1]
-            near = near + here_y * up_y(u) + down_y(here_y * u)
-            near = near + here_z * up_z(u) + down_z(here_z * u)
-            target[c, r] = keep * u + (b[c, r] + w[c, r] * near)
-
-    rows_loop(start, stop, one)
-
-
-def solve_and_diverge(b, one_buf, two_buf, w, kx, ky, kz, emit):
-    total = b.shape[1]
-    source, target = b, one_buf
+    here_x, past_x, here_y, here_z = kx[r], kx[r - 1], ky[r], kz[r]
+    for c in range(3):
+        u = source[c, r]
+        near = here_x * source[c, r + 1] + past_x * source[c, r - 1]
+        near = near + here_y * up_y(u) + down_y(here_y * u)
+        near = near + here_z * up_z(u) + down_z(here_z * u)
+        target[c, r] = keep * u + (b[c, r] + w[c, r] * near)
+
+
+def diverge(v, r):
+    vy, vz = v[1, r], v[2, r]
+    lane = lax.broadcasted_iota(jnp.int32, vz.shape, 1)
+    out = v[0, r - 1] - v[0, r]
+    out = out + (down_y(vy) - vy)
+    return out + (jnp.where(lane == 0, 0.0, down_z(vz)) - vz)
+
+
+def inner_solve(b, levels, out, inner, w, kx, ky, kz):
+    source = b
     for s in range(1, SWEEPS):
-        sweep(source, target, b, w, kx, ky, kz, s, total - 1 - s)
-        source, target = target, (two_buf if s % 2 == 1 else one_buf)
-    v = source
-    h = SWEEPS
-
-    def one(r):
-        vy, vz = v[1, r], v[2, r]
-        lane = lax.broadcasted_iota(jnp.int32, vz.shape, 1)
-        out = v[0, r - 1] - v[0, r]
-        out = out + (down_y(vy) - vy)
-        out = out + (jnp.where(lane == 0, 0.0, down_z(vz)) - vz)
-        emit(r - h, out)
-
-    rows_loop(h, total - h, one, 2)
-
-
-def emit_result(v_own, v_others, p_out, send_a, send_b, eta_at, sums):
+        target = levels[s - 1]
+
+        def one(r, source=source, target=target):
+            update(source, b, w, kx, ky, kz, target, r)
+
+        rows_loop(*inner[s], one)
+        source = target
+
+    def last(r):
+        out[r - HALO] = diverge(source, r)
+
+    rows_loop(*inner[SWEEPS], last, 2)
+
+
+def outer_solve(b, levels, buffers, inner, full, w, kx, ky, kz, emit):
+    source = b
+    for s in range(1, SWEEPS):
+        target = buffers[s - 1]
+        for r in outside(full[s], inner[s]):
+            update(source, b, w, kx, ky, kz, target, r)
+        source = Rows(levels[s - 1], target, *inner[s])
+    for r in outside(full[SWEEPS], inner[SWEEPS]):
+        emit(r - HALO, diverge(source, r))
+
+
+def emit_result(v_own, v_others, p_out, send_a, send_b, eta_at, sums=None):
     n = 1 + len(v_others)
     core = lax.axis_index("gz")
     odd = lax.rem(lax.axis_index("gy"), 2) == 1
@@ -253,57 +286,129 @@
         v_own[r] = parts[0]
         for ref, part in zip(v_others, parts[1:]):
             ref[r] = part
-        p = eta_at(r) * out
         if p_out is not None:
+            p = eta_at(r) * out
             p_out[r] = p
             low, high = p[:h], p[ys - h :]
             send_a[r] = jnp.where(odd, low, high)
             send_b[r] = jnp.where(odd, high, low)
-        sums(r, out, p)
+        if sums is not None:
+            sums(r, out)
 
     return emit
 
 
-def fold(acc, moment, index):
-    value = acc[index]
+def fold(value):
     total = value[:8]
     for k in range(1, value.shape[0] // 8):
         total = total + value[8 * k : 8 * k + 8]
     lanes = total[:, :LANES]
     for t in range(1, total.shape[1] // LANES):
         lanes = lanes + total[:, t * LANES : (t + 1) * LANES]
-    moment[index] = lanes
-
-
-def first_kernel(n, sizes, *refs):
-    full, ya, yb, xa, xb, flags = refs[:6]
-    v_own, *rest = refs[6:]
-    v_others, rest = rest[: n - 1], rest[n - 1 :]
-    p_out, send_a, send_b, moment, kx, ky, kz, w = rest[:8]
-    force, eta, line, b, one_buf, two_buf, acc = rest[8:]
+    return lanes
+
+
+def odd_places():
+    place = lax.axis_index("gx") * lax.axis_size("gz") + lax.axis_index("gz")
+    return lax.rem(lax.axis_index("gy"), 2) == 1, lax.rem(place, 2) == 1, place
+
+
+def set_row(ref, index, row, a, b, odd_y):
+    ys, h = row.shape[0], a.shape[0]
+    ref[(*index, slice(0, ys), slice(None))] = row
+    ref[(*index, slice(ys, ys + h), slice(None))] = jnp.where(odd_y, b, a)
+    ref[(*index, slice(ys + h, ys + 2 * h), slice(None))] = jnp.where(odd_y, a, b)
+
+
+def coefs_at(sizes, place, slots, lanes, rows, ys, flags):
+    h = HALO
+    slot = lax.broadcasted_iota(jnp.int32, (slots, lanes), 0)
+    at_y = lax.axis_index("gy") * ys + slot - jnp.where(slot >= ys + h, slots, 0)
+    at_z = lax.broadcasted_iota(jnp.int32, (slots, lanes), 1)
+    in_y = (at_y >= 0) & (at_y < sizes[1])
+    y_up, y_low = at_y + 1 < sizes[1], at_y >= 1
+    z_up, z_low = at_z + 1 < sizes[2], at_z >= 1
+    wall = [jnp.where(flags[k] == 0, 1.0, 0.0).astype(F32) for k in range(6)]
+
+    def coefs(r, mid, before, after, line, force_at, kx, ky, kz, w, b):
+        at_x = place * rows - h + r
+        x_up = jnp.full(mid.shape, at_x + 1, jnp.int32) < sizes[0]
+        x_low = jnp.full(mid.shape, at_x, jnp.int32) >= 1
+        inside = in_y & jnp.broadcast_to((at_x >= 0) & (at_x < sizes[0]), mid.shape)
+        y_before = jnp.where(slot == ys + h, line, down_y(mid))
+        sides = (
+            (x_up, after, x_low, before),
+            (y_up, up_y(mid), y_low, y_before),
+            (z_up, up_z(mid), z_low, down_z(mid)),
+        )
+        diag = [jnp.zeros_like(mid) for _ in range(3)]
+        for axis, (up_in, up, low_in, low) in enumerate(sides):
+            up, low = 0.5 * (mid + up), 0.5 * (mid + low)
+            (kx, ky, kz)[axis][r] = jnp.where(up_in, up, 0.0)
+            for c in range(3):
+                low_wall = 1.0 if c == axis else wall[2 * axis]
+                up_wall = 1.0 if c == axis else wall[2 * axis + 1]
+                diag[c] = diag[c] + jnp.where(up_in, up, up_wall * mid)
+                diag[c] = diag[c] + jnp.where(low_in, low, low_wall * mid)
+        for c in range(3):
+            weight = jnp.where(inside, OMEGA / diag[c], 0.0)
+            w[c, r] = weight
+            b[c, r] = weight * force_at(c)
+
+    return coefs
+
+
+def first_inner(sizes, full, ya, yb, flags, kx, ky, kz, w, b, *rest):
+    levels, (out, force, eta, line) = rest[: SWEEPS - 1], rest[SWEEPS - 1 :]
     fields, rows, ys, lanes = full.shape
     h = HALO
-    odd_y = lax.rem(lax.axis_index("gy"), 2) == 1
-    place = lax.axis_index("gx") * lax.axis_size("gz") + lax.axis_index("gz")
-    odd_x = lax.rem(place, 2) == 1
-    slots = ys + 2 * h
-    total = rows + 2 * h
-
-    def set_row(ref, index, row, a, b_):
-        ref[(*index, slice(0, ys), slice(None))] = row
-        ref[(*index, slice(ys, ys + h), slice(None))] = jnp.where(odd_y, b_, a)
-        ref[(*index, slice(ys + h, slots), slice(None))] = jnp.where(odd_y, a, b_)
-
+    odd_y, _, place = odd_places()
+    slots, total = ys + 2 * h, rows + 2 * h
     for c in range(fields):
 
         def one(r, c=c):
             row, a, b_ = full[c, r], ya[c * rows + r], yb[c * rows + r]
             if c < 3:
-                set_row(force, (c, r + h), row, a, b_)
+                set_row(force, (c, r + h), row, a, b_, odd_y)
             else:
-                set_row(eta, (r + h + 1,), row, a, b_)
+                set_row(eta, (r + h,), row, a, b_, odd_y)
 
         rows_loop(0, rows, one, 4)
+    for q in range(rows // 4):
+        block = jnp.where(odd_y, ya[fields * rows + q], yb[fields * rows + q])
+        for k in range(4):
+            line[h + 4 * q + k] = block[k : k + 1]
+    coefs = coefs_at(sizes, place, slots, lanes, rows, ys, flags)
+
+    def at(r):
+        coefs(r, eta[r], eta[r - 1], eta[r + 1], line[r], lambda c: force[c, r], kx, ky, kz, w, b)
+
+    _, inner = spans(h + 1, h + rows - 1, total)
+    rows_loop(*inner[0], at, 1)
+    inner_solve(b, levels, out, inner, w, kx, ky, kz)
+
+
+def first_outer(n, sizes, *refs):
+    full, ya, yb, xa, xb, flags, *early = refs[: 11 + SWEEPS]
+    kx0, ky0, kz0, w0, b0, *levels, out0 = early
+    refs = refs[11 + SWEEPS :]
+    v_own, v_others, refs = refs[0], refs[1:n], refs[n:]
+    p_out, send_a, send_b, kx, ky, kz, w = refs[:7]
+    force, eta, line, b, *buffers = refs[7:]
+    fields, rows, ys, lanes = full.shape
+    h = HALO
+    odd_y, odd_x, place = odd_places()
+    slots, total = ys + 2 * h, rows + 2 * h
+    ranges, inner = spans(h + 1, h + rows - 1, total)
+    todo = outside((0, total), inner[0])
+    for r in sorted({min(max(q + d, h), h + rows - 1) for q in todo for d in (-1, 0, 1)}):
+        k = r - h
+        for c in range(3):
+            set_row(force, (c, r), full[c, k], ya[c * rows + k], yb[c * rows + k], odd_y)
+        set_row(eta, (r + 1,), full[3, k], ya[3 * rows + k], yb[3 * rows + k], odd_y)
+        block = fields * rows + k // 4
+        line[r] = jnp.where(odd_y, ya[block], yb[block])[k % 4 : k % 4 + 1]
+    for c in range(fields):
         for k in range(h):
             t = 3 * (c * h + k)
             for q in range(3):
@@ -324,114 +429,98 @@
     for k in range(h):
         line[k] = lower[k : k + 1]
         line[h + rows + k] = upper[k : k + 1]
-    for q in range(rows // 4):
-        block = jnp.where(odd_y, ya[fields * rows + q], yb[fields * rows + q])
-        for k in range(4):
-            line[h + 4 * q + k] = block[k : k + 1]
-
-    first_x = place * rows - h
-    first_y = lax.axis_index("gy") * ys
-    slot = lax.broadcasted_iota(jnp.int32, (slots, lanes), 0)
-    at_y = first_y + slot - jnp.where(slot >= ys + h, slots, 0)
-    at_z = lax.broadcasted_iota(jnp.int32, (slots, lanes), 1)
-    in_y = (at_y >= 0) & (at_y < sizes[1])
-    y_up, y_low = at_y + 1 < sizes[1], at_y >= 1
-    z_up, z_low = at_z + 1 < sizes[2], at_z >= 1
-    wall = [jnp.where(flags[k] == 0, 1.0, 0.0).astype(F32) for k in range(6)]
-
-    def coefs(r):
-        mid, before, after = eta[r + 1], eta[r], eta[jnp.minimum(r + 2, total)]
-        at_x = first_x + r
-        x_up = jnp.full(mid.shape, at_x + 1, jnp.int32) < sizes[0]
-        x_low = jnp.full(mid.shape, at_x, jnp.int32) >= 1
-        inside = in_y & jnp.broadcast_to((at_x >= 0) & (at_x < sizes[0]), mid.shape)
-        y_before = jnp.where(slot == ys + h, line[r], down_y(mid))
-        sides = (
-            (x_up, after, x_low, before),
-            (y_up, up_y(mid), y_low, y_before),
-            (z_up, up_z(mid), z_low, down_z(mid)),
-        )
-        diag = [jnp.zeros_like(mid) for _ in range(3)]
-        for axis, (up_in, up, low_in, low) in enumerate(sides):
-            up, low = 0.5 * (mid + up), 0.5 * (mid + low)
-            (kx, ky, kz)[axis][r] = jnp.where(up_in, up, 0.0)
-            for c in range(3):
-                low_wall = 1.0 if c == axis else wall[2 * axis]
-                up_wall = 1.0 if c == axis else wall[2 * axis + 1]
-                diag[c] = diag[c] + jnp.where(up_in, up, up_wall * mid)
-                diag[c] = diag[c] + jnp.where(low_in, low, low_wall * mid)
+    coefs = coefs_at(sizes, place, slots, lanes, rows, ys, flags)
+    for r in todo:
+        after = eta[min(r + 2, total)]
+        coefs(r, eta[r + 1], eta[r], after, line[r], lambda c: force[c, r], kx, ky, kz, w, b)
+
+    def carry(r):
+        kx[r], ky[r], kz[r] = kx0[r], ky0[r], kz0[r]
         for c in range(3):
-            weight = jnp.where(inside, OMEGA / diag[c], 0.0)
-            w[c, r] = weight
-            b[c, r] = weight * force[c, r]
-
-    rows_loop(0, total, coefs, 1)
-    acc[...] = jnp.zeros_like(acc)
-
-    def sums(r, v, p):
-        acc[0] = acc[0] + v * p
-        acc[1] = acc[1] + v * v
-
-    emit = emit_result(v_own, v_others, p_out, send_a, send_b, lambda r: full[3, r], sums)
-    solve_and_diverge(b, one_buf, two_buf, w, kx, ky, kz, emit)
-    for k in range(2):
-        fold(acc, moment, k)
-
-
-def next_kernel(n, step, *refs):
-    p_in, ya, yb, xa, xb, full, kx, ky, kz, w = refs[:10]
-    refs = refs[10:]
-    earlier = [refs[k * n : (k + 1) * n] for k in range(step if step < ITERS else 0)]
-    refs = refs[len(earlier) * n :]
+            w[c, r] = w0[c, r]
+
+    rows_loop(*inner[0], carry, 2)
+    b = Rows(b0, b, *inner[0])
+    emit = emit_result(v_own, v_others, p_out, send_a, send_b, lambda r: full[3, r])
+    outer_solve(b, levels, buffers, inner, ranges, w, kx, ky, kz, emit)
+    rows_loop(inner[SWEEPS][0] - h, inner[SWEEPS][1] - h, lambda r: emit(r, out0[r]), 4)
+
+
+def next_inner(p_in, ya, yb, kx, ky, kz, w, p, b, *rest):
+    levels, out = rest[: SWEEPS - 1], rest[SWEEPS - 1]
+    rows = p_in.shape[0]
+    h = HALO
+    odd_y, _, _ = odd_places()
+
+    def fill(r):
+        set_row(p, (r + h,), p_in[r], ya[r], yb[r], odd_y)
+
+    rows_loop(0, rows, fill, 4)
+    _, inner = spans(h, h + rows - 1, rows + 2 * h)
+    rows_loop(*inner[0], lambda r: grads(p, w, b, r), 2)
+    inner_solve(b, levels, out, inner, w, kx, ky, kz)
+
+
+def grads(p, w, b, r):
+    mid = p[r]
+    lanes = mid.shape[1]
+    lane = lax.broadcasted_iota(jnp.int32, mid.shape, 1)
+    b[0, r] = w[0, r] * (p[r + 1] - mid)
+    b[1, r] = w[1, r] * (up_y(mid) - mid)
+    b[2, r] = w[2, r] * (jnp.where(lane == lanes - 1, 0.0, up_z(mid)) - mid)
+
+
+def next_outer(n, last, p_in, xa, xb, full, kx, ky, kz, w, p0, b0, *refs):
+    levels, out0, refs = refs[: SWEEPS - 1], refs[SWEEPS - 1], refs[SWEEPS:]
     v_own, v_others, refs = refs[0], refs[1:n], refs[n:]
-    if step < ITERS:
-        p_out, send_a, send_b, refs = refs[0], refs[1], refs[2], refs[3:]
+    p_out = send_a = send_b = sums = None
+    if last:
+        moment, refs = refs[0], refs[1:]
+        acc, refs = refs[-1], refs[:-1]
+        acc[...] = jnp.zeros_like(acc)
+
+        def sums(r, v):
+            acc[...] = acc[...] + v * p_in[r]
     else:
-        p_out = send_a = send_b = None
-    moment, p, b, one_buf, two_buf, acc = refs
-    rows, ys, lanes = p_in.shape
-    h = HALO
-    core = lax.axis_index("gz")
-    odd_y = lax.rem(lax.axis_index("gy"), 2) == 1
-    place = lax.axis_index("gx") * lax.axis_size("gz") + lax.axis_index("gz")
-    odd_x = lax.rem(place, 2) == 1
-    total = rows + 2 * h
-    slots = ys + 2 * h
-
-    def fill(r):
-        a, b_ = ya[r], yb[r]
-        p[r + h, :ys, :] = p_in[r]
-        p[r + h, ys : ys + h, :] = jnp.where(odd_y, b_, a)
-        p[r + h, ys + h :, :] = jnp.where(odd_y, a, b_)
-
-    rows_loop(0, rows, fill, 4)
+        p_out, send_a, send_b, *refs = refs
+    p, b, *buffers = refs
+    rows = p_in.shape[0]
+    h = HALO
+    _, odd_x, _ = odd_places()
     for k in range(h):
         a, b_ = xa[k], xb[k]
         p[k] = jnp.where(odd_x, a, b_)
         p[h + rows + k] = jnp.where(odd_x, b_, a)
-
-    def grads(r):
-        mid = p[r]
-        lane = lax.broadcasted_iota(jnp.int32, mid.shape, 1)
-        b[0, r] = w[0, r] * (p[r + 1] - mid)
-        b[1, r] = w[1, r] * (up_y(mid) - mid)
-        b[2, r] = w[2, r] * (jnp.where(lane == lanes - 1, 0.0, up_z(mid)) - mid)
-
-    rows_loop(0, total - 1, grads, 2)
+    ranges, inner = spans(h, h + rows - 1, rows + 2 * h)
+    p = Rows(p0, p, h, h + rows)
+    for r in outside(ranges[0], inner[0]):
+        grads(p, w, b, r)
+    b = Rows(b0, b, *inner[0])
+    emit = emit_result(v_own, v_others, p_out, send_a, send_b, lambda r: full[3, r], sums)
+    outer_solve(b, levels, buffers, inner, ranges, w, kx, ky, kz, emit)
+    rows_loop(inner[SWEEPS][0] - h, inner[SWEEPS][1] - h, lambda r: emit(r, out0[r]), 4)
+    if last:
+        moment[0] = fold(acc[...])
+
+
+def moments_kernel(n, step, *refs):
+    moment, acc = refs[-2:]
+    p, refs = refs[0], refs[1:-2]
+    before, refs = (refs[0], refs[1:]) if step else (None, refs)
+    groups = [refs[k * n : (k + 1) * n] for k in range(step + 1)]
+    core = lax.axis_index("gz")
     acc[...] = jnp.zeros_like(acc)
 
-    def sums(r, v, pv):
-        acc[0] = acc[0] + v * p_in[r]
-        if step < ITERS:
-            acc[1] = acc[1] + v * pv
-            acc[2] = acc[2] + v * v
-            for k, parts in enumerate(earlier):
-                acc[3 + k] = acc[3 + k] + v * join_own([q[r] for q in parts], core)
-
-    emit = emit_result(v_own, v_others, p_out, send_a, send_b, lambda r: full[3, r], sums)
-    solve_and_diverge(b, one_buf, two_buf, w, kx, ky, kz, emit)
+    def one(r):
+        v = join_own([q[r] for q in groups[-1]], core)
+        others = ([before[r]] if step else []) + [p[r], v]
+        others += [join_own([q[r] for q in group], core) for group in groups[:-1]]
+        for k, other in enumerate(others):
+            acc[k] = acc[k] + v * other
+
+    rows_loop(0, p.shape[0], one, 4)
     for k in range(acc.shape[0]):
-        fold(acc, moment, k)
+        moment[k] = fold(acc[k])
 
 
 def two_sum(a, b):
@@ -586,54 +675,75 @@
 
     v_shape = [sds(rows, ys, lanes)] * nz
     sent = [sds(rows, ys, zs), sds(rows, h, zs), sds(rows, h, zs)]
+    scalar, vector = sds(total, slots, zs), sds(3, total, slots, zs)
     field = pltpu.VMEM((3, total, slots, zs), F32)
-    coefs = [sds(total, slots, zs)] * 3 + [sds(3, total, slots, zs)]
+    line = pltpu.VMEM((total, 1, zs), F32)
+    heavy = 4 * 10**7
+    early = call(
+        functools.partial(first_inner, sizes),
+        [scalar] * 3 + [vector] * (1 + SWEEPS) + [sds(rows, slots, zs)],
+        (full, ya, yb, flags),
+        [VMEM] * 3 + [SMEM],
+        [field, pltpu.VMEM((total, slots, zs), F32), line],
+        heavy,
+        "first_inner",
+    )
     outs = call(
-        functools.partial(first_kernel, nz, sizes),
-        v_shape + sent + [sds(2, 8, LANES)] + coefs,
-        (full, ya, yb, xa, xb, flags),
-        [VMEM] * 5 + [SMEM],
-        [
-            field,
-            pltpu.VMEM((total + 1, slots, zs), F32),
-            pltpu.VMEM((total, 1, zs), F32),
-            field,
-            field,
-            field,
-            pltpu.VMEM((2, ys, zs), F32),
-        ],
-        name="first",
+        functools.partial(first_outer, nz, sizes),
+        v_shape + sent + [scalar] * 3 + [vector],
+        (full, ya, yb, xa, xb, flags, *early),
+        [VMEM] * 5 + [SMEM] + [VMEM] * len(early),
+        [field, pltpu.VMEM((total + 1, slots, zs), F32), line] + [field] * SWEEPS,
+        heavy,
+        "first",
     )
-    vs = [list(outs[:nz])]
-    p, ya, yb, moment = outs[nz : nz + 4]
-    coefs = outs[nz + 4 :]
-    moments = [moment]
+    vs, ps, moments = [list(outs[:nz])], [outs[nz]], []
+    ya, yb = outs[nz + 1 : nz + 3]
+    coefs = outs[nz + 3 :]
     for step in range(1, ITERS + 1):
+        last = step == ITERS
+        p = ps[-1]
+        count = 2 if step == 1 else 2 + step
+        moments.append(
+            call(
+                functools.partial(moments_kernel, nz, step - 1),
+                [sds(count, 8, LANES)],
+                (p, *ps[:-1][-1:], *[q for v in vs for q in v]),
+                None,
+                [pltpu.VMEM((count, ys, zs), F32)],
+                name="moments",
+            )[0]
+        )
         ya, yb = exchange("gy", ny, ya, yb)
         edge = sds(h, slots, zs)
         xa, xb = call(edges_kernel, [edge, edge], (p, ya, yb), name="edges")
         xa, xb = exchange(("gx", "gz"), chain, xa, xb)
-        more = step < ITERS
-        earlier = [q for v in vs for q in v] if more else []
-        count = 3 + step if more else 1
+        early = call(
+            next_inner,
+            [scalar] + [vector] * SWEEPS + [sds(rows, slots, zs)],
+            (p, ya, yb, *coefs),
+            None,
+            (),
+            heavy,
+            "next_inner",
+        )
         outs = call(
-            functools.partial(next_kernel, nz, step),
-            v_shape + (sent if more else []) + [sds(count, 8, LANES)],
-            (p, ya, yb, xa, xb, full, *coefs, *earlier),
+            functools.partial(next_outer, nz, last),
+            v_shape + ([sds(1, 8, LANES)] if last else sent),
+            (p, xa, xb, full, *coefs, *early),
             None,
-            [
-                pltpu.VMEM((total, slots, zs), F32),
-                field,
-                field,
-                field,
-                pltpu.VMEM((count, ys, zs), F32),
-            ],
-            name="next",
+            [pltpu.VMEM((total, slots, zs), F32)]
+            + [field] * SWEEPS
+            + ([pltpu.VMEM((ys, zs), F32)] if last else []),
+            heavy,
+            "next",
         )
         vs.append(list(outs[:nz]))
-        if more:
-            p, ya, yb = outs[nz : nz + 3]
-        moments.append(outs[-1])
+        if last:
+            moments.append(outs[nz])
+        else:
+            ps.append(outs[nz])
+            ya, yb = outs[nz + 1 : nz + 3]
 
     placed = [[v[0]] + [core_shift(v[j], nz, j) for j in range(1, nz)] for v in vs]
     flat = call(sums_kernel, sds(16, LANES), moments, name="sums")

time: 121 us -> 102 us (0.84)
  starting transfers between devices: 64.2 us -> 50.8 us
  waiting for transfers between devices: 23.3 us -> 20.1 us
  Pallas kernels: 29.1 us -> 26 us
    ppermute x8, starting transfers between devices: 38.2 us -> 28.9 us  [exchange(): lax.ppermute(a, axis, pair_perm(n, 0))]
    ppermute x5, starting transfers between devices: 19.1 us -> 14.8 us  [reduce_all(): other = lax.ppermute(pair, axis, [(i, i ^ step) for i in range(n)])]
    pallas_call x12 -> x19, Pallas kernels: 29.1 us -> 26 us  [call(): pl.pallas_call(kernel, out_shape=outs, in_specs=specs or [VMEM] * len(ins...]
    ppermute x8, waiting for transfers between devices: 13.9 us -> 11.1 us  [exchange(): lax.ppermute(a, axis, pair_perm(n, 0))]
  transfers between devices with their start and end apart: 26 -> 26, of which waited for: 14 -> 12; matrix products, arithmetic and copies ran while one was open for 0% -> 0% of each run, Pallas kernels for 0% -> 16%
where the time goes in v2:
time: 102 us; the launch traced here: 101 us
  starting transfers between devices  50.8 us (50%)
  Pallas kernels  26 us (25%)
  waiting for transfers between devices  20.1 us (20%)
  local copies, waits for them, and re-layouts  3.36 us (3%)
    ppermute x8, starting transfers between devices, exchange(): lax.ppermute(a, axis, pair_perm(n, 0))  28.9 us
    pallas_call x19, Pallas kernels, call(): pl.pallas_call(kernel, out_shape=outs, in_specs=specs or [VMEM] * len(ins...  26 us
    ppermute x5, starting transfers between devices, reduce_all(): other = lax.ppermute(pair, axis, [(i, i ^ step) for i in range(n)])  14.8 us
    ppermute x8, waiting for transfers between devices, exchange(): lax.ppermute(a, axis, pair_perm(n, 0))  11.1 us
    ppermute x5, waiting for transfers between devices, reduce_all(): other = lax.ppermute(pair, axis, [(i, i ^ step) for i in range(n)])  7.17 us
    ppermute x8, starting transfers between devices, exchange(): lax.ppermute(b, axis, pair_perm(n, 1))  5.46 us
    unnamed x8, local copies, waits for them, and re-layouts  2.73 us
  transfers between devices with their start and end apart: 26, of which 12 were waited for; matrix products, arithmetic and copies ran while one was open for 0% of the time, Pallas kernels for 16%

profile of v2, /device:TPU:0, one launch (start us, length us, event | category | flops | bytes accessed | tf_op | source)
XLA Modules:
  0.0 101.2 jit_solution(16235627123994516699)
XLA Ops:
  0.6 1.1 %copy-done = f32[3,32,16,128]{3,2,1,0:T(8,128)S(1)} copy-done((f32[3,32,16,128]{3,2,1,0:T(8,128)S(1)}, f32[3,32,16,128]{3,2,1,0:T(8,128)}, u32[]{:S(2)}) %copy-start) | copy-done | bytes 786456
  1.8 0.9 copy-done.1
  4.8 1.5 %collective-permute-done.refs_1_ = f32[4,16,16,128]{3,2,1,0:T(8,128)S(1)} collective-permute-done((f32[4,16,16,128]{3,2,1,0:T(8,128)S(1)}, f32[4,16,16,128]{3,2,1,0:T(8,128)S(1)}, u32[]{:S(2)}, u32[]{:S(2)}) %collective-permute-start) | collective-permute-done | bytes 524320 | tf_op jit(solution)/shard_map/ppermute | solution.py:109
  6.5 3.0 %collective-permute-start.1 = (f32[68,4,256]{2,1,0:T(4,128)S(1)}, f32[68,4,256]{2,1,0:T(4,128)S(1)}, u32[]{:S(2)}, u32[]{:S(2)}) collective-permute-start(f32[68,4,256]{2,1,0:T(4,128)S(1)} %get-tuple-element.72), channel_id=1, source_target_pairs={{0,2},{2,0},{4,6},{6,4},{1,3},{3,1},{5,7},{7,5},{8,10},{10,8},{12,... | collective-permute-start | bytes 835592 | tf_op jit(solution)/shard_map/ppermute | solution.py:103
  10.2 6.3 %collective-permute-done.1.got_a.ya.refs_1_ = f32[68,4,256]{2,1,0:T(4,128)S(1)} collective-permute-done((f32[68,4,256]{2,1,0:T(4,128)S(1)}, f32[68,4,256]{2,1,0:T(4,128)S(1)}, u32[]{:S(2)}, u32[]{:S(2)}) %collective-permute-start.1) | collective-permute-done | bytes 278560 | tf_op jit(solution)/shard_map/ppermute | solution.py:103
  17.4 4.7 %first_inner.1 = (f32[24,24,256]{2,1,0:T(8,128)S(1)}, f32[24,24,256]{2,1,0:T(8,128)S(1)}, f32[24,24,256]{2,1,0:T(8,128)S(1)}, f32[3,24,24,256]{3,2,1,0:T(8,128)S...) custom-call(f32[4,16,16,256]{3,2,1,0:T(8,128)S(1)} %get-tuple-elemen, ...), custom_call_target="tpu_custom_call" | custom-call | flops 40000000 | bytes 1048576 | tf_op jit(solution)/shard_map/first_inner/pallas_call | solution.py:26
  22.1 2.9 %first.1 = (f32[16,16,128]{2,1,0:T(8,128)S(1)}, f32[16,16,128]{2,1,0:T(8,128)S(1)}, f32[16,16,256]{2,1,0:T(8,128)S(1)}, f32[16,4,256]{2,1,0:T(4,128)S(1)}, f32[1...) custom-call(f32[4,16,16,256]{3,2,1,0:T(8,128)S(1)} %get-tuple-elemen, ...), custom_call_target="tpu_custom_call" | custom-call | flops 40000000 | bytes 1048576 | tf_op jit(solution)/shard_map/first/pallas_call | solution.py:26
  24.9 4.8 %collective-permute-start.5 = (f32[16,4,256]{2,1,0:T(4,128)S(1)}, f32[16,4,256]{2,1,0:T(4,128)S(1)}, u32[]{:S(2)}, u32[]{:S(2)}) collective-permute-start(f32[16,4,256]{2,1,0:T(4,128)S(1)} %get-tuple-element.88), channel_id=1, source_target_pairs={{0,2},{2,0},{4,6},{6,4},{1,3},{3,1},{5,7},{7,5},{8,10},{10,8},{12,... | collective-permute-start | bytes 196616 | tf_op jit(solution)/shard_map/ppermute | solution.py:103
  30.4 1.6 %collective-permute-done.5.got_a.ya = f32[16,4,256]{2,1,0:T(4,128)S(1)} collective-permute-done((f32[16,4,256]{2,1,0:T(4,128)S(1)}, f32[16,4,256]{2,1,0:T(4,128)S(1)}, u32[]{:S(2)}, u32[]{:S(2)}) %collective-permute-start.5) | collective-permute-done | bytes 65568 | tf_op jit(solution)/shard_map/ppermute | solution.py:103
  32.0 8.2 %collective-permute-start.7 = (f32[4,24,256]{2,1,0:T(8,128)S(1)}, f32[4,24,256]{2,1,0:T(8,128)S(1)}, u32[]{:S(2)}, u32[]{:S(2)}) collective-permute-start(f32[4,24,256]{2,1,0:T(8,128)S(1)} %get-tuple-element.90), channel_id=1, source_target_pairs={{0,1},{1,0},{8,9},{9,8},{16,17},{17,16},{24,25},{25,24},{2,3},{3,2... | collective-permute-start | bytes 294920 | tf_op jit(solution)/shard_map/ppermute | solution.py:103
  40.9 3.6 %next_inner.3 = (f32[24,24,256]{2,1,0:T(8,128)S(1)}, f32[3,24,24,256]{3,2,1,0:T(8,128)S(1)}, f32[3,24,24,256]{3,2,1,0:T(8,128)S(1)}, f32[3,24,24,256]{3,2,1,0:T(...) custom-call(f32[16,16,256]{2,1,0:T(8,128)S(1)} %get-tuple-element.85.refs_0_.p.p_in.refs_1_, ...), custom_call_target="tpu_custom_call" | custom-call | flops 40000000 | bytes 1048576 | tf_op jit(solution)/shard_map/next_inner/pallas_call | solution.py:26
  44.5 1.4 %next.3 = (f32[16,16,128]{2,1,0:T(8,128)S(1)}, f32[16,16,128]{2,1,0:T(8,128)S(1)}, f32[16,16,256]{2,1,0:T(8,128)S(1)}, f32[16,4,256]{2,1,0:T(4,128)S(1)}, f32[16,4,256]{2,1,0:T(4,128)S(1)}) custom-call(f32[16,16,256]{2,1,0:T(8,128)S(1)} %get-tuple-element.85.refs_0_.p.p_in.refs_1_, f32[4,24,256]{2,1,0:T(8,128)S(1)} %collective-permute-done.7.xa, ...), custom_call_target="tpu_custom_call" | custom-call | flops 40000000 | bytes 1048576 | tf_op jit(solution)/shard_map/next/pallas_call | solution.py:26
  45.9 3.7 %collective-permute-start.9 = (f32[16,4,256]{2,1,0:T(4,128)S(1)}, f32[16,4,256]{2,1,0:T(4,128)S(1)}, u32[]{:S(2)}, u32[]{:S(2)}) collective-permute-start(f32[16,4,256]{2,1,0:T(4,128)S(1)} %get-tuple-element.105), channel_id=1, source_target_pairs={{0,2},{2,0},{4,6},{6,4},{1,3},{3,1},{5,7},{7,5},{8,10},{10,8},{12,... | collective-permute-start | bytes 196616 | tf_op jit(solution)/shard_map/ppermute | solution.py:103
  50.3 1.6 %collective-permute-done.9.got_a.ya = f32[16,4,256]{2,1,0:T(4,128)S(1)} collective-permute-done((f32[16,4,256]{2,1,0:T(4,128)S(1)}, f32[16,4,256]{2,1,0:T(4,128)S(1)}, u32[]{:S(2)}, u32[]{:S(2)}) %collective-permute-start.9) | collective-permute-done | bytes 65568 | tf_op jit(solution)/shard_map/ppermute | solution.py:103
  51.9 2.3 %collective-permute-start.11 = (f32[4,24,256]{2,1,0:T(8,128)S(1)}, f32[4,24,256]{2,1,0:T(8,128)S(1)}, u32[]{:S(2)}, u32[]{:S(2)}) collective-permute-start(f32[4,24,256]{2,1,0:T(8,128)S(1)} %get-tuple-element.107), channel_id=1, source_target_pairs={{0,1},{1,0},{8,9},{9,8},{16,17},{17,16},{24,25},{25,24},{2,3},{3,2... | collective-permute-start | bytes 294920 | tf_op jit(solution)/shard_map/ppermute | solution.py:103
  54.9 3.6 %next_inner.4 = (f32[24,24,256]{2,1,0:T(8,128)S(1)}, f32[3,24,24,256]{3,2,1,0:T(8,128)S(1)}, f32[3,24,24,256]{3,2,1,0:T(8,128)S(1)}, f32[3,24,24,256]{3,2,1,0:T(...) custom-call(f32[16,16,256]{2,1,0:T(8,128)S(1)} %get-tuple-element.102.refs_0_.p.p_in.refs_1_, ...), custom_call_target="tpu_custom_call" | custom-call | flops 40000000 | bytes 1048576 | tf_op jit(solution)/shard_map/next_inner/pallas_call | solution.py:26
  58.5 1.4 %next.4 = (f32[16,16,128]{2,1,0:T(8,128)S(1)}, f32[16,16,128]{2,1,0:T(8,128)S(1)}, f32[16,16,256]{2,1,0:T(8,128)S(1)}, f32[16,4,256]{2,1,0:T(4,128)S(1)}, f32[16,4,256]{2,1,0:T(4,128)S(1)}) custom-call(f32[16,16,256]{2,1,0:T(8,128)S(1)} %get-tuple-element.102.refs_0_.p.p_in.refs_1_, f32[4,24,256]{2,1,0:T(8,128)S(1)} %collective-permute-done.11.xa, ...), custom_call_target="tpu_custom_call" | custom-call | flops 40000000 | bytes 1048576 | tf_op jit(solution)/shard_map/next/pallas_call | solution.py:26
  60.0 3.7 %collective-permute-start.13 = (f32[16,4,256]{2,1,0:T(4,128)S(1)}, f32[16,4,256]{2,1,0:T(4,128)S(1)}, u32[]{:S(2)}, u32[]{:S(2)}) collective-permute-start(f32[16,4,256]{2,1,0:T(4,128)S(1)} %get-tuple-element.118), channel_id=1, source_target_pairs={{0,2},{2,0},{4,6},{6,4},{1,3},{3,1},{5,7},{7,5},{8,10},{10,8},{12,... | collective-permute-start | bytes 196616 | tf_op jit(solution)/shard_map/ppermute | solution.py:103
  64.3 1.6 %collective-permute-done.13.got_a.ya = f32[16,4,256]{2,1,0:T(4,128)S(1)} collective-permute-done((f32[16,4,256]{2,1,0:T(4,128)S(1)}, f32[16,4,256]{2,1,0:T(4,128)S(1)}, u32[]{:S(2)}, u32[]{:S(2)}) %collective-permute-start.13) | collective-permute-done | bytes 65568 | tf_op jit(solution)/shard_map/ppermute | solution.py:103
  65.9 3.0 %collective-permute-start.15 = (f32[4,24,256]{2,1,0:T(8,128)S(1)}, f32[4,24,256]{2,1,0:T(8,128)S(1)}, u32[]{:S(2)}, u32[]{:S(2)}) collective-permute-start(f32[4,24,256]{2,1,0:T(8,128)S(1)} %get-tuple-element.120), channel_id=1, source_target_pairs={{0,1},{1,0},{8,9},{9,8},{16,17},{17,16},{24,25},{25,24},{2,3},{3,2... | collective-permute-start | bytes 294920 | tf_op jit(solution)/shard_map/ppermute | solution.py:103
  70.2 3.6 %next_inner.5 = (f32[24,24,256]{2,1,0:T(8,128)S(1)}, f32[3,24,24,256]{3,2,1,0:T(8,128)S(1)}, f32[3,24,24,256]{3,2,1,0:T(8,128)S(1)}, f32[3,24,24,256]{3,2,1,0:T(...) custom-call(f32[16,16,256]{2,1,0:T(8,128)S(1)} %get-tuple-element.115.refs_0_.p.p_in, ...), custom_call_target="tpu_custom_call" | custom-call | flops 40000000 | bytes 1048576 | tf_op jit(solution)/shard_map/next_inner/pallas_call | solution.py:26
  73.8 1.4 %next.5 = (f32[16,16,128]{2,1,0:T(8,128)S(1)}, f32[16,16,128]{2,1,0:T(8,128)S(1)}, f32[1,8,128]{2,1,0:T(8,128)S(1)}) custom-call(f32[16,16,256]{2,1,0:T(8,128)S(1)} %get-tuple-element.115.refs_0_.p.p_in, f32[4,24,256]{2,1,0:T(8,128)S(1)} %collective-permute-done.15.xa, f32[4,24,256]{2,1,0:T(8,128)S(1)} %collective-permute-done.16.xb, ...), custom_call_target="tpu_custom_call" | custom-call | flops 40000000 | bytes 1048576 | tf_op jit(solution)/shard_map/next/pallas_call | solution.py:26
  75.3 3.8 %collective-permute-start.17 = (f32[2,16,128]{2,1,0:T(8,128)S(1)}, f32[2,16,128]{2,1,0:T(8,128)S(1)}, u32[]{:S(2)}, u32[]{:S(2)}) collective-permute-start(f32[2,16,128]{2,1,0:T(8,128)S(1)} %stack.52), channel_id=1, source_target_pairs={{0,1},{1,0},{2,3},{3,2},{4,5},{5,4},{6,7},{7,6},{8,9},{9,8},{10,11... | collective-permute-start | bytes 49160 | tf_op jit(solution)/shard_map/ppermute | solution.py:638
  79.1 0.8 collective-permute-done.17
  79.9 2.2 %collective-permute-start.18 = (f32[2,16,128]{2,1,0:T(8,128)S(1)}, f32[2,16,128]{2,1,0:T(8,128)S(1)}, u32[]{:S(2)}, u32[]{:S(2)}) collective-permute-start(f32[2,16,128]{2,1,0:T(8,128)S(1)} %pad_maximum_fusion), channel_id=1, source_target_pairs={{0,8},{8,0},{16,24},{24,16},{1,9},{9,1},{17,25},{25,17},{2,10},{10... | collective-permute-start | bytes 49160 | tf_op jit(solution)/shard_map/ppermute | solution.py:638
  82.1 1.7 %collective-permute-done.18 = f32[2,16,128]{2,1,0:T(8,128)S(1)} collective-permute-done((f32[2,16,128]{2,1,0:T(8,128)S(1)}, f32[2,16,128]{2,1,0:T(8,128)S(1)}, u32[]{:S(2)}, u32[]{:S(2)}) %collective-permute-start.18) | collective-permute-done | bytes 16416 | tf_op jit(solution)/shard_map/ppermute | solution.py:638
  83.8 1.6 %collective-permute-start.19 = (f32[2,16,128]{2,1,0:T(8,128)S(1)}, f32[2,16,128]{2,1,0:T(8,128)S(1)}, u32[]{:S(2)}, u32[]{:S(2)}) collective-permute-start(f32[2,16,128]{2,1,0:T(8,128)S(1)} %pad_maximum_fusion.1), channel_id=1, source_target_pairs={{0,16},{8,24},{16,0},{24,8},{1,17},{9,25},{17,1},{25,9},{2,18},{10... | collective-permute-start | bytes 49160 | tf_op jit(solution)/shard_map/ppermute | solution.py:638
  85.4 2.2 %collective-permute-done.19 = f32[2,16,128]{2,1,0:T(8,128)S(1)} collective-permute-done((f32[2,16,128]{2,1,0:T(8,128)S(1)}, f32[2,16,128]{2,1,0:T(8,128)S(1)}, u32[]{:S(2)}, u32[]{:S(2)}) %collective-permute-start.19) | collective-permute-done | bytes 16416 | tf_op jit(solution)/shard_map/ppermute | solution.py:638
  87.7 4.0 %collective-permute-start.20 = (f32[2,16,128]{2,1,0:T(8,128)S(1)}, f32[2,16,128]{2,1,0:T(8,128)S(1)}, u32[]{:S(2)}, u32[]{:S(2)}) collective-permute-start(f32[2,16,128]{2,1,0:T(8,128)S(1)} %pad_maximum_fusion.2), channel_id=1, source_target_pairs={{0,2},{2,0},{4,6},{6,4},{1,3},{3,1},{5,7},{7,5},{8,10},{10,8},{12,... | collective-permute-start | bytes 49160 | tf_op jit(solution)/shard_map/ppermute | solution.py:638
  91.6 1.7 %collective-permute-done.20 = f32[2,16,128]{2,1,0:T(8,128)S(1)} collective-permute-done((f32[2,16,128]{2,1,0:T(8,128)S(1)}, f32[2,16,128]{2,1,0:T(8,128)S(1)}, u32[]{:S(2)}, u32[]{:S(2)}) %collective-permute-start.20) | collective-permute-done | bytes 16416 | tf_op jit(solution)/shard_map/ppermute | solution.py:638
  93.4 3.3 %collective-permute-start.21 = (f32[2,16,128]{2,1,0:T(8,128)S(1)}, f32[2,16,128]{2,1,0:T(8,128)S(1)}, u32[]{:S(2)}, u32[]{:S(2)}) collective-permute-start(f32[2,16,128]{2,1,0:T(8,128)S(1)} %pad_maximum_fusion.3), channel_id=1, source_target_pairs={{0,4},{2,6},{4,0},{6,2},{1,5},{3,7},{5,1},{7,3},{8,12},{10,14},{12... | collective-permute-start | bytes 49160 | tf_op jit(solution)/shard_map/ppermute | solution.py:638
  98.7 1.9 %last.1 = (f32[32,16,128]{2,1,0:T(8,128)}, f32[32,16,128]{2,1,0:T(8,128)}, f32[8,128]{1,0:T(8,128)S(1)}) custom-call(f32[2,16,128]{2,1,0:T(8,128)S(1)} %pad_maximum_fusion.4.sums, f32[32,16,128]{2,1,0:T(8,128)S(1)} %get-tuple-element.129.eta, f32[16,16,128]{2,1,0:T(8,128)S(1)} %get-tuple-element.86.refs_1_.refs_2_.refs_0_, ...), custom_call_target="tpu_custom_call" | custom-call | flops 1000000 | bytes 1048576 | tf_op jit(solution)/shard_map/last/pallas_call | solution.py:26
  (59 shorter events, 11.1 us)
Async XLA Ops:
  0.6 1.1 %copy-start = (f32[3,32,16,128]{3,2,1,0:T(8,128)S(1)}, f32[3,32,16,128]{3,2,1,0:T(8,128)}, u32[]{:S(2)}) copy-start(f32[3,32,16,128]{3,2,1,0:T(8,128)} %force.1) | copy-start | bytes 2359300
  1.8 0.9 copy-start.1
  2.7 0.7 copy-start.3
  3.4 14.0 %copy-start.2 = (s32[6]{0:T(128)S(1)}, s32[6]{0:T(128)}, u32[]{:S(2)}) copy-start(s32[6]{0:T(128)} %refs_5_.1) | copy-start | bytes 76
  4.2 2.1 %collective-permute-start = (f32[4,16,16,128]{3,2,1,0:T(8,128)S(1)}, f32[4,16,16,128]{3,2,1,0:T(8,128)S(1)}, u32[]{:S(2)}, u32[]{:S(2)}) collective-permute-start(f32[4,16,16,128]{3,2,1,0:T(8,128)S(1)} %get-tuple-element.70), channel_id=1, source_target_pairs={{0,1},{1,0},{2,3},{3,2},{4,5},{5,4},{6,7},{7,6},{8,9},{9,8},{10,11... | collective-permute-start | bytes 1572872 | tf_op jit(solution)/shard_map/ppermute | solution.py:109
  6.5 10.0 %collective-permute-start.1 = (f32[68,4,256]{2,1,0:T(4,128)S(1)}, f32[68,4,256]{2,1,0:T(4,128)S(1)}, u32[]{:S(2)}, u32[]{:S(2)}) collective-permute-start(f32[68,4,256]{2,1,0:T(4,128)S(1)} %get-tuple-element.72), channel_id=1, source_target_pairs={{0,2},{2,0},{4,6},{6,4},{1,3},{3,1},{5,7},{7,5},{8,10},{10,8},{12,... | collective-permute-start | bytes 835592 | tf_op jit(solution)/shard_map/ppermute | solution.py:103
  9.5 7.0 %collective-permute-start.2 = (f32[68,4,256]{2,1,0:T(4,128)S(1)}, f32[68,4,256]{2,1,0:T(4,128)S(1)}, u32[]{:S(2)}, u32[]{:S(2)}) collective-permute-start(f32[68,4,256]{2,1,0:T(4,128)S(1)} %get-tuple-element.73), channel_id=1, source_target_pairs={{2,4},{4,2},{3,5},{5,3},{10,12},{12,10},{11,13},{13,11},{18,20},{2... | collective-permute-start | bytes 835592 | tf_op jit(solution)/shard_map/ppermute | solution.py:104
  16.6 5.5 %collective-permute-start.3 = (f32[52,8,256]{2,1,0:T(8,128)S(1)}, f32[52,8,256]{2,1,0:T(8,128)S(1)}, u32[]{:S(2)}, u32[]{:S(2)}) collective-permute-start(f32[52,8,256]{2,1,0:T(8,128)S(1)} %get-tuple-element.74), channel_id=1, source_target_pairs={{0,1},{1,0},{8,9},{9,8},{16,17},{17,16},{24,25},{25,24},{2,3},{3,2... | collective-permute-start | bytes 1277960 | tf_op jit(solution)/shard_map/ppermute | solution.py:103
  16.6 5.4 %collective-permute-start.4 = (f32[52,8,256]{2,1,0:T(8,128)S(1)}, f32[52,8,256]{2,1,0:T(8,128)S(1)}, u32[]{:S(2)}, u32[]{:S(2)}) collective-permute-start(f32[52,8,256]{2,1,0:T(8,128)S(1)} %get-tuple-element.75), channel_id=1, source_target_pairs={{1,8},{8,1},{9,16},{16,9},{17,24},{24,17},{3,10},{10,3},{11,18},{1... | collective-permute-start | bytes 1277960 | tf_op jit(solution)/shard_map/ppermute | solution.py:104
  24.9 7.1 %collective-permute-start.5 = (f32[16,4,256]{2,1,0:T(4,128)S(1)}, f32[16,4,256]{2,1,0:T(4,128)S(1)}, u32[]{:S(2)}, u32[]{:S(2)}) collective-permute-start(f32[16,4,256]{2,1,0:T(4,128)S(1)} %get-tuple-element.88), channel_id=1, source_target_pairs={{0,2},{2,0},{4,6},{6,4},{1,3},{3,1},{5,7},{7,5},{8,10},{10,8},{12,... | collective-permute-start | bytes 196616 | tf_op jit(solution)/shard_map/ppermute | solution.py:103
  29.8 2.2 %collective-permute-start.6 = (f32[16,4,256]{2,1,0:T(4,128)S(1)}, f32[16,4,256]{2,1,0:T(4,128)S(1)}, u32[]{:S(2)}, u32[]{:S(2)}) collective-permute-start(f32[16,4,256]{2,1,0:T(4,128)S(1)} %get-tuple-element.89), channel_id=1, source_target_pairs={{2,4},{4,2},{3,5},{5,3},{10,12},{12,10},{11,13},{13,11},{18,20},{2... | collective-permute-start | bytes 196616 | tf_op jit(solution)/shard_map/ppermute | solution.py:104
  32.0 12.5 %collective-permute-start.7 = (f32[4,24,256]{2,1,0:T(8,128)S(1)}, f32[4,24,256]{2,1,0:T(8,128)S(1)}, u32[]{:S(2)}, u32[]{:S(2)}) collective-permute-start(f32[4,24,256]{2,1,0:T(8,128)S(1)} %get-tuple-element.90), channel_id=1, source_target_pairs={{0,1},{1,0},{8,9},{9,8},{16,17},{17,16},{24,25},{25,24},{2,3},{3,2... | collective-permute-start | bytes 294920 | tf_op jit(solution)/shard_map/ppermute | solution.py:103
  40.3 4.2 %collective-permute-start.8 = (f32[4,24,256]{2,1,0:T(8,128)S(1)}, f32[4,24,256]{2,1,0:T(8,128)S(1)}, u32[]{:S(2)}, u32[]{:S(2)}) collective-permute-start(f32[4,24,256]{2,1,0:T(8,128)S(1)} %get-tuple-element.91), channel_id=1, source_target_pairs={{1,8},{8,1},{9,16},{16,9},{17,24},{24,17},{3,10},{10,3},{11,18},{1... | collective-permute-start | bytes 294920 | tf_op jit(solution)/shard_map/ppermute | solution.py:104
  45.9 6.0 %collective-permute-start.9 = (f32[16,4,256]{2,1,0:T(4,128)S(1)}, f32[16,4,256]{2,1,0:T(4,128)S(1)}, u32[]{:S(2)}, u32[]{:S(2)}) collective-permute-start(f32[16,4,256]{2,1,0:T(4,128)S(1)} %get-tuple-element.105), channel_id=1, source_target_pairs={{0,2},{2,0},{4,6},{6,4},{1,3},{3,1},{5,7},{7,5},{8,10},{10,8},{12,... | collective-permute-start | bytes 196616 | tf_op jit(solution)/shard_map/ppermute | solution.py:103
  49.7 2.2 %collective-permute-start.10 = (f32[16,4,256]{2,1,0:T(4,128)S(1)}, f32[16,4,256]{2,1,0:T(4,128)S(1)}, u32[]{:S(2)}, u32[]{:S(2)}) collective-permute-start(f32[16,4,256]{2,1,0:T(4,128)S(1)} %get-tuple-element.106), channel_id=1, source_target_pairs={{2,4},{4,2},{3,5},{5,3},{10,12},{12,10},{11,13},{13,11},{18,20},{2... | collective-permute-start | bytes 196616 | tf_op jit(solution)/shard_map/ppermute | solution.py:104
  51.9 6.6 %collective-permute-start.11 = (f32[4,24,256]{2,1,0:T(8,128)S(1)}, f32[4,24,256]{2,1,0:T(8,128)S(1)}, u32[]{:S(2)}, u32[]{:S(2)}) collective-permute-start(f32[4,24,256]{2,1,0:T(8,128)S(1)} %get-tuple-element.107), channel_id=1, source_target_pairs={{0,1},{1,0},{8,9},{9,8},{16,17},{17,16},{24,25},{25,24},{2,3},{3,2... | collective-permute-start | bytes 294920 | tf_op jit(solution)/shard_map/ppermute | solution.py:103
  54.3 4.2 %collective-permute-start.12 = (f32[4,24,256]{2,1,0:T(8,128)S(1)}, f32[4,24,256]{2,1,0:T(8,128)S(1)}, u32[]{:S(2)}, u32[]{:S(2)}) collective-permute-start(f32[4,24,256]{2,1,0:T(8,128)S(1)} %get-tuple-element.108), channel_id=1, source_target_pairs={{1,8},{8,1},{9,16},{16,9},{17,24},{24,17},{3,10},{10,3},{11,18},{1... | collective-permute-start | bytes 294920 | tf_op jit(solution)/shard_map/ppermute | solution.py:104
  60.0 6.0 %collective-permute-start.13 = (f32[16,4,256]{2,1,0:T(4,128)S(1)}, f32[16,4,256]{2,1,0:T(4,128)S(1)}, u32[]{:S(2)}, u32[]{:S(2)}) collective-permute-start(f32[16,4,256]{2,1,0:T(4,128)S(1)} %get-tuple-element.118), channel_id=1, source_target_pairs={{0,2},{2,0},{4,6},{6,4},{1,3},{3,1},{5,7},{7,5},{8,10},{10,8},{12,... | collective-permute-start | bytes 196616 | tf_op jit(solution)/shard_map/ppermute | solution.py:103
  63.7 2.2 %collective-permute-start.14 = (f32[16,4,256]{2,1,0:T(4,128)S(1)}, f32[16,4,256]{2,1,0:T(4,128)S(1)}, u32[]{:S(2)}, u32[]{:S(2)}) collective-permute-start(f32[16,4,256]{2,1,0:T(4,128)S(1)} %get-tuple-element.119), channel_id=1, source_target_pairs={{2,4},{4,2},{3,5},{5,3},{10,12},{12,10},{11,13},{13,11},{18,20},{2... | collective-permute-start | bytes 196616 | tf_op jit(solution)/shard_map/ppermute | solution.py:104
  65.9 7.9 %collective-permute-start.15 = (f32[4,24,256]{2,1,0:T(8,128)S(1)}, f32[4,24,256]{2,1,0:T(8,128)S(1)}, u32[]{:S(2)}, u32[]{:S(2)}) collective-permute-start(f32[4,24,256]{2,1,0:T(8,128)S(1)} %get-tuple-element.120), channel_id=1, source_target_pairs={{0,1},{1,0},{8,9},{9,8},{16,17},{17,16},{24,25},{25,24},{2,3},{3,2... | collective-permute-start | bytes 294920 | tf_op jit(solution)/shard_map/ppermute | solution.py:103
  69.0 4.8 %collective-permute-start.16 = (f32[4,24,256]{2,1,0:T(8,128)S(1)}, f32[4,24,256]{2,1,0:T(8,128)S(1)}, u32[]{:S(2)}, u32[]{:S(2)}) collective-permute-start(f32[4,24,256]{2,1,0:T(8,128)S(1)} %get-tuple-element.121), channel_id=1, source_target_pairs={{1,8},{8,1},{9,16},{16,9},{17,24},{24,17},{3,10},{10,3},{11,18},{1... | collective-permute-start | bytes 294920 | tf_op jit(solution)/shard_map/ppermute | solution.py:104
  75.3 4.6 %collective-permute-start.17 = (f32[2,16,128]{2,1,0:T(8,128)S(1)}, f32[2,16,128]{2,1,0:T(8,128)S(1)}, u32[]{:S(2)}, u32[]{:S(2)}) collective-permute-start(f32[2,16,128]{2,1,0:T(8,128)S(1)} %stack.52), channel_id=1, source_target_pairs={{0,1},{1,0},{2,3},{3,2},{4,5},{5,4},{6,7},{7,6},{8,9},{9,8},{10,11... | collective-permute-start | bytes 49160 | tf_op jit(solution)/shard_map/ppermute | solution.py:638
  79.9 3.9 %collective-permute-start.18 = (f32[2,16,128]{2,1,0:T(8,128)S(1)}, f32[2,16,128]{2,1,0:T(8,128)S(1)}, u32[]{:S(2)}, u32[]{:S(2)}) collective-permute-start(f32[2,16,128]{2,1,0:T(8,128)S(1)} %pad_maximum_fusion), channel_id=1, source_target_pairs={{0,8},{8,0},{16,24},{24,16},{1,9},{9,1},{17,25},{25,17},{2,10},{10... | collective-permute-start | bytes 49160 | tf_op jit(solution)/shard_map/ppermute | solution.py:638
  83.8 3.8 %collective-permute-start.19 = (f32[2,16,128]{2,1,0:T(8,128)S(1)}, f32[2,16,128]{2,1,0:T(8,128)S(1)}, u32[]{:S(2)}, u32[]{:S(2)}) collective-permute-start(f32[2,16,128]{2,1,0:T(8,128)S(1)} %pad_maximum_fusion.1), channel_id=1, source_target_pairs={{0,16},{8,24},{16,0},{24,8},{1,17},{9,25},{17,1},{25,9},{2,18},{10... | collective-permute-start | bytes 49160 | tf_op jit(solution)/shard_map/ppermute | solution.py:638
  87.7 5.7 %collective-permute-start.20 = (f32[2,16,128]{2,1,0:T(8,128)S(1)}, f32[2,16,128]{2,1,0:T(8,128)S(1)}, u32[]{:S(2)}, u32[]{:S(2)}) collective-permute-start(f32[2,16,128]{2,1,0:T(8,128)S(1)} %pad_maximum_fusion.2), channel_id=1, source_target_pairs={{0,2},{2,0},{4,6},{6,4},{1,3},{3,1},{5,7},{7,5},{8,10},{10,8},{12,... | collective-permute-start | bytes 49160 | tf_op jit(solution)/shard_map/ppermute | solution.py:638
  93.4 5.0 %collective-permute-start.21 = (f32[2,16,128]{2,1,0:T(8,128)S(1)}, f32[2,16,128]{2,1,0:T(8,128)S(1)}, u32[]{:S(2)}, u32[]{:S(2)}) collective-permute-start(f32[2,16,128]{2,1,0:T(8,128)S(1)} %pad_maximum_fusion.3), channel_id=1, source_target_pairs={{0,4},{2,6},{4,0},{6,2},{1,5},{3,7},{5,1},{7,3},{8,12},{10,14},{12... | collective-permute-start | bytes 49160 | tf_op jit(solution)/shard_map/ppermute | solution.py:638
  96.6 1.7 %collective-permute-start.22 = (f32[16,16,128]{2,1,0:T(8,128)S(1)}, f32[16,16,128]{2,1,0:T(8,128)S(1)}, u32[]{:S(2)}, u32[]{:S(2)}) collective-permute-start(f32[16,16,128]{2,1,0:T(8,128)S(1)} %get-tuple-element.87.refs_2_.refs_3_), channel_id=1, source_target_pairs={{0,1},{1,0},{2,3},{3,2},{4,5},{5,4},{6,7},{7,6},{8,9},{9,8},{10,11... | collective-permute-start | bytes 393224 | tf_op jit(solution)/shard_map/ppermute | solution.py:109
  96.6 1.8 %collective-permute-start.23 = (f32[16,16,128]{2,1,0:T(8,128)S(1)}, f32[16,16,128]{2,1,0:T(8,128)S(1)}, u32[]{:S(2)}, u32[]{:S(2)}) collective-permute-start(f32[16,16,128]{2,1,0:T(8,128)S(1)} %get-tuple-element.104.refs_5_), channel_id=1, source_target_pairs={{0,1},{1,0},{2,3},{3,2},{4,5},{5,4},{6,7},{7,6},{8,9},{9,8},{10,11... | collective-permute-start | bytes 393224 | tf_op jit(solution)/shard_map/ppermute | solution.py:109
  97.1 1.3 %collective-permute-start.24 = (f32[16,16,128]{2,1,0:T(8,128)S(1)}, f32[16,16,128]{2,1,0:T(8,128)S(1)}, u32[]{:S(2)}, u32[]{:S(2)}) collective-permute-start(f32[16,16,128]{2,1,0:T(8,128)S(1)} %get-tuple-element.117.refs_7_), channel_id=1, source_target_pairs={{0,1},{1,0},{2,3},{3,2},{4,5},{5,4},{6,7},{7,6},{8,9},{9,8},{10,11... | collective-permute-start | bytes 393224 | tf_op jit(solution)/shard_map/ppermute | solution.py:109
  97.1 1.5 %collective-permute-start.25 = (f32[16,16,128]{2,1,0:T(8,128)S(1)}, f32[16,16,128]{2,1,0:T(8,128)S(1)}, u32[]{:S(2)}, u32[]{:S(2)}) collective-permute-start(f32[16,16,128]{2,1,0:T(8,128)S(1)} %get-tuple-element.131), channel_id=1, source_target_pairs={{0,1},{1,0},{2,3},{3,2},{4,5},{5,4},{6,7},{7,6},{8,9},{9,8},{10,11... | collective-permute-start | bytes 393224 | tf_op jit(solution)/shard_map/ppermute | solution.py:109

commit v3 on v2

--- a/solution.py
+++ b/solution.py
@@ -16,18 +16,19 @@
 
 VMEM = pl.BlockSpec(memory_space=pltpu.VMEM)
 SMEM = pl.BlockSpec(memory_space=pltpu.SMEM)
+HBM = pl.BlockSpec(memory_space=pltpu.HBM)
 
 
 def sds(*shape):
     return jax.ShapeDtypeStruct(shape, F32)
 
 
-def call(kernel, outs, ins, specs=None, scratch=(), flops=10**6, name=None):
+def call(kernel, outs, ins, specs=None, scratch=(), flops=10**6, name=None, out_specs=None):
     return pl.pallas_call(
         kernel,
         out_shape=outs,
         in_specs=specs or [VMEM] * len(ins),
-        out_specs=jax.tree.map(lambda _: VMEM, outs),
+        out_specs=out_specs or jax.tree.map(lambda _: VMEM, outs),
         scratch_shapes=list(scratch),
         compiler_params=pltpu.CompilerParams(vmem_limit_bytes=24 * 2**20),
         cost_estimate=pl.CostEstimate(flops=flops, bytes_accessed=2**20, transcendentals=0),
@@ -109,14 +110,24 @@
     return lax.ppermute(value, "gz", [(i, (i + j) % n) for i in range(n)])
 
 
-def prep_kernel(n, force, phase, table, *outs):
+def prep_kernel(n, force, phase, table, *refs):
+    parts, eta_out, ids_buf, sems = refs[:n], refs[n], refs[n + 1], refs[n + 2]
     core = lax.axis_index("gz")
-    rows = outs[0].shape[1]
-    eta_out = outs[n]
+    rows = parts[0].shape[1]
     levels = table.shape[0]
+    fetch = pltpu.make_async_copy(phase, ids_buf, sems.at[3 * n])
+    fetch.start()
+    copies = []
+    for j in range(n):
+        base = lax.rem(core + j, n) * rows
+        for c in range(3):
+            source = force.at[c, pl.ds(base, rows)]
+            copies.append(pltpu.make_async_copy(source, parts[j].at[c], sems.at[3 * j + c]))
+            copies[-1].start()
+    fetch.wait()
 
     def one(r):
-        ids = phase[r]
+        ids = ids_buf[r]
         eta = jnp.zeros(ids.shape, F32)
         for level in range(levels):
             eta = jnp.where(ids == level, table[level], eta)
@@ -127,11 +138,11 @@
         base = lax.rem(core + j, n) * rows
 
         def two(r, j=j, base=base):
-            for c in range(3):
-                outs[j][c, r] = force[c, base + r]
-            outs[j][3, r] = eta_out[base + r]
+            parts[j][3, r] = eta_out[base + r]
 
         rows_loop(0, rows, two, 4)
+    for copy in copies:
+        copy.wait()
 
 
 def gather_kernel(n, *refs):
@@ -158,38 +169,34 @@
         send_b[fields * rows + r // 4, r % 4 : r % 4 + 1, :] = line
 
 
+def edge_list(h):
+    tiles = []
+    for c in range(4):
+        for k in range(h):
+            if c in (1, 2) and k == 0:
+                continue
+            for q in range(2 if c == 0 and k == 0 else 3):
+                tiles.append((c, k, q))
+    return tiles + [(3, -1, 0), (3, -1, 1)]
+
+
 def force_edges_kernel(full, got_a, got_b, send_a, send_b):
-    odd_y = lax.rem(lax.axis_index("gy"), 2) == 1
-    place = lax.axis_index("gx") * lax.axis_size("gz") + lax.axis_index("gz")
-    odd_x = lax.rem(place, 2) == 1
-    fields, rows, ys, _ = full.shape
+    odd_y, odd_x, _ = odd_places()
+    _, rows, ys, _ = full.shape
     h = HALO
     for send, first in ((send_a, odd_x), (send_b, jnp.logical_not(odd_x))):
-        start = jnp.where(first, 0, rows - h)
-        for c in range(fields):
-            for k in range(h):
-                r = start + k
-                t = 3 * (c * h + k)
-                row = full[c, r]
+        for t, (c, k, q) in enumerate(edge_list(h)):
+            r = jnp.where(first, h - 1 - k, rows - h + k)
+            if q < 2:
+                send[t] = full[c, r, 8 * q : 8 * q + 8, :]
+            else:
                 a, b = got_a[c * rows + r], got_b[c * rows + r]
-                send[t] = row[:8]
-                send[t + 1] = row[8:]
-                send[t + 2, :4, :] = jnp.where(odd_y, b, a)
-                send[t + 2, 4:, :] = jnp.where(odd_y, a, b)
-        t = 3 * fields * h
-        r = jnp.where(first, h, rows - h - 1)
-        row = full[3, r]
-        a, b = got_a[3 * rows + r], got_b[3 * rows + r]
-        send[t] = row[:8]
-        send[t + 1] = row[8:]
-        send[t + 2, :4, :] = jnp.where(odd_y, b, a)
-        send[t + 2, 4:, :] = jnp.where(odd_y, a, b)
-        line = fields * rows + start // 4
-        send[t + 3, :4, :] = jnp.where(odd_y, got_a[line], got_b[line])
-        send[t + 3, 4:, :] = jnp.zeros_like(send[t + 3, 4:, :])
-
-
-def edges_kernel(p, got_a, got_b, send_a, send_b):
+                send[t, :h, :] = jnp.where(odd_y, b, a)
+                send[t, h:, :] = jnp.where(odd_y, a, b)
+
+
+def edges_kernel(p, got_a, got_b, *rest):
+    send_a, send_b = rest[-2:]
     odd_y = lax.rem(lax.axis_index("gy"), 2) == 1
     place = lax.axis_index("gx") * lax.axis_size("gz") + lax.axis_index("gz")
     odd_x = lax.rem(place, 2) == 1
@@ -408,27 +415,25 @@
         set_row(eta, (r + 1,), full[3, k], ya[3 * rows + k], yb[3 * rows + k], odd_y)
         block = fields * rows + k // 4
         line[r] = jnp.where(odd_y, ya[block], yb[block])[k % 4 : k % 4 + 1]
-    for c in range(fields):
-        for k in range(h):
-            t = 3 * (c * h + k)
-            for q in range(3):
-                a, b_ = xa[t + q], xb[t + q]
-                lower, upper = jnp.where(odd_x, a, b_), jnp.where(odd_x, b_, a)
-                where = slice(8 * q, 8 * q + 8)
-                if c < 3:
-                    force[c, k, where, :] = lower
-                    force[c, h + rows + k, where, :] = upper
-                else:
-                    eta[1 + k, where, :] = lower
-                    eta[1 + h + rows + k, where, :] = upper
-    t = 3 * fields * h
-    for q in range(3):
-        eta[0, 8 * q : 8 * q + 8, :] = jnp.where(odd_x, xa[t + q], xb[t + q])
-    lower = jnp.where(odd_x, xa[t + 3], xb[t + 3])
-    upper = jnp.where(odd_x, xb[t + 3], xa[t + 3])
+    blank = jnp.zeros((slots, lanes), F32)
+    line_blank = jnp.zeros((1, lanes), F32)
     for k in range(h):
-        line[k] = lower[k : k + 1]
-        line[h + rows + k] = upper[k : k + 1]
+        for r in (k, h + rows + k):
+            line[r] = line_blank
+    for c in range(3):
+        force[c, 0] = blank
+        force[c, total - 1] = blank
+    eta[0] = blank
+    for t, (c, k, q) in enumerate(edge_list(h)):
+        lower, upper = jnp.where(odd_x, xa[t], xb[t]), jnp.where(odd_x, xb[t], xa[t])
+        where = slice(8 * q, 8 * q + 8)
+        if c < 3:
+            force[c, k, where, :] = lower
+            force[c, total - 1 - k, where, :] = upper
+        else:
+            eta[1 + k, where, :] = lower
+            if k >= 0:
+                eta[total - k, where, :] = upper
     coefs = coefs_at(sizes, place, slots, lanes, rows, ys, flags)
     for r in todo:
         after = eta[min(r + 2, total)]
@@ -446,7 +451,8 @@
     rows_loop(inner[SWEEPS][0] - h, inner[SWEEPS][1] - h, lambda r: emit(r, out0[r]), 4)
 
 
-def next_inner(p_in, ya, yb, kx, ky, kz, w, p, b, *rest):
+def next_inner(extra, p_in, ya, yb, kx, ky, kz, w, *rest):
+    p, b, *rest = rest[extra:]
     levels, out = rest[: SWEEPS - 1], rest[SWEEPS - 1]
     rows = p_in.shape[0]
     h = HALO
@@ -472,11 +478,12 @@
 
 def next_outer(n, last, p_in, xa, xb, full, kx, ky, kz, w, p0, b0, *refs):
     levels, out0, refs = refs[: SWEEPS - 1], refs[SWEEPS - 1], refs[SWEEPS:]
+    if last:
+        partials, refs = refs[:ITERS], refs[ITERS:]
     v_own, v_others, refs = refs[0], refs[1:n], refs[n:]
     p_out = send_a = send_b = sums = None
     if last:
-        moment, refs = refs[0], refs[1:]
-        acc, refs = refs[-1], refs[:-1]
+        moment, acc, refs = v_others[-1].at[p_in.shape[0]], refs[-1], refs[:-1]
         acc[...] = jnp.zeros_like(acc)
 
         def sums(r, v):
@@ -500,7 +507,13 @@
     outer_solve(b, levels, buffers, inner, ranges, w, kx, ky, kz, emit)
     rows_loop(inner[SWEEPS][0] - h, inner[SWEEPS][1] - h, lambda r: emit(r, out0[r]), 4)
     if last:
-        moment[0] = fold(acc[...])
+        moment[...] = jnp.zeros_like(moment)
+        at = 0
+        for ref in partials:
+            for k in range(ref.shape[0]):
+                moment[at : at + 1, :] = jnp.sum(ref[k], 0, keepdims=True)
+                at += 1
+        moment[at : at + 1, :] = jnp.sum(fold(acc[...]), 0, keepdims=True)
 
 
 def moments_kernel(n, step, *refs):
@@ -605,9 +618,8 @@
     norm1 = add(n00, mul(c11, add(twice(n01), mul(c11, n11))))
     norm2 = add(n00, mul(c21, add(twice(n01), mul(c21, n11))))
     norm2 = add(norm2, mul(c22, add(twice(n02), add(mul(twice(c21), n12), mul(c22, n22)))))
-    row = lax.broadcasted_iota(jnp.int32, norms.shape, 0)
-    value = jnp.where(row == 0, n00[0], jnp.where(row == 1, norm1[0], norm2[0]))
-    norms[...] = value / cells
+    for k, value in enumerate((n00, norm1, norm2)):
+        norms[k] = (value[0] / cells)[0, 0]
     rows = own[0].shape[0]
     for j in range(n):
         base = lax.rem(core - j + n, n) * rows
@@ -621,25 +633,27 @@
         rows_loop(0, rows, one_row, 4)
 
 
-def sums_kernel(m0, m1, m2, m3, out):
-    at = 0
-    for ref in (m0, m1, m2, m3):
-        for k in range(ref.shape[0]):
-            out[at : at + 1, :] = jnp.sum(ref[k], 0, keepdims=True)
-            at += 1
-    out[at:, :] = jnp.zeros_like(out[at:, :])
-
-
-def reduce_all(value, counts):
-    pair = jnp.stack([value, jnp.zeros_like(value)])
-    for axis, n in counts:
-        step = 1
+def add_pairs(a, b):
+    s, e = two_sum(a[0], b[0])
+    return jnp.stack([s, e + (a[1] + b[1])])
+
+
+def reduce_all(pair, nx, ny, nz):
+    axes = ("gx", "gy", "gz")
+    places = [(x, y, z) for x in range(nx) for y in range(ny) for z in range(nz)]
+    number = {place: k for k, place in enumerate(places)}
+    for axis, n, step in ((0, nx, 1), (1, ny, 1), (2, nz, 2)):
         while step < n:
-            other = lax.ppermute(pair, axis, [(i, i ^ step) for i in range(n)])
-            s, e = two_sum(pair[0], other[0])
-            pair = jnp.stack([s, e + (pair[1] + other[1])])
+            moves = []
+            for place in places:
+                other = list(place)
+                other[axis] ^= step
+                if place[2] % 2 == 1:
+                    moves.append((number[place], number[tuple(other)]))
+            pair = add_pairs(pair, lax.ppermute(pair, axes, moves))
             step *= 2
-    return pair
+    handed = lax.ppermute(pair, "gz", [(k, k - 1) for k in range(1, nz, 2)])
+    return jnp.where(lax.rem(lax.axis_index("gz"), 2) == 1, pair, handed)
 
 
 def per_device(nx, ny, nz, force, phase, table, flags):
@@ -656,7 +670,8 @@
         functools.partial(prep_kernel, nz),
         [sds(4, rows, ys, lanes)] * nz + [sds(*phase.shape)],
         (force, phase, table),
-        [VMEM, VMEM, SMEM],
+        [HBM, HBM, SMEM],
+        [pltpu.VMEM(phase.shape, jnp.int32), pltpu.SemaphoreType.DMA((3 * nz + 1,))],
         name="prep",
     )
     eta = parts[-1]
@@ -669,7 +684,7 @@
         name="gather",
     )
     ya, yb = exchange("gy", ny, ya, yb)
-    edge = sds(3 * 4 * h + 4, 8, zs)
+    edge = sds(len(edge_list(h)), 8, zs)
     xa, xb = call(force_edges_kernel, [edge, edge], (full, ya, yb), name="force_edges")
     xa, xb = exchange(("gx", "gz"), chain, xa, xb)
 
@@ -700,9 +715,11 @@
     vs, ps, moments = [list(outs[:nz])], [outs[nz]], []
     ya, yb = outs[nz + 1 : nz + 3]
     coefs = outs[nz + 3 :]
+    placed = []
     for step in range(1, ITERS + 1):
         last = step == ITERS
-        p = ps[-1]
+        p, v = ps[-1], vs[-1]
+        placed.append([v[0]] + [core_shift(v[j], nz, j) for j in range(1, nz)])
         count = 2 if step == 1 else 2 + step
         moments.append(
             call(
@@ -716,21 +733,22 @@
         )
         ya, yb = exchange("gy", ny, ya, yb)
         edge = sds(h, slots, zs)
-        xa, xb = call(edges_kernel, [edge, edge], (p, ya, yb), name="edges")
+        xa, xb = call(edges_kernel, [edge, edge], (p, ya, yb, moments[-1]), name="edges")
         xa, xb = exchange(("gx", "gz"), chain, xa, xb)
         early = call(
-            next_inner,
+            functools.partial(next_inner, nz - 1),
             [scalar] + [vector] * SWEEPS + [sds(rows, slots, zs)],
-            (p, ya, yb, *coefs),
+            (p, ya, yb, *coefs, *placed[-1][1:]),
             None,
             (),
             heavy,
             "next_inner",
         )
+        joint = v_shape[:-1] + [sds(rows + 1, ys, lanes)]
         outs = call(
             functools.partial(next_outer, nz, last),
-            v_shape + ([sds(1, 8, LANES)] if last else sent),
-            (p, xa, xb, full, *coefs, *early),
+            joint if last else v_shape + sent,
+            (p, xa, xb, full, *coefs, *early, *(moments if last else ())),
             None,
             [pltpu.VMEM((total, slots, zs), F32)]
             + [field] * SWEEPS
@@ -739,22 +757,26 @@
             "next",
         )
         vs.append(list(outs[:nz]))
-        if last:
-            moments.append(outs[nz])
-        else:
+        if not last:
             ps.append(outs[nz])
             ya, yb = outs[nz + 1 : nz + 3]
 
-    placed = [[v[0]] + [core_shift(v[j], nz, j) for j in range(1, nz)] for v in vs]
-    flat = call(sums_kernel, sds(16, LANES), moments, name="sums")
-    pair = reduce_all(flat, (("gz", nz), ("gx", nx), ("gy", ny)))
+    v = vs[-1]
+    moved = [v[0]] + [core_shift(v[j], nz, j) for j in range(1, nz)]
+    placed.append(moved)
+    mine, theirs = v[-1][rows], moved[-1][rows]
+    if nz > 2:
+        theirs = lax.ppermute(mine, "gz", [(k, k ^ 1) for k in range(nz)])
+    pair = jnp.stack(two_sum(mine, theirs))
+    pair = reduce_all(pair, nx, ny, nz)
     pressure, residual, norms = call(
         functools.partial(last_kernel, nz, cells),
-        [sds(*phase.shape), sds(*phase.shape), sds(8, LANES)],
+        [sds(*phase.shape), sds(*phase.shape), sds(ITERS)],
         (pair, eta, *[q for v in placed for q in v]),
         name="last",
+        out_specs=[VMEM, VMEM, SMEM],
     )
-    return pressure, residual, norms[:ITERS, 0]
+    return pressure, residual, norms
 
 
 def solution(mesh):

time: 102 us -> 106 us (1.039)
  waiting for transfers between devices: 20.1 us -> 28.8 us
  starting transfers between devices: 50.8 us -> 45.3 us
  Pallas kernels: 26 us -> 27.2 us
    ppermute x5, starting transfers between devices: 1.58 us -> 18.2 us  [core_shift(): return lax.ppermute(value, 'gz', [(i, (i + j) % n) for i in range(n)])]
    ppermute x5, waiting for transfers between devices: 7.17 us -> 19.9 us  [the longest x1 19.9 us: reduce_all(): handed = lax.ppermute(pair, 'gz', [(k, k - 1) for k in range(1, nz, 2)])]
    ppermute x8, starting transfers between devices: 28.9 us -> 17.8 us  [exchange(): lax.ppermute(a, axis, pair_perm(n, 0))]
    ppermute x5, starting transfers between devices: 14.8 us -> 3.93 us  [the longest x4 2.64 us: reduce_all(): pair = add_pairs(pair, lax.ppermute(pair, axes, moves))]
    ppermute x8, waiting for transfers between devices: 11.1 us -> 6.31 us  [exchange(): lax.ppermute(a, axis, pair_perm(n, 0))]
    pallas_call x19 -> x18, Pallas kernels: 26 us -> 27.2 us  [call(): pl.pallas_call(kernel, out_shape=outs, in_specs=specs or [VMEM] * len(ins...]
  transfers between devices with their start and end apart: 26 -> 26, of which waited for: 12 -> 4; matrix products, arithmetic and copies ran while one was open for 0% -> 0% of each run, Pallas kernels for 16% -> 15%
where the time goes in v3:
time: 106 us; the launch traced here: 105 us
  starting transfers between devices  45.3 us (43%)
  waiting for transfers between devices  28.8 us (27%)
  Pallas kernels  27.2 us (26%)
  local copies, waits for them, and re-layouts  2.73 us (3%)
  between operations  1.23 us (1%)
    pallas_call x18, Pallas kernels, call(): pl.pallas_call(kernel, out_shape=outs, in_specs=specs or [VMEM] * len(ins...  27.2 us
    ppermute x1, waiting for transfers between devices, reduce_all(): handed = lax.ppermute(pair, 'gz', [(k, k - 1) for k in range(1, nz, 2)])  19.9 us
    ppermute x5, starting transfers between devices, core_shift(): return lax.ppermute(value, 'gz', [(i, (i + j) % n) for i in range(n)])  18.2 us
    ppermute x8, starting transfers between devices, exchange(): lax.ppermute(a, axis, pair_perm(n, 0))  17.8 us
    ppermute x8, waiting for transfers between devices, exchange(): lax.ppermute(a, axis, pair_perm(n, 0))  6.31 us
    ppermute x8, starting transfers between devices, exchange(): lax.ppermute(b, axis, pair_perm(n, 1))  5.45 us
    unnamed x8, local copies, waits for them, and re-layouts  2.73 us
    ppermute x4, starting transfers between devices, reduce_all(): pair = add_pairs(pair, lax.ppermute(pair, axes, moves))  2.64 us
  transfers between devices with their start and end apart: 26, of which 4 were waited for; matrix products, arithmetic and copies ran while one was open for 0% of the time, Pallas kernels for 15%

profile of v3, /device:TPU:0, one launch (start us, length us, event | category | flops | bytes accessed | tf_op | source)
XLA Modules:
  0.0 105.4 jit_solution(6105884686980157156)
XLA Ops:
  0.6 1.1 %copy-done = f32[3,32,16,128]{3,2,1,0:T(8,128)S(1)} copy-done((f32[3,32,16,128]{3,2,1,0:T(8,128)S(1)}, f32[3,32,16,128]{3,2,1,0:T(8,128)}, u32[]{:S(2)}) %copy-start) | copy-done | bytes 786456
  1.8 0.9 copy-done.1
  3.4 1.9 %prep.1 = (f32[4,16,16,128]{3,2,1,0:T(8,128)S(1)}, f32[4,16,16,128]{3,2,1,0:T(8,128)S(1)}, f32[32,16,128]{2,1,0:T(8,128)S(1)}) custom-call(f32[3,32,16,128]{3,2,1,0:T(8,128)S(1)} %copy-done, s32[32,16,128]{2,1,0:T(8,128)S(1)} %copy-done.1, f32[8]{0:T(128)S(1)} %copy-done.3), custom_call_target="tpu_custom_call" | custom-call | flops 1000000 | bytes 1048576 | tf_op jit(solution)/shard_map/prep/pallas_call | solution.py:27
  5.8 1.5 %collective-permute-done.refs_1_ = f32[4,16,16,128]{3,2,1,0:T(8,128)S(1)} collective-permute-done((f32[4,16,16,128]{3,2,1,0:T(8,128)S(1)}, f32[4,16,16,128]{3,2,1,0:T(8,128)S(1)}, u32[]{:S(2)}, u32[]{:S(2)}) %collective-permute-start) | collective-permute-done | bytes 524320 | tf_op jit(solution)/shard_map/ppermute | solution.py:110
  7.6 3.0 %collective-permute-start.1 = (f32[68,4,256]{2,1,0:T(4,128)S(1)}, f32[68,4,256]{2,1,0:T(4,128)S(1)}, u32[]{:S(2)}, u32[]{:S(2)}) collective-permute-start(f32[68,4,256]{2,1,0:T(4,128)S(1)} %get-tuple-element.68), channel_id=1, source_target_pairs={{0,2},{2,0},{4,6},{6,4},{1,3},{3,1},{5,7},{7,5},{8,10},{10,8},{12,... | collective-permute-start | bytes 835592 | tf_op jit(solution)/shard_map/ppermute | solution.py:104
  10.6 0.7 collective-permute-start.2
  11.3 6.3 %collective-permute-done.1.got_a.ya.refs_1_ = f32[68,4,256]{2,1,0:T(4,128)S(1)} collective-permute-done((f32[68,4,256]{2,1,0:T(4,128)S(1)}, f32[68,4,256]{2,1,0:T(4,128)S(1)}, u32[]{:S(2)}, u32[]{:S(2)}) %collective-permute-start.1) | collective-permute-done | bytes 278560 | tf_op jit(solution)/shard_map/ppermute | solution.py:104
  17.7 0.7 collective-permute-start.4
  18.4 4.7 %first_inner.1 = (f32[24,24,256]{2,1,0:T(8,128)S(1)}, f32[24,24,256]{2,1,0:T(8,128)S(1)}, f32[24,24,256]{2,1,0:T(8,128)S(1)}, f32[3,24,24,256]{3,2,1,0:T(8,128)S...) custom-call(f32[4,16,16,256]{3,2,1,0:T(8,128)S(1)} %get-tuple-elemen, ...), custom_call_target="tpu_custom_call" | custom-call | flops 40000000 | bytes 1048576 | tf_op jit(solution)/shard_map/first_inner/pallas_call | solution.py:27
  23.1 2.8 %first.1 = (f32[16,16,128]{2,1,0:T(8,128)S(1)}, f32[16,16,128]{2,1,0:T(8,128)S(1)}, f32[16,16,256]{2,1,0:T(8,128)S(1)}, f32[16,4,256]{2,1,0:T(4,128)S(1)}, f32[1...) custom-call(f32[4,16,16,256]{3,2,1,0:T(8,128)S(1)} %get-tuple-elemen, ...), custom_call_target="tpu_custom_call" | custom-call | flops 40000000 | bytes 1048576 | tf_op jit(solution)/shard_map/first/pallas_call | solution.py:27
  26.0 4.8 %collective-permute-start.5 = (f32[16,4,256]{2,1,0:T(4,128)S(1)}, f32[16,4,256]{2,1,0:T(4,128)S(1)}, u32[]{:S(2)}, u32[]{:S(2)}) collective-permute-start(f32[16,4,256]{2,1,0:T(4,128)S(1)} %get-tuple-element.82), channel_id=1, source_target_pairs={{0,2},{2,0},{4,6},{6,4},{1,3},{3,1},{5,7},{7,5},{8,10},{10,8},{12,... | collective-permute-start | bytes 196616 | tf_op jit(solution)/shard_map/ppermute | solution.py:104
  31.5 7.1 %collective-permute-start.9 = (f32[16,16,128]{2,1,0:T(8,128)S(1)}, f32[16,16,128]{2,1,0:T(8,128)S(1)}, u32[]{:S(2)}, u32[]{:S(2)}) collective-permute-start(f32[16,16,128]{2,1,0:T(8,128)S(1)} %get-tuple-element.85.refs_2_.refs_3_), channel_id=1, source_target_pairs={{0,1},{1,0},{2,3},{3,2},{4,5},{5,4},{6,7},{7,6},{8,9},{9,8},{10,11... | collective-permute-start | bytes 393224 | tf_op jit(solution)/shard_map/ppermute | solution.py:110
  38.7 0.9 collective-permute-start.7
  40.2 3.6 %next_inner.3 = (f32[24,24,256]{2,1,0:T(8,128)S(1)}, f32[3,24,24,256]{3,2,1,0:T(8,128)S(1)}, f32[3,24,24,256]{3,2,1,0:T(8,128)S(1)}, f32[3,24,24,256]{3,2,1,0:T(...) custom-call(f32[16,16,256]{2,1,0:T(8,128)S(1)} %get-tuple-element.81.refs_0_.p.p_in.refs_1_, ...), custom_call_target="tpu_custom_call" | custom-call | flops 40000000 | bytes 1048576 | tf_op jit(solution)/shard_map/next_inner/pallas_call | solution.py:27
  43.8 1.4 %next.3 = (f32[16,16,128]{2,1,0:T(8,128)S(1)}, f32[16,16,128]{2,1,0:T(8,128)S(1)}, f32[16,16,256]{2,1,0:T(8,128)S(1)}, f32[16,4,256]{2,1,0:T(4,128)S(1)}, f32[16,4,256]{2,1,0:T(4,128)S(1)}) custom-call(f32[16,16,256]{2,1,0:T(8,128)S(1)} %get-tuple-element.81.refs_0_.p.p_in.refs_1_, f32[4,24,256]{2,1,0:T(8,128)S(1)} %collective-permute-done.7.xa, ...), custom_call_target="tpu_custom_call" | custom-call | flops 40000000 | bytes 1048576 | tf_op jit(solution)/shard_map/next/pallas_call | solution.py:27
  45.2 3.7 %collective-permute-start.10 = (f32[16,4,256]{2,1,0:T(4,128)S(1)}, f32[16,4,256]{2,1,0:T(4,128)S(1)}, u32[]{:S(2)}, u32[]{:S(2)}) collective-permute-start(f32[16,4,256]{2,1,0:T(4,128)S(1)} %get-tuple-element.99), channel_id=1, source_target_pairs={{0,2},{2,0},{4,6},{6,4},{1,3},{3,1},{5,7},{7,5},{8,10},{10,8},{12,... | collective-permute-start | bytes 196616 | tf_op jit(solution)/shard_map/ppermute | solution.py:104
  49.6 3.1 %collective-permute-start.14 = (f32[16,16,128]{2,1,0:T(8,128)S(1)}, f32[16,16,128]{2,1,0:T(8,128)S(1)}, u32[]{:S(2)}, u32[]{:S(2)}) collective-permute-start(f32[16,16,128]{2,1,0:T(8,128)S(1)} %get-tuple-element.102.refs_5_), channel_id=1, source_target_pairs={{0,1},{1,0},{2,3},{3,2},{4,5},{5,4},{6,7},{7,6},{8,9},{9,8},{10,11... | collective-permute-start | bytes 393224 | tf_op jit(solution)/shard_map/ppermute | solution.py:110
  52.9 0.8 collective-permute-start.12
  54.4 3.6 %next_inner.4 = (f32[24,24,256]{2,1,0:T(8,128)S(1)}, f32[3,24,24,256]{3,2,1,0:T(8,128)S(1)}, f32[3,24,24,256]{3,2,1,0:T(8,128)S(1)}, f32[3,24,24,256]{3,2,1,0:T(...) custom-call(f32[16,16,256]{2,1,0:T(8,128)S(1)} %get-tuple-element.98.refs_0_.p.p_in.refs_1_, ...), custom_call_target="tpu_custom_call" | custom-call | flops 40000000 | bytes 1048576 | tf_op jit(solution)/shard_map/next_inner/pallas_call | solution.py:27
  58.0 1.4 %next.4 = (f32[16,16,128]{2,1,0:T(8,128)S(1)}, f32[16,16,128]{2,1,0:T(8,128)S(1)}, f32[16,16,256]{2,1,0:T(8,128)S(1)}, f32[16,4,256]{2,1,0:T(4,128)S(1)}, f32[16,4,256]{2,1,0:T(4,128)S(1)}) custom-call(f32[16,16,256]{2,1,0:T(8,128)S(1)} %get-tuple-element.98.refs_0_.p.p_in.refs_1_, f32[4,24,256]{2,1,0:T(8,128)S(1)} %collective-permute-done.12.xa, ...), custom_call_target="tpu_custom_call" | custom-call | flops 40000000 | bytes 1048576 | tf_op jit(solution)/shard_map/next/pallas_call | solution.py:27
  59.5 3.7 %collective-permute-start.15 = (f32[16,4,256]{2,1,0:T(4,128)S(1)}, f32[16,4,256]{2,1,0:T(4,128)S(1)}, u32[]{:S(2)}, u32[]{:S(2)}) collective-permute-start(f32[16,4,256]{2,1,0:T(4,128)S(1)} %get-tuple-element.112), channel_id=1, source_target_pairs={{0,2},{2,0},{4,6},{6,4},{1,3},{3,1},{5,7},{7,5},{8,10},{10,8},{12,... | collective-permute-start | bytes 196616 | tf_op jit(solution)/shard_map/ppermute | solution.py:104
  63.8 3.6 %collective-permute-start.19 = (f32[16,16,128]{2,1,0:T(8,128)S(1)}, f32[16,16,128]{2,1,0:T(8,128)S(1)}, u32[]{:S(2)}, u32[]{:S(2)}) collective-permute-start(f32[16,16,128]{2,1,0:T(8,128)S(1)} %get-tuple-element.115.refs_7_), channel_id=1, source_target_pairs={{0,1},{1,0},{2,3},{3,2},{4,5},{5,4},{6,7},{7,6},{8,9},{9,8},{10,11... | collective-permute-start | bytes 393224 | tf_op jit(solution)/shard_map/ppermute | solution.py:110
  67.7 0.8 collective-permute-start.17
  68.5 0.8 collective-permute-start.18
  69.3 3.6 %next_inner.5 = (f32[24,24,256]{2,1,0:T(8,128)S(1)}, f32[3,24,24,256]{3,2,1,0:T(8,128)S(1)}, f32[3,24,24,256]{3,2,1,0:T(8,128)S(1)}, f32[3,24,24,256]{3,2,1,0:T(...) custom-call(f32[16,16,256]{2,1,0:T(8,128)S(1)} %get-tuple-element.111.refs_0_.p.p_in, ...), custom_call_target="tpu_custom_call" | custom-call | flops 40000000 | bytes 1048576 | tf_op jit(solution)/shard_map/next_inner/pallas_call | solution.py:27
  73.0 1.4 %next.5 = (f32[16,16,128]{2,1,0:T(8,128)S(1)}, f32[17,16,128]{2,1,0:T(8,128)S(1)}) custom-call(f32[16,16,256]{2,1,0:T(8,128)S(1)} %get-tuple-element.111.refs_0_.p.p_in, f32[4,24,256]{2,1,0:T(8,128)S(1)} %collective-permute-done.17.xa, f32[4,24,256]{2,1,0:T(8,128)S(1)} %collective-permute-done.18.xb, f32[4,16,16,256]{3,2,1,0:T(8,128)S(1)} %get-tuple-element.67.full.refs_0_, ...), custom_call_target="tpu_custom_call" | custom-call | flops 40000000 | bytes 1048576 | tf_op jit(solution)/shard_map/next/pallas_call | solution.py:27
  74.4 3.8 %collective-permute-start.20 = (f32[17,16,128]{2,1,0:T(8,128)S(1)}, f32[17,16,128]{2,1,0:T(8,128)S(1)}, u32[]{:S(2)}, u32[]{:S(2)}) collective-permute-start(f32[17,16,128]{2,1,0:T(8,128)S(1)} %get-tuple-element.124), channel_id=1, source_target_pairs={{0,1},{1,0},{2,3},{3,2},{4,5},{5,4},{6,7},{7,6},{8,9},{9,8},{10,11... | collective-permute-start | bytes 417800 | tf_op jit(solution)/shard_map/ppermute | solution.py:110
  78.2 1.0 collective-permute-done.20.refs_7_
  81.3 0.7 collective-permute-start.24
  82.1 1.3 %collective-permute-start.25 = (f32[2,16,128]{2,1,0:T(8,128)S(1)}, f32[2,16,128]{2,1,0:T(8,128)S(1)}, u32[]{:S(2)}, u32[]{:S(2)}) collective-permute-start(f32[2,16,128]{2,1,0:T(8,128)S(1)} %pad_maximum_fusion.4), channel_id=1, source_target_pairs={{1,0},{3,2},{5,4},{7,6},{9,8},{11,10},{13,12},{15,14},{17,16},{19,... | collective-permute-start | bytes 49160 | tf_op jit(solution)/shard_map/ppermute | solution.py:655
  83.4 19.9 %collective-permute-done.25 = f32[2,16,128]{2,1,0:T(8,128)S(1)} collective-permute-done((f32[2,16,128]{2,1,0:T(8,128)S(1)}, f32[2,16,128]{2,1,0:T(8,128)S(1)}, u32[]{:S(2)}, u32[]{:S(2)}) %collective-permute-start.25) | collective-permute-done | bytes 16416 | tf_op jit(solution)/shard_map/ppermute | solution.py:655
  103.3 1.9 %last.1 = (f32[32,16,128]{2,1,0:T(8,128)}, f32[32,16,128]{2,1,0:T(8,128)}, f32[3]{0:T(128)}) custom-call(f32[2,16,128]{2,1,0:T(8,128)S(1)} %broadcast_select_fusion.sums, f32[32,16,128]{2,1,0:T(8,128)S(1)} %get-tuple-element.125.eta, f32[16,16,128]{2,1,0:T(8,128)S(1)} %get-tuple-element.84.refs_1_.refs_2_.refs_0_, ...), custom_call_target="tpu_custom_call" | custom-call | flops 1000000 | bytes 1048576 | tf_op jit(solution)/shard_map/last/pallas_call | solution.py:27
  (57 shorter events, 7.5 us)
Async XLA Ops:
  0.6 1.1 %copy-start = (f32[3,32,16,128]{3,2,1,0:T(8,128)S(1)}, f32[3,32,16,128]{3,2,1,0:T(8,128)}, u32[]{:S(2)}) copy-start(f32[3,32,16,128]{3,2,1,0:T(8,128)} %force.1) | copy-start | bytes 2359300
  1.8 0.9 copy-start.1
  2.7 0.7 copy-start.3
  3.4 15.0 %copy-start.2 = (s32[6]{0:T(128)S(1)}, s32[6]{0:T(128)}, u32[]{:S(2)}) copy-start(s32[6]{0:T(128)} %refs_5_.1) | copy-start | bytes 76
  5.3 2.1 %collective-permute-start = (f32[4,16,16,128]{3,2,1,0:T(8,128)S(1)}, f32[4,16,16,128]{3,2,1,0:T(8,128)S(1)}, u32[]{:S(2)}, u32[]{:S(2)}) collective-permute-start(f32[4,16,16,128]{3,2,1,0:T(8,128)S(1)} %get-tuple-element.66), channel_id=1, source_target_pairs={{0,1},{1,0},{2,3},{3,2},{4,5},{5,4},{6,7},{7,6},{8,9},{9,8},{10,11... | collective-permute-start | bytes 1572872 | tf_op jit(solution)/shard_map/ppermute | solution.py:110
  7.6 10.0 %collective-permute-start.1 = (f32[68,4,256]{2,1,0:T(4,128)S(1)}, f32[68,4,256]{2,1,0:T(4,128)S(1)}, u32[]{:S(2)}, u32[]{:S(2)}) collective-permute-start(f32[68,4,256]{2,1,0:T(4,128)S(1)} %get-tuple-element.68), channel_id=1, source_target_pairs={{0,2},{2,0},{4,6},{6,4},{1,3},{3,1},{5,7},{7,5},{8,10},{10,8},{12,... | collective-permute-start | bytes 835592 | tf_op jit(solution)/shard_map/ppermute | solution.py:104
  10.6 7.0 %collective-permute-start.2 = (f32[68,4,256]{2,1,0:T(4,128)S(1)}, f32[68,4,256]{2,1,0:T(4,128)S(1)}, u32[]{:S(2)}, u32[]{:S(2)}) collective-permute-start(f32[68,4,256]{2,1,0:T(4,128)S(1)} %get-tuple-element.69), channel_id=1, source_target_pairs={{2,4},{4,2},{3,5},{5,3},{10,12},{12,10},{11,13},{13,11},{18,20},{2... | collective-permute-start | bytes 835592 | tf_op jit(solution)/shard_map/ppermute | solution.py:105
  17.6 5.5 %collective-permute-start.3 = (f32[43,8,256]{2,1,0:T(8,128)S(1)}, f32[43,8,256]{2,1,0:T(8,128)S(1)}, u32[]{:S(2)}, u32[]{:S(2)}) collective-permute-start(f32[43,8,256]{2,1,0:T(8,128)S(1)} %get-tuple-element.70), channel_id=1, source_target_pairs={{0,1},{1,0},{8,9},{9,8},{16,17},{17,16},{24,25},{25,24},{2,3},{3,2... | collective-permute-start | bytes 1056776 | tf_op jit(solution)/shard_map/ppermute | solution.py:104
  17.7 5.4 %collective-permute-start.4 = (f32[43,8,256]{2,1,0:T(8,128)S(1)}, f32[43,8,256]{2,1,0:T(8,128)S(1)}, u32[]{:S(2)}, u32[]{:S(2)}) collective-permute-start(f32[43,8,256]{2,1,0:T(8,128)S(1)} %get-tuple-element.71), channel_id=1, source_target_pairs={{1,8},{8,1},{9,16},{16,9},{17,24},{24,17},{3,10},{10,3},{11,18},{1... | collective-permute-start | bytes 1056776 | tf_op jit(solution)/shard_map/ppermute | solution.py:105
  26.0 12.6 %collective-permute-start.5 = (f32[16,4,256]{2,1,0:T(4,128)S(1)}, f32[16,4,256]{2,1,0:T(4,128)S(1)}, u32[]{:S(2)}, u32[]{:S(2)}) collective-permute-start(f32[16,4,256]{2,1,0:T(4,128)S(1)} %get-tuple-element.82), channel_id=1, source_target_pairs={{0,2},{2,0},{4,6},{6,4},{1,3},{3,1},{5,7},{7,5},{8,10},{10,8},{12,... | collective-permute-start | bytes 196616 | tf_op jit(solution)/shard_map/ppermute | solution.py:104
  30.8 7.8 %collective-permute-start.6 = (f32[16,4,256]{2,1,0:T(4,128)S(1)}, f32[16,4,256]{2,1,0:T(4,128)S(1)}, u32[]{:S(2)}, u32[]{:S(2)}) collective-permute-start(f32[16,4,256]{2,1,0:T(4,128)S(1)} %get-tuple-element.83), channel_id=1, source_target_pairs={{2,4},{4,2},{3,5},{5,3},{10,12},{12,10},{11,13},{13,11},{18,20},{2... | collective-permute-start | bytes 196616 | tf_op jit(solution)/shard_map/ppermute | solution.py:105
  31.5 8.8 %collective-permute-start.9 = (f32[16,16,128]{2,1,0:T(8,128)S(1)}, f32[16,16,128]{2,1,0:T(8,128)S(1)}, u32[]{:S(2)}, u32[]{:S(2)}) collective-permute-start(f32[16,16,128]{2,1,0:T(8,128)S(1)} %get-tuple-element.85.refs_2_.refs_3_), channel_id=1, source_target_pairs={{0,1},{1,0},{2,3},{3,2},{4,5},{5,4},{6,7},{7,6},{8,9},{9,8},{10,11... | collective-permute-start | bytes 393224 | tf_op jit(solution)/shard_map/ppermute | solution.py:110
  38.7 5.1 %collective-permute-start.7 = (f32[4,24,256]{2,1,0:T(8,128)S(1)}, f32[4,24,256]{2,1,0:T(8,128)S(1)}, u32[]{:S(2)}, u32[]{:S(2)}) collective-permute-start(f32[4,24,256]{2,1,0:T(8,128)S(1)} %get-tuple-element.86), channel_id=1, source_target_pairs={{0,1},{1,0},{8,9},{9,8},{16,17},{17,16},{24,25},{25,24},{2,3},{3,2... | collective-permute-start | bytes 294920 | tf_op jit(solution)/shard_map/ppermute | solution.py:104
  39.6 4.3 %collective-permute-start.8 = (f32[4,24,256]{2,1,0:T(8,128)S(1)}, f32[4,24,256]{2,1,0:T(8,128)S(1)}, u32[]{:S(2)}, u32[]{:S(2)}) collective-permute-start(f32[4,24,256]{2,1,0:T(8,128)S(1)} %get-tuple-element.87), channel_id=1, source_target_pairs={{1,8},{8,1},{9,16},{16,9},{17,24},{24,17},{3,10},{10,3},{11,18},{1... | collective-permute-start | bytes 294920 | tf_op jit(solution)/shard_map/ppermute | solution.py:105
  45.2 7.6 %collective-permute-start.10 = (f32[16,4,256]{2,1,0:T(4,128)S(1)}, f32[16,4,256]{2,1,0:T(4,128)S(1)}, u32[]{:S(2)}, u32[]{:S(2)}) collective-permute-start(f32[16,4,256]{2,1,0:T(4,128)S(1)} %get-tuple-element.99), channel_id=1, source_target_pairs={{0,2},{2,0},{4,6},{6,4},{1,3},{3,1},{5,7},{7,5},{8,10},{10,8},{12,... | collective-permute-start | bytes 196616 | tf_op jit(solution)/shard_map/ppermute | solution.py:104
  49.0 3.9 %collective-permute-start.11 = (f32[16,4,256]{2,1,0:T(4,128)S(1)}, f32[16,4,256]{2,1,0:T(4,128)S(1)}, u32[]{:S(2)}, u32[]{:S(2)}) collective-permute-start(f32[16,4,256]{2,1,0:T(4,128)S(1)} %get-tuple-element.100), channel_id=1, source_target_pairs={{2,4},{4,2},{3,5},{5,3},{10,12},{12,10},{11,13},{13,11},{18,20},{2... | collective-permute-start | bytes 196616 | tf_op jit(solution)/shard_map/ppermute | solution.py:105
  49.6 4.8 %collective-permute-start.14 = (f32[16,16,128]{2,1,0:T(8,128)S(1)}, f32[16,16,128]{2,1,0:T(8,128)S(1)}, u32[]{:S(2)}, u32[]{:S(2)}) collective-permute-start(f32[16,16,128]{2,1,0:T(8,128)S(1)} %get-tuple-element.102.refs_5_), channel_id=1, source_target_pairs={{0,1},{1,0},{2,3},{3,2},{4,5},{5,4},{6,7},{7,6},{8,9},{9,8},{10,11... | collective-permute-start | bytes 393224 | tf_op jit(solution)/shard_map/ppermute | solution.py:110
  52.9 5.1 %collective-permute-start.12 = (f32[4,24,256]{2,1,0:T(8,128)S(1)}, f32[4,24,256]{2,1,0:T(8,128)S(1)}, u32[]{:S(2)}, u32[]{:S(2)}) collective-permute-start(f32[4,24,256]{2,1,0:T(8,128)S(1)} %get-tuple-element.103), channel_id=1, source_target_pairs={{0,1},{1,0},{8,9},{9,8},{16,17},{17,16},{24,25},{25,24},{2,3},{3,2... | collective-permute-start | bytes 294920 | tf_op jit(solution)/shard_map/ppermute | solution.py:104
  53.8 4.3 %collective-permute-start.13 = (f32[4,24,256]{2,1,0:T(8,128)S(1)}, f32[4,24,256]{2,1,0:T(8,128)S(1)}, u32[]{:S(2)}, u32[]{:S(2)}) collective-permute-start(f32[4,24,256]{2,1,0:T(8,128)S(1)} %get-tuple-element.104), channel_id=1, source_target_pairs={{1,8},{8,1},{9,16},{16,9},{17,24},{24,17},{3,10},{10,3},{11,18},{1... | collective-permute-start | bytes 294920 | tf_op jit(solution)/shard_map/ppermute | solution.py:105
  59.5 8.2 %collective-permute-start.15 = (f32[16,4,256]{2,1,0:T(4,128)S(1)}, f32[16,4,256]{2,1,0:T(4,128)S(1)}, u32[]{:S(2)}, u32[]{:S(2)}) collective-permute-start(f32[16,4,256]{2,1,0:T(4,128)S(1)} %get-tuple-element.112), channel_id=1, source_target_pairs={{0,2},{2,0},{4,6},{6,4},{1,3},{3,1},{5,7},{7,5},{8,10},{10,8},{12,... | collective-permute-start | bytes 196616 | tf_op jit(solution)/shard_map/ppermute | solution.py:104
  63.2 4.5 %collective-permute-start.16 = (f32[16,4,256]{2,1,0:T(4,128)S(1)}, f32[16,4,256]{2,1,0:T(4,128)S(1)}, u32[]{:S(2)}, u32[]{:S(2)}) collective-permute-start(f32[16,4,256]{2,1,0:T(4,128)S(1)} %get-tuple-element.113), channel_id=1, source_target_pairs={{2,4},{4,2},{3,5},{5,3},{10,12},{12,10},{11,13},{13,11},{18,20},{2... | collective-permute-start | bytes 196616 | tf_op jit(solution)/shard_map/ppermute | solution.py:105
  63.8 5.5 %collective-permute-start.19 = (f32[16,16,128]{2,1,0:T(8,128)S(1)}, f32[16,16,128]{2,1,0:T(8,128)S(1)}, u32[]{:S(2)}, u32[]{:S(2)}) collective-permute-start(f32[16,16,128]{2,1,0:T(8,128)S(1)} %get-tuple-element.115.refs_7_), channel_id=1, source_target_pairs={{0,1},{1,0},{2,3},{3,2},{4,5},{5,4},{6,7},{7,6},{8,9},{9,8},{10,11... | collective-permute-start | bytes 393224 | tf_op jit(solution)/shard_map/ppermute | solution.py:110
  67.7 5.3 %collective-permute-start.17 = (f32[4,24,256]{2,1,0:T(8,128)S(1)}, f32[4,24,256]{2,1,0:T(8,128)S(1)}, u32[]{:S(2)}, u32[]{:S(2)}) collective-permute-start(f32[4,24,256]{2,1,0:T(8,128)S(1)} %get-tuple-element.116), channel_id=1, source_target_pairs={{0,1},{1,0},{8,9},{9,8},{16,17},{17,16},{24,25},{25,24},{2,3},{3,2... | collective-permute-start | bytes 294920 | tf_op jit(solution)/shard_map/ppermute | solution.py:104
  68.5 4.5 %collective-permute-start.18 = (f32[4,24,256]{2,1,0:T(8,128)S(1)}, f32[4,24,256]{2,1,0:T(8,128)S(1)}, u32[]{:S(2)}, u32[]{:S(2)}) collective-permute-start(f32[4,24,256]{2,1,0:T(8,128)S(1)} %get-tuple-element.117), channel_id=1, source_target_pairs={{1,8},{8,1},{9,16},{16,9},{17,24},{24,17},{3,10},{10,3},{11,18},{1... | collective-permute-start | bytes 294920 | tf_op jit(solution)/shard_map/ppermute | solution.py:105
  74.4 4.8 %collective-permute-start.20 = (f32[17,16,128]{2,1,0:T(8,128)S(1)}, f32[17,16,128]{2,1,0:T(8,128)S(1)}, u32[]{:S(2)}, u32[]{:S(2)}) collective-permute-start(f32[17,16,128]{2,1,0:T(8,128)S(1)} %get-tuple-element.124), channel_id=1, source_target_pairs={{0,1},{1,0},{2,3},{3,2},{4,5},{5,4},{6,7},{7,6},{8,9},{9,8},{10,11... | collective-permute-start | bytes 417800 | tf_op jit(solution)/shard_map/ppermute | solution.py:110
  79.2 0.7 collective-permute-start.21
  79.9 0.7 collective-permute-start.22
  80.6 0.7 collective-permute-start.23
  81.3 0.7 collective-permute-start.24
  82.1 21.2 %collective-permute-start.25 = (f32[2,16,128]{2,1,0:T(8,128)S(1)}, f32[2,16,128]{2,1,0:T(8,128)S(1)}, u32[]{:S(2)}, u32[]{:S(2)}) collective-permute-start(f32[2,16,128]{2,1,0:T(8,128)S(1)} %pad_maximum_fusion.4), channel_id=1, source_target_pairs={{1,0},{3,2},{5,4},{7,6},{9,8},{11,10},{13,12},{15,14},{17,16},{19,... | collective-permute-start | bytes 49160 | tf_op jit(solution)/shard_map/ppermute | solution.py:655

commit v4 on v3

--- a/solution.py
+++ b/solution.py
@@ -16,7 +16,6 @@
 
 VMEM = pl.BlockSpec(memory_space=pltpu.VMEM)
 SMEM = pl.BlockSpec(memory_space=pltpu.SMEM)
-HBM = pl.BlockSpec(memory_space=pltpu.HBM)
 
 
 def sds(*shape):
@@ -92,42 +91,30 @@
         body(r)
 
 
-def pair_perm(n, first):
-    pairs = []
-    for i in range(first, n - 1, 2):
-        pairs += [(i, i + 1), (i + 1, i)]
-    return pairs
-
-
-def exchange(axis, n, a, b):
-    return (
-        lax.ppermute(a, axis, pair_perm(n, 0)),
-        lax.ppermute(b, axis, pair_perm(n, 1)),
-    )
+def exchange_y(up, low, n):
+    from_below = lax.ppermute(up, "gy", [(i, (i + 1) % n) for i in range(n)])
+    from_above = lax.ppermute(low, "gy", [(i, (i - 1) % n) for i in range(n)])
+    return from_above, from_below
+
+
+def exchange_x(a, b, n):
+    even = [(i, i ^ 1) for i in range(n)]
+    odd = [(i, (i + (1 if i % 2 else -1)) % n) for i in range(n)]
+    return lax.ppermute(a, ("gx", "gz"), even), lax.ppermute(b, ("gx", "gz"), odd)
 
 
 def core_shift(value, n, j):
     return lax.ppermute(value, "gz", [(i, (i + j) % n) for i in range(n)])
 
 
-def prep_kernel(n, force, phase, table, *refs):
-    parts, eta_out, ids_buf, sems = refs[:n], refs[n], refs[n + 1], refs[n + 2]
+def prep_kernel(n, force, phase, table, *outs):
     core = lax.axis_index("gz")
-    rows = parts[0].shape[1]
+    rows = outs[0].shape[1]
+    eta_out = outs[n]
     levels = table.shape[0]
-    fetch = pltpu.make_async_copy(phase, ids_buf, sems.at[3 * n])
-    fetch.start()
-    copies = []
-    for j in range(n):
-        base = lax.rem(core + j, n) * rows
-        for c in range(3):
-            source = force.at[c, pl.ds(base, rows)]
-            copies.append(pltpu.make_async_copy(source, parts[j].at[c], sems.at[3 * j + c]))
-            copies[-1].start()
-    fetch.wait()
 
     def one(r):
-        ids = ids_buf[r]
+        ids = phase[r]
         eta = jnp.zeros(ids.shape, F32)
         for level in range(levels):
             eta = jnp.where(ids == level, table[level], eta)
@@ -138,18 +125,17 @@
         base = lax.rem(core + j, n) * rows
 
         def two(r, j=j, base=base):
-            parts[j][3, r] = eta_out[base + r]
+            for c in range(3):
+                outs[j][c, r] = force[c, base + r]
+            outs[j][3, r] = eta_out[base + r]
 
         rows_loop(0, rows, two, 4)
-    for copy in copies:
-        copy.wait()
 
 
 def gather_kernel(n, *refs):
     parts = refs[:n]
-    full, send_a, send_b = refs[n:]
+    full, send_up, send_low = refs[n:]
     core = lax.axis_index("gz")
-    odd = lax.rem(lax.axis_index("gy"), 2) == 1
     fields, rows, ys, _ = full.shape
     h = HALO
 
@@ -158,15 +144,13 @@
         def one(r, c=c):
             row = join_received([p[c, r] for p in parts], core)
             full[c, r] = row
-            low, high = row[:h], row[ys - h :]
-            send_a[c * rows + r] = jnp.where(odd, low, high)
-            send_b[c * rows + r] = jnp.where(odd, high, low)
+            send_low[c * rows + r] = row[:h]
+            send_up[c * rows + r] = row[ys - h :]
 
         rows_loop(0, rows, one, 4)
     for r in range(rows):
         line = full[3, r, ys - h - 1 : ys - h, :]
-        send_a[fields * rows + r // 4, r % 4 : r % 4 + 1, :] = line
-        send_b[fields * rows + r // 4, r % 4 : r % 4 + 1, :] = line
+        send_up[fields * rows + r // 4, r % 4 : r % 4 + 1, :] = line
 
 
 def edge_list(h):
@@ -180,8 +164,8 @@
     return tiles + [(3, -1, 0), (3, -1, 1)]
 
 
-def force_edges_kernel(full, got_a, got_b, send_a, send_b):
-    odd_y, odd_x, _ = odd_places()
+def force_edges_kernel(full, up, low, send_a, send_b):
+    odd_x = Place().odd
     _, rows, ys, _ = full.shape
     h = HALO
     for send, first in ((send_a, odd_x), (send_b, jnp.logical_not(odd_x))):
@@ -190,26 +174,19 @@
             if q < 2:
                 send[t] = full[c, r, 8 * q : 8 * q + 8, :]
             else:
-                a, b = got_a[c * rows + r], got_b[c * rows + r]
-                send[t, :h, :] = jnp.where(odd_y, b, a)
-                send[t, h:, :] = jnp.where(odd_y, a, b)
-
-
-def edges_kernel(p, got_a, got_b, *rest):
+                send[t, :h, :] = up[c * rows + r]
+                send[t, h:, :] = low[c * rows + r]
+
+
+def edges_kernel(p, up, low, *rest):
     send_a, send_b = rest[-2:]
-    odd_y = lax.rem(lax.axis_index("gy"), 2) == 1
-    place = lax.axis_index("gx") * lax.axis_size("gz") + lax.axis_index("gz")
-    odd_x = lax.rem(place, 2) == 1
-    rows, ys, _ = p.shape
-    h = HALO
-    for send, first in ((send_a, odd_x), (send_b, jnp.logical_not(odd_x))):
+    place = Place()
+    rows = p.shape[0]
+    h = HALO
+    for send, first in ((send_a, place.odd), (send_b, jnp.logical_not(place.odd))):
         start = jnp.where(first, 0, rows - h)
         for k in range(h):
-            r = start + k
-            a, b = got_a[r], got_b[r]
-            send[k, :ys, :] = p[r]
-            send[k, ys : ys + h, :] = jnp.where(odd_y, b, a)
-            send[k, ys + h :, :] = jnp.where(odd_y, a, b)
+            set_row(send, (k,), p[start + k], up[start + k], low[start + k], place)
 
 
 class Rows:
@@ -280,10 +257,9 @@
         emit(r - HALO, diverge(source, r))
 
 
-def emit_result(v_own, v_others, p_out, send_a, send_b, eta_at, sums=None):
+def emit_result(v_own, v_others, p_out, send_up, send_low, eta_at, sums=None):
     n = 1 + len(v_others)
     core = lax.axis_index("gz")
-    odd = lax.rem(lax.axis_index("gy"), 2) == 1
     h = HALO
 
     def emit(r, out):
@@ -296,9 +272,8 @@
         if p_out is not None:
             p = eta_at(r) * out
             p_out[r] = p
-            low, high = p[:h], p[ys - h :]
-            send_a[r] = jnp.where(odd, low, high)
-            send_b[r] = jnp.where(odd, high, low)
+            send_up[r] = p[ys - h :]
+            send_low[r] = p[:h]
         if sums is not None:
             sums(r, out)
 
@@ -315,16 +290,23 @@
     return lanes
 
 
-def odd_places():
-    place = lax.axis_index("gx") * lax.axis_size("gz") + lax.axis_index("gz")
-    return lax.rem(lax.axis_index("gy"), 2) == 1, lax.rem(place, 2) == 1, place
-
-
-def set_row(ref, index, row, a, b, odd_y):
-    ys, h = row.shape[0], a.shape[0]
+class Place:
+    def __init__(self):
+        chain = lax.axis_size("gx") * lax.axis_size("gz")
+        self.x = lax.axis_index("gx") * lax.axis_size("gz") + lax.axis_index("gz")
+        self.odd = lax.rem(self.x, 2) == 1
+        self.below_x, self.above_x = self.x > 0, self.x < chain - 1
+        y = lax.axis_index("gy")
+        self.below_y, self.above_y = y > 0, y < lax.axis_size("gy") - 1
+
+
+def set_row(ref, index, row, up, low, place=None):
+    ys, h = row.shape[0], up.shape[0]
+    if place is not None:
+        up, low = jnp.where(place.above_y, up, 0.0), jnp.where(place.below_y, low, 0.0)
     ref[(*index, slice(0, ys), slice(None))] = row
-    ref[(*index, slice(ys, ys + h), slice(None))] = jnp.where(odd_y, b, a)
-    ref[(*index, slice(ys + h, ys + 2 * h), slice(None))] = jnp.where(odd_y, a, b)
+    ref[(*index, slice(ys, ys + h), slice(None))] = up
+    ref[(*index, slice(ys + h, ys + 2 * h), slice(None))] = low
 
 
 def coefs_at(sizes, place, slots, lanes, rows, ys, flags):
@@ -365,24 +347,21 @@
     return coefs
 
 
-def first_inner(sizes, full, ya, yb, flags, kx, ky, kz, w, b, *rest):
+def first_inner(sizes, full, up, low, flags, kx, ky, kz, w, b, *rest):
     levels, (out, force, eta, line) = rest[: SWEEPS - 1], rest[SWEEPS - 1 :]
     fields, rows, ys, lanes = full.shape
     h = HALO
-    odd_y, _, place = odd_places()
+    place = Place().x
     slots, total = ys + 2 * h, rows + 2 * h
     for c in range(fields):
 
         def one(r, c=c):
-            row, a, b_ = full[c, r], ya[c * rows + r], yb[c * rows + r]
-            if c < 3:
-                set_row(force, (c, r + h), row, a, b_, odd_y)
-            else:
-                set_row(eta, (r + h,), row, a, b_, odd_y)
+            to, index = (force, (c, r + h)) if c < 3 else (eta, (r + h,))
+            set_row(to, index, full[c, r], up[c * rows + r], low[c * rows + r])
 
         rows_loop(0, rows, one, 4)
     for q in range(rows // 4):
-        block = jnp.where(odd_y, ya[fields * rows + q], yb[fields * rows + q])
+        block = low[fields * rows + q]
         for k in range(4):
             line[h + 4 * q + k] = block[k : k + 1]
     coefs = coefs_at(sizes, place, slots, lanes, rows, ys, flags)
@@ -396,25 +375,24 @@
 
 
 def first_outer(n, sizes, *refs):
-    full, ya, yb, xa, xb, flags, *early = refs[: 11 + SWEEPS]
+    full, up, low, xa, xb, flags, *early = refs[: 11 + SWEEPS]
     kx0, ky0, kz0, w0, b0, *levels, out0 = early
     refs = refs[11 + SWEEPS :]
     v_own, v_others, refs = refs[0], refs[1:n], refs[n:]
-    p_out, send_a, send_b, kx, ky, kz, w = refs[:7]
+    p_out, send_up, send_low, kx, ky, kz, w = refs[:7]
     force, eta, line, b, *buffers = refs[7:]
     fields, rows, ys, lanes = full.shape
     h = HALO
-    odd_y, odd_x, place = odd_places()
+    place, odd_x = Place().x, Place().odd
     slots, total = ys + 2 * h, rows + 2 * h
     ranges, inner = spans(h + 1, h + rows - 1, total)
     todo = outside((0, total), inner[0])
     for r in sorted({min(max(q + d, h), h + rows - 1) for q in todo for d in (-1, 0, 1)}):
         k = r - h
-        for c in range(3):
-            set_row(force, (c, r), full[c, k], ya[c * rows + k], yb[c * rows + k], odd_y)
-        set_row(eta, (r + 1,), full[3, k], ya[3 * rows + k], yb[3 * rows + k], odd_y)
-        block = fields * rows + k // 4
-        line[r] = jnp.where(odd_y, ya[block], yb[block])[k % 4 : k % 4 + 1]
+        for c in range(fields):
+            to, index = (force, (c, r)) if c < 3 else (eta, (r + 1,))
+            set_row(to, index, full[c, k], up[c * rows + k], low[c * rows + k])
+        line[r] = low[fields * rows + k // 4, k % 4 : k % 4 + 1, :]
     blank = jnp.zeros((slots, lanes), F32)
     line_blank = jnp.zeros((1, lanes), F32)
     for k in range(h):
@@ -446,20 +424,20 @@
 
     rows_loop(*inner[0], carry, 2)
     b = Rows(b0, b, *inner[0])
-    emit = emit_result(v_own, v_others, p_out, send_a, send_b, lambda r: full[3, r])
+    emit = emit_result(v_own, v_others, p_out, send_up, send_low, lambda r: full[3, r])
     outer_solve(b, levels, buffers, inner, ranges, w, kx, ky, kz, emit)
     rows_loop(inner[SWEEPS][0] - h, inner[SWEEPS][1] - h, lambda r: emit(r, out0[r]), 4)
 
 
-def next_inner(extra, p_in, ya, yb, kx, ky, kz, w, *rest):
+def next_inner(extra, p_in, up, low, kx, ky, kz, w, *rest):
     p, b, *rest = rest[extra:]
     levels, out = rest[: SWEEPS - 1], rest[SWEEPS - 1]
     rows = p_in.shape[0]
     h = HALO
-    odd_y, _, _ = odd_places()
+    place = Place()
 
     def fill(r):
-        set_row(p, (r + h,), p_in[r], ya[r], yb[r], odd_y)
+        set_row(p, (r + h,), p_in[r], up[r], low[r], place)
 
     rows_loop(0, rows, fill, 4)
     _, inner = spans(h, h + rows - 1, rows + 2 * h)
@@ -481,7 +459,7 @@
     if last:
         partials, refs = refs[:ITERS], refs[ITERS:]
     v_own, v_others, refs = refs[0], refs[1:n], refs[n:]
-    p_out = send_a = send_b = sums = None
+    p_out = send_up = send_low = sums = None
     if last:
         moment, acc, refs = v_others[-1].at[p_in.shape[0]], refs[-1], refs[:-1]
         acc[...] = jnp.zeros_like(acc)
@@ -489,21 +467,21 @@
         def sums(r, v):
             acc[...] = acc[...] + v * p_in[r]
     else:
-        p_out, send_a, send_b, *refs = refs
+        p_out, send_up, send_low, *refs = refs
     p, b, *buffers = refs
     rows = p_in.shape[0]
     h = HALO
-    _, odd_x, _ = odd_places()
+    place = Place()
     for k in range(h):
-        a, b_ = xa[k], xb[k]
-        p[k] = jnp.where(odd_x, a, b_)
-        p[h + rows + k] = jnp.where(odd_x, b_, a)
+        lower, upper = jnp.where(place.odd, xa[k], xb[k]), jnp.where(place.odd, xb[k], xa[k])
+        p[k] = jnp.where(place.below_x, lower, 0.0)
+        p[h + rows + k] = jnp.where(place.above_x, upper, 0.0)
     ranges, inner = spans(h, h + rows - 1, rows + 2 * h)
     p = Rows(p0, p, h, h + rows)
     for r in outside(ranges[0], inner[0]):
         grads(p, w, b, r)
     b = Rows(b0, b, *inner[0])
-    emit = emit_result(v_own, v_others, p_out, send_a, send_b, lambda r: full[3, r], sums)
+    emit = emit_result(v_own, v_others, p_out, send_up, send_low, lambda r: full[3, r], sums)
     outer_solve(b, levels, buffers, inner, ranges, w, kx, ky, kz, emit)
     rows_loop(inner[SWEEPS][0] - h, inner[SWEEPS][1] - h, lambda r: emit(r, out0[r]), 4)
     if last:
@@ -638,22 +616,20 @@
     return jnp.stack([s, e + (a[1] + b[1])])
 
 
-def reduce_all(pair, nx, ny, nz):
-    axes = ("gx", "gy", "gz")
-    places = [(x, y, z) for x in range(nx) for y in range(ny) for z in range(nz)]
-    number = {place: k for k, place in enumerate(places)}
-    for axis, n, step in ((0, nx, 1), (1, ny, 1), (2, nz, 2)):
-        while step < n:
-            moves = []
-            for place in places:
-                other = list(place)
-                other[axis] ^= step
-                if place[2] % 2 == 1:
-                    moves.append((number[place], number[tuple(other)]))
-            pair = add_pairs(pair, lax.ppermute(pair, axes, moves))
-            step *= 2
-    handed = lax.ppermute(pair, "gz", [(k, k - 1) for k in range(1, nz, 2)])
-    return jnp.where(lax.rem(lax.axis_index("gz"), 2) == 1, pair, handed)
+def sum_along(pair, axis, n, stride=1):
+    count = n // stride
+    if count < 2:
+        return pair
+    terms = [pair]
+    for k in range(1, count):
+        moves = [(i, (i + k * stride) % n) for i in range(n)]
+        terms.append(lax.ppermute(pair, axis, moves))
+    me = lax.axis_index(axis) // stride
+    terms = [pick(terms, lax.rem(me - j + count, count)) for j in range(count)]
+    while len(terms) > 1:
+        rest = terms[len(terms) // 2 * 2 :]
+        terms = [add_pairs(a, b) for a, b in zip(terms[::2], terms[1::2])] + rest
+    return terms[0]
 
 
 def per_device(nx, ny, nz, force, phase, table, flags):
@@ -670,23 +646,25 @@
         functools.partial(prep_kernel, nz),
         [sds(4, rows, ys, lanes)] * nz + [sds(*phase.shape)],
         (force, phase, table),
-        [HBM, HBM, SMEM],
-        [pltpu.VMEM(phase.shape, jnp.int32), pltpu.SemaphoreType.DMA((3 * nz + 1,))],
+        [VMEM, VMEM, SMEM],
         name="prep",
     )
     eta = parts[-1]
     parts = [parts[0]] + [core_shift(parts[j], nz, j) for j in range(1, nz)]
-    edge = sds(4 * rows + rows // 4, h, zs)
     full, ya, yb = call(
         functools.partial(gather_kernel, nz),
-        [sds(4, rows, ys, zs), edge, edge],
+        [
+            sds(4, rows, ys, zs),
+            sds(4 * rows + rows // 4, h, zs),
+            sds(4 * rows, h, zs),
+        ],
         parts,
         name="gather",
     )
-    ya, yb = exchange("gy", ny, ya, yb)
+    ya, yb = exchange_y(ya, yb, ny)
     edge = sds(len(edge_list(h)), 8, zs)
     xa, xb = call(force_edges_kernel, [edge, edge], (full, ya, yb), name="force_edges")
-    xa, xb = exchange(("gx", "gz"), chain, xa, xb)
+    xa, xb = exchange_x(xa, xb, chain)
 
     v_shape = [sds(rows, ys, lanes)] * nz
     sent = [sds(rows, ys, zs), sds(rows, h, zs), sds(rows, h, zs)]
@@ -731,10 +709,10 @@
                 name="moments",
             )[0]
         )
-        ya, yb = exchange("gy", ny, ya, yb)
+        ya, yb = exchange_y(ya, yb, ny)
         edge = sds(h, slots, zs)
         xa, xb = call(edges_kernel, [edge, edge], (p, ya, yb, moments[-1]), name="edges")
-        xa, xb = exchange(("gx", "gz"), chain, xa, xb)
+        xa, xb = exchange_x(xa, xb, chain)
         early = call(
             functools.partial(next_inner, nz - 1),
             [scalar] + [vector] * SWEEPS + [sds(rows, slots, zs)],
@@ -768,7 +746,8 @@
     if nz > 2:
         theirs = lax.ppermute(mine, "gz", [(k, k ^ 1) for k in range(nz)])
     pair = jnp.stack(two_sum(mine, theirs))
-    pair = reduce_all(pair, nx, ny, nz)
+    pair = sum_along(pair, "gz", nz, 2)
+    pair = sum_along(sum_along(pair, "gx", nx), "gy", ny)
     pressure, residual, norms = call(
         functools.partial(last_kernel, nz, cells),
         [sds(*phase.shape), sds(*phase.shape), sds(ITERS)],

time: 106 us -> 98 us (0.925)
  starting transfers between devices: 45.3 us -> 25.9 us
  waiting for transfers between devices: 28.8 us -> 42.2 us
  Pallas kernels: 27.2 us -> 25.9 us
    ppermute x5, starting transfers between devices: 18.2 us -> 0.64 us  [core_shift(): return lax.ppermute(value, 'gz', [(i, (i + j) % n) for i in range(n)])]
    ppermute x21 -> x22, waiting for transfers between devices: 26.2 us -> 39.3 us  [the longest x4 18.3 us: exchange_y(): from_above = lax.ppermute(low, 'gy', [(i, (i - 1) % n) for i in range(n)])]
    ppermute x21 -> x22, starting transfers between devices: 27.2 us -> 25.2 us  [the longest x4 7.24 us: exchange_x(): lax.ppermute(b, ('gx', 'gz'), odd)]
    pallas_call x18, Pallas kernels: 27.2 us -> 25.9 us  [call(): pl.pallas_call(kernel, out_shape=outs, in_specs=specs or [VMEM] * len(ins...]
  transfers between devices with their start and end apart: 26 -> 27, of which waited for: 4 -> 16; matrix products, arithmetic and copies ran while one was open for 0% -> 0% of each run, Pallas kernels for 15% -> 16%
where the time goes in v4:
time: 98 us; the launch traced here: 97.8 us
  waiting for transfers between devices  42.2 us (43%)
  Pallas kernels  25.9 us (26%)
  starting transfers between devices  25.9 us (26%)
  local copies, waits for them, and re-layouts  2.73 us (3%)
  between operations  1.03 us (1%)
    pallas_call x18, Pallas kernels, call(): pl.pallas_call(kernel, out_shape=outs, in_specs=specs or [VMEM] * len(ins...  25.9 us
    ppermute x4, waiting for transfers between devices, exchange_y(): from_above = lax.ppermute(low, 'gy', [(i, (i - 1) % n) for i in range(n)])  18.3 us
    ppermute x4, waiting for transfers between devices, exchange_y(): from_below = lax.ppermute(up, 'gy', [(i, (i + 1) % n) for i in range(n)])  8.71 us
    ppermute x6, waiting for transfers between devices, sum_along(): terms.append(lax.ppermute(pair, axis, moves))  8.29 us
    ppermute x4, starting transfers between devices, exchange_x(): lax.ppermute(b, ('gx', 'gz'), odd)  7.24 us
    ppermute x6, starting transfers between devices, sum_along(): terms.append(lax.ppermute(pair, axis, moves))  6.11 us
    ppermute x4, starting transfers between devices, exchange_y(): from_above = lax.ppermute(low, 'gy', [(i, (i - 1) % n) for i in range(n)])  5.93 us
    ppermute x4, starting transfers between devices, exchange_y(): from_below = lax.ppermute(up, 'gy', [(i, (i + 1) % n) for i in range(n)])  5.66 us
  transfers between devices with their start and end apart: 27, of which 16 were waited for; matrix products, arithmetic and copies ran while one was open for 0% of the time, Pallas kernels for 16%

profile of v4, /device:TPU:0, one launch (start us, length us, event | category | flops | bytes accessed | tf_op | source)
XLA Modules:
  0.0 97.8 jit_solution(8920816275380858808)
XLA Ops:
  4.8 1.5 %collective-permute-done.refs_1_ = f32[4,16,16,128]{3,2,1,0:T(8,128)S(1)} collective-permute-done((f32[4,16,16,128]{3,2,1,0:T(8,128)S(1)}, f32[4,16,16,128]{3,2,1,0:T(8,128)S(1)}, u32[]{:S(2)}, u32[]{:S(2)}) %collective-permute-start) | collective-permute-done | bytes 524320 | tf_op jit(solution)/shard_map/ppermute | solution.py:107
  6.5 3.0 %collective-permute-start.2 = (f32[68,4,256]{2,1,0:T(4,128)S(1)}, f32[68,4,256]{2,1,0:T(4,128)S(1)}, u32[]{:S(2)}, u32[]{:S(2)}) collective-permute-start(f32[68,4,256]{2,1,0:T(4,128)S(1)} %get-tuple-element.69), channel_id=1, source_target_pairs={{0,2},{2,4},{4,6},{6,0},{1,3},{3,5},{5,7},{7,1},{8,10},{10,12},{12... | collective-permute-start | bytes 835592 | tf_op jit(solution)/shard_map/ppermute | solution.py:95
  9.4 2.1 %collective-permute-start.1 = (f32[64,4,256]{2,1,0:T(4,128)S(1)}, f32[64,4,256]{2,1,0:T(4,128)S(1)}, u32[]{:S(2)}, u32[]{:S(2)}) collective-permute-start(f32[64,4,256]{2,1,0:T(4,128)S(1)} %get-tuple-element.68), channel_id=1, source_target_pairs={{0,6},{2,0},{4,2},{6,4},{1,7},{3,1},{5,3},{7,5},{8,14},{10,8},{12,... | collective-permute-start | bytes 786440 | tf_op jit(solution)/shard_map/ppermute | solution.py:96
  11.5 11.9 %collective-permute-done.1.up.refs_1_ = f32[64,4,256]{2,1,0:T(4,128)S(1)} collective-permute-done((f32[64,4,256]{2,1,0:T(4,128)S(1)}, f32[64,4,256]{2,1,0:T(4,128)S(1)}, u32[]{:S(2)}, u32[]{:S(2)}) %collective-permute-start.1) | collective-permute-done | bytes 262176 | tf_op jit(solution)/shard_map/ppermute | solution.py:96
  23.6 2.5 %collective-permute-start.4 = (f32[43,8,256]{2,1,0:T(8,128)S(1)}, f32[43,8,256]{2,1,0:T(8,128)S(1)}, u32[]{:S(2)}, u32[]{:S(2)}) collective-permute-start(f32[43,8,256]{2,1,0:T(8,128)S(1)} %get-tuple-element.71), channel_id=1, source_target_pairs={{0,25},{1,8},{8,1},{9,16},{16,9},{17,24},{24,17},{25,0},{2,27},{3,... | collective-permute-start | bytes 1056776 | tf_op jit(solution)/shard_map/ppermute | solution.py:103
  26.2 4.7 %first_inner.1 = (f32[24,24,256]{2,1,0:T(8,128)S(1)}, f32[24,24,256]{2,1,0:T(8,128)S(1)}, f32[24,24,256]{2,1,0:T(8,128)S(1)}, f32[3,24,24,256]{3,2,1,0:T(8,128)S...) custom-call(f32[4,16,16,256]{3,2,1,0:T(8,128)S(1)} %get-tuple-elemen, ...), custom_call_target="tpu_custom_call" | custom-call | flops 40000000 | bytes 1048576 | tf_op jit(solution)/shard_map/first_inner/pallas_call | solution.py:26
  30.9 3.6 %collective-permute-done.4.refs_4_ = f32[43,8,256]{2,1,0:T(8,128)S(1)} collective-permute-done((f32[43,8,256]{2,1,0:T(8,128)S(1)}, f32[43,8,256]{2,1,0:T(8,128)S(1)}, u32[]{:S(2)}, u32[]{:S(2)}) %collective-permute-start.4) | collective-permute-done | bytes 352288 | tf_op jit(solution)/shard_map/ppermute | solution.py:103
  34.5 2.8 %first.1 = (f32[16,16,128]{2,1,0:T(8,128)S(1)}, f32[16,16,128]{2,1,0:T(8,128)S(1)}, f32[16,16,256]{2,1,0:T(8,128)S(1)}, f32[16,4,256]{2,1,0:T(4,128)S(1)}, f32[1...) custom-call(f32[4,16,16,256]{3,2,1,0:T(8,128)S(1)} %get-tuple-elemen, ...), custom_call_target="tpu_custom_call" | custom-call | flops 40000000 | bytes 1048576 | tf_op jit(solution)/shard_map/first/pallas_call | solution.py:26
  37.3 2.4 %collective-permute-start.5 = (f32[16,4,256]{2,1,0:T(4,128)S(1)}, f32[16,4,256]{2,1,0:T(4,128)S(1)}, u32[]{:S(2)}, u32[]{:S(2)}) collective-permute-start(f32[16,4,256]{2,1,0:T(4,128)S(1)} %get-tuple-element.82), channel_id=1, source_target_pairs={{0,6},{2,0},{4,2},{6,4},{1,7},{3,1},{5,3},{7,5},{8,14},{10,8},{12,... | collective-permute-start | bytes 196616 | tf_op jit(solution)/shard_map/ppermute | solution.py:96
  39.7 2.2 %collective-permute-done.5.up = f32[16,4,256]{2,1,0:T(4,128)S(1)} collective-permute-done((f32[16,4,256]{2,1,0:T(4,128)S(1)}, f32[16,4,256]{2,1,0:T(4,128)S(1)}, u32[]{:S(2)}, u32[]{:S(2)}) %collective-permute-start.5) | collective-permute-done | bytes 65568 | tf_op jit(solution)/shard_map/ppermute | solution.py:96
  42.0 3.7 %collective-permute-done.6.low = f32[16,4,256]{2,1,0:T(4,128)S(1)} collective-permute-done((f32[16,4,256]{2,1,0:T(4,128)S(1)}, f32[16,4,256]{2,1,0:T(4,128)S(1)}, u32[]{:S(2)}, u32[]{:S(2)}) %collective-permute-start.6) | collective-permute-done | bytes 65568 | tf_op jit(solution)/shard_map/ppermute | solution.py:95
  45.8 1.8 %collective-permute-start.8 = (f32[4,24,256]{2,1,0:T(8,128)S(1)}, f32[4,24,256]{2,1,0:T(8,128)S(1)}, u32[]{:S(2)}, u32[]{:S(2)}) collective-permute-start(f32[4,24,256]{2,1,0:T(8,128)S(1)} %get-tuple-element.87), channel_id=1, source_target_pairs={{0,25},{1,8},{8,1},{9,16},{16,9},{17,24},{24,17},{25,0},{2,27},{3,... | collective-permute-start | bytes 294920 | tf_op jit(solution)/shard_map/ppermute | solution.py:103
  47.6 3.5 %next_inner.3 = (f32[24,24,256]{2,1,0:T(8,128)S(1)}, f32[3,24,24,256]{3,2,1,0:T(8,128)S(1)}, f32[3,24,24,256]{3,2,1,0:T(8,128)S(1)}, f32[3,24,24,256]{3,2,1,0:T(...) custom-call(f32[16,16,256]{2,1,0:T(8,128)S(1)} %get-tuple-element.81.refs_0_.p.p_in.refs_1_, ...), custom_call_target="tpu_custom_call" | custom-call | flops 40000000 | bytes 1048576 | tf_op jit(solution)/shard_map/next_inner/pallas_call | solution.py:26
  51.1 1.4 %next.3 = (f32[16,16,128]{2,1,0:T(8,128)S(1)}, f32[16,16,128]{2,1,0:T(8,128)S(1)}, f32[16,16,256]{2,1,0:T(8,128)S(1)}, f32[16,4,256]{2,1,0:T(4,128)S(1)}, f32[16,4,256]{2,1,0:T(4,128)S(1)}) custom-call(f32[16,16,256]{2,1,0:T(8,128)S(1)} %get-tuple-element.81.refs_0_.p.p_in.refs_1_, f32[4,24,256]{2,1,0:T(8,128)S(1)} %collective-permute-done.7.xa, ...), custom_call_target="tpu_custom_call" | custom-call | flops 40000000 | bytes 1048576 | tf_op jit(solution)/shard_map/next/pallas_call | solution.py:26
  53.3 1.3 %collective-permute-start.11 = (f32[16,4,256]{2,1,0:T(4,128)S(1)}, f32[16,4,256]{2,1,0:T(4,128)S(1)}, u32[]{:S(2)}, u32[]{:S(2)}) collective-permute-start(f32[16,4,256]{2,1,0:T(4,128)S(1)} %get-tuple-element.100), channel_id=1, source_target_pairs={{0,2},{2,4},{4,6},{6,0},{1,3},{3,5},{5,7},{7,1},{8,10},{10,12},{12... | collective-permute-start | bytes 196616 | tf_op jit(solution)/shard_map/ppermute | solution.py:95
  54.8 2.1 %collective-permute-done.10.up = f32[16,4,256]{2,1,0:T(4,128)S(1)} collective-permute-done((f32[16,4,256]{2,1,0:T(4,128)S(1)}, f32[16,4,256]{2,1,0:T(4,128)S(1)}, u32[]{:S(2)}, u32[]{:S(2)}) %collective-permute-start.10) | collective-permute-done | bytes 65568 | tf_op jit(solution)/shard_map/ppermute | solution.py:96
  56.9 2.5 %collective-permute-done.11.low = f32[16,4,256]{2,1,0:T(4,128)S(1)} collective-permute-done((f32[16,4,256]{2,1,0:T(4,128)S(1)}, f32[16,4,256]{2,1,0:T(4,128)S(1)}, u32[]{:S(2)}, u32[]{:S(2)}) %collective-permute-start.11) | collective-permute-done | bytes 65568 | tf_op jit(solution)/shard_map/ppermute | solution.py:95
  60.8 3.5 %next_inner.4 = (f32[24,24,256]{2,1,0:T(8,128)S(1)}, f32[3,24,24,256]{3,2,1,0:T(8,128)S(1)}, f32[3,24,24,256]{3,2,1,0:T(8,128)S(1)}, f32[3,24,24,256]{3,2,1,0:T(...) custom-call(f32[16,16,256]{2,1,0:T(8,128)S(1)} %get-tuple-element.98.refs_0_.p.p_in.refs_1_, ...), custom_call_target="tpu_custom_call" | custom-call | flops 40000000 | bytes 1048576 | tf_op jit(solution)/shard_map/next_inner/pallas_call | solution.py:26
  64.7 1.4 %next.4 = (f32[16,16,128]{2,1,0:T(8,128)S(1)}, f32[16,16,128]{2,1,0:T(8,128)S(1)}, f32[16,16,256]{2,1,0:T(8,128)S(1)}, f32[16,4,256]{2,1,0:T(4,128)S(1)}, f32[16,4,256]{2,1,0:T(4,128)S(1)}) custom-call(f32[16,16,256]{2,1,0:T(8,128)S(1)} %get-tuple-element.98.refs_0_.p.p_in.refs_1_, f32[4,24,256]{2,1,0:T(8,128)S(1)} %collective-permute-done.12.xa, ...), custom_call_target="tpu_custom_call" | custom-call | flops 40000000 | bytes 1048576 | tf_op jit(solution)/shard_map/next/pallas_call | solution.py:26
  66.8 1.4 %collective-permute-start.16 = (f32[16,4,256]{2,1,0:T(4,128)S(1)}, f32[16,4,256]{2,1,0:T(4,128)S(1)}, u32[]{:S(2)}, u32[]{:S(2)}) collective-permute-start(f32[16,4,256]{2,1,0:T(4,128)S(1)} %get-tuple-element.113), channel_id=1, source_target_pairs={{0,2},{2,4},{4,6},{6,0},{1,3},{3,5},{5,7},{7,1},{8,10},{10,12},{12... | collective-permute-start | bytes 196616 | tf_op jit(solution)/shard_map/ppermute | solution.py:95
  68.4 2.1 %collective-permute-done.15.up = f32[16,4,256]{2,1,0:T(4,128)S(1)} collective-permute-done((f32[16,4,256]{2,1,0:T(4,128)S(1)}, f32[16,4,256]{2,1,0:T(4,128)S(1)}, u32[]{:S(2)}, u32[]{:S(2)}) %collective-permute-start.15) | collective-permute-done | bytes 65568 | tf_op jit(solution)/shard_map/ppermute | solution.py:96
  70.4 2.4 %collective-permute-done.16.low = f32[16,4,256]{2,1,0:T(4,128)S(1)} collective-permute-done((f32[16,4,256]{2,1,0:T(4,128)S(1)}, f32[16,4,256]{2,1,0:T(4,128)S(1)}, u32[]{:S(2)}, u32[]{:S(2)}) %collective-permute-start.16) | collective-permute-done | bytes 65568 | tf_op jit(solution)/shard_map/ppermute | solution.py:95
  73.0 1.6 %collective-permute-start.18 = (f32[4,24,256]{2,1,0:T(8,128)S(1)}, f32[4,24,256]{2,1,0:T(8,128)S(1)}, u32[]{:S(2)}, u32[]{:S(2)}) collective-permute-start(f32[4,24,256]{2,1,0:T(8,128)S(1)} %get-tuple-element.117), channel_id=1, source_target_pairs={{0,25},{1,8},{8,1},{9,16},{16,9},{17,24},{24,17},{25,0},{2,27},{3,... | collective-permute-start | bytes 294920 | tf_op jit(solution)/shard_map/ppermute | solution.py:103
  74.6 3.6 %next_inner.5 = (f32[24,24,256]{2,1,0:T(8,128)S(1)}, f32[3,24,24,256]{3,2,1,0:T(8,128)S(1)}, f32[3,24,24,256]{3,2,1,0:T(8,128)S(1)}, f32[3,24,24,256]{3,2,1,0:T(...) custom-call(f32[16,16,256]{2,1,0:T(8,128)S(1)} %get-tuple-element.111.refs_0_.p.p_in, ...), custom_call_target="tpu_custom_call" | custom-call | flops 40000000 | bytes 1048576 | tf_op jit(solution)/shard_map/next_inner/pallas_call | solution.py:26
  78.3 1.4 %next.5 = (f32[16,16,128]{2,1,0:T(8,128)S(1)}, f32[17,16,128]{2,1,0:T(8,128)S(1)}) custom-call(f32[16,16,256]{2,1,0:T(8,128)S(1)} %get-tuple-element.111.refs_0_.p.p_in, f32[4,24,256]{2,1,0:T(8,128)S(1)} %collective-permute-done.17.xa, f32[4,24,256]{2,1,0:T(8,128)S(1)} %collective-permute-done.18.xb, f32[4,16,16,256]{3,2,1,0:T(8,128)S(1)} %get-tuple-element.67.full.refs_0_, ...), custom_call_target="tpu_custom_call" | custom-call | flops 40000000 | bytes 1048576 | tf_op jit(solution)/shard_map/next/pallas_call | solution.py:26
  79.8 1.3 %collective-permute-done.20.refs_7_ = f32[17,16,128]{2,1,0:T(8,128)S(1)} collective-permute-done((f32[17,16,128]{2,1,0:T(8,128)S(1)}, f32[17,16,128]{2,1,0:T(8,128)S(1)}, u32[]{:S(2)}, u32[]{:S(2)}) %collective-permute-start.20) | collective-permute-done | bytes 139296 | tf_op jit(solution)/shard_map/ppermute | solution.py:107
  81.2 1.9 %collective-permute-start.21 = (f32[2,16,128]{2,1,0:T(8,128)S(1)}, f32[2,16,128]{2,1,0:T(8,128)S(1)}, u32[]{:S(2)}, u32[]{:S(2)}) collective-permute-start(f32[2,16,128]{2,1,0:T(8,128)S(1)} %pad_maximum_fusion), channel_id=1, source_target_pairs={{0,24},{8,0},{16,8},{24,16},{1,25},{9,1},{17,9},{25,17},{2,26},{10... | collective-permute-start | bytes 49160 | tf_op jit(solution)/shard_map/ppermute | solution.py:626
  85.2 1.7 %collective-permute-done.22 = f32[2,16,128]{2,1,0:T(8,128)S(1)} collective-permute-done((f32[2,16,128]{2,1,0:T(8,128)S(1)}, f32[2,16,128]{2,1,0:T(8,128)S(1)}, u32[]{:S(2)}, u32[]{:S(2)}) %collective-permute-start.22) | collective-permute-done | bytes 16416 | tf_op jit(solution)/shard_map/ppermute | solution.py:626
  86.8 2.0 %collective-permute-done.23 = f32[2,16,128]{2,1,0:T(8,128)S(1)} collective-permute-done((f32[2,16,128]{2,1,0:T(8,128)S(1)}, f32[2,16,128]{2,1,0:T(8,128)S(1)}, u32[]{:S(2)}, u32[]{:S(2)}) %collective-permute-start.23) | collective-permute-done | bytes 16416 | tf_op jit(solution)/shard_map/ppermute | solution.py:626
  91.0 1.9 %collective-permute-done.24 = f32[2,16,128]{2,1,0:T(8,128)S(1)} collective-permute-done((f32[2,16,128]{2,1,0:T(8,128)S(1)}, f32[2,16,128]{2,1,0:T(8,128)S(1)}, u32[]{:S(2)}, u32[]{:S(2)}) %collective-permute-start.24) | collective-permute-done | bytes 16416 | tf_op jit(solution)/shard_map/ppermute | solution.py:626
  94.1 1.5 %collective-permute-done.26 = f32[2,16,128]{2,1,0:T(8,128)S(1)} collective-permute-done((f32[2,16,128]{2,1,0:T(8,128)S(1)}, f32[2,16,128]{2,1,0:T(8,128)S(1)}, u32[]{:S(2)}, u32[]{:S(2)}) %collective-permute-start.26) | collective-permute-done | bytes 16416 | tf_op jit(solution)/shard_map/ppermute | solution.py:626
  95.7 2.0 %last.1 = (f32[32,16,128]{2,1,0:T(8,128)}, f32[32,16,128]{2,1,0:T(8,128)}, f32[3]{0:T(128)}) custom-call(f32[2,16,128]{2,1,0:T(8,128)S(1)} %pad_maximum_fusion.2.sums, f32[32,16,128]{2,1,0:T(8,128)S(1)} %get-tuple-element.125.eta, f32[16,16,128]{2,1,0:T(8,128)S(1)} %get-tuple-element.84.refs_1_.refs_2_.refs_0_, ...), custom_call_target="tpu_custom_call" | custom-call | flops 1000000 | bytes 1048576 | tf_op jit(solution)/shard_map/last/pallas_call | solution.py:26
  (58 shorter events, 13.8 us)
Async XLA Ops:
  0.6 1.1 %copy-start = (f32[3,32,16,128]{3,2,1,0:T(8,128)S(1)}, f32[3,32,16,128]{3,2,1,0:T(8,128)}, u32[]{:S(2)}) copy-start(f32[3,32,16,128]{3,2,1,0:T(8,128)} %force.1) | copy-start | bytes 2359300
  1.8 0.9 copy-start.1
  2.7 0.7 copy-start.3
  3.4 22.8 %copy-start.2 = (s32[6]{0:T(128)S(1)}, s32[6]{0:T(128)}, u32[]{:S(2)}) copy-start(s32[6]{0:T(128)} %refs_5_.1) | copy-start | bytes 76
  4.2 2.1 %collective-permute-start = (f32[4,16,16,128]{3,2,1,0:T(8,128)S(1)}, f32[4,16,16,128]{3,2,1,0:T(8,128)S(1)}, u32[]{:S(2)}, u32[]{:S(2)}) collective-permute-start(f32[4,16,16,128]{3,2,1,0:T(8,128)S(1)} %get-tuple-element.66), channel_id=1, source_target_pairs={{0,1},{1,0},{2,3},{3,2},{4,5},{5,4},{6,7},{7,6},{8,9},{9,8},{10,11... | collective-permute-start | bytes 1572872 | tf_op jit(solution)/shard_map/ppermute | solution.py:107
  6.5 17.0 %collective-permute-start.2 = (f32[68,4,256]{2,1,0:T(4,128)S(1)}, f32[68,4,256]{2,1,0:T(4,128)S(1)}, u32[]{:S(2)}, u32[]{:S(2)}) collective-permute-start(f32[68,4,256]{2,1,0:T(4,128)S(1)} %get-tuple-element.69), channel_id=1, source_target_pairs={{0,2},{2,4},{4,6},{6,0},{1,3},{3,5},{5,7},{7,1},{8,10},{10,12},{12... | collective-permute-start | bytes 835592 | tf_op jit(solution)/shard_map/ppermute | solution.py:95
  9.4 14.0 %collective-permute-start.1 = (f32[64,4,256]{2,1,0:T(4,128)S(1)}, f32[64,4,256]{2,1,0:T(4,128)S(1)}, u32[]{:S(2)}, u32[]{:S(2)}) collective-permute-start(f32[64,4,256]{2,1,0:T(4,128)S(1)} %get-tuple-element.68), channel_id=1, source_target_pairs={{0,6},{2,0},{4,2},{6,4},{1,7},{3,1},{5,3},{7,5},{8,14},{10,8},{12,... | collective-permute-start | bytes 786440 | tf_op jit(solution)/shard_map/ppermute | solution.py:96
  23.6 7.3 %collective-permute-start.3 = (f32[43,8,256]{2,1,0:T(8,128)S(1)}, f32[43,8,256]{2,1,0:T(8,128)S(1)}, u32[]{:S(2)}, u32[]{:S(2)}) collective-permute-start(f32[43,8,256]{2,1,0:T(8,128)S(1)} %get-tuple-element.70), channel_id=1, source_target_pairs={{0,1},{1,0},{8,9},{9,8},{16,17},{17,16},{24,25},{25,24},{2,3},{3,2... | collective-permute-start | bytes 1056776 | tf_op jit(solution)/shard_map/ppermute | solution.py:103
  23.6 10.8 %collective-permute-start.4 = (f32[43,8,256]{2,1,0:T(8,128)S(1)}, f32[43,8,256]{2,1,0:T(8,128)S(1)}, u32[]{:S(2)}, u32[]{:S(2)}) collective-permute-start(f32[43,8,256]{2,1,0:T(8,128)S(1)} %get-tuple-element.71), channel_id=1, source_target_pairs={{0,25},{1,8},{8,1},{9,16},{16,9},{17,24},{24,17},{25,0},{2,27},{3,... | collective-permute-start | bytes 1056776 | tf_op jit(solution)/shard_map/ppermute | solution.py:103
  37.3 4.7 %collective-permute-start.5 = (f32[16,4,256]{2,1,0:T(4,128)S(1)}, f32[16,4,256]{2,1,0:T(4,128)S(1)}, u32[]{:S(2)}, u32[]{:S(2)}) collective-permute-start(f32[16,4,256]{2,1,0:T(4,128)S(1)} %get-tuple-element.82), channel_id=1, source_target_pairs={{0,6},{2,0},{4,2},{6,4},{1,7},{3,1},{5,3},{7,5},{8,14},{10,8},{12,... | collective-permute-start | bytes 196616 | tf_op jit(solution)/shard_map/ppermute | solution.py:96
  39.6 6.1 %collective-permute-start.6 = (f32[16,4,256]{2,1,0:T(4,128)S(1)}, f32[16,4,256]{2,1,0:T(4,128)S(1)}, u32[]{:S(2)}, u32[]{:S(2)}) collective-permute-start(f32[16,4,256]{2,1,0:T(4,128)S(1)} %get-tuple-element.83), channel_id=1, source_target_pairs={{0,2},{2,4},{4,6},{6,0},{1,3},{3,5},{5,7},{7,1},{8,10},{10,12},{12... | collective-permute-start | bytes 196616 | tf_op jit(solution)/shard_map/ppermute | solution.py:95
  39.6 7.9 %collective-permute-start.9 = (f32[16,16,128]{2,1,0:T(8,128)S(1)}, f32[16,16,128]{2,1,0:T(8,128)S(1)}, u32[]{:S(2)}, u32[]{:S(2)}) collective-permute-start(f32[16,16,128]{2,1,0:T(8,128)S(1)} %get-tuple-element.85.refs_2_.refs_3_), channel_id=1, source_target_pairs={{0,1},{1,0},{2,3},{3,2},{4,5},{5,4},{6,7},{7,6},{8,9},{9,8},{10,11... | collective-permute-start | bytes 393224 | tf_op jit(solution)/shard_map/ppermute | solution.py:107
  45.7 5.4 %collective-permute-start.7 = (f32[4,24,256]{2,1,0:T(8,128)S(1)}, f32[4,24,256]{2,1,0:T(8,128)S(1)}, u32[]{:S(2)}, u32[]{:S(2)}) collective-permute-start(f32[4,24,256]{2,1,0:T(8,128)S(1)} %get-tuple-element.86), channel_id=1, source_target_pairs={{0,1},{1,0},{8,9},{9,8},{16,17},{17,16},{24,25},{25,24},{2,3},{3,2... | collective-permute-start | bytes 294920 | tf_op jit(solution)/shard_map/ppermute | solution.py:103
  45.8 5.3 %collective-permute-start.8 = (f32[4,24,256]{2,1,0:T(8,128)S(1)}, f32[4,24,256]{2,1,0:T(8,128)S(1)}, u32[]{:S(2)}, u32[]{:S(2)}) collective-permute-start(f32[4,24,256]{2,1,0:T(8,128)S(1)} %get-tuple-element.87), channel_id=1, source_target_pairs={{0,25},{1,8},{8,1},{9,16},{16,9},{17,24},{24,17},{25,0},{2,27},{3,... | collective-permute-start | bytes 294920 | tf_op jit(solution)/shard_map/ppermute | solution.py:103
  52.5 4.3 %collective-permute-start.10 = (f32[16,4,256]{2,1,0:T(4,128)S(1)}, f32[16,4,256]{2,1,0:T(4,128)S(1)}, u32[]{:S(2)}, u32[]{:S(2)}) collective-permute-start(f32[16,4,256]{2,1,0:T(4,128)S(1)} %get-tuple-element.99), channel_id=1, source_target_pairs={{0,6},{2,0},{4,2},{6,4},{1,7},{3,1},{5,3},{7,5},{8,14},{10,8},{12,... | collective-permute-start | bytes 196616 | tf_op jit(solution)/shard_map/ppermute | solution.py:96
  53.3 6.1 %collective-permute-start.11 = (f32[16,4,256]{2,1,0:T(4,128)S(1)}, f32[16,4,256]{2,1,0:T(4,128)S(1)}, u32[]{:S(2)}, u32[]{:S(2)}) collective-permute-start(f32[16,4,256]{2,1,0:T(4,128)S(1)} %get-tuple-element.100), channel_id=1, source_target_pairs={{0,2},{2,4},{4,6},{6,0},{1,3},{3,5},{5,7},{7,1},{8,10},{10,12},{12... | collective-permute-start | bytes 196616 | tf_op jit(solution)/shard_map/ppermute | solution.py:95
  54.6 6.2 %collective-permute-start.14 = (f32[16,16,128]{2,1,0:T(8,128)S(1)}, f32[16,16,128]{2,1,0:T(8,128)S(1)}, u32[]{:S(2)}, u32[]{:S(2)}) collective-permute-start(f32[16,16,128]{2,1,0:T(8,128)S(1)} %get-tuple-element.102.refs_5_), channel_id=1, source_target_pairs={{0,1},{1,0},{2,3},{3,2},{4,5},{5,4},{6,7},{7,6},{8,9},{9,8},{10,11... | collective-permute-start | bytes 393224 | tf_op jit(solution)/shard_map/ppermute | solution.py:107
  59.4 4.9 %collective-permute-start.12 = (f32[4,24,256]{2,1,0:T(8,128)S(1)}, f32[4,24,256]{2,1,0:T(8,128)S(1)}, u32[]{:S(2)}, u32[]{:S(2)}) collective-permute-start(f32[4,24,256]{2,1,0:T(8,128)S(1)} %get-tuple-element.103), channel_id=1, source_target_pairs={{0,1},{1,0},{8,9},{9,8},{16,17},{17,16},{24,25},{25,24},{2,3},{3,2... | collective-permute-start | bytes 294920 | tf_op jit(solution)/shard_map/ppermute | solution.py:103
  59.5 5.2 %collective-permute-start.13 = (f32[4,24,256]{2,1,0:T(8,128)S(1)}, f32[4,24,256]{2,1,0:T(8,128)S(1)}, u32[]{:S(2)}, u32[]{:S(2)}) collective-permute-start(f32[4,24,256]{2,1,0:T(8,128)S(1)} %get-tuple-element.104), channel_id=1, source_target_pairs={{0,25},{1,8},{8,1},{9,16},{16,9},{17,24},{24,17},{25,0},{2,27},{3,... | collective-permute-start | bytes 294920 | tf_op jit(solution)/shard_map/ppermute | solution.py:103
  66.1 4.3 %collective-permute-start.15 = (f32[16,4,256]{2,1,0:T(4,128)S(1)}, f32[16,4,256]{2,1,0:T(4,128)S(1)}, u32[]{:S(2)}, u32[]{:S(2)}) collective-permute-start(f32[16,4,256]{2,1,0:T(4,128)S(1)} %get-tuple-element.112), channel_id=1, source_target_pairs={{0,6},{2,0},{4,2},{6,4},{1,7},{3,1},{5,3},{7,5},{8,14},{10,8},{12,... | collective-permute-start | bytes 196616 | tf_op jit(solution)/shard_map/ppermute | solution.py:96
  66.8 6.1 %collective-permute-start.16 = (f32[16,4,256]{2,1,0:T(4,128)S(1)}, f32[16,4,256]{2,1,0:T(4,128)S(1)}, u32[]{:S(2)}, u32[]{:S(2)}) collective-permute-start(f32[16,4,256]{2,1,0:T(4,128)S(1)} %get-tuple-element.113), channel_id=1, source_target_pairs={{0,2},{2,4},{4,6},{6,0},{1,3},{3,5},{5,7},{7,1},{8,10},{10,12},{12... | collective-permute-start | bytes 196616 | tf_op jit(solution)/shard_map/ppermute | solution.py:95
  68.2 6.4 %collective-permute-start.19 = (f32[16,16,128]{2,1,0:T(8,128)S(1)}, f32[16,16,128]{2,1,0:T(8,128)S(1)}, u32[]{:S(2)}, u32[]{:S(2)}) collective-permute-start(f32[16,16,128]{2,1,0:T(8,128)S(1)} %get-tuple-element.115.refs_7_), channel_id=1, source_target_pairs={{0,1},{1,0},{2,3},{3,2},{4,5},{5,4},{6,7},{7,6},{8,9},{9,8},{10,11... | collective-permute-start | bytes 393224 | tf_op jit(solution)/shard_map/ppermute | solution.py:107
  72.9 5.3 %collective-permute-start.17 = (f32[4,24,256]{2,1,0:T(8,128)S(1)}, f32[4,24,256]{2,1,0:T(8,128)S(1)}, u32[]{:S(2)}, u32[]{:S(2)}) collective-permute-start(f32[4,24,256]{2,1,0:T(8,128)S(1)} %get-tuple-element.116), channel_id=1, source_target_pairs={{0,1},{1,0},{8,9},{9,8},{16,17},{17,16},{24,25},{25,24},{2,3},{3,2... | collective-permute-start | bytes 294920 | tf_op jit(solution)/shard_map/ppermute | solution.py:103
  73.0 5.3 %collective-permute-start.18 = (f32[4,24,256]{2,1,0:T(8,128)S(1)}, f32[4,24,256]{2,1,0:T(8,128)S(1)}, u32[]{:S(2)}, u32[]{:S(2)}) collective-permute-start(f32[4,24,256]{2,1,0:T(8,128)S(1)} %get-tuple-element.117), channel_id=1, source_target_pairs={{0,25},{1,8},{8,1},{9,16},{16,9},{17,24},{24,17},{25,0},{2,27},{3,... | collective-permute-start | bytes 294920 | tf_op jit(solution)/shard_map/ppermute | solution.py:103
  79.7 1.4 %collective-permute-start.20 = (f32[17,16,128]{2,1,0:T(8,128)S(1)}, f32[17,16,128]{2,1,0:T(8,128)S(1)}, u32[]{:S(2)}, u32[]{:S(2)}) collective-permute-start(f32[17,16,128]{2,1,0:T(8,128)S(1)} %get-tuple-element.124), channel_id=1, source_target_pairs={{0,1},{1,0},{2,3},{3,2},{4,5},{5,4},{6,7},{7,6},{8,9},{9,8},{10,11... | collective-permute-start | bytes 417800 | tf_op jit(solution)/shard_map/ppermute | solution.py:107
  81.2 4.0 %collective-permute-start.21 = (f32[2,16,128]{2,1,0:T(8,128)S(1)}, f32[2,16,128]{2,1,0:T(8,128)S(1)}, u32[]{:S(2)}, u32[]{:S(2)}) collective-permute-start(f32[2,16,128]{2,1,0:T(8,128)S(1)} %pad_maximum_fusion), channel_id=1, source_target_pairs={{0,24},{8,0},{16,8},{24,16},{1,25},{9,1},{17,9},{25,17},{2,26},{10... | collective-permute-start | bytes 49160 | tf_op jit(solution)/shard_map/ppermute | solution.py:626
  83.1 3.7 %collective-permute-start.22 = (f32[2,16,128]{2,1,0:T(8,128)S(1)}, f32[2,16,128]{2,1,0:T(8,128)S(1)}, u32[]{:S(2)}, u32[]{:S(2)}) collective-permute-start(f32[2,16,128]{2,1,0:T(8,128)S(1)} %pad_maximum_fusion), channel_id=1, source_target_pairs={{0,16},{8,24},{16,0},{24,8},{1,17},{9,25},{17,1},{25,9},{2,18},{10... | collective-permute-start | bytes 49160 | tf_op jit(solution)/shard_map/ppermute | solution.py:626
  84.2 4.6 %collective-permute-start.23 = (f32[2,16,128]{2,1,0:T(8,128)S(1)}, f32[2,16,128]{2,1,0:T(8,128)S(1)}, u32[]{:S(2)}, u32[]{:S(2)}) collective-permute-start(f32[2,16,128]{2,1,0:T(8,128)S(1)} %pad_maximum_fusion), channel_id=1, source_target_pairs={{0,8},{8,16},{16,24},{24,0},{1,9},{9,17},{17,25},{25,1},{2,10},{10... | collective-permute-start | bytes 49160 | tf_op jit(solution)/shard_map/ppermute | solution.py:626
  88.9 4.0 %collective-permute-start.24 = (f32[2,16,128]{2,1,0:T(8,128)S(1)}, f32[2,16,128]{2,1,0:T(8,128)S(1)}, u32[]{:S(2)}, u32[]{:S(2)}) collective-permute-start(f32[2,16,128]{2,1,0:T(8,128)S(1)} %pad_maximum_fusion.1), channel_id=1, source_target_pairs={{0,6},{2,0},{4,2},{6,4},{1,7},{3,1},{5,3},{7,5},{8,14},{10,8},{12,... | collective-permute-start | bytes 49160 | tf_op jit(solution)/shard_map/ppermute | solution.py:626
  89.5 4.6 %collective-permute-start.25 = (f32[2,16,128]{2,1,0:T(8,128)S(1)}, f32[2,16,128]{2,1,0:T(8,128)S(1)}, u32[]{:S(2)}, u32[]{:S(2)}) collective-permute-start(f32[2,16,128]{2,1,0:T(8,128)S(1)} %pad_maximum_fusion.1), channel_id=1, source_target_pairs={{0,4},{2,6},{4,0},{6,2},{1,5},{3,7},{5,1},{7,3},{8,12},{10,14},{12... | collective-permute-start | bytes 49160 | tf_op jit(solution)/shard_map/ppermute | solution.py:626
  90.1 5.5 %collective-permute-start.26 = (f32[2,16,128]{2,1,0:T(8,128)S(1)}, f32[2,16,128]{2,1,0:T(8,128)S(1)}, u32[]{:S(2)}, u32[]{:S(2)}) collective-permute-start(f32[2,16,128]{2,1,0:T(8,128)S(1)} %pad_maximum_fusion.1), channel_id=1, source_target_pairs={{0,2},{2,4},{4,6},{6,0},{1,3},{3,5},{5,7},{7,1},{8,10},{10,12},{12... | collective-permute-start | bytes 49160 | tf_op jit(solution)/shard_map/ppermute | solution.py:626

commit v5 on v4

--- a/solution.py
+++ b/solution.py
@@ -91,10 +91,10 @@
         body(r)
 
 
-def exchange_y(up, low, n):
-    from_below = lax.ppermute(up, "gy", [(i, (i + 1) % n) for i in range(n)])
-    from_above = lax.ppermute(low, "gy", [(i, (i - 1) % n) for i in range(n)])
-    return from_above, from_below
+def exchange_y(a, b, n):
+    even = [(i, i ^ 1) for i in range(n)]
+    odd = [(i, i + (1 if i % 2 else -1)) for i in range(1, n - 1)]
+    return lax.ppermute(a, "gy", even), lax.ppermute(b, "gy", odd)
 
 
 def exchange_x(a, b, n):
@@ -134,8 +134,9 @@
 
 def gather_kernel(n, *refs):
     parts = refs[:n]
-    full, send_up, send_low = refs[n:]
+    full, send_a, send_b = refs[n:]
     core = lax.axis_index("gz")
+    odd = Place().odd_y
     fields, rows, ys, _ = full.shape
     h = HALO
 
@@ -144,13 +145,14 @@
         def one(r, c=c):
             row = join_received([p[c, r] for p in parts], core)
             full[c, r] = row
-            send_low[c * rows + r] = row[:h]
-            send_up[c * rows + r] = row[ys - h :]
+            send_a[c * rows + r] = jnp.where(odd, row[:h], row[ys - h :])
+            send_b[c * rows + r] = jnp.where(odd, row[ys - h :], row[:h])
 
         rows_loop(0, rows, one, 4)
     for r in range(rows):
         line = full[3, r, ys - h - 1 : ys - h, :]
-        send_up[fields * rows + r // 4, r % 4 : r % 4 + 1, :] = line
+        send_a[fields * rows + r // 4, r % 4 : r % 4 + 1, :] = line
+        send_b[fields * rows + r // 4, r % 4 : r % 4 + 1, :] = line
 
 
 def edge_list(h):
@@ -164,8 +166,9 @@
     return tiles + [(3, -1, 0), (3, -1, 1)]
 
 
-def force_edges_kernel(full, up, low, send_a, send_b):
-    odd_x = Place().odd
+def force_edges_kernel(full, ya, yb, send_a, send_b):
+    place = Place()
+    odd_x = place.odd
     _, rows, ys, _ = full.shape
     h = HALO
     for send, first in ((send_a, odd_x), (send_b, jnp.logical_not(odd_x))):
@@ -174,11 +177,12 @@
             if q < 2:
                 send[t] = full[c, r, 8 * q : 8 * q + 8, :]
             else:
-                send[t, :h, :] = up[c * rows + r]
-                send[t, h:, :] = low[c * rows + r]
-
-
-def edges_kernel(p, up, low, *rest):
+                a, b = ya[c * rows + r], yb[c * rows + r]
+                send[t, :h, :] = place.up(a, b)
+                send[t, h:, :] = place.low(a, b)
+
+
+def edges_kernel(p, ya, yb, *rest):
     send_a, send_b = rest[-2:]
     place = Place()
     rows = p.shape[0]
@@ -186,7 +190,7 @@
     for send, first in ((send_a, place.odd), (send_b, jnp.logical_not(place.odd))):
         start = jnp.where(first, 0, rows - h)
         for k in range(h):
-            set_row(send, (k,), p[start + k], up[start + k], low[start + k], place)
+            set_row(send, (k,), p[start + k], ya[start + k], yb[start + k], place)
 
 
 class Rows:
@@ -257,9 +261,10 @@
         emit(r - HALO, diverge(source, r))
 
 
-def emit_result(v_own, v_others, p_out, send_up, send_low, eta_at, sums=None):
+def emit_result(v_own, v_others, p_out, send_a, send_b, eta_at, sums=None):
     n = 1 + len(v_others)
     core = lax.axis_index("gz")
+    odd = Place().odd_y
     h = HALO
 
     def emit(r, out):
@@ -272,8 +277,8 @@
         if p_out is not None:
             p = eta_at(r) * out
             p_out[r] = p
-            send_up[r] = p[ys - h :]
-            send_low[r] = p[:h]
+            send_a[r] = jnp.where(odd, p[:h], p[ys - h :])
+            send_b[r] = jnp.where(odd, p[ys - h :], p[:h])
         if sums is not None:
             sums(r, out)
 
@@ -296,17 +301,20 @@
         self.x = lax.axis_index("gx") * lax.axis_size("gz") + lax.axis_index("gz")
         self.odd = lax.rem(self.x, 2) == 1
         self.below_x, self.above_x = self.x > 0, self.x < chain - 1
-        y = lax.axis_index("gy")
-        self.below_y, self.above_y = y > 0, y < lax.axis_size("gy") - 1
-
-
-def set_row(ref, index, row, up, low, place=None):
-    ys, h = row.shape[0], up.shape[0]
-    if place is not None:
-        up, low = jnp.where(place.above_y, up, 0.0), jnp.where(place.below_y, low, 0.0)
+        self.odd_y = lax.rem(lax.axis_index("gy"), 2) == 1
+
+    def up(self, a, b):
+        return jnp.where(self.odd_y, b, a)
+
+    def low(self, a, b):
+        return jnp.where(self.odd_y, a, b)
+
+
+def set_row(ref, index, row, a, b, place):
+    ys, h = row.shape[0], a.shape[0]
     ref[(*index, slice(0, ys), slice(None))] = row
-    ref[(*index, slice(ys, ys + h), slice(None))] = up
-    ref[(*index, slice(ys + h, ys + 2 * h), slice(None))] = low
+    ref[(*index, slice(ys, ys + h), slice(None))] = place.up(a, b)
+    ref[(*index, slice(ys + h, ys + 2 * h), slice(None))] = place.low(a, b)
 
 
 def coefs_at(sizes, place, slots, lanes, rows, ys, flags):
@@ -347,24 +355,24 @@
     return coefs
 
 
-def first_inner(sizes, full, up, low, flags, kx, ky, kz, w, b, *rest):
+def first_inner(sizes, full, ya, yb, flags, kx, ky, kz, w, b, *rest):
     levels, (out, force, eta, line) = rest[: SWEEPS - 1], rest[SWEEPS - 1 :]
     fields, rows, ys, lanes = full.shape
     h = HALO
-    place = Place().x
+    place = Place()
     slots, total = ys + 2 * h, rows + 2 * h
     for c in range(fields):
 
         def one(r, c=c):
             to, index = (force, (c, r + h)) if c < 3 else (eta, (r + h,))
-            set_row(to, index, full[c, r], up[c * rows + r], low[c * rows + r])
+            set_row(to, index, full[c, r], ya[c * rows + r], yb[c * rows + r], place)
 
         rows_loop(0, rows, one, 4)
     for q in range(rows // 4):
-        block = low[fields * rows + q]
+        block = place.low(ya[fields * rows + q], yb[fields * rows + q])
         for k in range(4):
             line[h + 4 * q + k] = block[k : k + 1]
-    coefs = coefs_at(sizes, place, slots, lanes, rows, ys, flags)
+    coefs = coefs_at(sizes, place.x, slots, lanes, rows, ys, flags)
 
     def at(r):
         coefs(r, eta[r], eta[r - 1], eta[r + 1], line[r], lambda c: force[c, r], kx, ky, kz, w, b)
@@ -375,15 +383,16 @@
 
 
 def first_outer(n, sizes, *refs):
-    full, up, low, xa, xb, flags, *early = refs[: 11 + SWEEPS]
+    full, ya, yb, xa, xb, flags, *early = refs[: 11 + SWEEPS]
     kx0, ky0, kz0, w0, b0, *levels, out0 = early
     refs = refs[11 + SWEEPS :]
     v_own, v_others, refs = refs[0], refs[1:n], refs[n:]
-    p_out, send_up, send_low, kx, ky, kz, w = refs[:7]
+    p_out, send_a, send_b, kx, ky, kz, w = refs[:7]
     force, eta, line, b, *buffers = refs[7:]
     fields, rows, ys, lanes = full.shape
     h = HALO
-    place, odd_x = Place().x, Place().odd
+    place = Place()
+    odd_x = place.odd
     slots, total = ys + 2 * h, rows + 2 * h
     ranges, inner = spans(h + 1, h + rows - 1, total)
     todo = outside((0, total), inner[0])
@@ -391,8 +400,9 @@
         k = r - h
         for c in range(fields):
             to, index = (force, (c, r)) if c < 3 else (eta, (r + 1,))
-            set_row(to, index, full[c, k], up[c * rows + k], low[c * rows + k])
-        line[r] = low[fields * rows + k // 4, k % 4 : k % 4 + 1, :]
+            set_row(to, index, full[c, k], ya[c * rows + k], yb[c * rows + k], place)
+        block = fields * rows + k // 4
+        line[r] = place.low(ya[block], yb[block])[k % 4 : k % 4 + 1]
     blank = jnp.zeros((slots, lanes), F32)
     line_blank = jnp.zeros((1, lanes), F32)
     for k in range(h):
@@ -412,7 +422,7 @@
             eta[1 + k, where, :] = lower
             if k >= 0:
                 eta[total - k, where, :] = upper
-    coefs = coefs_at(sizes, place, slots, lanes, rows, ys, flags)
+    coefs = coefs_at(sizes, place.x, slots, lanes, rows, ys, flags)
     for r in todo:
         after = eta[min(r + 2, total)]
         coefs(r, eta[r + 1], eta[r], after, line[r], lambda c: force[c, r], kx, ky, kz, w, b)
@@ -424,12 +434,12 @@
 
     rows_loop(*inner[0], carry, 2)
     b = Rows(b0, b, *inner[0])
-    emit = emit_result(v_own, v_others, p_out, send_up, send_low, lambda r: full[3, r])
+    emit = emit_result(v_own, v_others, p_out, send_a, send_b, lambda r: full[3, r])
     outer_solve(b, levels, buffers, inner, ranges, w, kx, ky, kz, emit)
     rows_loop(inner[SWEEPS][0] - h, inner[SWEEPS][1] - h, lambda r: emit(r, out0[r]), 4)
 
 
-def next_inner(extra, p_in, up, low, kx, ky, kz, w, *rest):
+def next_inner(extra, p_in, ya, yb, kx, ky, kz, w, *rest):
     p, b, *rest = rest[extra:]
     levels, out = rest[: SWEEPS - 1], rest[SWEEPS - 1]
     rows = p_in.shape[0]
@@ -437,7 +447,7 @@
     place = Place()
 
     def fill(r):
-        set_row(p, (r + h,), p_in[r], up[r], low[r], place)
+        set_row(p, (r + h,), p_in[r], ya[r], yb[r], place)
 
     rows_loop(0, rows, fill, 4)
     _, inner = spans(h, h + rows - 1, rows + 2 * h)
@@ -459,7 +469,7 @@
     if last:
         partials, refs = refs[:ITERS], refs[ITERS:]
     v_own, v_others, refs = refs[0], refs[1:n], refs[n:]
-    p_out = send_up = send_low = sums = None
+    p_out = send_a = send_b = sums = None
     if last:
         moment, acc, refs = v_others[-1].at[p_in.shape[0]], refs[-1], refs[:-1]
         acc[...] = jnp.zeros_like(acc)
@@ -467,7 +477,7 @@
         def sums(r, v):
             acc[...] = acc[...] + v * p_in[r]
     else:
-        p_out, send_up, send_low, *refs = refs
+        p_out, send_a, send_b, *refs = refs
     p, b, *buffers = refs
     rows = p_in.shape[0]
     h = HALO
@@ -481,7 +491,7 @@
     for r in outside(ranges[0], inner[0]):
         grads(p, w, b, r)
     b = Rows(b0, b, *inner[0])
-    emit = emit_result(v_own, v_others, p_out, send_up, send_low, lambda r: full[3, r], sums)
+    emit = emit_result(v_own, v_others, p_out, send_a, send_b, lambda r: full[3, r], sums)
     outer_solve(b, levels, buffers, inner, ranges, w, kx, ky, kz, emit)
     rows_loop(inner[SWEEPS][0] - h, inner[SWEEPS][1] - h, lambda r: emit(r, out0[r]), 4)
     if last:
@@ -656,7 +666,7 @@
         [
             sds(4, rows, ys, zs),
             sds(4 * rows + rows // 4, h, zs),
-            sds(4 * rows, h, zs),
+            sds(4 * rows + rows // 4, h, zs),
         ],
         parts,
         name="gather",

time: 98 us -> 93 us (0.949)
  waiting for transfers between devices: 42.2 us -> 24 us
  starting transfers between devices: 25.9 us -> 38.8 us
    ppermute x8, waiting for transfers between devices: 27.1 us -> 10.4 us  [exchange_y(): return (lax.ppermute(a, 'gy', even), lax.ppermute(b, 'gy', odd))]
    ppermute x8, starting transfers between devices: 11.6 us -> 18.3 us  [exchange_y(): return (lax.ppermute(a, 'gy', even), lax.ppermute(b, 'gy', odd))]
    ppermute x6, starting transfers between devices: 6.11 us -> 11 us  [sum_along(): terms.append(lax.ppermute(pair, axis, moves))]
    ppermute x4, starting transfers between devices: 7.24 us -> 8.42 us  [exchange_x(): lax.ppermute(b, ('gx', 'gz'), odd)]
  transfers between devices with their start and end apart: 27 -> 27, of which waited for: 16 -> 11; matrix products, arithmetic and copies ran while one was open for 0% -> 0% of each run, Pallas kernels for 16% -> 17%
where the time goes in v5:
time: 93 us; the launch traced here: 92.7 us
  starting transfers between devices  38.8 us (42%)
  Pallas kernels  26 us (28%)
  waiting for transfers between devices  24 us (26%)
  local copies, waits for them, and re-layouts  2.73 us (3%)
  between operations  1.09 us (1%)
    pallas_call x18, Pallas kernels, call(): pl.pallas_call(kernel, out_shape=outs, in_specs=specs or [VMEM] * len(ins...  26 us
    ppermute x8, starting transfers between devices, exchange_y(): return (lax.ppermute(a, 'gy', even), lax.ppermute(b, 'gy', odd))  18.3 us
    ppermute x6, starting transfers between devices, sum_along(): terms.append(lax.ppermute(pair, axis, moves))  11 us
    ppermute x8, waiting for transfers between devices, exchange_y(): return (lax.ppermute(a, 'gy', even), lax.ppermute(b, 'gy', odd))  10.4 us
    ppermute x4, starting transfers between devices, exchange_x(): lax.ppermute(b, ('gx', 'gz'), odd)  8.42 us
    ppermute x6, waiting for transfers between devices, sum_along(): terms.append(lax.ppermute(pair, axis, moves))  7.47 us
    ppermute x4, waiting for transfers between devices, exchange_x(): lax.ppermute(b, ('gx', 'gz'), odd)  3.25 us
    ppermute x5, waiting for transfers between devices, core_shift(): return lax.ppermute(value, 'gz', [(i, (i + j) % n) for i in range(n)])  2.89 us
  transfers between devices with their start and end apart: 27, of which 11 were waited for; matrix products, arithmetic and copies ran while one was open for 0% of the time, Pallas kernels for 17%

profile of v5, /device:TPU:0, one launch (start us, length us, event | category | flops | bytes accessed | tf_op | source)
XLA Modules:
  0.0 92.7 jit_solution(14798033316156371641)
XLA Ops:
  4.8 1.5 %collective-permute-done.refs_1_ = f32[4,16,16,128]{3,2,1,0:T(8,128)S(1)} collective-permute-done((f32[4,16,16,128]{3,2,1,0:T(8,128)S(1)}, f32[4,16,16,128]{3,2,1,0:T(8,128)S(1)}, u32[]{:S(2)}, u32[]{:S(2)}) %collective-permute-start) | collective-permute-done | bytes 524320 | tf_op jit(solution)/shard_map/ppermute | solution.py:107
  6.5 3.0 %collective-permute-start.1 = (f32[68,4,256]{2,1,0:T(4,128)S(1)}, f32[68,4,256]{2,1,0:T(4,128)S(1)}, u32[]{:S(2)}, u32[]{:S(2)}) collective-permute-start(f32[68,4,256]{2,1,0:T(4,128)S(1)} %get-tuple-element.68), channel_id=1, source_target_pairs={{0,2},{2,0},{4,6},{6,4},{1,3},{3,1},{5,7},{7,5},{8,10},{10,8},{12,... | collective-permute-start | bytes 835592 | tf_op jit(solution)/shard_map/ppermute | solution.py:97
  10.2 6.3 %collective-permute-done.1.ya.refs_1_ = f32[68,4,256]{2,1,0:T(4,128)S(1)} collective-permute-done((f32[68,4,256]{2,1,0:T(4,128)S(1)}, f32[68,4,256]{2,1,0:T(4,128)S(1)}, u32[]{:S(2)}, u32[]{:S(2)}) %collective-permute-start.1) | collective-permute-done | bytes 278560 | tf_op jit(solution)/shard_map/ppermute | solution.py:97
  16.6 2.7 %collective-permute-start.4 = (f32[43,8,256]{2,1,0:T(8,128)S(1)}, f32[43,8,256]{2,1,0:T(8,128)S(1)}, u32[]{:S(2)}, u32[]{:S(2)}) collective-permute-start(f32[43,8,256]{2,1,0:T(8,128)S(1)} %get-tuple-element.71), channel_id=1, source_target_pairs={{0,25},{1,8},{8,1},{9,16},{16,9},{17,24},{24,17},{25,0},{2,27},{3,... | collective-permute-start | bytes 1056776 | tf_op jit(solution)/shard_map/ppermute | solution.py:103
  19.3 4.7 %first_inner.1 = (f32[24,24,256]{2,1,0:T(8,128)S(1)}, f32[24,24,256]{2,1,0:T(8,128)S(1)}, f32[24,24,256]{2,1,0:T(8,128)S(1)}, f32[3,24,24,256]{3,2,1,0:T(8,128)S...) custom-call(f32[4,16,16,256]{3,2,1,0:T(8,128)S(1)} %get-tuple-elemen, ...), custom_call_target="tpu_custom_call" | custom-call | flops 40000000 | bytes 1048576 | tf_op jit(solution)/shard_map/first_inner/pallas_call | solution.py:26
  24.1 3.2 %collective-permute-done.4.refs_4_ = f32[43,8,256]{2,1,0:T(8,128)S(1)} collective-permute-done((f32[43,8,256]{2,1,0:T(8,128)S(1)}, f32[43,8,256]{2,1,0:T(8,128)S(1)}, u32[]{:S(2)}, u32[]{:S(2)}) %collective-permute-start.4) | collective-permute-done | bytes 352288 | tf_op jit(solution)/shard_map/ppermute | solution.py:103
  27.3 2.8 %first.1 = (f32[16,16,128]{2,1,0:T(8,128)S(1)}, f32[16,16,128]{2,1,0:T(8,128)S(1)}, f32[16,16,256]{2,1,0:T(8,128)S(1)}, f32[16,4,256]{2,1,0:T(4,128)S(1)}, f32[1...) custom-call(f32[4,16,16,256]{3,2,1,0:T(8,128)S(1)} %get-tuple-elemen, ...), custom_call_target="tpu_custom_call" | custom-call | flops 40000000 | bytes 1048576 | tf_op jit(solution)/shard_map/first/pallas_call | solution.py:26
  30.1 5.0 %collective-permute-start.5 = (f32[16,4,256]{2,1,0:T(4,128)S(1)}, f32[16,4,256]{2,1,0:T(4,128)S(1)}, u32[]{:S(2)}, u32[]{:S(2)}) collective-permute-start(f32[16,4,256]{2,1,0:T(4,128)S(1)} %get-tuple-element.82), channel_id=1, source_target_pairs={{0,2},{2,0},{4,6},{6,4},{1,3},{3,1},{5,7},{7,5},{8,10},{10,8},{12,... | collective-permute-start | bytes 196616 | tf_op jit(solution)/shard_map/ppermute | solution.py:97
  36.0 1.5 %collective-permute-done.5.ya = f32[16,4,256]{2,1,0:T(4,128)S(1)} collective-permute-done((f32[16,4,256]{2,1,0:T(4,128)S(1)}, f32[16,4,256]{2,1,0:T(4,128)S(1)}, u32[]{:S(2)}, u32[]{:S(2)}) %collective-permute-start.5) | collective-permute-done | bytes 65568 | tf_op jit(solution)/shard_map/ppermute | solution.py:97
  37.6 2.0 %collective-permute-start.8 = (f32[4,24,256]{2,1,0:T(8,128)S(1)}, f32[4,24,256]{2,1,0:T(8,128)S(1)}, u32[]{:S(2)}, u32[]{:S(2)}) collective-permute-start(f32[4,24,256]{2,1,0:T(8,128)S(1)} %get-tuple-element.87), channel_id=1, source_target_pairs={{0,25},{1,8},{8,1},{9,16},{16,9},{17,24},{24,17},{25,0},{2,27},{3,... | collective-permute-start | bytes 294920 | tf_op jit(solution)/shard_map/ppermute | solution.py:103
  39.6 3.5 %next_inner.3 = (f32[24,24,256]{2,1,0:T(8,128)S(1)}, f32[3,24,24,256]{3,2,1,0:T(8,128)S(1)}, f32[3,24,24,256]{3,2,1,0:T(8,128)S(1)}, f32[3,24,24,256]{3,2,1,0:T(...) custom-call(f32[16,16,256]{2,1,0:T(8,128)S(1)} %get-tuple-element.81.refs_0_.p.p_in.refs_1_, ...), custom_call_target="tpu_custom_call" | custom-call | flops 40000000 | bytes 1048576 | tf_op jit(solution)/shard_map/next_inner/pallas_call | solution.py:26
  43.1 1.4 %next.3 = (f32[16,16,128]{2,1,0:T(8,128)S(1)}, f32[16,16,128]{2,1,0:T(8,128)S(1)}, f32[16,16,256]{2,1,0:T(8,128)S(1)}, f32[16,4,256]{2,1,0:T(4,128)S(1)}, f32[16,4,256]{2,1,0:T(4,128)S(1)}) custom-call(f32[16,16,256]{2,1,0:T(8,128)S(1)} %get-tuple-element.81.refs_0_.p.p_in.refs_1_, f32[4,24,256]{2,1,0:T(8,128)S(1)} %collective-permute-done.7.xa, ...), custom_call_target="tpu_custom_call" | custom-call | flops 40000000 | bytes 1048576 | tf_op jit(solution)/shard_map/next/pallas_call | solution.py:26
  44.5 3.7 %collective-permute-start.10 = (f32[16,4,256]{2,1,0:T(4,128)S(1)}, f32[16,4,256]{2,1,0:T(4,128)S(1)}, u32[]{:S(2)}, u32[]{:S(2)}) collective-permute-start(f32[16,4,256]{2,1,0:T(4,128)S(1)} %get-tuple-element.99), channel_id=1, source_target_pairs={{0,2},{2,0},{4,6},{6,4},{1,3},{3,1},{5,7},{7,5},{8,10},{10,8},{12,... | collective-permute-start | bytes 196616 | tf_op jit(solution)/shard_map/ppermute | solution.py:97
  49.1 1.4 %collective-permute-done.10.ya = f32[16,4,256]{2,1,0:T(4,128)S(1)} collective-permute-done((f32[16,4,256]{2,1,0:T(4,128)S(1)}, f32[16,4,256]{2,1,0:T(4,128)S(1)}, u32[]{:S(2)}, u32[]{:S(2)}) %collective-permute-start.10) | collective-permute-done | bytes 65568 | tf_op jit(solution)/shard_map/ppermute | solution.py:97
  50.6 1.9 %collective-permute-start.13 = (f32[4,24,256]{2,1,0:T(8,128)S(1)}, f32[4,24,256]{2,1,0:T(8,128)S(1)}, u32[]{:S(2)}, u32[]{:S(2)}) collective-permute-start(f32[4,24,256]{2,1,0:T(8,128)S(1)} %get-tuple-element.104), channel_id=1, source_target_pairs={{0,25},{1,8},{8,1},{9,16},{16,9},{17,24},{24,17},{25,0},{2,27},{3,... | collective-permute-start | bytes 294920 | tf_op jit(solution)/shard_map/ppermute | solution.py:103
  52.5 3.5 %next_inner.4 = (f32[24,24,256]{2,1,0:T(8,128)S(1)}, f32[3,24,24,256]{3,2,1,0:T(8,128)S(1)}, f32[3,24,24,256]{3,2,1,0:T(8,128)S(1)}, f32[3,24,24,256]{3,2,1,0:T(...) custom-call(f32[16,16,256]{2,1,0:T(8,128)S(1)} %get-tuple-element.98.refs_0_.p.p_in.refs_1_, ...), custom_call_target="tpu_custom_call" | custom-call | flops 40000000 | bytes 1048576 | tf_op jit(solution)/shard_map/next_inner/pallas_call | solution.py:26
  56.1 1.4 %next.4 = (f32[16,16,128]{2,1,0:T(8,128)S(1)}, f32[16,16,128]{2,1,0:T(8,128)S(1)}, f32[16,16,256]{2,1,0:T(8,128)S(1)}, f32[16,4,256]{2,1,0:T(4,128)S(1)}, f32[16,4,256]{2,1,0:T(4,128)S(1)}) custom-call(f32[16,16,256]{2,1,0:T(8,128)S(1)} %get-tuple-element.98.refs_0_.p.p_in.refs_1_, f32[4,24,256]{2,1,0:T(8,128)S(1)} %collective-permute-done.12.xa, ...), custom_call_target="tpu_custom_call" | custom-call | flops 40000000 | bytes 1048576 | tf_op jit(solution)/shard_map/next/pallas_call | solution.py:26
  57.5 3.8 %collective-permute-start.15 = (f32[16,4,256]{2,1,0:T(4,128)S(1)}, f32[16,4,256]{2,1,0:T(4,128)S(1)}, u32[]{:S(2)}, u32[]{:S(2)}) collective-permute-start(f32[16,4,256]{2,1,0:T(4,128)S(1)} %get-tuple-element.112), channel_id=1, source_target_pairs={{0,2},{2,0},{4,6},{6,4},{1,3},{3,1},{5,7},{7,5},{8,10},{10,8},{12,... | collective-permute-start | bytes 196616 | tf_op jit(solution)/shard_map/ppermute | solution.py:97
  62.4 1.2 %collective-permute-done.15.ya = f32[16,4,256]{2,1,0:T(4,128)S(1)} collective-permute-done((f32[16,4,256]{2,1,0:T(4,128)S(1)}, f32[16,4,256]{2,1,0:T(4,128)S(1)}, u32[]{:S(2)}, u32[]{:S(2)}) %collective-permute-start.15) | collective-permute-done | bytes 65568 | tf_op jit(solution)/shard_map/ppermute | solution.py:97
  63.6 1.9 %collective-permute-start.18 = (f32[4,24,256]{2,1,0:T(8,128)S(1)}, f32[4,24,256]{2,1,0:T(8,128)S(1)}, u32[]{:S(2)}, u32[]{:S(2)}) collective-permute-start(f32[4,24,256]{2,1,0:T(8,128)S(1)} %get-tuple-element.117), channel_id=1, source_target_pairs={{0,25},{1,8},{8,1},{9,16},{16,9},{17,24},{24,17},{25,0},{2,27},{3,... | collective-permute-start | bytes 294920 | tf_op jit(solution)/shard_map/ppermute | solution.py:103
  65.5 3.6 %next_inner.5 = (f32[24,24,256]{2,1,0:T(8,128)S(1)}, f32[3,24,24,256]{3,2,1,0:T(8,128)S(1)}, f32[3,24,24,256]{3,2,1,0:T(8,128)S(1)}, f32[3,24,24,256]{3,2,1,0:T(...) custom-call(f32[16,16,256]{2,1,0:T(8,128)S(1)} %get-tuple-element.111.refs_0_.p.p_in, ...), custom_call_target="tpu_custom_call" | custom-call | flops 40000000 | bytes 1048576 | tf_op jit(solution)/shard_map/next_inner/pallas_call | solution.py:26
  69.1 1.4 %next.5 = (f32[16,16,128]{2,1,0:T(8,128)S(1)}, f32[17,16,128]{2,1,0:T(8,128)S(1)}) custom-call(f32[16,16,256]{2,1,0:T(8,128)S(1)} %get-tuple-element.111.refs_0_.p.p_in, f32[4,24,256]{2,1,0:T(8,128)S(1)} %collective-permute-done.17.xa, f32[4,24,256]{2,1,0:T(8,128)S(1)} %collective-permute-done.18.xb, f32[4,16,16,256]{3,2,1,0:T(8,128)S(1)} %get-tuple-element.67.full.refs_0_, ...), custom_call_target="tpu_custom_call" | custom-call | flops 40000000 | bytes 1048576 | tf_op jit(solution)/shard_map/next/pallas_call | solution.py:26
  70.7 1.3 %collective-permute-done.20.refs_7_ = f32[17,16,128]{2,1,0:T(8,128)S(1)} collective-permute-done((f32[17,16,128]{2,1,0:T(8,128)S(1)}, f32[17,16,128]{2,1,0:T(8,128)S(1)}, u32[]{:S(2)}, u32[]{:S(2)}) %collective-permute-start.20) | collective-permute-done | bytes 139296 | tf_op jit(solution)/shard_map/ppermute | solution.py:107
  72.0 1.7 %collective-permute-start.21 = (f32[2,16,128]{2,1,0:T(8,128)S(1)}, f32[2,16,128]{2,1,0:T(8,128)S(1)}, u32[]{:S(2)}, u32[]{:S(2)}) collective-permute-start(f32[2,16,128]{2,1,0:T(8,128)S(1)} %pad_maximum_fusion), channel_id=1, source_target_pairs={{0,24},{8,0},{16,8},{24,16},{1,25},{9,1},{17,9},{25,17},{2,26},{10... | collective-permute-start | bytes 49160 | tf_op jit(solution)/shard_map/ppermute | solution.py:636
  73.7 1.1 %collective-permute-start.22 = (f32[2,16,128]{2,1,0:T(8,128)S(1)}, f32[2,16,128]{2,1,0:T(8,128)S(1)}, u32[]{:S(2)}, u32[]{:S(2)}) collective-permute-start(f32[2,16,128]{2,1,0:T(8,128)S(1)} %pad_maximum_fusion), channel_id=1, source_target_pairs={{0,16},{8,24},{16,0},{24,8},{1,17},{9,25},{17,1},{25,9},{2,18},{10... | collective-permute-start | bytes 49160 | tf_op jit(solution)/shard_map/ppermute | solution.py:636
  75.8 1.6 %collective-permute-done.22 = f32[2,16,128]{2,1,0:T(8,128)S(1)} collective-permute-done((f32[2,16,128]{2,1,0:T(8,128)S(1)}, f32[2,16,128]{2,1,0:T(8,128)S(1)}, u32[]{:S(2)}, u32[]{:S(2)}) %collective-permute-start.22) | collective-permute-done | bytes 16416 | tf_op jit(solution)/shard_map/ppermute | solution.py:636
  77.5 2.0 %collective-permute-done.23 = f32[2,16,128]{2,1,0:T(8,128)S(1)} collective-permute-done((f32[2,16,128]{2,1,0:T(8,128)S(1)}, f32[2,16,128]{2,1,0:T(8,128)S(1)}, u32[]{:S(2)}, u32[]{:S(2)}) %collective-permute-start.23) | collective-permute-done | bytes 16416 | tf_op jit(solution)/shard_map/ppermute | solution.py:636
  79.6 2.7 %collective-permute-start.24 = (f32[2,16,128]{2,1,0:T(8,128)S(1)}, f32[2,16,128]{2,1,0:T(8,128)S(1)}, u32[]{:S(2)}, u32[]{:S(2)}) collective-permute-start(f32[2,16,128]{2,1,0:T(8,128)S(1)} %pad_maximum_fusion.1), channel_id=1, source_target_pairs={{0,6},{2,0},{4,2},{6,4},{1,7},{3,1},{5,3},{7,5},{8,14},{10,8},{12,... | collective-permute-start | bytes 49160 | tf_op jit(solution)/shard_map/ppermute | solution.py:636
  82.2 2.8 %collective-permute-start.25 = (f32[2,16,128]{2,1,0:T(8,128)S(1)}, f32[2,16,128]{2,1,0:T(8,128)S(1)}, u32[]{:S(2)}, u32[]{:S(2)}) collective-permute-start(f32[2,16,128]{2,1,0:T(8,128)S(1)} %pad_maximum_fusion.1), channel_id=1, source_target_pairs={{0,4},{2,6},{4,0},{6,2},{1,5},{3,7},{5,1},{7,3},{8,12},{10,14},{12... | collective-permute-start | bytes 49160 | tf_op jit(solution)/shard_map/ppermute | solution.py:636
  85.0 1.7 %collective-permute-start.26 = (f32[2,16,128]{2,1,0:T(8,128)S(1)}, f32[2,16,128]{2,1,0:T(8,128)S(1)}, u32[]{:S(2)}, u32[]{:S(2)}) collective-permute-start(f32[2,16,128]{2,1,0:T(8,128)S(1)} %pad_maximum_fusion.1), channel_id=1, source_target_pairs={{0,2},{2,4},{4,6},{6,0},{1,3},{3,5},{5,7},{7,1},{8,10},{10,12},{12... | collective-permute-start | bytes 49160 | tf_op jit(solution)/shard_map/ppermute | solution.py:636
  86.9 3.6 %collective-permute-done.26 = f32[2,16,128]{2,1,0:T(8,128)S(1)} collective-permute-done((f32[2,16,128]{2,1,0:T(8,128)S(1)}, f32[2,16,128]{2,1,0:T(8,128)S(1)}, u32[]{:S(2)}, u32[]{:S(2)}) %collective-permute-start.26) | collective-permute-done | bytes 16416 | tf_op jit(solution)/shard_map/ppermute | solution.py:636
  90.6 2.0 %last.1 = (f32[32,16,128]{2,1,0:T(8,128)}, f32[32,16,128]{2,1,0:T(8,128)}, f32[3]{0:T(128)}) custom-call(f32[2,16,128]{2,1,0:T(8,128)S(1)} %pad_maximum_fusion.2.sums, f32[32,16,128]{2,1,0:T(8,128)S(1)} %get-tuple-element.125.eta, f32[16,16,128]{2,1,0:T(8,128)S(1)} %get-tuple-element.84.refs_1_.refs_2_.refs_0_, ...), custom_call_target="tpu_custom_call" | custom-call | flops 1000000 | bytes 1048576 | tf_op jit(solution)/shard_map/last/pallas_call | solution.py:26
  (58 shorter events, 9.5 us)
Async XLA Ops:
  0.6 1.1 %copy-start = (f32[3,32,16,128]{3,2,1,0:T(8,128)S(1)}, f32[3,32,16,128]{3,2,1,0:T(8,128)}, u32[]{:S(2)}) copy-start(f32[3,32,16,128]{3,2,1,0:T(8,128)} %force.1) | copy-start | bytes 2359300
  1.8 0.9 %copy-start.1 = (s32[32,16,128]{2,1,0:T(8,128)S(1)}, s32[32,16,128]{2,1,0:T(8,128)}, u32[]{:S(2)}) copy-start(s32[32,16,128]{2,1,0:T(8,128)} %phase.1) | copy-start | bytes 786436
  2.7 0.7 copy-start.3
  3.4 16.0 %copy-start.2 = (s32[6]{0:T(128)S(1)}, s32[6]{0:T(128)}, u32[]{:S(2)}) copy-start(s32[6]{0:T(128)} %refs_5_.1) | copy-start | bytes 76
  4.2 2.1 %collective-permute-start = (f32[4,16,16,128]{3,2,1,0:T(8,128)S(1)}, f32[4,16,16,128]{3,2,1,0:T(8,128)S(1)}, u32[]{:S(2)}, u32[]{:S(2)}) collective-permute-start(f32[4,16,16,128]{3,2,1,0:T(8,128)S(1)} %get-tuple-element.66), channel_id=1, source_target_pairs={{0,1},{1,0},{2,3},{3,2},{4,5},{5,4},{6,7},{7,6},{8,9},{9,8},{10,11... | collective-permute-start | bytes 1572872 | tf_op jit(solution)/shard_map/ppermute | solution.py:107
  6.5 10.0 %collective-permute-start.1 = (f32[68,4,256]{2,1,0:T(4,128)S(1)}, f32[68,4,256]{2,1,0:T(4,128)S(1)}, u32[]{:S(2)}, u32[]{:S(2)}) collective-permute-start(f32[68,4,256]{2,1,0:T(4,128)S(1)} %get-tuple-element.68), channel_id=1, source_target_pairs={{0,2},{2,0},{4,6},{6,4},{1,3},{3,1},{5,7},{7,5},{8,10},{10,8},{12,... | collective-permute-start | bytes 835592 | tf_op jit(solution)/shard_map/ppermute | solution.py:97
  9.5 7.0 %collective-permute-start.2 = (f32[68,4,256]{2,1,0:T(4,128)S(1)}, f32[68,4,256]{2,1,0:T(4,128)S(1)}, u32[]{:S(2)}, u32[]{:S(2)}) collective-permute-start(f32[68,4,256]{2,1,0:T(4,128)S(1)} %get-tuple-element.69), channel_id=1, source_target_pairs={{2,4},{4,2},{3,5},{5,3},{10,12},{12,10},{11,13},{13,11},{18,20},{2... | collective-permute-start | bytes 835592 | tf_op jit(solution)/shard_map/ppermute | solution.py:97
  16.5 7.5 %collective-permute-start.3 = (f32[43,8,256]{2,1,0:T(8,128)S(1)}, f32[43,8,256]{2,1,0:T(8,128)S(1)}, u32[]{:S(2)}, u32[]{:S(2)}) collective-permute-start(f32[43,8,256]{2,1,0:T(8,128)S(1)} %get-tuple-element.70), channel_id=1, source_target_pairs={{0,1},{1,0},{8,9},{9,8},{16,17},{17,16},{24,25},{25,24},{2,3},{3,2... | collective-permute-start | bytes 1056776 | tf_op jit(solution)/shard_map/ppermute | solution.py:103
  16.6 10.7 %collective-permute-start.4 = (f32[43,8,256]{2,1,0:T(8,128)S(1)}, f32[43,8,256]{2,1,0:T(8,128)S(1)}, u32[]{:S(2)}, u32[]{:S(2)}) collective-permute-start(f32[43,8,256]{2,1,0:T(8,128)S(1)} %get-tuple-element.71), channel_id=1, source_target_pairs={{0,25},{1,8},{8,1},{9,16},{16,9},{17,24},{24,17},{25,0},{2,27},{3,... | collective-permute-start | bytes 1056776 | tf_op jit(solution)/shard_map/ppermute | solution.py:103
  30.1 7.3 %collective-permute-start.5 = (f32[16,4,256]{2,1,0:T(4,128)S(1)}, f32[16,4,256]{2,1,0:T(4,128)S(1)}, u32[]{:S(2)}, u32[]{:S(2)}) collective-permute-start(f32[16,4,256]{2,1,0:T(4,128)S(1)} %get-tuple-element.82), channel_id=1, source_target_pairs={{0,2},{2,0},{4,6},{6,4},{1,3},{3,1},{5,7},{7,5},{8,10},{10,8},{12,... | collective-permute-start | bytes 196616 | tf_op jit(solution)/shard_map/ppermute | solution.py:97
  35.1 2.4 %collective-permute-start.6 = (f32[16,4,256]{2,1,0:T(4,128)S(1)}, f32[16,4,256]{2,1,0:T(4,128)S(1)}, u32[]{:S(2)}, u32[]{:S(2)}) collective-permute-start(f32[16,4,256]{2,1,0:T(4,128)S(1)} %get-tuple-element.83), channel_id=1, source_target_pairs={{2,4},{4,2},{3,5},{5,3},{10,12},{12,10},{11,13},{13,11},{18,20},{2... | collective-permute-start | bytes 196616 | tf_op jit(solution)/shard_map/ppermute | solution.py:97
  35.8 3.8 %collective-permute-start.9 = (f32[16,16,128]{2,1,0:T(8,128)S(1)}, f32[16,16,128]{2,1,0:T(8,128)S(1)}, u32[]{:S(2)}, u32[]{:S(2)}) collective-permute-start(f32[16,16,128]{2,1,0:T(8,128)S(1)} %get-tuple-element.85.refs_2_.refs_3_), channel_id=1, source_target_pairs={{0,1},{1,0},{2,3},{3,2},{4,5},{5,4},{6,7},{7,6},{8,9},{9,8},{10,11... | collective-permute-start | bytes 393224 | tf_op jit(solution)/shard_map/ppermute | solution.py:107
  37.5 5.6 %collective-permute-start.7 = (f32[4,24,256]{2,1,0:T(8,128)S(1)}, f32[4,24,256]{2,1,0:T(8,128)S(1)}, u32[]{:S(2)}, u32[]{:S(2)}) collective-permute-start(f32[4,24,256]{2,1,0:T(8,128)S(1)} %get-tuple-element.86), channel_id=1, source_target_pairs={{0,1},{1,0},{8,9},{9,8},{16,17},{17,16},{24,25},{25,24},{2,3},{3,2... | collective-permute-start | bytes 294920 | tf_op jit(solution)/shard_map/ppermute | solution.py:103
  37.6 5.5 %collective-permute-start.8 = (f32[4,24,256]{2,1,0:T(8,128)S(1)}, f32[4,24,256]{2,1,0:T(8,128)S(1)}, u32[]{:S(2)}, u32[]{:S(2)}) collective-permute-start(f32[4,24,256]{2,1,0:T(8,128)S(1)} %get-tuple-element.87), channel_id=1, source_target_pairs={{0,25},{1,8},{8,1},{9,16},{16,9},{17,24},{24,17},{25,0},{2,27},{3,... | collective-permute-start | bytes 294920 | tf_op jit(solution)/shard_map/ppermute | solution.py:103
  44.5 6.0 %collective-permute-start.10 = (f32[16,4,256]{2,1,0:T(4,128)S(1)}, f32[16,4,256]{2,1,0:T(4,128)S(1)}, u32[]{:S(2)}, u32[]{:S(2)}) collective-permute-start(f32[16,4,256]{2,1,0:T(4,128)S(1)} %get-tuple-element.99), channel_id=1, source_target_pairs={{0,2},{2,0},{4,6},{6,4},{1,3},{3,1},{5,7},{7,5},{8,10},{10,8},{12,... | collective-permute-start | bytes 196616 | tf_op jit(solution)/shard_map/ppermute | solution.py:97
  48.3 2.2 %collective-permute-start.11 = (f32[16,4,256]{2,1,0:T(4,128)S(1)}, f32[16,4,256]{2,1,0:T(4,128)S(1)}, u32[]{:S(2)}, u32[]{:S(2)}) collective-permute-start(f32[16,4,256]{2,1,0:T(4,128)S(1)} %get-tuple-element.100), channel_id=1, source_target_pairs={{2,4},{4,2},{3,5},{5,3},{10,12},{12,10},{11,13},{13,11},{18,20},{2... | collective-permute-start | bytes 196616 | tf_op jit(solution)/shard_map/ppermute | solution.py:97
  48.9 3.6 %collective-permute-start.14 = (f32[16,16,128]{2,1,0:T(8,128)S(1)}, f32[16,16,128]{2,1,0:T(8,128)S(1)}, u32[]{:S(2)}, u32[]{:S(2)}) collective-permute-start(f32[16,16,128]{2,1,0:T(8,128)S(1)} %get-tuple-element.102.refs_5_), channel_id=1, source_target_pairs={{0,1},{1,0},{2,3},{3,2},{4,5},{5,4},{6,7},{7,6},{8,9},{9,8},{10,11... | collective-permute-start | bytes 393224 | tf_op jit(solution)/shard_map/ppermute | solution.py:107
  50.5 5.5 %collective-permute-start.12 = (f32[4,24,256]{2,1,0:T(8,128)S(1)}, f32[4,24,256]{2,1,0:T(8,128)S(1)}, u32[]{:S(2)}, u32[]{:S(2)}) collective-permute-start(f32[4,24,256]{2,1,0:T(8,128)S(1)} %get-tuple-element.103), channel_id=1, source_target_pairs={{0,1},{1,0},{8,9},{9,8},{16,17},{17,16},{24,25},{25,24},{2,3},{3,2... | collective-permute-start | bytes 294920 | tf_op jit(solution)/shard_map/ppermute | solution.py:103
  50.6 5.4 %collective-permute-start.13 = (f32[4,24,256]{2,1,0:T(8,128)S(1)}, f32[4,24,256]{2,1,0:T(8,128)S(1)}, u32[]{:S(2)}, u32[]{:S(2)}) collective-permute-start(f32[4,24,256]{2,1,0:T(8,128)S(1)} %get-tuple-element.104), channel_id=1, source_target_pairs={{0,25},{1,8},{8,1},{9,16},{16,9},{17,24},{24,17},{25,0},{2,27},{3,... | collective-permute-start | bytes 294920 | tf_op jit(solution)/shard_map/ppermute | solution.py:103
  57.5 6.1 %collective-permute-start.15 = (f32[16,4,256]{2,1,0:T(4,128)S(1)}, f32[16,4,256]{2,1,0:T(4,128)S(1)}, u32[]{:S(2)}, u32[]{:S(2)}) collective-permute-start(f32[16,4,256]{2,1,0:T(4,128)S(1)} %get-tuple-element.112), channel_id=1, source_target_pairs={{0,2},{2,0},{4,6},{6,4},{1,3},{3,1},{5,7},{7,5},{8,10},{10,8},{12,... | collective-permute-start | bytes 196616 | tf_op jit(solution)/shard_map/ppermute | solution.py:97
  61.3 2.2 %collective-permute-start.16 = (f32[16,4,256]{2,1,0:T(4,128)S(1)}, f32[16,4,256]{2,1,0:T(4,128)S(1)}, u32[]{:S(2)}, u32[]{:S(2)}) collective-permute-start(f32[16,4,256]{2,1,0:T(4,128)S(1)} %get-tuple-element.113), channel_id=1, source_target_pairs={{2,4},{4,2},{3,5},{5,3},{10,12},{12,10},{11,13},{13,11},{18,20},{2... | collective-permute-start | bytes 196616 | tf_op jit(solution)/shard_map/ppermute | solution.py:97
  62.1 3.4 %collective-permute-start.19 = (f32[16,16,128]{2,1,0:T(8,128)S(1)}, f32[16,16,128]{2,1,0:T(8,128)S(1)}, u32[]{:S(2)}, u32[]{:S(2)}) collective-permute-start(f32[16,16,128]{2,1,0:T(8,128)S(1)} %get-tuple-element.115.refs_7_), channel_id=1, source_target_pairs={{0,1},{1,0},{2,3},{3,2},{4,5},{5,4},{6,7},{7,6},{8,9},{9,8},{10,11... | collective-permute-start | bytes 393224 | tf_op jit(solution)/shard_map/ppermute | solution.py:107
  63.6 5.6 %collective-permute-start.17 = (f32[4,24,256]{2,1,0:T(8,128)S(1)}, f32[4,24,256]{2,1,0:T(8,128)S(1)}, u32[]{:S(2)}, u32[]{:S(2)}) collective-permute-start(f32[4,24,256]{2,1,0:T(8,128)S(1)} %get-tuple-element.116), channel_id=1, source_target_pairs={{0,1},{1,0},{8,9},{9,8},{16,17},{17,16},{24,25},{25,24},{2,3},{3,2... | collective-permute-start | bytes 294920 | tf_op jit(solution)/shard_map/ppermute | solution.py:103
  63.6 5.5 %collective-permute-start.18 = (f32[4,24,256]{2,1,0:T(8,128)S(1)}, f32[4,24,256]{2,1,0:T(8,128)S(1)}, u32[]{:S(2)}, u32[]{:S(2)}) collective-permute-start(f32[4,24,256]{2,1,0:T(8,128)S(1)} %get-tuple-element.117), channel_id=1, source_target_pairs={{0,25},{1,8},{8,1},{9,16},{16,9},{17,24},{24,17},{25,0},{2,27},{3,... | collective-permute-start | bytes 294920 | tf_op jit(solution)/shard_map/ppermute | solution.py:103
  70.6 1.4 %collective-permute-start.20 = (f32[17,16,128]{2,1,0:T(8,128)S(1)}, f32[17,16,128]{2,1,0:T(8,128)S(1)}, u32[]{:S(2)}, u32[]{:S(2)}) collective-permute-start(f32[17,16,128]{2,1,0:T(8,128)S(1)} %get-tuple-element.124), channel_id=1, source_target_pairs={{0,1},{1,0},{2,3},{3,2},{4,5},{5,4},{6,7},{7,6},{8,9},{9,8},{10,11... | collective-permute-start | bytes 417800 | tf_op jit(solution)/shard_map/ppermute | solution.py:107
  72.0 3.8 %collective-permute-start.21 = (f32[2,16,128]{2,1,0:T(8,128)S(1)}, f32[2,16,128]{2,1,0:T(8,128)S(1)}, u32[]{:S(2)}, u32[]{:S(2)}) collective-permute-start(f32[2,16,128]{2,1,0:T(8,128)S(1)} %pad_maximum_fusion), channel_id=1, source_target_pairs={{0,24},{8,0},{16,8},{24,16},{1,25},{9,1},{17,9},{25,17},{2,26},{10... | collective-permute-start | bytes 49160 | tf_op jit(solution)/shard_map/ppermute | solution.py:636
  73.7 3.7 %collective-permute-start.22 = (f32[2,16,128]{2,1,0:T(8,128)S(1)}, f32[2,16,128]{2,1,0:T(8,128)S(1)}, u32[]{:S(2)}, u32[]{:S(2)}) collective-permute-start(f32[2,16,128]{2,1,0:T(8,128)S(1)} %pad_maximum_fusion), channel_id=1, source_target_pairs={{0,16},{8,24},{16,0},{24,8},{1,17},{9,25},{17,1},{25,9},{2,18},{10... | collective-permute-start | bytes 49160 | tf_op jit(solution)/shard_map/ppermute | solution.py:636
  74.9 4.6 %collective-permute-start.23 = (f32[2,16,128]{2,1,0:T(8,128)S(1)}, f32[2,16,128]{2,1,0:T(8,128)S(1)}, u32[]{:S(2)}, u32[]{:S(2)}) collective-permute-start(f32[2,16,128]{2,1,0:T(8,128)S(1)} %pad_maximum_fusion), channel_id=1, source_target_pairs={{0,8},{8,16},{16,24},{24,0},{1,9},{9,17},{17,25},{25,1},{2,10},{10... | collective-permute-start | bytes 49160 | tf_op jit(solution)/shard_map/ppermute | solution.py:636
  79.6 7.2 %collective-permute-start.24 = (f32[2,16,128]{2,1,0:T(8,128)S(1)}, f32[2,16,128]{2,1,0:T(8,128)S(1)}, u32[]{:S(2)}, u32[]{:S(2)}) collective-permute-start(f32[2,16,128]{2,1,0:T(8,128)S(1)} %pad_maximum_fusion.1), channel_id=1, source_target_pairs={{0,6},{2,0},{4,2},{6,4},{1,7},{3,1},{5,3},{7,5},{8,14},{10,8},{12,... | collective-permute-start | bytes 49160 | tf_op jit(solution)/shard_map/ppermute | solution.py:636
  82.2 4.6 %collective-permute-start.25 = (f32[2,16,128]{2,1,0:T(8,128)S(1)}, f32[2,16,128]{2,1,0:T(8,128)S(1)}, u32[]{:S(2)}, u32[]{:S(2)}) collective-permute-start(f32[2,16,128]{2,1,0:T(8,128)S(1)} %pad_maximum_fusion.1), channel_id=1, source_target_pairs={{0,4},{2,6},{4,0},{6,2},{1,5},{3,7},{5,1},{7,3},{8,12},{10,14},{12... | collective-permute-start | bytes 49160 | tf_op jit(solution)/shard_map/ppermute | solution.py:636
  85.0 5.5 %collective-permute-start.26 = (f32[2,16,128]{2,1,0:T(8,128)S(1)}, f32[2,16,128]{2,1,0:T(8,128)S(1)}, u32[]{:S(2)}, u32[]{:S(2)}) collective-permute-start(f32[2,16,128]{2,1,0:T(8,128)S(1)} %pad_maximum_fusion.1), channel_id=1, source_target_pairs={{0,2},{2,4},{4,6},{6,0},{1,3},{3,5},{5,7},{7,1},{8,10},{10,12},{12... | collective-permute-start | bytes 49160 | tf_op jit(solution)/shard_map/ppermute | solution.py:636

commit v6 on v5

--- a/solution.py
+++ b/solution.py
@@ -91,10 +91,14 @@
         body(r)
 
 
-def exchange_y(a, b, n):
-    even = [(i, i ^ 1) for i in range(n)]
-    odd = [(i, i + (1 if i % 2 else -1)) for i in range(1, n - 1)]
-    return lax.ppermute(a, "gy", even), lax.ppermute(b, "gy", odd)
+def exchange_y(a, b, ny, nz):
+    even = [(i, i ^ 1) for i in range(ny)]
+    odd = []
+    for y in range(ny):
+        for z in range(nz):
+            other = (y + (1 if y % 2 else -1), z) if 0 < y < ny - 1 else (y, z ^ 1)
+            odd.append((y * nz + z, other[0] * nz + other[1]))
+    return lax.ppermute(a, "gy", even), lax.ppermute(b, ("gy", "gz"), odd)
 
 
 def exchange_x(a, b, n):
@@ -301,13 +305,15 @@
         self.x = lax.axis_index("gx") * lax.axis_size("gz") + lax.axis_index("gz")
         self.odd = lax.rem(self.x, 2) == 1
         self.below_x, self.above_x = self.x > 0, self.x < chain - 1
-        self.odd_y = lax.rem(lax.axis_index("gy"), 2) == 1
+        y = lax.axis_index("gy")
+        self.odd_y = lax.rem(y, 2) == 1
+        self.below_y, self.above_y = y > 0, y < lax.axis_size("gy") - 1
 
     def up(self, a, b):
-        return jnp.where(self.odd_y, b, a)
+        return jnp.where(self.above_y, jnp.where(self.odd_y, b, a), 0.0)
 
     def low(self, a, b):
-        return jnp.where(self.odd_y, a, b)
+        return jnp.where(self.below_y, jnp.where(self.odd_y, a, b), 0.0)
 
 
 def set_row(ref, index, row, a, b, place):
@@ -671,7 +677,7 @@
         parts,
         name="gather",
     )
-    ya, yb = exchange_y(ya, yb, ny)
+    ya, yb = exchange_y(ya, yb, ny, nz)
     edge = sds(len(edge_list(h)), 8, zs)
     xa, xb = call(force_edges_kernel, [edge, edge], (full, ya, yb), name="force_edges")
     xa, xb = exchange_x(xa, xb, chain)
@@ -719,7 +725,7 @@
                 name="moments",
             )[0]
         )
-        ya, yb = exchange_y(ya, yb, ny)
+        ya, yb = exchange_y(ya, yb, ny, nz)
         edge = sds(h, slots, zs)
         xa, xb = call(edges_kernel, [edge, edge], (p, ya, yb, moments[-1]), name="edges")
         xa, xb = exchange_x(xa, xb, chain)

time: 93 us -> 85.5 us (0.919)
  starting transfers between devices: 38.8 us -> 29.8 us
  waiting for transfers between devices: 24 us -> 25.8 us
    ppermute x8, starting transfers between devices: 18.3 us -> 10 us  [exchange_y(): return (lax.ppermute(a, 'gy', even), lax.ppermute(b, ('gy', 'gz'), odd))]
    ppermute x8, waiting for transfers between devices: 10.4 us -> 12.2 us  [exchange_y(): return (lax.ppermute(a, 'gy', even), lax.ppermute(b, ('gy', 'gz'), odd))]
    ppermute x6, starting transfers between devices: 11 us -> 9.31 us  [sum_along(): terms.append(lax.ppermute(pair, axis, moves))]
    ppermute x5, starting transfers between devices: 0.84 us -> 2.15 us  [core_shift(): return lax.ppermute(value, 'gz', [(i, (i + j) % n) for i in range(n)])]
  transfers between devices with their start and end apart: 27 -> 27, of which waited for: 11 -> 11; matrix products, arithmetic and copies ran while one was open for 0% -> 0% of each run, Pallas kernels for 17% -> 19%
where the time goes in v6:
time: 85.5 us; the launch traced here: 85.3 us
  starting transfers between devices  29.8 us (35%)
  Pallas kernels  26 us (30%)
  waiting for transfers between devices  25.8 us (30%)
  local copies, waits for them, and re-layouts  2.73 us (3%)
  between operations  0.88 us (1%)
    pallas_call x18, Pallas kernels, call(): pl.pallas_call(kernel, out_shape=outs, in_specs=specs or [VMEM] * len(ins...  26 us
    ppermute x8, waiting for transfers between devices, exchange_y(): return (lax.ppermute(a, 'gy', even), lax.ppermute(b, ('gy', 'gz'), odd))  12.2 us
    ppermute x8, starting transfers between devices, exchange_y(): return (lax.ppermute(a, 'gy', even), lax.ppermute(b, ('gy', 'gz'), odd))  10 us
    ppermute x6, starting transfers between devices, sum_along(): terms.append(lax.ppermute(pair, axis, moves))  9.31 us
    ppermute x4, starting transfers between devices, exchange_x(): lax.ppermute(b, ('gx', 'gz'), odd)  8.08 us
    ppermute x6, waiting for transfers between devices, sum_along(): terms.append(lax.ppermute(pair, axis, moves))  7.38 us
    ppermute x4, waiting for transfers between devices, exchange_x(): lax.ppermute(b, ('gx', 'gz'), odd)  3.25 us
    ppermute x5, waiting for transfers between devices, core_shift(): return lax.ppermute(value, 'gz', [(i, (i + j) % n) for i in range(n)])  2.89 us
  transfers between devices with their start and end apart: 27, of which 11 were waited for; matrix products, arithmetic and copies ran while one was open for 0% of the time, Pallas kernels for 19%

profile of v6, /device:TPU:0, one launch (start us, length us, event | category | flops | bytes accessed | tf_op | source)
XLA Modules:
  0.0 85.3 jit_solution(1102077725811786687)
XLA Ops:
  4.8 1.5 %collective-permute-done.refs_1_ = f32[4,16,16,128]{3,2,1,0:T(8,128)S(1)} collective-permute-done((f32[4,16,16,128]{3,2,1,0:T(8,128)S(1)}, f32[4,16,16,128]{3,2,1,0:T(8,128)S(1)}, u32[]{:S(2)}, u32[]{:S(2)}) %collective-permute-start) | collective-permute-done | bytes 524320 | tf_op jit(solution)/shard_map/ppermute | solution.py:111
  6.5 3.0 %collective-permute-start.1 = (f32[68,4,256]{2,1,0:T(4,128)S(1)}, f32[68,4,256]{2,1,0:T(4,128)S(1)}, u32[]{:S(2)}, u32[]{:S(2)}) collective-permute-start(f32[68,4,256]{2,1,0:T(4,128)S(1)} %get-tuple-element.68), channel_id=1, source_target_pairs={{0,2},{2,0},{4,6},{6,4},{1,3},{3,1},{5,7},{7,5},{8,10},{10,8},{12,... | collective-permute-start | bytes 835592 | tf_op jit(solution)/shard_map/ppermute | solution.py:101
  9.5 7.0 %collective-permute-done.1.ya.refs_1_ = f32[68,4,256]{2,1,0:T(4,128)S(1)} collective-permute-done((f32[68,4,256]{2,1,0:T(4,128)S(1)}, f32[68,4,256]{2,1,0:T(4,128)S(1)}, u32[]{:S(2)}, u32[]{:S(2)}) %collective-permute-start.1) | collective-permute-done | bytes 278560 | tf_op jit(solution)/shard_map/ppermute | solution.py:101
  16.6 2.7 %collective-permute-start.4 = (f32[43,8,256]{2,1,0:T(8,128)S(1)}, f32[43,8,256]{2,1,0:T(8,128)S(1)}, u32[]{:S(2)}, u32[]{:S(2)}) collective-permute-start(f32[43,8,256]{2,1,0:T(8,128)S(1)} %get-tuple-element.71), channel_id=1, source_target_pairs={{0,25},{1,8},{8,1},{9,16},{16,9},{17,24},{24,17},{25,0},{2,27},{3,... | collective-permute-start | bytes 1056776 | tf_op jit(solution)/shard_map/ppermute | solution.py:107
  19.3 4.7 %first_inner.1 = (f32[24,24,256]{2,1,0:T(8,128)S(1)}, f32[24,24,256]{2,1,0:T(8,128)S(1)}, f32[24,24,256]{2,1,0:T(8,128)S(1)}, f32[3,24,24,256]{3,2,1,0:T(8,128)S...) custom-call(f32[4,16,16,256]{3,2,1,0:T(8,128)S(1)} %get-tuple-elemen, ...), custom_call_target="tpu_custom_call" | custom-call | flops 40000000 | bytes 1048576 | tf_op jit(solution)/shard_map/first_inner/pallas_call | solution.py:26
  24.1 3.2 %collective-permute-done.4.refs_4_ = f32[43,8,256]{2,1,0:T(8,128)S(1)} collective-permute-done((f32[43,8,256]{2,1,0:T(8,128)S(1)}, f32[43,8,256]{2,1,0:T(8,128)S(1)}, u32[]{:S(2)}, u32[]{:S(2)}) %collective-permute-start.4) | collective-permute-done | bytes 352288 | tf_op jit(solution)/shard_map/ppermute | solution.py:107
  27.3 2.8 %first.1 = (f32[16,16,128]{2,1,0:T(8,128)S(1)}, f32[16,16,128]{2,1,0:T(8,128)S(1)}, f32[16,16,256]{2,1,0:T(8,128)S(1)}, f32[16,4,256]{2,1,0:T(4,128)S(1)}, f32[1...) custom-call(f32[4,16,16,256]{3,2,1,0:T(8,128)S(1)} %get-tuple-elemen, ...), custom_call_target="tpu_custom_call" | custom-call | flops 40000000 | bytes 1048576 | tf_op jit(solution)/shard_map/first/pallas_call | solution.py:26
  30.2 3.1 %collective-permute-start.5 = (f32[16,4,256]{2,1,0:T(4,128)S(1)}, f32[16,4,256]{2,1,0:T(4,128)S(1)}, u32[]{:S(2)}, u32[]{:S(2)}) collective-permute-start(f32[16,4,256]{2,1,0:T(4,128)S(1)} %get-tuple-element.82), channel_id=1, source_target_pairs={{0,2},{2,0},{4,6},{6,4},{1,3},{3,1},{5,7},{7,5},{8,10},{10,8},{12,... | collective-permute-start | bytes 196616 | tf_op jit(solution)/shard_map/ppermute | solution.py:101
  33.8 1.8 %collective-permute-done.5.ya = f32[16,4,256]{2,1,0:T(4,128)S(1)} collective-permute-done((f32[16,4,256]{2,1,0:T(4,128)S(1)}, f32[16,4,256]{2,1,0:T(4,128)S(1)}, u32[]{:S(2)}, u32[]{:S(2)}) %collective-permute-start.5) | collective-permute-done | bytes 65568 | tf_op jit(solution)/shard_map/ppermute | solution.py:101
  35.7 2.0 %collective-permute-start.8 = (f32[4,24,256]{2,1,0:T(8,128)S(1)}, f32[4,24,256]{2,1,0:T(8,128)S(1)}, u32[]{:S(2)}, u32[]{:S(2)}) collective-permute-start(f32[4,24,256]{2,1,0:T(8,128)S(1)} %get-tuple-element.87), channel_id=1, source_target_pairs={{0,25},{1,8},{8,1},{9,16},{16,9},{17,24},{24,17},{25,0},{2,27},{3,... | collective-permute-start | bytes 294920 | tf_op jit(solution)/shard_map/ppermute | solution.py:107
  37.7 3.5 %next_inner.3 = (f32[24,24,256]{2,1,0:T(8,128)S(1)}, f32[3,24,24,256]{3,2,1,0:T(8,128)S(1)}, f32[3,24,24,256]{3,2,1,0:T(8,128)S(1)}, f32[3,24,24,256]{3,2,1,0:T(...) custom-call(f32[16,16,256]{2,1,0:T(8,128)S(1)} %get-tuple-element.81.refs_0_.p.p_in.refs_1_, ...), custom_call_target="tpu_custom_call" | custom-call | flops 40000000 | bytes 1048576 | tf_op jit(solution)/shard_map/next_inner/pallas_call | solution.py:26
  41.3 1.4 %next.3 = (f32[16,16,128]{2,1,0:T(8,128)S(1)}, f32[16,16,128]{2,1,0:T(8,128)S(1)}, f32[16,16,256]{2,1,0:T(8,128)S(1)}, f32[16,4,256]{2,1,0:T(4,128)S(1)}, f32[16,4,256]{2,1,0:T(4,128)S(1)}) custom-call(f32[16,16,256]{2,1,0:T(8,128)S(1)} %get-tuple-element.81.refs_0_.p.p_in.refs_1_, f32[4,24,256]{2,1,0:T(8,128)S(1)} %collective-permute-done.7.xa, ...), custom_call_target="tpu_custom_call" | custom-call | flops 40000000 | bytes 1048576 | tf_op jit(solution)/shard_map/next/pallas_call | solution.py:26
  42.7 1.9 %collective-permute-start.10 = (f32[16,4,256]{2,1,0:T(4,128)S(1)}, f32[16,4,256]{2,1,0:T(4,128)S(1)}, u32[]{:S(2)}, u32[]{:S(2)}) collective-permute-start(f32[16,4,256]{2,1,0:T(4,128)S(1)} %get-tuple-element.99), channel_id=1, source_target_pairs={{0,2},{2,0},{4,6},{6,4},{1,3},{3,1},{5,7},{7,5},{8,10},{10,8},{12,... | collective-permute-start | bytes 196616 | tf_op jit(solution)/shard_map/ppermute | solution.py:101
  45.2 1.8 %collective-permute-done.10.ya = f32[16,4,256]{2,1,0:T(4,128)S(1)} collective-permute-done((f32[16,4,256]{2,1,0:T(4,128)S(1)}, f32[16,4,256]{2,1,0:T(4,128)S(1)}, u32[]{:S(2)}, u32[]{:S(2)}) %collective-permute-start.10) | collective-permute-done | bytes 65568 | tf_op jit(solution)/shard_map/ppermute | solution.py:101
  47.1 1.7 %collective-permute-start.13 = (f32[4,24,256]{2,1,0:T(8,128)S(1)}, f32[4,24,256]{2,1,0:T(8,128)S(1)}, u32[]{:S(2)}, u32[]{:S(2)}) collective-permute-start(f32[4,24,256]{2,1,0:T(8,128)S(1)} %get-tuple-element.104), channel_id=1, source_target_pairs={{0,25},{1,8},{8,1},{9,16},{16,9},{17,24},{24,17},{25,0},{2,27},{3,... | collective-permute-start | bytes 294920 | tf_op jit(solution)/shard_map/ppermute | solution.py:107
  48.8 3.5 %next_inner.4 = (f32[24,24,256]{2,1,0:T(8,128)S(1)}, f32[3,24,24,256]{3,2,1,0:T(8,128)S(1)}, f32[3,24,24,256]{3,2,1,0:T(8,128)S(1)}, f32[3,24,24,256]{3,2,1,0:T(...) custom-call(f32[16,16,256]{2,1,0:T(8,128)S(1)} %get-tuple-element.98.refs_0_.p.p_in.refs_1_, ...), custom_call_target="tpu_custom_call" | custom-call | flops 40000000 | bytes 1048576 | tf_op jit(solution)/shard_map/next_inner/pallas_call | solution.py:26
  52.4 1.4 %next.4 = (f32[16,16,128]{2,1,0:T(8,128)S(1)}, f32[16,16,128]{2,1,0:T(8,128)S(1)}, f32[16,16,256]{2,1,0:T(8,128)S(1)}, f32[16,4,256]{2,1,0:T(4,128)S(1)}, f32[16,4,256]{2,1,0:T(4,128)S(1)}) custom-call(f32[16,16,256]{2,1,0:T(8,128)S(1)} %get-tuple-element.98.refs_0_.p.p_in.refs_1_, f32[4,24,256]{2,1,0:T(8,128)S(1)} %collective-permute-done.12.xa, ...), custom_call_target="tpu_custom_call" | custom-call | flops 40000000 | bytes 1048576 | tf_op jit(solution)/shard_map/next/pallas_call | solution.py:26
  53.8 2.0 %collective-permute-start.15 = (f32[16,4,256]{2,1,0:T(4,128)S(1)}, f32[16,4,256]{2,1,0:T(4,128)S(1)}, u32[]{:S(2)}, u32[]{:S(2)}) collective-permute-start(f32[16,4,256]{2,1,0:T(4,128)S(1)} %get-tuple-element.112), channel_id=1, source_target_pairs={{0,2},{2,0},{4,6},{6,4},{1,3},{3,1},{5,7},{7,5},{8,10},{10,8},{12,... | collective-permute-start | bytes 196616 | tf_op jit(solution)/shard_map/ppermute | solution.py:101
  56.5 1.7 %collective-permute-done.15.ya = f32[16,4,256]{2,1,0:T(4,128)S(1)} collective-permute-done((f32[16,4,256]{2,1,0:T(4,128)S(1)}, f32[16,4,256]{2,1,0:T(4,128)S(1)}, u32[]{:S(2)}, u32[]{:S(2)}) %collective-permute-start.15) | collective-permute-done | bytes 65568 | tf_op jit(solution)/shard_map/ppermute | solution.py:101
  58.3 1.7 %collective-permute-start.18 = (f32[4,24,256]{2,1,0:T(8,128)S(1)}, f32[4,24,256]{2,1,0:T(8,128)S(1)}, u32[]{:S(2)}, u32[]{:S(2)}) collective-permute-start(f32[4,24,256]{2,1,0:T(8,128)S(1)} %get-tuple-element.117), channel_id=1, source_target_pairs={{0,25},{1,8},{8,1},{9,16},{16,9},{17,24},{24,17},{25,0},{2,27},{3,... | collective-permute-start | bytes 294920 | tf_op jit(solution)/shard_map/ppermute | solution.py:107
  60.0 3.6 %next_inner.5 = (f32[24,24,256]{2,1,0:T(8,128)S(1)}, f32[3,24,24,256]{3,2,1,0:T(8,128)S(1)}, f32[3,24,24,256]{3,2,1,0:T(8,128)S(1)}, f32[3,24,24,256]{3,2,1,0:T(...) custom-call(f32[16,16,256]{2,1,0:T(8,128)S(1)} %get-tuple-element.111.refs_0_.p.p_in, ...), custom_call_target="tpu_custom_call" | custom-call | flops 40000000 | bytes 1048576 | tf_op jit(solution)/shard_map/next_inner/pallas_call | solution.py:26
  63.7 1.4 %next.5 = (f32[16,16,128]{2,1,0:T(8,128)S(1)}, f32[17,16,128]{2,1,0:T(8,128)S(1)}) custom-call(f32[16,16,256]{2,1,0:T(8,128)S(1)} %get-tuple-element.111.refs_0_.p.p_in, f32[4,24,256]{2,1,0:T(8,128)S(1)} %collective-permute-done.17.xa, f32[4,24,256]{2,1,0:T(8,128)S(1)} %collective-permute-done.18.xb, f32[4,16,16,256]{3,2,1,0:T(8,128)S(1)} %get-tuple-element.67.full.refs_0_, ...), custom_call_target="tpu_custom_call" | custom-call | flops 40000000 | bytes 1048576 | tf_op jit(solution)/shard_map/next/pallas_call | solution.py:26
  65.2 1.3 %collective-permute-done.20.refs_7_ = f32[17,16,128]{2,1,0:T(8,128)S(1)} collective-permute-done((f32[17,16,128]{2,1,0:T(8,128)S(1)}, f32[17,16,128]{2,1,0:T(8,128)S(1)}, u32[]{:S(2)}, u32[]{:S(2)}) %collective-permute-start.20) | collective-permute-done | bytes 139296 | tf_op jit(solution)/shard_map/ppermute | solution.py:111
  66.6 1.8 %collective-permute-start.21 = (f32[2,16,128]{2,1,0:T(8,128)S(1)}, f32[2,16,128]{2,1,0:T(8,128)S(1)}, u32[]{:S(2)}, u32[]{:S(2)}) collective-permute-start(f32[2,16,128]{2,1,0:T(8,128)S(1)} %pad_maximum_fusion), channel_id=1, source_target_pairs={{0,24},{8,0},{16,8},{24,16},{1,25},{9,1},{17,9},{25,17},{2,26},{10... | collective-permute-start | bytes 49160 | tf_op jit(solution)/shard_map/ppermute | solution.py:642
  68.3 1.1 %collective-permute-start.22 = (f32[2,16,128]{2,1,0:T(8,128)S(1)}, f32[2,16,128]{2,1,0:T(8,128)S(1)}, u32[]{:S(2)}, u32[]{:S(2)}) collective-permute-start(f32[2,16,128]{2,1,0:T(8,128)S(1)} %pad_maximum_fusion), channel_id=1, source_target_pairs={{0,16},{8,24},{16,0},{24,8},{1,17},{9,25},{17,1},{25,9},{2,18},{10... | collective-permute-start | bytes 49160 | tf_op jit(solution)/shard_map/ppermute | solution.py:642
  70.5 1.6 %collective-permute-done.22 = f32[2,16,128]{2,1,0:T(8,128)S(1)} collective-permute-done((f32[2,16,128]{2,1,0:T(8,128)S(1)}, f32[2,16,128]{2,1,0:T(8,128)S(1)}, u32[]{:S(2)}, u32[]{:S(2)}) %collective-permute-start.22) | collective-permute-done | bytes 16416 | tf_op jit(solution)/shard_map/ppermute | solution.py:642
  72.1 2.0 %collective-permute-done.23 = f32[2,16,128]{2,1,0:T(8,128)S(1)} collective-permute-done((f32[2,16,128]{2,1,0:T(8,128)S(1)}, f32[2,16,128]{2,1,0:T(8,128)S(1)}, u32[]{:S(2)}, u32[]{:S(2)}) %collective-permute-start.23) | collective-permute-done | bytes 16416 | tf_op jit(solution)/shard_map/ppermute | solution.py:642
  74.2 2.7 %collective-permute-start.24 = (f32[2,16,128]{2,1,0:T(8,128)S(1)}, f32[2,16,128]{2,1,0:T(8,128)S(1)}, u32[]{:S(2)}, u32[]{:S(2)}) collective-permute-start(f32[2,16,128]{2,1,0:T(8,128)S(1)} %pad_maximum_fusion.1), channel_id=1, source_target_pairs={{0,6},{2,0},{4,2},{6,4},{1,7},{3,1},{5,3},{7,5},{8,14},{10,8},{12,... | collective-permute-start | bytes 49160 | tf_op jit(solution)/shard_map/ppermute | solution.py:642
  77.8 1.8 %collective-permute-start.26 = (f32[2,16,128]{2,1,0:T(8,128)S(1)}, f32[2,16,128]{2,1,0:T(8,128)S(1)}, u32[]{:S(2)}, u32[]{:S(2)}) collective-permute-start(f32[2,16,128]{2,1,0:T(8,128)S(1)} %pad_maximum_fusion.1), channel_id=1, source_target_pairs={{0,2},{2,4},{4,6},{6,0},{1,3},{3,5},{5,7},{7,1},{8,10},{10,12},{12... | collective-permute-start | bytes 49160 | tf_op jit(solution)/shard_map/ppermute | solution.py:642
  79.5 2.0 %collective-permute-done.25 = f32[2,16,128]{2,1,0:T(8,128)S(1)} collective-permute-done((f32[2,16,128]{2,1,0:T(8,128)S(1)}, f32[2,16,128]{2,1,0:T(8,128)S(1)}, u32[]{:S(2)}, u32[]{:S(2)}) %collective-permute-start.25) | collective-permute-done | bytes 16416 | tf_op jit(solution)/shard_map/ppermute | solution.py:642
  81.5 1.8 %collective-permute-done.26 = f32[2,16,128]{2,1,0:T(8,128)S(1)} collective-permute-done((f32[2,16,128]{2,1,0:T(8,128)S(1)}, f32[2,16,128]{2,1,0:T(8,128)S(1)}, u32[]{:S(2)}, u32[]{:S(2)}) %collective-permute-start.26) | collective-permute-done | bytes 16416 | tf_op jit(solution)/shard_map/ppermute | solution.py:642
  83.4 2.0 %last.1 = (f32[32,16,128]{2,1,0:T(8,128)}, f32[32,16,128]{2,1,0:T(8,128)}, f32[3]{0:T(128)}) custom-call(f32[2,16,128]{2,1,0:T(8,128)S(1)} %pad_maximum_fusion.2.sums, f32[32,16,128]{2,1,0:T(8,128)S(1)} %get-tuple-element.125.eta, f32[16,16,128]{2,1,0:T(8,128)S(1)} %get-tuple-element.84.refs_1_.refs_2_.refs_0_, ...), custom_call_target="tpu_custom_call" | custom-call | flops 1000000 | bytes 1048576 | tf_op jit(solution)/shard_map/last/pallas_call | solution.py:26
  (58 shorter events, 8.8 us)
Async XLA Ops:
  0.6 1.1 %copy-start = (f32[3,32,16,128]{3,2,1,0:T(8,128)S(1)}, f32[3,32,16,128]{3,2,1,0:T(8,128)}, u32[]{:S(2)}) copy-start(f32[3,32,16,128]{3,2,1,0:T(8,128)} %force.1) | copy-start | bytes 2359300
  1.8 0.9 %copy-start.1 = (s32[32,16,128]{2,1,0:T(8,128)S(1)}, s32[32,16,128]{2,1,0:T(8,128)}, u32[]{:S(2)}) copy-start(s32[32,16,128]{2,1,0:T(8,128)} %phase.1) | copy-start | bytes 786436
  2.7 0.7 copy-start.3
  3.4 16.0 %copy-start.2 = (s32[6]{0:T(128)S(1)}, s32[6]{0:T(128)}, u32[]{:S(2)}) copy-start(s32[6]{0:T(128)} %refs_5_.1) | copy-start | bytes 76
  4.2 2.1 %collective-permute-start = (f32[4,16,16,128]{3,2,1,0:T(8,128)S(1)}, f32[4,16,16,128]{3,2,1,0:T(8,128)S(1)}, u32[]{:S(2)}, u32[]{:S(2)}) collective-permute-start(f32[4,16,16,128]{3,2,1,0:T(8,128)S(1)} %get-tuple-element.66), channel_id=1, source_target_pairs={{0,1},{1,0},{2,3},{3,2},{4,5},{5,4},{6,7},{7,6},{8,9},{9,8},{10,11... | collective-permute-start | bytes 1572872 | tf_op jit(solution)/shard_map/ppermute | solution.py:111
  6.5 10.0 %collective-permute-start.1 = (f32[68,4,256]{2,1,0:T(4,128)S(1)}, f32[68,4,256]{2,1,0:T(4,128)S(1)}, u32[]{:S(2)}, u32[]{:S(2)}) collective-permute-start(f32[68,4,256]{2,1,0:T(4,128)S(1)} %get-tuple-element.68), channel_id=1, source_target_pairs={{0,2},{2,0},{4,6},{6,4},{1,3},{3,1},{5,7},{7,5},{8,10},{10,8},{12,... | collective-permute-start | bytes 835592 | tf_op jit(solution)/shard_map/ppermute | solution.py:101
  9.5 7.0 %collective-permute-start.2 = (f32[68,4,256]{2,1,0:T(4,128)S(1)}, f32[68,4,256]{2,1,0:T(4,128)S(1)}, u32[]{:S(2)}, u32[]{:S(2)}) collective-permute-start(f32[68,4,256]{2,1,0:T(4,128)S(1)} %get-tuple-element.69), channel_id=1, source_target_pairs={{0,1},{1,0},{2,4},{3,5},{4,2},{5,3},{6,7},{7,6},{8,9},{9,8},{10,12... | collective-permute-start | bytes 835592 | tf_op jit(solution)/shard_map/ppermute | solution.py:101
  16.6 7.5 %collective-permute-start.3 = (f32[43,8,256]{2,1,0:T(8,128)S(1)}, f32[43,8,256]{2,1,0:T(8,128)S(1)}, u32[]{:S(2)}, u32[]{:S(2)}) collective-permute-start(f32[43,8,256]{2,1,0:T(8,128)S(1)} %get-tuple-element.70), channel_id=1, source_target_pairs={{0,1},{1,0},{8,9},{9,8},{16,17},{17,16},{24,25},{25,24},{2,3},{3,2... | collective-permute-start | bytes 1056776 | tf_op jit(solution)/shard_map/ppermute | solution.py:107
  16.6 10.7 %collective-permute-start.4 = (f32[43,8,256]{2,1,0:T(8,128)S(1)}, f32[43,8,256]{2,1,0:T(8,128)S(1)}, u32[]{:S(2)}, u32[]{:S(2)}) collective-permute-start(f32[43,8,256]{2,1,0:T(8,128)S(1)} %get-tuple-element.71), channel_id=1, source_target_pairs={{0,25},{1,8},{8,1},{9,16},{16,9},{17,24},{24,17},{25,0},{2,27},{3,... | collective-permute-start | bytes 1056776 | tf_op jit(solution)/shard_map/ppermute | solution.py:107
  30.2 5.5 %collective-permute-start.5 = (f32[16,4,256]{2,1,0:T(4,128)S(1)}, f32[16,4,256]{2,1,0:T(4,128)S(1)}, u32[]{:S(2)}, u32[]{:S(2)}) collective-permute-start(f32[16,4,256]{2,1,0:T(4,128)S(1)} %get-tuple-element.82), channel_id=1, source_target_pairs={{0,2},{2,0},{4,6},{6,4},{1,3},{3,1},{5,7},{7,5},{8,10},{10,8},{12,... | collective-permute-start | bytes 196616 | tf_op jit(solution)/shard_map/ppermute | solution.py:101
  33.2 2.4 %collective-permute-start.6 = (f32[16,4,256]{2,1,0:T(4,128)S(1)}, f32[16,4,256]{2,1,0:T(4,128)S(1)}, u32[]{:S(2)}, u32[]{:S(2)}) collective-permute-start(f32[16,4,256]{2,1,0:T(4,128)S(1)} %get-tuple-element.83), channel_id=1, source_target_pairs={{0,1},{1,0},{2,4},{3,5},{4,2},{5,3},{6,7},{7,6},{8,9},{9,8},{10,12... | collective-permute-start | bytes 196616 | tf_op jit(solution)/shard_map/ppermute | solution.py:101
  33.2 4.4 %collective-permute-start.9 = (f32[16,16,128]{2,1,0:T(8,128)S(1)}, f32[16,16,128]{2,1,0:T(8,128)S(1)}, u32[]{:S(2)}, u32[]{:S(2)}) collective-permute-start(f32[16,16,128]{2,1,0:T(8,128)S(1)} %get-tuple-element.85.refs_2_.refs_3_), channel_id=1, source_target_pairs={{0,1},{1,0},{2,3},{3,2},{4,5},{5,4},{6,7},{7,6},{8,9},{9,8},{10,11... | collective-permute-start | bytes 393224 | tf_op jit(solution)/shard_map/ppermute | solution.py:111
  35.6 5.6 %collective-permute-start.7 = (f32[4,24,256]{2,1,0:T(8,128)S(1)}, f32[4,24,256]{2,1,0:T(8,128)S(1)}, u32[]{:S(2)}, u32[]{:S(2)}) collective-permute-start(f32[4,24,256]{2,1,0:T(8,128)S(1)} %get-tuple-element.86), channel_id=1, source_target_pairs={{0,1},{1,0},{8,9},{9,8},{16,17},{17,16},{24,25},{25,24},{2,3},{3,2... | collective-permute-start | bytes 294920 | tf_op jit(solution)/shard_map/ppermute | solution.py:107
  35.7 5.5 %collective-permute-start.8 = (f32[4,24,256]{2,1,0:T(8,128)S(1)}, f32[4,24,256]{2,1,0:T(8,128)S(1)}, u32[]{:S(2)}, u32[]{:S(2)}) collective-permute-start(f32[4,24,256]{2,1,0:T(8,128)S(1)} %get-tuple-element.87), channel_id=1, source_target_pairs={{0,25},{1,8},{8,1},{9,16},{16,9},{17,24},{24,17},{25,0},{2,27},{3,... | collective-permute-start | bytes 294920 | tf_op jit(solution)/shard_map/ppermute | solution.py:107
  42.7 4.3 %collective-permute-start.10 = (f32[16,4,256]{2,1,0:T(4,128)S(1)}, f32[16,4,256]{2,1,0:T(4,128)S(1)}, u32[]{:S(2)}, u32[]{:S(2)}) collective-permute-start(f32[16,4,256]{2,1,0:T(4,128)S(1)} %get-tuple-element.99), channel_id=1, source_target_pairs={{0,2},{2,0},{4,6},{6,4},{1,3},{3,1},{5,7},{7,5},{8,10},{10,8},{12,... | collective-permute-start | bytes 196616 | tf_op jit(solution)/shard_map/ppermute | solution.py:101
  44.6 2.5 %collective-permute-start.11 = (f32[16,4,256]{2,1,0:T(4,128)S(1)}, f32[16,4,256]{2,1,0:T(4,128)S(1)}, u32[]{:S(2)}, u32[]{:S(2)}) collective-permute-start(f32[16,4,256]{2,1,0:T(4,128)S(1)} %get-tuple-element.100), channel_id=1, source_target_pairs={{0,1},{1,0},{2,4},{3,5},{4,2},{5,3},{6,7},{7,6},{8,9},{9,8},{10,12... | collective-permute-start | bytes 196616 | tf_op jit(solution)/shard_map/ppermute | solution.py:101
  44.6 4.2 %collective-permute-start.14 = (f32[16,16,128]{2,1,0:T(8,128)S(1)}, f32[16,16,128]{2,1,0:T(8,128)S(1)}, u32[]{:S(2)}, u32[]{:S(2)}) collective-permute-start(f32[16,16,128]{2,1,0:T(8,128)S(1)} %get-tuple-element.102.refs_5_), channel_id=1, source_target_pairs={{0,1},{1,0},{2,3},{3,2},{4,5},{5,4},{6,7},{7,6},{8,9},{9,8},{10,11... | collective-permute-start | bytes 393224 | tf_op jit(solution)/shard_map/ppermute | solution.py:111
  47.0 5.3 %collective-permute-start.12 = (f32[4,24,256]{2,1,0:T(8,128)S(1)}, f32[4,24,256]{2,1,0:T(8,128)S(1)}, u32[]{:S(2)}, u32[]{:S(2)}) collective-permute-start(f32[4,24,256]{2,1,0:T(8,128)S(1)} %get-tuple-element.103), channel_id=1, source_target_pairs={{0,1},{1,0},{8,9},{9,8},{16,17},{17,16},{24,25},{25,24},{2,3},{3,2... | collective-permute-start | bytes 294920 | tf_op jit(solution)/shard_map/ppermute | solution.py:107
  47.1 5.2 %collective-permute-start.13 = (f32[4,24,256]{2,1,0:T(8,128)S(1)}, f32[4,24,256]{2,1,0:T(8,128)S(1)}, u32[]{:S(2)}, u32[]{:S(2)}) collective-permute-start(f32[4,24,256]{2,1,0:T(8,128)S(1)} %get-tuple-element.104), channel_id=1, source_target_pairs={{0,25},{1,8},{8,1},{9,16},{16,9},{17,24},{24,17},{25,0},{2,27},{3,... | collective-permute-start | bytes 294920 | tf_op jit(solution)/shard_map/ppermute | solution.py:107
  53.8 4.4 %collective-permute-start.15 = (f32[16,4,256]{2,1,0:T(4,128)S(1)}, f32[16,4,256]{2,1,0:T(4,128)S(1)}, u32[]{:S(2)}, u32[]{:S(2)}) collective-permute-start(f32[16,4,256]{2,1,0:T(4,128)S(1)} %get-tuple-element.112), channel_id=1, source_target_pairs={{0,2},{2,0},{4,6},{6,4},{1,3},{3,1},{5,7},{7,5},{8,10},{10,8},{12,... | collective-permute-start | bytes 196616 | tf_op jit(solution)/shard_map/ppermute | solution.py:101
  55.8 2.4 %collective-permute-start.16 = (f32[16,4,256]{2,1,0:T(4,128)S(1)}, f32[16,4,256]{2,1,0:T(4,128)S(1)}, u32[]{:S(2)}, u32[]{:S(2)}) collective-permute-start(f32[16,4,256]{2,1,0:T(4,128)S(1)} %get-tuple-element.113), channel_id=1, source_target_pairs={{0,1},{1,0},{2,4},{3,5},{4,2},{5,3},{6,7},{7,6},{8,9},{9,8},{10,12... | collective-permute-start | bytes 196616 | tf_op jit(solution)/shard_map/ppermute | solution.py:101
  55.8 4.2 %collective-permute-start.19 = (f32[16,16,128]{2,1,0:T(8,128)S(1)}, f32[16,16,128]{2,1,0:T(8,128)S(1)}, u32[]{:S(2)}, u32[]{:S(2)}) collective-permute-start(f32[16,16,128]{2,1,0:T(8,128)S(1)} %get-tuple-element.115.refs_7_), channel_id=1, source_target_pairs={{0,1},{1,0},{2,3},{3,2},{4,5},{5,4},{6,7},{7,6},{8,9},{9,8},{10,11... | collective-permute-start | bytes 393224 | tf_op jit(solution)/shard_map/ppermute | solution.py:111
  58.2 5.4 %collective-permute-start.17 = (f32[4,24,256]{2,1,0:T(8,128)S(1)}, f32[4,24,256]{2,1,0:T(8,128)S(1)}, u32[]{:S(2)}, u32[]{:S(2)}) collective-permute-start(f32[4,24,256]{2,1,0:T(8,128)S(1)} %get-tuple-element.116), channel_id=1, source_target_pairs={{0,1},{1,0},{8,9},{9,8},{16,17},{17,16},{24,25},{25,24},{2,3},{3,2... | collective-permute-start | bytes 294920 | tf_op jit(solution)/shard_map/ppermute | solution.py:107
  58.3 5.4 %collective-permute-start.18 = (f32[4,24,256]{2,1,0:T(8,128)S(1)}, f32[4,24,256]{2,1,0:T(8,128)S(1)}, u32[]{:S(2)}, u32[]{:S(2)}) collective-permute-start(f32[4,24,256]{2,1,0:T(8,128)S(1)} %get-tuple-element.117), channel_id=1, source_target_pairs={{0,25},{1,8},{8,1},{9,16},{16,9},{17,24},{24,17},{25,0},{2,27},{3,... | collective-permute-start | bytes 294920 | tf_op jit(solution)/shard_map/ppermute | solution.py:107
  65.1 1.4 %collective-permute-start.20 = (f32[17,16,128]{2,1,0:T(8,128)S(1)}, f32[17,16,128]{2,1,0:T(8,128)S(1)}, u32[]{:S(2)}, u32[]{:S(2)}) collective-permute-start(f32[17,16,128]{2,1,0:T(8,128)S(1)} %get-tuple-element.124), channel_id=1, source_target_pairs={{0,1},{1,0},{2,3},{3,2},{4,5},{5,4},{6,7},{7,6},{8,9},{9,8},{10,11... | collective-permute-start | bytes 417800 | tf_op jit(solution)/shard_map/ppermute | solution.py:111
  66.6 3.9 %collective-permute-start.21 = (f32[2,16,128]{2,1,0:T(8,128)S(1)}, f32[2,16,128]{2,1,0:T(8,128)S(1)}, u32[]{:S(2)}, u32[]{:S(2)}) collective-permute-start(f32[2,16,128]{2,1,0:T(8,128)S(1)} %pad_maximum_fusion), channel_id=1, source_target_pairs={{0,24},{8,0},{16,8},{24,16},{1,25},{9,1},{17,9},{25,17},{2,26},{10... | collective-permute-start | bytes 49160 | tf_op jit(solution)/shard_map/ppermute | solution.py:642
  68.3 3.7 %collective-permute-start.22 = (f32[2,16,128]{2,1,0:T(8,128)S(1)}, f32[2,16,128]{2,1,0:T(8,128)S(1)}, u32[]{:S(2)}, u32[]{:S(2)}) collective-permute-start(f32[2,16,128]{2,1,0:T(8,128)S(1)} %pad_maximum_fusion), channel_id=1, source_target_pairs={{0,16},{8,24},{16,0},{24,8},{1,17},{9,25},{17,1},{25,9},{2,18},{10... | collective-permute-start | bytes 49160 | tf_op jit(solution)/shard_map/ppermute | solution.py:642
  69.5 4.6 %collective-permute-start.23 = (f32[2,16,128]{2,1,0:T(8,128)S(1)}, f32[2,16,128]{2,1,0:T(8,128)S(1)}, u32[]{:S(2)}, u32[]{:S(2)}) collective-permute-start(f32[2,16,128]{2,1,0:T(8,128)S(1)} %pad_maximum_fusion), channel_id=1, source_target_pairs={{0,8},{8,16},{16,24},{24,0},{1,9},{9,17},{17,25},{25,1},{2,10},{10... | collective-permute-start | bytes 49160 | tf_op jit(solution)/shard_map/ppermute | solution.py:642
  74.2 5.4 %collective-permute-start.24 = (f32[2,16,128]{2,1,0:T(8,128)S(1)}, f32[2,16,128]{2,1,0:T(8,128)S(1)}, u32[]{:S(2)}, u32[]{:S(2)}) collective-permute-start(f32[2,16,128]{2,1,0:T(8,128)S(1)} %pad_maximum_fusion.1), channel_id=1, source_target_pairs={{0,6},{2,0},{4,2},{6,4},{1,7},{3,1},{5,3},{7,5},{8,14},{10,8},{12,... | collective-permute-start | bytes 49160 | tf_op jit(solution)/shard_map/ppermute | solution.py:642
  76.9 4.6 %collective-permute-start.25 = (f32[2,16,128]{2,1,0:T(8,128)S(1)}, f32[2,16,128]{2,1,0:T(8,128)S(1)}, u32[]{:S(2)}, u32[]{:S(2)}) collective-permute-start(f32[2,16,128]{2,1,0:T(8,128)S(1)} %pad_maximum_fusion.1), channel_id=1, source_target_pairs={{0,4},{2,6},{4,0},{6,2},{1,5},{3,7},{5,1},{7,3},{8,12},{10,14},{12... | collective-permute-start | bytes 49160 | tf_op jit(solution)/shard_map/ppermute | solution.py:642
  77.8 5.5 %collective-permute-start.26 = (f32[2,16,128]{2,1,0:T(8,128)S(1)}, f32[2,16,128]{2,1,0:T(8,128)S(1)}, u32[]{:S(2)}, u32[]{:S(2)}) collective-permute-start(f32[2,16,128]{2,1,0:T(8,128)S(1)} %pad_maximum_fusion.1), channel_id=1, source_target_pairs={{0,2},{2,4},{4,6},{6,0},{1,3},{3,5},{5,7},{7,1},{8,10},{10,12},{12... | collective-permute-start | bytes 49160 | tf_op jit(solution)/shard_map/ppermute | solution.py:642

commit v7 on v6

--- a/solution.py
+++ b/solution.py
@@ -214,8 +214,14 @@
     return full, inner
 
 
-def outside(full, inner):
-    return list(range(full[0], inner[0])) + list(range(inner[1], full[1]))
+def outside(full, inner, side):
+    return range(full[0], inner[0]) if side == "low" else range(inner[1], full[1])
+
+
+def on_side(near, body):
+    odd = Place().odd
+    pl.when(odd)(lambda: body("low" if near else "high"))
+    pl.when(jnp.logical_not(odd))(lambda: body("high" if near else "low"))
 
 
 def update(source, b, w, kx, ky, kz, target, r):
@@ -237,6 +243,12 @@
     return out + (jnp.where(lane == 0, 0.0, down_z(vz)) - vz)
 
 
+def emit_early(emit, near_side, full, inner, out_inner, out_near):
+    for r in outside(full[SWEEPS], inner[SWEEPS], near_side):
+        emit(r - HALO, out_near[r - HALO])
+    rows_loop(inner[SWEEPS][0] - HALO, inner[SWEEPS][1] - HALO, lambda r: emit(r, out_inner[r]), 4)
+
+
 def inner_solve(b, levels, out, inner, w, kx, ky, kz):
     source = b
     for s in range(1, SWEEPS):
@@ -254,14 +266,14 @@
     rows_loop(*inner[SWEEPS], last, 2)
 
 
-def outer_solve(b, levels, buffers, inner, full, w, kx, ky, kz, emit):
+def outer_solve(side, b, levels, buffers, inner, full, w, kx, ky, kz, emit):
     source = b
     for s in range(1, SWEEPS):
         target = buffers[s - 1]
-        for r in outside(full[s], inner[s]):
+        for r in outside(full[s], inner[s], side):
             update(source, b, w, kx, ky, kz, target, r)
         source = Rows(levels[s - 1], target, *inner[s])
-    for r in outside(full[SWEEPS], inner[SWEEPS]):
+    for r in outside(full[SWEEPS], inner[SWEEPS], side):
         emit(r - HALO, diverge(source, r))
 
 
@@ -388,61 +400,84 @@
     inner_solve(b, levels, out, inner, w, kx, ky, kz)
 
 
-def first_outer(n, sizes, *refs):
-    full, ya, yb, xa, xb, flags, *early = refs[: 11 + SWEEPS]
+def first_side(n, sizes, near, *refs):
+    count = 10 + SWEEPS
+    full, ya, yb, xs, flags, *early = refs[:count]
     kx0, ky0, kz0, w0, b0, *levels, out0 = early
-    refs = refs[11 + SWEEPS :]
-    v_own, v_others, refs = refs[0], refs[1:n], refs[n:]
-    p_out, send_a, send_b, kx, ky, kz, w = refs[:7]
-    force, eta, line, b, *buffers = refs[7:]
+    if near:
+        kx, ky, kz, w, out, *scratch = refs[count:]
+    else:
+        out_near, refs = refs[count], refs[count + 1 :]
+        v_own, v_others, refs = refs[0], refs[1:n], refs[n:]
+        p_out, send_a, send_b, kx, ky, kz, w, *scratch = refs
+    force, eta, line, b, *buffers = scratch
     fields, rows, ys, lanes = full.shape
     h = HALO
     place = Place()
-    odd_x = place.odd
     slots, total = ys + 2 * h, rows + 2 * h
     ranges, inner = spans(h + 1, h + rows - 1, total)
-    todo = outside((0, total), inner[0])
-    for r in sorted({min(max(q + d, h), h + rows - 1) for q in todo for d in (-1, 0, 1)}):
-        k = r - h
-        for c in range(fields):
-            to, index = (force, (c, r)) if c < 3 else (eta, (r + 1,))
-            set_row(to, index, full[c, k], ya[c * rows + k], yb[c * rows + k], place)
-        block = fields * rows + k // 4
-        line[r] = place.low(ya[block], yb[block])[k % 4 : k % 4 + 1]
-    blank = jnp.zeros((slots, lanes), F32)
-    line_blank = jnp.zeros((1, lanes), F32)
-    for k in range(h):
-        for r in (k, h + rows + k):
-            line[r] = line_blank
-    for c in range(3):
-        force[c, 0] = blank
-        force[c, total - 1] = blank
-    eta[0] = blank
-    for t, (c, k, q) in enumerate(edge_list(h)):
-        lower, upper = jnp.where(odd_x, xa[t], xb[t]), jnp.where(odd_x, xb[t], xa[t])
-        where = slice(8 * q, 8 * q + 8)
-        if c < 3:
-            force[c, k, where, :] = lower
-            force[c, total - 1 - k, where, :] = upper
+    coefs = coefs_at(sizes, place.x, slots, lanes, rows, ys, flags)
+
+    def body(side):
+        todo = outside((0, total), inner[0], side)
+        for r in sorted({min(max(q + d, h), h + rows - 1) for q in todo for d in (-1, 0, 1)}):
+            k = r - h
+            for c in range(fields):
+                to, index = (force, (c, r)) if c < 3 else (eta, (r + 1,))
+                set_row(to, index, full[c, k], ya[c * rows + k], yb[c * rows + k], place)
+            block = fields * rows + k // 4
+            line[r] = place.low(ya[block], yb[block])[k % 4 : k % 4 + 1]
+        low = side == "low"
+        blank = jnp.zeros((slots, lanes), F32)
+        for k in range(h):
+            line[k if low else h + rows + k] = jnp.zeros((1, lanes), F32)
+        for c in range(3):
+            force[c, 0 if low else total - 1] = blank
+        if low:
+            eta[0] = blank
+        for t, (c, k, q) in enumerate(edge_list(h)):
+            where = slice(8 * q, 8 * q + 8)
+            if c < 3:
+                force[c, k if low else total - 1 - k, where, :] = xs[t]
+            elif low or k >= 0:
+                eta[1 + k if low else total - k, where, :] = xs[t]
+        for r in todo:
+            after = eta[min(r + 2, total)]
+            coefs(r, eta[r + 1], eta[r], after, line[r], lambda c: force[c, r], kx, ky, kz, w, b)
+        early_late = [(kx0, kx), (ky0, ky), (kz0, kz), (w0, w), (b0, b)]
+        kxs, kys, kzs, ws, bs = (Rows(e, f, *inner[0]) for e, f in early_late)
+        if near:
+
+            def emit(r, value):
+                out[r] = value
+
+            outer_solve(side, bs, levels, buffers, inner, ranges, ws, kxs, kys, kzs, emit)
         else:
-            eta[1 + k, where, :] = lower
-            if k >= 0:
-                eta[total - k, where, :] = upper
-    coefs = coefs_at(sizes, place.x, slots, lanes, rows, ys, flags)
-    for r in todo:
-        after = eta[min(r + 2, total)]
-        coefs(r, eta[r + 1], eta[r], after, line[r], lambda c: force[c, r], kx, ky, kz, w, b)
-
-    def carry(r):
-        kx[r], ky[r], kz[r] = kx0[r], ky0[r], kz0[r]
+            emit = emit_result(v_own, v_others, p_out, send_a, send_b, lambda r: full[3, r])
+            outer_solve(side, bs, levels, buffers, inner, ranges, ws, kxs, kys, kzs, emit)
+            emit_early(emit, "high" if low else "low", ranges, inner, out0, out_near)
+
+    on_side(near, body)
+
+
+def join_kernel(total, rows, *refs):
+    inner_refs, near_refs, far_refs, outs = (refs[4 * k : 4 * k + 4] for k in range(4))
+    _, inner = spans(HALO + 1, HALO + rows - 1, total)
+
+    def carry(source, r):
+        for k in range(3):
+            outs[k][r] = source[k][r]
         for c in range(3):
-            w[c, r] = w0[c, r]
-
-    rows_loop(*inner[0], carry, 2)
-    b = Rows(b0, b, *inner[0])
-    emit = emit_result(v_own, v_others, p_out, send_a, send_b, lambda r: full[3, r])
-    outer_solve(b, levels, buffers, inner, ranges, w, kx, ky, kz, emit)
-    rows_loop(inner[SWEEPS][0] - h, inner[SWEEPS][1] - h, lambda r: emit(r, out0[r]), 4)
+            outs[3][c, r] = source[3][c, r]
+
+    rows_loop(*inner[0], lambda r: carry(inner_refs, r), 2)
+    for near, source in ((True, near_refs), (False, far_refs)):
+
+        def body(side, source=source):
+            for r in outside((0, total), inner[0], side):
+                carry(source, r)
+
+        on_side(near, body)
 
 
 def next_inner(extra, p_in, ya, yb, kx, ky, kz, w, *rest):
@@ -470,37 +505,55 @@
     b[2, r] = w[2, r] * (jnp.where(lane == lanes - 1, 0.0, up_z(mid)) - mid)
 
 
-def next_outer(n, last, p_in, xa, xb, full, kx, ky, kz, w, p0, b0, *refs):
-    levels, out0, refs = refs[: SWEEPS - 1], refs[SWEEPS - 1], refs[SWEEPS:]
-    if last:
-        partials, refs = refs[:ITERS], refs[ITERS:]
-    v_own, v_others, refs = refs[0], refs[1:n], refs[n:]
-    p_out = send_a = send_b = sums = None
-    if last:
-        moment, acc, refs = v_others[-1].at[p_in.shape[0]], refs[-1], refs[:-1]
-        acc[...] = jnp.zeros_like(acc)
-
-        def sums(r, v):
-            acc[...] = acc[...] + v * p_in[r]
+def next_side(n, near, last, p_in, xs, kx, ky, kz, w, p0, b0, *refs):
+    levels, refs = refs[: SWEEPS - 1], refs[SWEEPS - 1 :]
+    if near:
+        out, *scratch = refs
     else:
-        p_out, send_a, send_b, *refs = refs
-    p, b, *buffers = refs
+        full, out0, out_near, refs = refs[0], refs[1], refs[2], refs[3:]
+        sums = p_out = send_a = send_b = None
+        if last:
+            partials, refs = refs[:ITERS], refs[ITERS:]
+        v_own, v_others, refs = refs[0], refs[1:n], refs[n:]
+        if last:
+            moment, acc, refs = v_others[-1].at[p_in.shape[0]], refs[-1], refs[:-1]
+            acc[...] = jnp.zeros_like(acc)
+
+            def sums(r, v):
+                acc[...] = acc[...] + v * p_in[r]
+        else:
+            p_out, send_a, send_b, *refs = refs
+        scratch = refs
+    p, b, *buffers = scratch
     rows = p_in.shape[0]
     h = HALO
     place = Place()
-    for k in range(h):
-        lower, upper = jnp.where(place.odd, xa[k], xb[k]), jnp.where(place.odd, xb[k], xa[k])
-        p[k] = jnp.where(place.below_x, lower, 0.0)
-        p[h + rows + k] = jnp.where(place.above_x, upper, 0.0)
     ranges, inner = spans(h, h + rows - 1, rows + 2 * h)
-    p = Rows(p0, p, h, h + rows)
-    for r in outside(ranges[0], inner[0]):
-        grads(p, w, b, r)
-    b = Rows(b0, b, *inner[0])
-    emit = emit_result(v_own, v_others, p_out, send_a, send_b, lambda r: full[3, r], sums)
-    outer_solve(b, levels, buffers, inner, ranges, w, kx, ky, kz, emit)
-    rows_loop(inner[SWEEPS][0] - h, inner[SWEEPS][1] - h, lambda r: emit(r, out0[r]), 4)
-    if last:
+
+    def body(side):
+        low = side == "low"
+        for k in range(h):
+            row = xs[k]
+            if not near:
+                row = jnp.where(place.below_x if low else place.above_x, row, 0.0)
+            p[k if low else h + rows + k] = row
+        ps = Rows(p0, p, h, h + rows)
+        for r in outside(ranges[0], inner[0], side):
+            grads(ps, w, b, r)
+        bs = Rows(b0, b, *inner[0])
+        if near:
+
+            def emit(r, value):
+                out[r] = value
+
+            outer_solve(side, bs, levels, buffers, inner, ranges, w, kx, ky, kz, emit)
+        else:
+            emit = emit_result(v_own, v_others, p_out, send_a, send_b, lambda r: full[3, r], sums)
+            outer_solve(side, bs, levels, buffers, inner, ranges, w, kx, ky, kz, emit)
+            emit_early(emit, "high" if low else "low", ranges, inner, out0, out_near)
+
+    on_side(near, body)
+    if not near and last:
         moment[...] = jnp.zeros_like(moment)
         at = 0
         for ref in partials:
@@ -697,18 +750,34 @@
         heavy,
         "first_inner",
     )
+    scratch = [field, pltpu.VMEM((total + 1, slots, zs), F32), line] + [field] * SWEEPS
+    result = sds(rows, slots, zs)
+    near = call(
+        functools.partial(first_side, nz, sizes, True),
+        [scalar] * 3 + [vector, result],
+        (full, ya, yb, xa, flags, *early),
+        [VMEM] * 4 + [SMEM] + [VMEM] * len(early),
+        scratch,
+        heavy // 2,
+        "first_near",
+    )
     outs = call(
-        functools.partial(first_outer, nz, sizes),
+        functools.partial(first_side, nz, sizes, False),
         v_shape + sent + [scalar] * 3 + [vector],
-        (full, ya, yb, xa, xb, flags, *early),
-        [VMEM] * 5 + [SMEM] + [VMEM] * len(early),
-        [field, pltpu.VMEM((total + 1, slots, zs), F32), line] + [field] * SWEEPS,
-        heavy,
+        (full, ya, yb, xb, flags, *early, near[-1]),
+        [VMEM] * 4 + [SMEM] + [VMEM] * (len(early) + 1),
+        scratch,
+        heavy // 2,
         "first",
+    )
+    coefs = call(
+        functools.partial(join_kernel, total, rows),
+        [scalar] * 3 + [vector],
+        (*early[:4], *near[:4], *outs[nz + 3 :]),
+        name="join",
     )
     vs, ps, moments = [list(outs[:nz])], [outs[nz]], []
     ya, yb = outs[nz + 1 : nz + 3]
-    coefs = outs[nz + 3 :]
     placed = []
     for step in range(1, ITERS + 1):
         last = step == ITERS
@@ -738,16 +807,24 @@
             heavy,
             "next_inner",
         )
+        scratch = [pltpu.VMEM((total, slots, zs), F32)] + [field] * SWEEPS
+        near = call(
+            functools.partial(next_side, nz, True, last),
+            [result],
+            (p, xa, *coefs, *early[:-1]),
+            None,
+            scratch,
+            heavy // 4,
+            "next_near",
+        )
         joint = v_shape[:-1] + [sds(rows + 1, ys, lanes)]
         outs = call(
-            functools.partial(next_outer, nz, last),
+            functools.partial(next_side, nz, False, last),
             joint if last else v_shape + sent,
-            (p, xa, xb, full, *coefs, *early, *(moments if last else ())),
+            (p, xb, *coefs, *early[:-1], full, early[-1], *near, *(moments if last else ())),
             None,
-            [pltpu.VMEM((total, slots, zs), F32)]
-            + [field] * SWEEPS
-            + ([pltpu.VMEM((ys, zs), F32)] if last else []),
-            heavy,
+            scratch + ([pltpu.VMEM((ys, zs), F32)] if last else []),
+            heavy // 4,
             "next",
         )
         vs.append(list(outs[:nz]))

time: 85.5 us -> 84.7 us (level)
  waiting for transfers between devices: 25.8 us -> 23.9 us
  Pallas kernels: 26 us -> 27.9 us
  starting transfers between devices: 29.8 us -> 28.8 us
    pallas_call x18 -> x23, Pallas kernels: 26 us -> 27.9 us  [call(): pl.pallas_call(kernel, out_shape=outs, in_specs=specs or [VMEM] * len(ins...]
    ppermute x4, waiting for transfers between devices: 3.25 us -> 1.64 us  [exchange_x(): lax.ppermute(b, ('gx', 'gz'), odd)]
  transfers between devices with their start and end apart: 27 -> 27, of which waited for: 11 -> 13; matrix products, arithmetic and copies ran while one was open for 0% -> 0% of each run, Pallas kernels for 19% -> 24%
where the time goes in v7:
time: 84.7 us; the launch traced here: 84.5 us
  starting transfers between devices  28.8 us (34%)
  Pallas kernels  27.9 us (33%)
  waiting for transfers between devices  23.9 us (28%)
  local copies, waits for them, and re-layouts  2.73 us (3%)
  between operations  1.07 us (1%)
    pallas_call x23, Pallas kernels, call(): pl.pallas_call(kernel, out_shape=outs, in_specs=specs or [VMEM] * len(ins...  27.9 us
    ppermute x8, waiting for transfers between devices, exchange_y(): return (lax.ppermute(a, 'gy', even), lax.ppermute(b, ('gy', 'gz'), odd))  11.8 us
    ppermute x8, starting transfers between devices, exchange_y(): return (lax.ppermute(a, 'gy', even), lax.ppermute(b, ('gy', 'gz'), odd))  10.3 us
    ppermute x6, starting transfers between devices, sum_along(): terms.append(lax.ppermute(pair, axis, moves))  8.47 us
    ppermute x4, starting transfers between devices, exchange_x(): lax.ppermute(b, ('gx', 'gz'), odd)  7.56 us
    ppermute x6, waiting for transfers between devices, sum_along(): terms.append(lax.ppermute(pair, axis, moves))  7.55 us
    ppermute x5, waiting for transfers between devices, core_shift(): return lax.ppermute(value, 'gz', [(i, (i + j) % n) for i in range(n)])  2.89 us
    unnamed x8, local copies, waits for them, and re-layouts  2.73 us
  transfers between devices with their start and end apart: 27, of which 13 were waited for; matrix products, arithmetic and copies ran while one was open for 0% of the time, Pallas kernels for 24%

profile of v7, /device:TPU:0, one launch (start us, length us, event | category | flops | bytes accessed | tf_op | source)
XLA Modules:
  0.0 84.5 jit_solution(2883443192702560056)
XLA Ops:
  0.6 1.1 %copy-done = f32[3,32,16,128]{3,2,1,0:T(8,128)S(1)} copy-done((f32[3,32,16,128]{3,2,1,0:T(8,128)S(1)}, f32[3,32,16,128]{3,2,1,0:T(8,128)}, u32[]{:S(2)}) %copy-start) | copy-done | bytes 786456
  1.8 0.9 %copy-done.1 = s32[32,16,128]{2,1,0:T(8,128)S(1)} copy-done((s32[32,16,128]{2,1,0:T(8,128)S(1)}, s32[32,16,128]{2,1,0:T(8,128)}, u32[]{:S(2)}) %copy-start.1) | copy-done | bytes 262168
  4.8 1.5 %collective-permute-done.refs_1_ = f32[4,16,16,128]{3,2,1,0:T(8,128)S(1)} collective-permute-done((f32[4,16,16,128]{3,2,1,0:T(8,128)S(1)}, f32[4,16,16,128]{3,2,1,0:T(8,128)S(1)}, u32[]{:S(2)}, u32[]{:S(2)}) %collective-permute-start) | collective-permute-done | bytes 524320 | tf_op jit(solution)/shard_map/ppermute | solution.py:111
  6.5 3.0 %collective-permute-start.1 = (f32[68,4,256]{2,1,0:T(4,128)S(1)}, f32[68,4,256]{2,1,0:T(4,128)S(1)}, u32[]{:S(2)}, u32[]{:S(2)}) collective-permute-start(f32[68,4,256]{2,1,0:T(4,128)S(1)} %get-tuple-element.77), channel_id=1, source_target_pairs={{0,2},{2,0},{4,6},{6,4},{1,3},{3,1},{5,7},{7,5},{8,10},{10,8},{12,... | collective-permute-start | bytes 835592 | tf_op jit(solution)/shard_map/ppermute | solution.py:101
  9.5 7.0 %collective-permute-done.1.ya.refs_1_ = f32[68,4,256]{2,1,0:T(4,128)S(1)} collective-permute-done((f32[68,4,256]{2,1,0:T(4,128)S(1)}, f32[68,4,256]{2,1,0:T(4,128)S(1)}, u32[]{:S(2)}, u32[]{:S(2)}) %collective-permute-start.1) | collective-permute-done | bytes 278560 | tf_op jit(solution)/shard_map/ppermute | solution.py:101
  16.6 2.7 %collective-permute-start.3 = (f32[43,8,256]{2,1,0:T(8,128)S(1)}, f32[43,8,256]{2,1,0:T(8,128)S(1)}, u32[]{:S(2)}, u32[]{:S(2)}) collective-permute-start(f32[43,8,256]{2,1,0:T(8,128)S(1)} %get-tuple-element.79), channel_id=1, source_target_pairs={{0,25},{1,8},{8,1},{9,16},{16,9},{17,24},{24,17},{25,0},{2,27},{3,... | collective-permute-start | bytes 1056776 | tf_op jit(solution)/shard_map/ppermute | solution.py:107
  19.3 4.8 %first_inner.1 = (f32[24,24,256]{2,1,0:T(8,128)S(1)}, f32[24,24,256]{2,1,0:T(8,128)S(1)}, f32[24,24,256]{2,1,0:T(8,128)S(1)}, f32[3,24,24,256]{3,2,1,0:T(8,128)S...) custom-call(f32[4,16,16,256]{3,2,1,0:T(8,128)S(1)} %get-tuple-elemen, ...), custom_call_target="tpu_custom_call" | custom-call | flops 40000000 | bytes 1048576 | tf_op jit(solution)/shard_map/first_inner/pallas_call | solution.py:26
  24.2 1.7 %first_near.1 = (f32[24,24,256]{2,1,0:T(8,128)S(1)}, f32[24,24,256]{2,1,0:T(8,128)S(1)}, f32[24,24,256]{2,1,0:T(8,128)S(1)}, f32[3,24,24,256]{3,2,1,0:T(8,128)S(1)}, f32[16,24,256]{2,1,0:T(8,128)S(1)}) custom-call(f32[4,16,16,256]{3,2,1,0:T(8,128)S(1)} %get-tuple-element.76.full.refs_0_.refs_3_, f32[68,4,256]{2,1,0:T(4,128)S(1)} %collective-permute-done.1.ya.refs_1_, ...), custom_call_target="tpu_custom_call" | custom-call | flops 20000000 | bytes 1048576 | tf_op jit(solution)/shard_map/first_near/pallas_call | solution.py:26
  25.8 1.5 %collective-permute-done.3.refs_3_ = f32[43,8,256]{2,1,0:T(8,128)S(1)} collective-permute-done((f32[43,8,256]{2,1,0:T(8,128)S(1)}, f32[43,8,256]{2,1,0:T(8,128)S(1)}, u32[]{:S(2)}, u32[]{:S(2)}) %collective-permute-start.3) | collective-permute-done | bytes 352288 | tf_op jit(solution)/shard_map/ppermute | solution.py:107
  27.3 1.9 %first.1 = (f32[16,16,128]{2,1,0:T(8,128)S(1)}, f32[16,16,128]{2,1,0:T(8,128)S(1)}, f32[16,16,256]{2,1,0:T(8,128)S(1)}, f32[16,4,256]{2,1,0:T(4,128)S(1)}, f32[1...) custom-call(f32[4,16,16,256]{3,2,1,0:T(8,128)S(1)} %get-tuple-elemen, ...), custom_call_target="tpu_custom_call" | custom-call | flops 20000000 | bytes 1048576 | tf_op jit(solution)/shard_map/first/pallas_call | solution.py:26
  29.2 3.1 %collective-permute-start.5 = (f32[16,4,256]{2,1,0:T(4,128)S(1)}, f32[16,4,256]{2,1,0:T(4,128)S(1)}, u32[]{:S(2)}, u32[]{:S(2)}) collective-permute-start(f32[16,4,256]{2,1,0:T(4,128)S(1)} %get-tuple-element.92), channel_id=1, source_target_pairs={{0,2},{2,0},{4,6},{6,4},{1,3},{3,1},{5,7},{7,5},{8,10},{10,8},{12,... | collective-permute-start | bytes 196616 | tf_op jit(solution)/shard_map/ppermute | solution.py:101
  32.9 1.6 %collective-permute-done.5.ya = f32[16,4,256]{2,1,0:T(4,128)S(1)} collective-permute-done((f32[16,4,256]{2,1,0:T(4,128)S(1)}, f32[16,4,256]{2,1,0:T(4,128)S(1)}, u32[]{:S(2)}, u32[]{:S(2)}) %collective-permute-start.5) | collective-permute-done | bytes 65568 | tf_op jit(solution)/shard_map/ppermute | solution.py:101
  34.6 1.9 %collective-permute-start.7 = (f32[4,24,256]{2,1,0:T(8,128)S(1)}, f32[4,24,256]{2,1,0:T(8,128)S(1)}, u32[]{:S(2)}, u32[]{:S(2)}) collective-permute-start(f32[4,24,256]{2,1,0:T(8,128)S(1)} %get-tuple-element.96), channel_id=1, source_target_pairs={{0,25},{1,8},{8,1},{9,16},{16,9},{17,24},{24,17},{25,0},{2,27},{3,... | collective-permute-start | bytes 294920 | tf_op jit(solution)/shard_map/ppermute | solution.py:107
  36.8 3.5 %next_inner.3 = (f32[24,24,256]{2,1,0:T(8,128)S(1)}, f32[3,24,24,256]{3,2,1,0:T(8,128)S(1)}, f32[3,24,24,256]{3,2,1,0:T(8,128)S(1)}, f32[3,24,24,256]{3,2,1,0:T(...) custom-call(f32[16,16,256]{2,1,0:T(8,128)S(1)} %get-tuple-element.91.refs_0_.p.p_in.refs_1_, ...), custom_call_target="tpu_custom_call" | custom-call | flops 40000000 | bytes 1048576 | tf_op jit(solution)/shard_map/next_inner/pallas_call | solution.py:26
  41.2 1.0 %next.3 = (f32[16,16,128]{2,1,0:T(8,128)S(1)}, f32[16,16,128]{2,1,0:T(8,128)S(1)}, f32[16,16,256]{2,1,0:T(8,128)S(1)}, f32[16,4,256]{2,1,0:T(4,128)S(1)}, f32[16,4,256]{2,1,0:T(4,128)S(1)}) custom-call(f32[16,16,256]{2,1,0:T(8,128)S(1)} %get-tuple-element.91.refs_0_.p.p_in.refs_1_, f32[4,24,256]{2,1,0:T(8,128)S(1)} %collective-permute-done.7.xs, ...), custom_call_target="tpu_custom_call" | custom-call | flops 10000000 | bytes 1048576 | tf_op jit(solution)/shard_map/next/pallas_call | solution.py:26
  42.3 2.0 %collective-permute-start.10 = (f32[16,4,256]{2,1,0:T(4,128)S(1)}, f32[16,4,256]{2,1,0:T(4,128)S(1)}, u32[]{:S(2)}, u32[]{:S(2)}) collective-permute-start(f32[16,4,256]{2,1,0:T(4,128)S(1)} %get-tuple-element.117), channel_id=1, source_target_pairs={{0,2},{2,0},{4,6},{6,4},{1,3},{3,1},{5,7},{7,5},{8,10},{10,8},{12,... | collective-permute-start | bytes 196616 | tf_op jit(solution)/shard_map/ppermute | solution.py:101
  44.9 1.7 %collective-permute-done.10.ya = f32[16,4,256]{2,1,0:T(4,128)S(1)} collective-permute-done((f32[16,4,256]{2,1,0:T(4,128)S(1)}, f32[16,4,256]{2,1,0:T(4,128)S(1)}, u32[]{:S(2)}, u32[]{:S(2)}) %collective-permute-start.10) | collective-permute-done | bytes 65568 | tf_op jit(solution)/shard_map/ppermute | solution.py:101
  46.7 1.7 %collective-permute-start.12 = (f32[4,24,256]{2,1,0:T(8,128)S(1)}, f32[4,24,256]{2,1,0:T(8,128)S(1)}, u32[]{:S(2)}, u32[]{:S(2)}) collective-permute-start(f32[4,24,256]{2,1,0:T(8,128)S(1)} %get-tuple-element.121), channel_id=1, source_target_pairs={{0,25},{1,8},{8,1},{9,16},{16,9},{17,24},{24,17},{25,0},{2,27},{3,... | collective-permute-start | bytes 294920 | tf_op jit(solution)/shard_map/ppermute | solution.py:107
  48.4 3.4 %next_inner.4 = (f32[24,24,256]{2,1,0:T(8,128)S(1)}, f32[3,24,24,256]{3,2,1,0:T(8,128)S(1)}, f32[3,24,24,256]{3,2,1,0:T(8,128)S(1)}, f32[3,24,24,256]{3,2,1,0:T(...) custom-call(f32[16,16,256]{2,1,0:T(8,128)S(1)} %get-tuple-element.116.refs_0_.p.p_in.refs_1_, ...), custom_call_target="tpu_custom_call" | custom-call | flops 40000000 | bytes 1048576 | tf_op jit(solution)/shard_map/next_inner/pallas_call | solution.py:26
  53.5 2.2 %collective-permute-start.15 = (f32[16,4,256]{2,1,0:T(4,128)S(1)}, f32[16,4,256]{2,1,0:T(4,128)S(1)}, u32[]{:S(2)}, u32[]{:S(2)}) collective-permute-start(f32[16,4,256]{2,1,0:T(4,128)S(1)} %get-tuple-element.130), channel_id=1, source_target_pairs={{0,2},{2,0},{4,6},{6,4},{1,3},{3,1},{5,7},{7,5},{8,10},{10,8},{12,... | collective-permute-start | bytes 196616 | tf_op jit(solution)/shard_map/ppermute | solution.py:101
  56.4 1.6 %collective-permute-done.15.ya = f32[16,4,256]{2,1,0:T(4,128)S(1)} collective-permute-done((f32[16,4,256]{2,1,0:T(4,128)S(1)}, f32[16,4,256]{2,1,0:T(4,128)S(1)}, u32[]{:S(2)}, u32[]{:S(2)}) %collective-permute-start.15) | collective-permute-done | bytes 65568 | tf_op jit(solution)/shard_map/ppermute | solution.py:101
  58.0 1.3 %collective-permute-start.17 = (f32[4,24,256]{2,1,0:T(8,128)S(1)}, f32[4,24,256]{2,1,0:T(8,128)S(1)}, u32[]{:S(2)}, u32[]{:S(2)}) collective-permute-start(f32[4,24,256]{2,1,0:T(8,128)S(1)} %get-tuple-element.134), channel_id=1, source_target_pairs={{0,25},{1,8},{8,1},{9,16},{16,9},{17,24},{24,17},{25,0},{2,27},{3,... | collective-permute-start | bytes 294920 | tf_op jit(solution)/shard_map/ppermute | solution.py:107
  59.3 3.5 %next_inner.5 = (f32[24,24,256]{2,1,0:T(8,128)S(1)}, f32[3,24,24,256]{3,2,1,0:T(8,128)S(1)}, f32[3,24,24,256]{3,2,1,0:T(8,128)S(1)}, f32[3,24,24,256]{3,2,1,0:T(...) custom-call(f32[16,16,256]{2,1,0:T(8,128)S(1)} %get-tuple-element.129.refs_0_.p.p_in, ...), custom_call_target="tpu_custom_call" | custom-call | flops 40000000 | bytes 1048576 | tf_op jit(solution)/shard_map/next_inner/pallas_call | solution.py:26
  64.9 1.3 %collective-permute-done.20.refs_7_ = f32[17,16,128]{2,1,0:T(8,128)S(1)} collective-permute-done((f32[17,16,128]{2,1,0:T(8,128)S(1)}, f32[17,16,128]{2,1,0:T(8,128)S(1)}, u32[]{:S(2)}, u32[]{:S(2)}) %collective-permute-start.20) | collective-permute-done | bytes 139296 | tf_op jit(solution)/shard_map/ppermute | solution.py:111
  66.2 1.3 %collective-permute-start.21 = (f32[2,16,128]{2,1,0:T(8,128)S(1)}, f32[2,16,128]{2,1,0:T(8,128)S(1)}, u32[]{:S(2)}, u32[]{:S(2)}) collective-permute-start(f32[2,16,128]{2,1,0:T(8,128)S(1)} %pad_maximum_fusion), channel_id=1, source_target_pairs={{0,24},{8,0},{16,8},{24,16},{1,25},{9,1},{17,9},{25,17},{2,26},{10... | collective-permute-start | bytes 49160 | tf_op jit(solution)/shard_map/ppermute | solution.py:695
  70.0 1.3 %collective-permute-done.22 = f32[2,16,128]{2,1,0:T(8,128)S(1)} collective-permute-done((f32[2,16,128]{2,1,0:T(8,128)S(1)}, f32[2,16,128]{2,1,0:T(8,128)S(1)}, u32[]{:S(2)}, u32[]{:S(2)}) %collective-permute-start.22) | collective-permute-done | bytes 16416 | tf_op jit(solution)/shard_map/ppermute | solution.py:695
  71.3 1.8 %collective-permute-done.23 = f32[2,16,128]{2,1,0:T(8,128)S(1)} collective-permute-done((f32[2,16,128]{2,1,0:T(8,128)S(1)}, f32[2,16,128]{2,1,0:T(8,128)S(1)}, u32[]{:S(2)}, u32[]{:S(2)}) %collective-permute-start.23) | collective-permute-done | bytes 16416 | tf_op jit(solution)/shard_map/ppermute | solution.py:695
  73.2 2.9 %collective-permute-start.24 = (f32[2,16,128]{2,1,0:T(8,128)S(1)}, f32[2,16,128]{2,1,0:T(8,128)S(1)}, u32[]{:S(2)}, u32[]{:S(2)}) collective-permute-start(f32[2,16,128]{2,1,0:T(8,128)S(1)} %pad_maximum_fusion.1), channel_id=1, source_target_pairs={{0,6},{2,0},{4,2},{6,4},{1,7},{3,1},{5,3},{7,5},{8,14},{10,8},{12,... | collective-permute-start | bytes 49160 | tf_op jit(solution)/shard_map/ppermute | solution.py:695
  76.8 1.9 %collective-permute-start.26 = (f32[2,16,128]{2,1,0:T(8,128)S(1)}, f32[2,16,128]{2,1,0:T(8,128)S(1)}, u32[]{:S(2)}, u32[]{:S(2)}) collective-permute-start(f32[2,16,128]{2,1,0:T(8,128)S(1)} %pad_maximum_fusion.1), channel_id=1, source_target_pairs={{0,2},{2,4},{4,6},{6,0},{1,3},{3,5},{5,7},{7,1},{8,10},{10,12},{12... | collective-permute-start | bytes 49160 | tf_op jit(solution)/shard_map/ppermute | solution.py:695
  78.7 2.0 %collective-permute-done.25 = f32[2,16,128]{2,1,0:T(8,128)S(1)} collective-permute-done((f32[2,16,128]{2,1,0:T(8,128)S(1)}, f32[2,16,128]{2,1,0:T(8,128)S(1)}, u32[]{:S(2)}, u32[]{:S(2)}) %collective-permute-start.25) | collective-permute-done | bytes 16416 | tf_op jit(solution)/shard_map/ppermute | solution.py:695
  80.7 1.6 %collective-permute-done.26 = f32[2,16,128]{2,1,0:T(8,128)S(1)} collective-permute-done((f32[2,16,128]{2,1,0:T(8,128)S(1)}, f32[2,16,128]{2,1,0:T(8,128)S(1)}, u32[]{:S(2)}, u32[]{:S(2)}) %collective-permute-start.26) | collective-permute-done | bytes 16416 | tf_op jit(solution)/shard_map/ppermute | solution.py:695
  82.4 2.0 %last.1 = (f32[32,16,128]{2,1,0:T(8,128)}, f32[32,16,128]{2,1,0:T(8,128)}, f32[3]{0:T(128)}) custom-call(f32[2,16,128]{2,1,0:T(8,128)S(1)} %pad_maximum_fusion.2.sums, f32[32,16,128]{2,1,0:T(8,128)S(1)} %get-tuple-element.143.eta, f32[16,16,128]{2,1,0:T(8,128)S(1)} %get-tuple-element.94.refs_1_.refs_2_.refs_0_, ...), custom_call_target="tpu_custom_call" | custom-call | flops 1000000 | bytes 1048576 | tf_op jit(solution)/shard_map/last/pallas_call | solution.py:26
  (63 shorter events, 12.6 us)
Async XLA Ops:
  0.6 1.1 %copy-start = (f32[3,32,16,128]{3,2,1,0:T(8,128)S(1)}, f32[3,32,16,128]{3,2,1,0:T(8,128)}, u32[]{:S(2)}) copy-start(f32[3,32,16,128]{3,2,1,0:T(8,128)} %force.1) | copy-start | bytes 2359300
  1.8 0.9 %copy-start.1 = (s32[32,16,128]{2,1,0:T(8,128)S(1)}, s32[32,16,128]{2,1,0:T(8,128)}, u32[]{:S(2)}) copy-start(s32[32,16,128]{2,1,0:T(8,128)} %phase.1) | copy-start | bytes 786436
  2.7 0.7 copy-start.3
  3.4 16.0 %copy-start.2 = (s32[6]{0:T(128)S(1)}, s32[6]{0:T(128)}, u32[]{:S(2)}) copy-start(s32[6]{0:T(128)} %refs_4_.3) | copy-start | bytes 76
  4.2 2.1 %collective-permute-start = (f32[4,16,16,128]{3,2,1,0:T(8,128)S(1)}, f32[4,16,16,128]{3,2,1,0:T(8,128)S(1)}, u32[]{:S(2)}, u32[]{:S(2)}) collective-permute-start(f32[4,16,16,128]{3,2,1,0:T(8,128)S(1)} %get-tuple-element.75), channel_id=1, source_target_pairs={{0,1},{1,0},{2,3},{3,2},{4,5},{5,4},{6,7},{7,6},{8,9},{9,8},{10,11... | collective-permute-start | bytes 1572872 | tf_op jit(solution)/shard_map/ppermute | solution.py:111
  6.5 10.0 %collective-permute-start.1 = (f32[68,4,256]{2,1,0:T(4,128)S(1)}, f32[68,4,256]{2,1,0:T(4,128)S(1)}, u32[]{:S(2)}, u32[]{:S(2)}) collective-permute-start(f32[68,4,256]{2,1,0:T(4,128)S(1)} %get-tuple-element.77), channel_id=1, source_target_pairs={{0,2},{2,0},{4,6},{6,4},{1,3},{3,1},{5,7},{7,5},{8,10},{10,8},{12,... | collective-permute-start | bytes 835592 | tf_op jit(solution)/shard_map/ppermute | solution.py:101
  9.5 7.0 %collective-permute-start.2 = (f32[68,4,256]{2,1,0:T(4,128)S(1)}, f32[68,4,256]{2,1,0:T(4,128)S(1)}, u32[]{:S(2)}, u32[]{:S(2)}) collective-permute-start(f32[68,4,256]{2,1,0:T(4,128)S(1)} %get-tuple-element.78), channel_id=1, source_target_pairs={{0,1},{1,0},{2,4},{3,5},{4,2},{5,3},{6,7},{7,6},{8,9},{9,8},{10,12... | collective-permute-start | bytes 835592 | tf_op jit(solution)/shard_map/ppermute | solution.py:101
  16.5 7.6 %collective-permute-start.4 = (f32[43,8,256]{2,1,0:T(8,128)S(1)}, f32[43,8,256]{2,1,0:T(8,128)S(1)}, u32[]{:S(2)}, u32[]{:S(2)}) collective-permute-start(f32[43,8,256]{2,1,0:T(8,128)S(1)} %get-tuple-element.89), channel_id=1, source_target_pairs={{0,1},{1,0},{8,9},{9,8},{16,17},{17,16},{24,25},{25,24},{2,3},{3,2... | collective-permute-start | bytes 1056776 | tf_op jit(solution)/shard_map/ppermute | solution.py:107
  16.6 10.7 %collective-permute-start.3 = (f32[43,8,256]{2,1,0:T(8,128)S(1)}, f32[43,8,256]{2,1,0:T(8,128)S(1)}, u32[]{:S(2)}, u32[]{:S(2)}) collective-permute-start(f32[43,8,256]{2,1,0:T(8,128)S(1)} %get-tuple-element.79), channel_id=1, source_target_pairs={{0,25},{1,8},{8,1},{9,16},{16,9},{17,24},{24,17},{25,0},{2,27},{3,... | collective-permute-start | bytes 1056776 | tf_op jit(solution)/shard_map/ppermute | solution.py:107
  29.2 5.3 %collective-permute-start.5 = (f32[16,4,256]{2,1,0:T(4,128)S(1)}, f32[16,4,256]{2,1,0:T(4,128)S(1)}, u32[]{:S(2)}, u32[]{:S(2)}) collective-permute-start(f32[16,4,256]{2,1,0:T(4,128)S(1)} %get-tuple-element.92), channel_id=1, source_target_pairs={{0,2},{2,0},{4,6},{6,4},{1,3},{3,1},{5,7},{7,5},{8,10},{10,8},{12,... | collective-permute-start | bytes 196616 | tf_op jit(solution)/shard_map/ppermute | solution.py:101
  32.3 2.2 %collective-permute-start.6 = (f32[16,4,256]{2,1,0:T(4,128)S(1)}, f32[16,4,256]{2,1,0:T(4,128)S(1)}, u32[]{:S(2)}, u32[]{:S(2)}) collective-permute-start(f32[16,4,256]{2,1,0:T(4,128)S(1)} %get-tuple-element.93), channel_id=1, source_target_pairs={{0,1},{1,0},{2,4},{3,5},{4,2},{5,3},{6,7},{7,6},{8,9},{9,8},{10,12... | collective-permute-start | bytes 196616 | tf_op jit(solution)/shard_map/ppermute | solution.py:101
  32.3 4.5 %collective-permute-start.8 = (f32[16,16,128]{2,1,0:T(8,128)S(1)}, f32[16,16,128]{2,1,0:T(8,128)S(1)}, u32[]{:S(2)}, u32[]{:S(2)}) collective-permute-start(f32[16,16,128]{2,1,0:T(8,128)S(1)} %get-tuple-element.95.refs_2_.refs_3_), channel_id=1, source_target_pairs={{0,1},{1,0},{2,3},{3,2},{4,5},{5,4},{6,7},{7,6},{8,9},{9,8},{10,11... | collective-permute-start | bytes 393224 | tf_op jit(solution)/shard_map/ppermute | solution.py:111
  34.6 5.8 %collective-permute-start.9 = (f32[4,24,256]{2,1,0:T(8,128)S(1)}, f32[4,24,256]{2,1,0:T(8,128)S(1)}, u32[]{:S(2)}, u32[]{:S(2)}) collective-permute-start(f32[4,24,256]{2,1,0:T(8,128)S(1)} %get-tuple-element.115), channel_id=1, source_target_pairs={{0,1},{1,0},{8,9},{9,8},{16,17},{17,16},{24,25},{25,24},{2,3},{3,2... | collective-permute-start | bytes 294920 | tf_op jit(solution)/shard_map/ppermute | solution.py:107
  34.6 6.6 %collective-permute-start.7 = (f32[4,24,256]{2,1,0:T(8,128)S(1)}, f32[4,24,256]{2,1,0:T(8,128)S(1)}, u32[]{:S(2)}, u32[]{:S(2)}) collective-permute-start(f32[4,24,256]{2,1,0:T(8,128)S(1)} %get-tuple-element.96), channel_id=1, source_target_pairs={{0,25},{1,8},{8,1},{9,16},{16,9},{17,24},{24,17},{25,0},{2,27},{3,... | collective-permute-start | bytes 294920 | tf_op jit(solution)/shard_map/ppermute | solution.py:107
  42.3 4.3 %collective-permute-start.10 = (f32[16,4,256]{2,1,0:T(4,128)S(1)}, f32[16,4,256]{2,1,0:T(4,128)S(1)}, u32[]{:S(2)}, u32[]{:S(2)}) collective-permute-start(f32[16,4,256]{2,1,0:T(4,128)S(1)} %get-tuple-element.117), channel_id=1, source_target_pairs={{0,2},{2,0},{4,6},{6,4},{1,3},{3,1},{5,7},{7,5},{8,10},{10,8},{12,... | collective-permute-start | bytes 196616 | tf_op jit(solution)/shard_map/ppermute | solution.py:101
  44.3 2.3 %collective-permute-start.11 = (f32[16,4,256]{2,1,0:T(4,128)S(1)}, f32[16,4,256]{2,1,0:T(4,128)S(1)}, u32[]{:S(2)}, u32[]{:S(2)}) collective-permute-start(f32[16,4,256]{2,1,0:T(4,128)S(1)} %get-tuple-element.118), channel_id=1, source_target_pairs={{0,1},{1,0},{2,4},{3,5},{4,2},{5,3},{6,7},{7,6},{8,9},{9,8},{10,12... | collective-permute-start | bytes 196616 | tf_op jit(solution)/shard_map/ppermute | solution.py:101
  44.3 4.1 %collective-permute-start.13 = (f32[16,16,128]{2,1,0:T(8,128)S(1)}, f32[16,16,128]{2,1,0:T(8,128)S(1)}, u32[]{:S(2)}, u32[]{:S(2)}) collective-permute-start(f32[16,16,128]{2,1,0:T(8,128)S(1)} %get-tuple-element.120.refs_5_), channel_id=1, source_target_pairs={{0,1},{1,0},{2,3},{3,2},{4,5},{5,4},{6,7},{7,6},{8,9},{9,8},{10,11... | collective-permute-start | bytes 393224 | tf_op jit(solution)/shard_map/ppermute | solution.py:111
  46.6 5.2 %collective-permute-start.14 = (f32[4,24,256]{2,1,0:T(8,128)S(1)}, f32[4,24,256]{2,1,0:T(8,128)S(1)}, u32[]{:S(2)}, u32[]{:S(2)}) collective-permute-start(f32[4,24,256]{2,1,0:T(8,128)S(1)} %get-tuple-element.128), channel_id=1, source_target_pairs={{0,1},{1,0},{8,9},{9,8},{16,17},{17,16},{24,25},{25,24},{2,3},{3,2... | collective-permute-start | bytes 294920 | tf_op jit(solution)/shard_map/ppermute | solution.py:107
  46.7 6.0 %collective-permute-start.12 = (f32[4,24,256]{2,1,0:T(8,128)S(1)}, f32[4,24,256]{2,1,0:T(8,128)S(1)}, u32[]{:S(2)}, u32[]{:S(2)}) collective-permute-start(f32[4,24,256]{2,1,0:T(8,128)S(1)} %get-tuple-element.121), channel_id=1, source_target_pairs={{0,25},{1,8},{8,1},{9,16},{16,9},{17,24},{24,17},{25,0},{2,27},{3,... | collective-permute-start | bytes 294920 | tf_op jit(solution)/shard_map/ppermute | solution.py:107
  53.5 4.4 %collective-permute-start.15 = (f32[16,4,256]{2,1,0:T(4,128)S(1)}, f32[16,4,256]{2,1,0:T(4,128)S(1)}, u32[]{:S(2)}, u32[]{:S(2)}) collective-permute-start(f32[16,4,256]{2,1,0:T(4,128)S(1)} %get-tuple-element.130), channel_id=1, source_target_pairs={{0,2},{2,0},{4,6},{6,4},{1,3},{3,1},{5,7},{7,5},{8,10},{10,8},{12,... | collective-permute-start | bytes 196616 | tf_op jit(solution)/shard_map/ppermute | solution.py:101
  55.7 2.2 %collective-permute-start.16 = (f32[16,4,256]{2,1,0:T(4,128)S(1)}, f32[16,4,256]{2,1,0:T(4,128)S(1)}, u32[]{:S(2)}, u32[]{:S(2)}) collective-permute-start(f32[16,4,256]{2,1,0:T(4,128)S(1)} %get-tuple-element.131), channel_id=1, source_target_pairs={{0,1},{1,0},{2,4},{3,5},{4,2},{5,3},{6,7},{7,6},{8,9},{9,8},{10,12... | collective-permute-start | bytes 196616 | tf_op jit(solution)/shard_map/ppermute | solution.py:101
  55.7 3.6 %collective-permute-start.18 = (f32[16,16,128]{2,1,0:T(8,128)S(1)}, f32[16,16,128]{2,1,0:T(8,128)S(1)}, u32[]{:S(2)}, u32[]{:S(2)}) collective-permute-start(f32[16,16,128]{2,1,0:T(8,128)S(1)} %get-tuple-element.133.refs_7_), channel_id=1, source_target_pairs={{0,1},{1,0},{2,3},{3,2},{4,5},{5,4},{6,7},{7,6},{8,9},{9,8},{10,11... | collective-permute-start | bytes 393224 | tf_op jit(solution)/shard_map/ppermute | solution.py:111
  58.0 4.9 %collective-permute-start.19 = (f32[4,24,256]{2,1,0:T(8,128)S(1)}, f32[4,24,256]{2,1,0:T(8,128)S(1)}, u32[]{:S(2)}, u32[]{:S(2)}) collective-permute-start(f32[4,24,256]{2,1,0:T(8,128)S(1)} %get-tuple-element.141), channel_id=1, source_target_pairs={{0,1},{1,0},{8,9},{9,8},{16,17},{17,16},{24,25},{25,24},{2,3},{3,2... | collective-permute-start | bytes 294920 | tf_op jit(solution)/shard_map/ppermute | solution.py:107
  58.0 5.9 %collective-permute-start.17 = (f32[4,24,256]{2,1,0:T(8,128)S(1)}, f32[4,24,256]{2,1,0:T(8,128)S(1)}, u32[]{:S(2)}, u32[]{:S(2)}) collective-permute-start(f32[4,24,256]{2,1,0:T(8,128)S(1)} %get-tuple-element.134), channel_id=1, source_target_pairs={{0,25},{1,8},{8,1},{9,16},{16,9},{17,24},{24,17},{25,0},{2,27},{3,... | collective-permute-start | bytes 294920 | tf_op jit(solution)/shard_map/ppermute | solution.py:107
  64.8 1.4 %collective-permute-start.20 = (f32[17,16,128]{2,1,0:T(8,128)S(1)}, f32[17,16,128]{2,1,0:T(8,128)S(1)}, u32[]{:S(2)}, u32[]{:S(2)}) collective-permute-start(f32[17,16,128]{2,1,0:T(8,128)S(1)} %get-tuple-element.142), channel_id=1, source_target_pairs={{0,1},{1,0},{2,3},{3,2},{4,5},{5,4},{6,7},{7,6},{8,9},{9,8},{10,11... | collective-permute-start | bytes 417800 | tf_op jit(solution)/shard_map/ppermute | solution.py:111
  66.2 3.8 %collective-permute-start.21 = (f32[2,16,128]{2,1,0:T(8,128)S(1)}, f32[2,16,128]{2,1,0:T(8,128)S(1)}, u32[]{:S(2)}, u32[]{:S(2)}) collective-permute-start(f32[2,16,128]{2,1,0:T(8,128)S(1)} %pad_maximum_fusion), channel_id=1, source_target_pairs={{0,24},{8,0},{16,8},{24,16},{1,25},{9,1},{17,9},{25,17},{2,26},{10... | collective-permute-start | bytes 49160 | tf_op jit(solution)/shard_map/ppermute | solution.py:695
  67.6 3.7 %collective-permute-start.22 = (f32[2,16,128]{2,1,0:T(8,128)S(1)}, f32[2,16,128]{2,1,0:T(8,128)S(1)}, u32[]{:S(2)}, u32[]{:S(2)}) collective-permute-start(f32[2,16,128]{2,1,0:T(8,128)S(1)} %pad_maximum_fusion), channel_id=1, source_target_pairs={{0,16},{8,24},{16,0},{24,8},{1,17},{9,25},{17,1},{25,9},{2,18},{10... | collective-permute-start | bytes 49160 | tf_op jit(solution)/shard_map/ppermute | solution.py:695
  68.5 4.6 %collective-permute-start.23 = (f32[2,16,128]{2,1,0:T(8,128)S(1)}, f32[2,16,128]{2,1,0:T(8,128)S(1)}, u32[]{:S(2)}, u32[]{:S(2)}) collective-permute-start(f32[2,16,128]{2,1,0:T(8,128)S(1)} %pad_maximum_fusion), channel_id=1, source_target_pairs={{0,8},{8,16},{16,24},{24,0},{1,9},{9,17},{17,25},{25,1},{2,10},{10... | collective-permute-start | bytes 49160 | tf_op jit(solution)/shard_map/ppermute | solution.py:695
  73.2 5.6 %collective-permute-start.24 = (f32[2,16,128]{2,1,0:T(8,128)S(1)}, f32[2,16,128]{2,1,0:T(8,128)S(1)}, u32[]{:S(2)}, u32[]{:S(2)}) collective-permute-start(f32[2,16,128]{2,1,0:T(8,128)S(1)} %pad_maximum_fusion.1), channel_id=1, source_target_pairs={{0,6},{2,0},{4,2},{6,4},{1,7},{3,1},{5,3},{7,5},{8,14},{10,8},{12,... | collective-permute-start | bytes 49160 | tf_op jit(solution)/shard_map/ppermute | solution.py:695
  76.1 4.6 %collective-permute-start.25 = (f32[2,16,128]{2,1,0:T(8,128)S(1)}, f32[2,16,128]{2,1,0:T(8,128)S(1)}, u32[]{:S(2)}, u32[]{:S(2)}) collective-permute-start(f32[2,16,128]{2,1,0:T(8,128)S(1)} %pad_maximum_fusion.1), channel_id=1, source_target_pairs={{0,4},{2,6},{4,0},{6,2},{1,5},{3,7},{5,1},{7,3},{8,12},{10,14},{12... | collective-permute-start | bytes 49160 | tf_op jit(solution)/shard_map/ppermute | solution.py:695
  76.8 5.5 %collective-permute-start.26 = (f32[2,16,128]{2,1,0:T(8,128)S(1)}, f32[2,16,128]{2,1,0:T(8,128)S(1)}, u32[]{:S(2)}, u32[]{:S(2)}) collective-permute-start(f32[2,16,128]{2,1,0:T(8,128)S(1)} %pad_maximum_fusion.1), channel_id=1, source_target_pairs={{0,2},{2,4},{4,6},{6,0},{1,3},{3,5},{5,7},{7,1},{8,10},{10,12},{12... | collective-permute-start | bytes 49160 | tf_op jit(solution)/shard_map/ppermute | solution.py:695

commit v8 on v7

--- a/solution.py
+++ b/solution.py
@@ -111,34 +111,16 @@
     return lax.ppermute(value, "gz", [(i, (i + j) % n) for i in range(n)])
 
 
-def prep_kernel(n, force, phase, table, *outs):
-    core = lax.axis_index("gz")
-    rows = outs[0].shape[1]
-    eta_out = outs[n]
-    levels = table.shape[0]
-
-    def one(r):
-        ids = phase[r]
-        eta = jnp.zeros(ids.shape, F32)
-        for level in range(levels):
-            eta = jnp.where(ids == level, table[level], eta)
-        eta_out[r] = eta
-
-    rows_loop(0, phase.shape[0], one, 4)
-    for j in range(n):
-        base = lax.rem(core + j, n) * rows
-
-        def two(r, j=j, base=base):
-            for c in range(3):
-                outs[j][c, r] = force[c, base + r]
-            outs[j][3, r] = eta_out[base + r]
-
-        rows_loop(0, rows, two, 4)
+def lookup(ids, table):
+    eta = jnp.zeros(ids.shape, F32)
+    for level in range(table.shape[0]):
+        eta = jnp.where(ids == level, table[level], eta)
+    return eta
 
 
 def gather_kernel(n, *refs):
-    parts = refs[:n]
-    full, send_a, send_b = refs[n:]
+    forces, etas = refs[:n], refs[n : 2 * n]
+    full, send_a, send_b = refs[2 * n :]
     core = lax.axis_index("gz")
     odd = Place().odd_y
     fields, rows, ys, _ = full.shape
@@ -147,7 +129,8 @@
     for c in range(fields):
 
         def one(r, c=c):
-            row = join_received([p[c, r] for p in parts], core)
+            parts = [q[c, r] for q in forces] if c < 3 else [q[r] for q in etas]
+            row = join_received(parts, core)
             full[c, r] = row
             send_a[c * rows + r] = jnp.where(odd, row[:h], row[ys - h :])
             send_b[c * rows + r] = jnp.where(odd, row[ys - h :], row[:h])
@@ -249,7 +232,7 @@
     rows_loop(inner[SWEEPS][0] - HALO, inner[SWEEPS][1] - HALO, lambda r: emit(r, out_inner[r]), 4)
 
 
-def inner_solve(b, levels, out, inner, w, kx, ky, kz):
+def inner_solve(b, levels, out, inner, w, kx, ky, kz, step):
     source = b
     for s in range(1, SWEEPS):
         target = levels[s - 1]
@@ -257,7 +240,7 @@
         def one(r, source=source, target=target):
             update(source, b, w, kx, ky, kz, target, r)
 
-        rows_loop(*inner[s], one)
+        rows_loop(*inner[s], one, step)
         source = target
 
     def last(r):
@@ -397,7 +380,7 @@
 
     _, inner = spans(h + 1, h + rows - 1, total)
     rows_loop(*inner[0], at, 1)
-    inner_solve(b, levels, out, inner, w, kx, ky, kz)
+    inner_solve(b, levels, out, inner, w, kx, ky, kz, 3)
 
 
 def first_side(n, sizes, near, *refs):
@@ -492,8 +475,8 @@
 
     rows_loop(0, rows, fill, 4)
     _, inner = spans(h, h + rows - 1, rows + 2 * h)
-    rows_loop(*inner[0], lambda r: grads(p, w, b, r), 2)
-    inner_solve(b, levels, out, inner, w, kx, ky, kz)
+    rows_loop(*inner[0], lambda r: grads(p, w, b, r), 16)
+    inner_solve(b, levels, out, inner, w, kx, ky, kz, 16)
 
 
 def grads(p, w, b, r):
@@ -711,15 +694,15 @@
     cells = float(sizes[0] * sizes[1] * sizes[2])
     chain = nx * nz
 
-    parts = call(
-        functools.partial(prep_kernel, nz),
-        [sds(4, rows, ys, lanes)] * nz + [sds(*phase.shape)],
-        (force, phase, table),
-        [VMEM, VMEM, SMEM],
-        name="prep",
-    )
-    eta = parts[-1]
-    parts = [parts[0]] + [core_shift(parts[j], nz, j) for j in range(1, nz)]
+    core = lax.axis_index("gz")
+    eta = lookup(phase, table)
+    forces, etas = [], []
+    for j in range(nz):
+        start = lax.rem(core + j, nz) * rows
+        forces.append(lax.dynamic_slice_in_dim(force, start, rows, 1))
+        etas.append(lax.dynamic_slice_in_dim(eta, start, rows, 0))
+    forces = forces[:1] + [core_shift(forces[j], nz, j) for j in range(1, nz)]
+    etas = etas[:1] + [core_shift(etas[j], nz, j) for j in range(1, nz)]
     full, ya, yb = call(
         functools.partial(gather_kernel, nz),
         [
@@ -727,7 +710,7 @@
             sds(4 * rows + rows // 4, h, zs),
             sds(4 * rows + rows // 4, h, zs),
         ],
-        parts,
+        (*forces, *etas),
         name="gather",
     )
     ya, yb = exchange_y(ya, yb, ny, nz)

time: 84.7 us -> 88.1 us (1.040)
  other arithmetic: 0.08 us -> 5.29 us
  Pallas kernels: 27.9 us -> 24.8 us
  starting transfers between devices: 28.8 us -> 29.7 us
    select_n x0 -> x1, other arithmetic: none -> 5.21 us  [lookup(): eta = jnp.where(ids == level, table[level], eta)]
    pallas_call x23 -> x22, Pallas kernels: 27.9 us -> 24.8 us  [call(): pl.pallas_call(kernel, out_shape=outs, in_specs=specs or [VMEM] * len(ins...]
    unnamed x8 -> x4, local copies, waits for them, and re-layouts: 2.73 us -> 0.01 us
    slice x0 -> x1, local copies, waits for them, and re-layouts: none -> 1.62 us  [lookup(): eta = jnp.where(ids == level, table[level], eta)]
    dynamic_slice x0 -> x2, local copies, waits for them, and re-layouts: none -> 1.24 us  [the longest x1 1.21 us: per_device(): forces.append(lax.dynamic_slice_in_dim(force, start, rows, 1))]
    ppermute x5 -> x6, waiting for transfers between devices: 2.89 us -> 2.69 us  [core_shift(): return lax.ppermute(value, 'gz', [(i, (i + j) % n) for i in range(n)])]
    ppermute x5 -> x6, starting transfers between devices: 2.15 us -> 2.23 us  [core_shift(): return lax.ppermute(value, 'gz', [(i, (i + j) % n) for i in range(n)])]
  transfers between devices with their start and end apart: 27 -> 28, of which waited for: 13 -> 13; matrix products, arithmetic and copies ran while one was open for 0% -> 8% of each run, Pallas kernels for 24% -> 20%
where the time goes in v8:
time: 88.1 us; the launch traced here: 87.9 us
  starting transfers between devices  29.7 us (34%)
  Pallas kernels  24.8 us (28%)
  waiting for transfers between devices  24.1 us (27%)
  other arithmetic  5.29 us (6%)
  local copies, waits for them, and re-layouts  2.87 us (3%)
  between operations  1.11 us (1%)
    pallas_call x22, Pallas kernels, call(): pl.pallas_call(kernel, out_shape=outs, in_specs=specs or [VMEM] * len(ins...  24.8 us
    ppermute x8, waiting for transfers between devices, exchange_y(): return (lax.ppermute(a, 'gy', even), lax.ppermute(b, ('gy', 'gz'), odd))  12.1 us
    ppermute x8, starting transfers between devices, exchange_y(): return (lax.ppermute(a, 'gy', even), lax.ppermute(b, ('gy', 'gz'), odd))  10 us
    ppermute x6, starting transfers between devices, sum_along(): terms.append(lax.ppermute(pair, axis, moves))  9.35 us
    ppermute x4, starting transfers between devices, exchange_x(): lax.ppermute(b, ('gx', 'gz'), odd)  7.82 us
    ppermute x6, waiting for transfers between devices, sum_along(): terms.append(lax.ppermute(pair, axis, moves))  7.22 us
    select_n x1, other arithmetic, lookup(): eta = jnp.where(ids == level, table[level], eta)  5.21 us
    ppermute x6, waiting for transfers between devices, core_shift(): return lax.ppermute(value, 'gz', [(i, (i + j) % n) for i in range(n)])  2.69 us
  transfers between devices with their start and end apart: 28, of which 13 were waited for; matrix products, arithmetic and copies ran while one was open for 8% of the time, Pallas kernels for 20%

profile of v8, /device:TPU:0, one launch (start us, length us, event | category | flops | bytes accessed | tf_op | source)
XLA Modules:
  0.0 87.9 jit_solution(4925129689456883852)
XLA Ops:
  0.7 1.2 %constant_dynamic-slice_fusion.2 = (f32[3,16,16,128]{3,2,1,0:T(8,128)S(1)}, f32[3,16,16,128]{3,2,1,0:T(8,128)S(1)}) fusion(f32[3,32,16,128]{3,2,1,0:T(8,128)} %param.4, s32[]{:T(128)S(6)} %select_n.186, s32[]{:T(128)S(6)} %select_n.185), kind=kLoop, calls=%fused_computation.34 | loop fusion | bytes 1572872 | tf_op jit(solution)/shard_map/dynamic_slice | solution.py:702
  2.4 1.6 %fusion.12 = (f32[1]{0:T(128)}, f32[1]{0:T(128)}, f32[1]{0:T(128)}, f32[1]{0:T(128)}, f32[1]{0:T(128)}, /*index=5*/f32[1]{0:T(128)}, f32[1]{0:T(128)}, f32[1]{0:T(128)}) fusion(f32[8]{0:T(128)} %param.6), kind=kLoop, calls=%fused_computation.36 | loop fusion | bytes 64 | tf_op jit(solution)/shard_map/slice | solution.py:117
  4.1 5.2 %select_select_fusion.eta = f32[32,16,128]{2,1,0:T(8,128)S(1)} fusion(s32[32,16,128]{2,1,0:T(8,128)S(1)} %copy-done.1, f32[]{:T(128)} %bitcast.7, f32[]{:T(128)} %bitcast.6, f32[]{:T(128)} %bitcast.5, f32[]{:T(128)} %bitcast.4, f32[]{:T(128)} %bitcast.3, f32[]{:T(128)} %bitcast.2, f32[]{:T(128)} %bitcast.1, f32[]{:T(128)} %bitcast), kind=kLoop, calls=%fused_computation | loop fusion | flops 1048576 | bytes 524320 | tf_op jit(solution)/shard_map/jit(_where)/select_n | solution.py:117
  9.4 1.3 %collective-permute-done.1.refs_3_ = f32[16,16,128]{2,1,0:T(8,128)S(1)} collective-permute-done((f32[16,16,128]{2,1,0:T(8,128)S(1)}, f32[16,16,128]{2,1,0:T(8,128)S(1)}, u32[]{:S(2)}, u32[]{:S(2)}) %collective-permute-start.1) | collective-permute-done | bytes 131104 | tf_op jit(solution)/shard_map/ppermute | solution.py:111
  11.0 2.8 %collective-permute-start.2 = (f32[68,4,256]{2,1,0:T(4,128)S(1)}, f32[68,4,256]{2,1,0:T(4,128)S(1)}, u32[]{:S(2)}, u32[]{:S(2)}) collective-permute-start(f32[68,4,256]{2,1,0:T(4,128)S(1)} %get-tuple-element.72), channel_id=1, source_target_pairs={{0,2},{2,0},{4,6},{6,4},{1,3},{3,1},{5,7},{7,5},{8,10},{10,8},{12,... | collective-permute-start | bytes 835592 | tf_op jit(solution)/shard_map/ppermute | solution.py:101
  13.8 7.1 %collective-permute-done.2.ya.refs_1_ = f32[68,4,256]{2,1,0:T(4,128)S(1)} collective-permute-done((f32[68,4,256]{2,1,0:T(4,128)S(1)}, f32[68,4,256]{2,1,0:T(4,128)S(1)}, u32[]{:S(2)}, u32[]{:S(2)}) %collective-permute-start.2) | collective-permute-done | bytes 278560 | tf_op jit(solution)/shard_map/ppermute | solution.py:101
  21.1 2.7 %collective-permute-start.4 = (f32[43,8,256]{2,1,0:T(8,128)S(1)}, f32[43,8,256]{2,1,0:T(8,128)S(1)}, u32[]{:S(2)}, u32[]{:S(2)}) collective-permute-start(f32[43,8,256]{2,1,0:T(8,128)S(1)} %get-tuple-element.74), channel_id=1, source_target_pairs={{0,25},{1,8},{8,1},{9,16},{16,9},{17,24},{24,17},{25,0},{2,27},{3,... | collective-permute-start | bytes 1056776 | tf_op jit(solution)/shard_map/ppermute | solution.py:107
  23.8 4.8 %first_inner.1 = (f32[24,24,256]{2,1,0:T(8,128)S(1)}, f32[24,24,256]{2,1,0:T(8,128)S(1)}, f32[24,24,256]{2,1,0:T(8,128)S(1)}, f32[3,24,24,256]{3,2,1,0:T(8,128)S...) custom-call(f32[4,16,16,256]{3,2,1,0:T(8,128)S(1)} %get-tuple-elemen, ...), custom_call_target="tpu_custom_call" | custom-call | flops 40000000 | bytes 1048576 | tf_op jit(solution)/shard_map/first_inner/pallas_call | solution.py:26
  28.6 1.7 %first_near.1 = (f32[24,24,256]{2,1,0:T(8,128)S(1)}, f32[24,24,256]{2,1,0:T(8,128)S(1)}, f32[24,24,256]{2,1,0:T(8,128)S(1)}, f32[3,24,24,256]{3,2,1,0:T(8,128)S(1)}, f32[16,24,256]{2,1,0:T(8,128)S(1)}) custom-call(f32[4,16,16,256]{3,2,1,0:T(8,128)S(1)} %get-tuple-element.71.full.refs_0_.refs_3_, f32[68,4,256]{2,1,0:T(4,128)S(1)} %collective-permute-done.2.ya.refs_1_, ...), custom_call_target="tpu_custom_call" | custom-call | flops 20000000 | bytes 1048576 | tf_op jit(solution)/shard_map/first_near/pallas_call | solution.py:26
  30.3 1.5 %collective-permute-done.4.refs_3_ = f32[43,8,256]{2,1,0:T(8,128)S(1)} collective-permute-done((f32[43,8,256]{2,1,0:T(8,128)S(1)}, f32[43,8,256]{2,1,0:T(8,128)S(1)}, u32[]{:S(2)}, u32[]{:S(2)}) %collective-permute-start.4) | collective-permute-done | bytes 352288 | tf_op jit(solution)/shard_map/ppermute | solution.py:107
  31.7 1.9 %first.1 = (f32[16,16,128]{2,1,0:T(8,128)S(1)}, f32[16,16,128]{2,1,0:T(8,128)S(1)}, f32[16,16,256]{2,1,0:T(8,128)S(1)}, f32[16,4,256]{2,1,0:T(4,128)S(1)}, f32[1...) custom-call(f32[4,16,16,256]{3,2,1,0:T(8,128)S(1)} %get-tuple-elemen, ...), custom_call_target="tpu_custom_call" | custom-call | flops 20000000 | bytes 1048576 | tf_op jit(solution)/shard_map/first/pallas_call | solution.py:26
  33.6 3.1 %collective-permute-start.6 = (f32[16,4,256]{2,1,0:T(4,128)S(1)}, f32[16,4,256]{2,1,0:T(4,128)S(1)}, u32[]{:S(2)}, u32[]{:S(2)}) collective-permute-start(f32[16,4,256]{2,1,0:T(4,128)S(1)} %get-tuple-element.87), channel_id=1, source_target_pairs={{0,2},{2,0},{4,6},{6,4},{1,3},{3,1},{5,7},{7,5},{8,10},{10,8},{12,... | collective-permute-start | bytes 196616 | tf_op jit(solution)/shard_map/ppermute | solution.py:101
  37.3 1.6 %collective-permute-done.6.ya = f32[16,4,256]{2,1,0:T(4,128)S(1)} collective-permute-done((f32[16,4,256]{2,1,0:T(4,128)S(1)}, f32[16,4,256]{2,1,0:T(4,128)S(1)}, u32[]{:S(2)}, u32[]{:S(2)}) %collective-permute-start.6) | collective-permute-done | bytes 65568 | tf_op jit(solution)/shard_map/ppermute | solution.py:101
  39.1 1.9 %collective-permute-start.8 = (f32[4,24,256]{2,1,0:T(8,128)S(1)}, f32[4,24,256]{2,1,0:T(8,128)S(1)}, u32[]{:S(2)}, u32[]{:S(2)}) collective-permute-start(f32[4,24,256]{2,1,0:T(8,128)S(1)} %get-tuple-element.91), channel_id=1, source_target_pairs={{0,25},{1,8},{8,1},{9,16},{16,9},{17,24},{24,17},{25,0},{2,27},{3,... | collective-permute-start | bytes 294920 | tf_op jit(solution)/shard_map/ppermute | solution.py:107
  41.2 2.7 %next_inner.3 = (f32[24,24,256]{2,1,0:T(8,128)S(1)}, f32[3,24,24,256]{3,2,1,0:T(8,128)S(1)}, f32[3,24,24,256]{3,2,1,0:T(8,128)S(1)}, f32[3,24,24,256]{3,2,1,0:T(...) custom-call(f32[16,16,256]{2,1,0:T(8,128)S(1)} %get-tuple-element.86.refs_0_.p.p_in.refs_1_, ...), custom_call_target="tpu_custom_call" | custom-call | flops 40000000 | bytes 1048576 | tf_op jit(solution)/shard_map/next_inner/pallas_call | solution.py:26
  45.9 2.0 %collective-permute-start.11 = (f32[16,4,256]{2,1,0:T(4,128)S(1)}, f32[16,4,256]{2,1,0:T(4,128)S(1)}, u32[]{:S(2)}, u32[]{:S(2)}) collective-permute-start(f32[16,4,256]{2,1,0:T(4,128)S(1)} %get-tuple-element.112), channel_id=1, source_target_pairs={{0,2},{2,0},{4,6},{6,4},{1,3},{3,1},{5,7},{7,5},{8,10},{10,8},{12,... | collective-permute-start | bytes 196616 | tf_op jit(solution)/shard_map/ppermute | solution.py:101
  48.6 1.7 %collective-permute-done.11.ya = f32[16,4,256]{2,1,0:T(4,128)S(1)} collective-permute-done((f32[16,4,256]{2,1,0:T(4,128)S(1)}, f32[16,4,256]{2,1,0:T(4,128)S(1)}, u32[]{:S(2)}, u32[]{:S(2)}) %collective-permute-start.11) | collective-permute-done | bytes 65568 | tf_op jit(solution)/shard_map/ppermute | solution.py:101
  50.3 1.7 %collective-permute-start.13 = (f32[4,24,256]{2,1,0:T(8,128)S(1)}, f32[4,24,256]{2,1,0:T(8,128)S(1)}, u32[]{:S(2)}, u32[]{:S(2)}) collective-permute-start(f32[4,24,256]{2,1,0:T(8,128)S(1)} %get-tuple-element.116), channel_id=1, source_target_pairs={{0,25},{1,8},{8,1},{9,16},{16,9},{17,24},{24,17},{25,0},{2,27},{3,... | collective-permute-start | bytes 294920 | tf_op jit(solution)/shard_map/ppermute | solution.py:107
  52.0 2.5 %next_inner.4 = (f32[24,24,256]{2,1,0:T(8,128)S(1)}, f32[3,24,24,256]{3,2,1,0:T(8,128)S(1)}, f32[3,24,24,256]{3,2,1,0:T(8,128)S(1)}, f32[3,24,24,256]{3,2,1,0:T(...) custom-call(f32[16,16,256]{2,1,0:T(8,128)S(1)} %get-tuple-element.111.refs_0_.p.p_in.refs_1_, ...), custom_call_target="tpu_custom_call" | custom-call | flops 40000000 | bytes 1048576 | tf_op jit(solution)/shard_map/next_inner/pallas_call | solution.py:26
  56.7 2.0 %collective-permute-start.16 = (f32[16,4,256]{2,1,0:T(4,128)S(1)}, f32[16,4,256]{2,1,0:T(4,128)S(1)}, u32[]{:S(2)}, u32[]{:S(2)}) collective-permute-start(f32[16,4,256]{2,1,0:T(4,128)S(1)} %get-tuple-element.125), channel_id=1, source_target_pairs={{0,2},{2,0},{4,6},{6,4},{1,3},{3,1},{5,7},{7,5},{8,10},{10,8},{12,... | collective-permute-start | bytes 196616 | tf_op jit(solution)/shard_map/ppermute | solution.py:101
  59.4 1.7 %collective-permute-done.16.ya = f32[16,4,256]{2,1,0:T(4,128)S(1)} collective-permute-done((f32[16,4,256]{2,1,0:T(4,128)S(1)}, f32[16,4,256]{2,1,0:T(4,128)S(1)}, u32[]{:S(2)}, u32[]{:S(2)}) %collective-permute-start.16) | collective-permute-done | bytes 65568 | tf_op jit(solution)/shard_map/ppermute | solution.py:101
  61.3 1.5 %collective-permute-start.18 = (f32[4,24,256]{2,1,0:T(8,128)S(1)}, f32[4,24,256]{2,1,0:T(8,128)S(1)}, u32[]{:S(2)}, u32[]{:S(2)}) collective-permute-start(f32[4,24,256]{2,1,0:T(8,128)S(1)} %get-tuple-element.129), channel_id=1, source_target_pairs={{0,25},{1,8},{8,1},{9,16},{16,9},{17,24},{24,17},{25,0},{2,27},{3,... | collective-permute-start | bytes 294920 | tf_op jit(solution)/shard_map/ppermute | solution.py:107
  62.8 2.8 %next_inner.5 = (f32[24,24,256]{2,1,0:T(8,128)S(1)}, f32[3,24,24,256]{3,2,1,0:T(8,128)S(1)}, f32[3,24,24,256]{3,2,1,0:T(8,128)S(1)}, f32[3,24,24,256]{3,2,1,0:T(...) custom-call(f32[16,16,256]{2,1,0:T(8,128)S(1)} %get-tuple-element.124.refs_0_.p.p_in, ...), custom_call_target="tpu_custom_call" | custom-call | flops 40000000 | bytes 1048576 | tf_op jit(solution)/shard_map/next_inner/pallas_call | solution.py:26
  67.7 1.3 %collective-permute-done.21.refs_7_ = f32[17,16,128]{2,1,0:T(8,128)S(1)} collective-permute-done((f32[17,16,128]{2,1,0:T(8,128)S(1)}, f32[17,16,128]{2,1,0:T(8,128)S(1)}, u32[]{:S(2)}, u32[]{:S(2)}) %collective-permute-start.21) | collective-permute-done | bytes 139296 | tf_op jit(solution)/shard_map/ppermute | solution.py:111
  69.1 1.7 %collective-permute-start.22 = (f32[2,16,128]{2,1,0:T(8,128)S(1)}, f32[2,16,128]{2,1,0:T(8,128)S(1)}, u32[]{:S(2)}, u32[]{:S(2)}) collective-permute-start(f32[2,16,128]{2,1,0:T(8,128)S(1)} %pad_maximum_fusion), channel_id=1, source_target_pairs={{0,24},{8,0},{16,8},{24,16},{1,25},{9,1},{17,9},{25,17},{2,26},{10... | collective-permute-start | bytes 49160 | tf_op jit(solution)/shard_map/ppermute | solution.py:678
  72.9 1.6 %collective-permute-done.23 = f32[2,16,128]{2,1,0:T(8,128)S(1)} collective-permute-done((f32[2,16,128]{2,1,0:T(8,128)S(1)}, f32[2,16,128]{2,1,0:T(8,128)S(1)}, u32[]{:S(2)}, u32[]{:S(2)}) %collective-permute-start.23) | collective-permute-done | bytes 16416 | tf_op jit(solution)/shard_map/ppermute | solution.py:678
  74.5 2.0 %collective-permute-done.24 = f32[2,16,128]{2,1,0:T(8,128)S(1)} collective-permute-done((f32[2,16,128]{2,1,0:T(8,128)S(1)}, f32[2,16,128]{2,1,0:T(8,128)S(1)}, u32[]{:S(2)}, u32[]{:S(2)}) %collective-permute-start.24) | collective-permute-done | bytes 16416 | tf_op jit(solution)/shard_map/ppermute | solution.py:678
  76.6 2.9 %collective-permute-start.25 = (f32[2,16,128]{2,1,0:T(8,128)S(1)}, f32[2,16,128]{2,1,0:T(8,128)S(1)}, u32[]{:S(2)}, u32[]{:S(2)}) collective-permute-start(f32[2,16,128]{2,1,0:T(8,128)S(1)} %pad_maximum_fusion.1), channel_id=1, source_target_pairs={{0,6},{2,0},{4,2},{6,4},{1,7},{3,1},{5,3},{7,5},{8,14},{10,8},{12,... | collective-permute-start | bytes 49160 | tf_op jit(solution)/shard_map/ppermute | solution.py:678
  80.2 1.9 %collective-permute-start.27 = (f32[2,16,128]{2,1,0:T(8,128)S(1)}, f32[2,16,128]{2,1,0:T(8,128)S(1)}, u32[]{:S(2)}, u32[]{:S(2)}) collective-permute-start(f32[2,16,128]{2,1,0:T(8,128)S(1)} %pad_maximum_fusion.1), channel_id=1, source_target_pairs={{0,2},{2,4},{4,6},{6,0},{1,3},{3,5},{5,7},{7,1},{8,10},{10,12},{12... | collective-permute-start | bytes 49160 | tf_op jit(solution)/shard_map/ppermute | solution.py:678
  82.1 2.0 %collective-permute-done.26 = f32[2,16,128]{2,1,0:T(8,128)S(1)} collective-permute-done((f32[2,16,128]{2,1,0:T(8,128)S(1)}, f32[2,16,128]{2,1,0:T(8,128)S(1)}, u32[]{:S(2)}, u32[]{:S(2)}) %collective-permute-start.26) | collective-permute-done | bytes 16416 | tf_op jit(solution)/shard_map/ppermute | solution.py:678
  84.1 1.6 %collective-permute-done.27 = f32[2,16,128]{2,1,0:T(8,128)S(1)} collective-permute-done((f32[2,16,128]{2,1,0:T(8,128)S(1)}, f32[2,16,128]{2,1,0:T(8,128)S(1)}, u32[]{:S(2)}, u32[]{:S(2)}) %collective-permute-start.27) | collective-permute-done | bytes 16416 | tf_op jit(solution)/shard_map/ppermute | solution.py:678
  85.8 2.0 %last.1 = (f32[32,16,128]{2,1,0:T(8,128)}, f32[32,16,128]{2,1,0:T(8,128)}, f32[3]{0:T(128)}) custom-call(f32[2,16,128]{2,1,0:T(8,128)S(1)} %pad_maximum_fusion.2.sums, f32[32,16,128]{2,1,0:T(8,128)S(1)} %select_select_fusion.eta, f32[16,16,128]{2,1,0:T(8,128)S(1)} %get-tuple-element.89.refs_1_.refs_2_.refs_0_, ...), custom_call_target="tpu_custom_call" | custom-call | flops 1000000 | bytes 1048576 | tf_op jit(solution)/shard_map/last/pallas_call | solution.py:26
  (64 shorter events, 12.6 us)
Async XLA Ops:
  0.6 3.4 %copy-start.1 = (s32[32,16,128]{2,1,0:T(8,128)S(1)}, s32[32,16,128]{2,1,0:T(8,128)}, u32[]{:S(2)}) copy-start(s32[32,16,128]{2,1,0:T(8,128)} %param.5) | copy-start | bytes 786436
  1.9 8.9 %collective-permute-start = (f32[3,16,16,128]{3,2,1,0:T(8,128)S(1)}, f32[3,16,16,128]{3,2,1,0:T(8,128)S(1)}, u32[]{:S(2)}, u32[]{:S(2)}) collective-permute-start(f32[3,16,16,128]{3,2,1,0:T(8,128)S(1)} %get-tuple-element.145), channel_id=1, source_target_pairs={{0,1},{1,0},{2,3},{3,2},{4,5},{5,4},{6,7},{7,6},{8,9},{9,8},{10,11... | collective-permute-start | bytes 1179656 | tf_op jit(solution)/shard_map/ppermute | solution.py:111
  4.1 19.7 %copy-start = (s32[6]{0:T(128)S(1)}, s32[6]{0:T(128)}, u32[]{:S(2)}) copy-start(s32[6]{0:T(128)} %refs_4_.3) | copy-start | bytes 76
  9.3 1.4 %collective-permute-start.1 = (f32[16,16,128]{2,1,0:T(8,128)S(1)}, f32[16,16,128]{2,1,0:T(8,128)S(1)}, u32[]{:S(2)}, u32[]{:S(2)}) collective-permute-start(f32[16,16,128]{2,1,0:T(8,128)S(1)} %get-tuple-element.147), channel_id=1, source_target_pairs={{0,1},{1,0},{2,3},{3,2},{4,5},{5,4},{6,7},{7,6},{8,9},{9,8},{10,11... | collective-permute-start | bytes 393224 | tf_op jit(solution)/shard_map/ppermute | solution.py:111
  11.0 10.0 %collective-permute-start.2 = (f32[68,4,256]{2,1,0:T(4,128)S(1)}, f32[68,4,256]{2,1,0:T(4,128)S(1)}, u32[]{:S(2)}, u32[]{:S(2)}) collective-permute-start(f32[68,4,256]{2,1,0:T(4,128)S(1)} %get-tuple-element.72), channel_id=1, source_target_pairs={{0,2},{2,0},{4,6},{6,4},{1,3},{3,1},{5,7},{7,5},{8,10},{10,8},{12,... | collective-permute-start | bytes 835592 | tf_op jit(solution)/shard_map/ppermute | solution.py:101
  13.7 7.2 %collective-permute-start.3 = (f32[68,4,256]{2,1,0:T(4,128)S(1)}, f32[68,4,256]{2,1,0:T(4,128)S(1)}, u32[]{:S(2)}, u32[]{:S(2)}) collective-permute-start(f32[68,4,256]{2,1,0:T(4,128)S(1)} %get-tuple-element.73), channel_id=1, source_target_pairs={{0,1},{1,0},{2,4},{3,5},{4,2},{5,3},{6,7},{7,6},{8,9},{9,8},{10,12... | collective-permute-start | bytes 835592 | tf_op jit(solution)/shard_map/ppermute | solution.py:101
  21.0 7.6 %collective-permute-start.5 = (f32[43,8,256]{2,1,0:T(8,128)S(1)}, f32[43,8,256]{2,1,0:T(8,128)S(1)}, u32[]{:S(2)}, u32[]{:S(2)}) collective-permute-start(f32[43,8,256]{2,1,0:T(8,128)S(1)} %get-tuple-element.84), channel_id=1, source_target_pairs={{0,1},{1,0},{8,9},{9,8},{16,17},{17,16},{24,25},{25,24},{2,3},{3,2... | collective-permute-start | bytes 1056776 | tf_op jit(solution)/shard_map/ppermute | solution.py:107
  21.1 10.7 %collective-permute-start.4 = (f32[43,8,256]{2,1,0:T(8,128)S(1)}, f32[43,8,256]{2,1,0:T(8,128)S(1)}, u32[]{:S(2)}, u32[]{:S(2)}) collective-permute-start(f32[43,8,256]{2,1,0:T(8,128)S(1)} %get-tuple-element.74), channel_id=1, source_target_pairs={{0,25},{1,8},{8,1},{9,16},{16,9},{17,24},{24,17},{25,0},{2,27},{3,... | collective-permute-start | bytes 1056776 | tf_op jit(solution)/shard_map/ppermute | solution.py:107
  33.6 5.3 %collective-permute-start.6 = (f32[16,4,256]{2,1,0:T(4,128)S(1)}, f32[16,4,256]{2,1,0:T(4,128)S(1)}, u32[]{:S(2)}, u32[]{:S(2)}) collective-permute-start(f32[16,4,256]{2,1,0:T(4,128)S(1)} %get-tuple-element.87), channel_id=1, source_target_pairs={{0,2},{2,0},{4,6},{6,4},{1,3},{3,1},{5,7},{7,5},{8,10},{10,8},{12,... | collective-permute-start | bytes 196616 | tf_op jit(solution)/shard_map/ppermute | solution.py:101
  36.7 2.2 %collective-permute-start.7 = (f32[16,4,256]{2,1,0:T(4,128)S(1)}, f32[16,4,256]{2,1,0:T(4,128)S(1)}, u32[]{:S(2)}, u32[]{:S(2)}) collective-permute-start(f32[16,4,256]{2,1,0:T(4,128)S(1)} %get-tuple-element.88), channel_id=1, source_target_pairs={{0,1},{1,0},{2,4},{3,5},{4,2},{5,3},{6,7},{7,6},{8,9},{9,8},{10,12... | collective-permute-start | bytes 196616 | tf_op jit(solution)/shard_map/ppermute | solution.py:101
  36.7 4.5 %collective-permute-start.9 = (f32[16,16,128]{2,1,0:T(8,128)S(1)}, f32[16,16,128]{2,1,0:T(8,128)S(1)}, u32[]{:S(2)}, u32[]{:S(2)}) collective-permute-start(f32[16,16,128]{2,1,0:T(8,128)S(1)} %get-tuple-element.90.refs_2_.refs_3_), channel_id=1, source_target_pairs={{0,1},{1,0},{2,3},{3,2},{4,5},{5,4},{6,7},{7,6},{8,9},{9,8},{10,11... | collective-permute-start | bytes 393224 | tf_op jit(solution)/shard_map/ppermute | solution.py:111
  39.0 5.0 %collective-permute-start.10 = (f32[4,24,256]{2,1,0:T(8,128)S(1)}, f32[4,24,256]{2,1,0:T(8,128)S(1)}, u32[]{:S(2)}, u32[]{:S(2)}) collective-permute-start(f32[4,24,256]{2,1,0:T(8,128)S(1)} %get-tuple-element.110), channel_id=1, source_target_pairs={{0,1},{1,0},{8,9},{9,8},{16,17},{17,16},{24,25},{25,24},{2,3},{3,2... | collective-permute-start | bytes 294920 | tf_op jit(solution)/shard_map/ppermute | solution.py:107
  39.1 5.8 %collective-permute-start.8 = (f32[4,24,256]{2,1,0:T(8,128)S(1)}, f32[4,24,256]{2,1,0:T(8,128)S(1)}, u32[]{:S(2)}, u32[]{:S(2)}) collective-permute-start(f32[4,24,256]{2,1,0:T(8,128)S(1)} %get-tuple-element.91), channel_id=1, source_target_pairs={{0,25},{1,8},{8,1},{9,16},{16,9},{17,24},{24,17},{25,0},{2,27},{3,... | collective-permute-start | bytes 294920 | tf_op jit(solution)/shard_map/ppermute | solution.py:107
  45.9 4.3 %collective-permute-start.11 = (f32[16,4,256]{2,1,0:T(4,128)S(1)}, f32[16,4,256]{2,1,0:T(4,128)S(1)}, u32[]{:S(2)}, u32[]{:S(2)}) collective-permute-start(f32[16,4,256]{2,1,0:T(4,128)S(1)} %get-tuple-element.112), channel_id=1, source_target_pairs={{0,2},{2,0},{4,6},{6,4},{1,3},{3,1},{5,7},{7,5},{8,10},{10,8},{12,... | collective-permute-start | bytes 196616 | tf_op jit(solution)/shard_map/ppermute | solution.py:101
  47.9 2.3 %collective-permute-start.12 = (f32[16,4,256]{2,1,0:T(4,128)S(1)}, f32[16,4,256]{2,1,0:T(4,128)S(1)}, u32[]{:S(2)}, u32[]{:S(2)}) collective-permute-start(f32[16,4,256]{2,1,0:T(4,128)S(1)} %get-tuple-element.113), channel_id=1, source_target_pairs={{0,1},{1,0},{2,4},{3,5},{4,2},{5,3},{6,7},{7,6},{8,9},{9,8},{10,12... | collective-permute-start | bytes 196616 | tf_op jit(solution)/shard_map/ppermute | solution.py:101
  47.9 4.1 %collective-permute-start.14 = (f32[16,16,128]{2,1,0:T(8,128)S(1)}, f32[16,16,128]{2,1,0:T(8,128)S(1)}, u32[]{:S(2)}, u32[]{:S(2)}) collective-permute-start(f32[16,16,128]{2,1,0:T(8,128)S(1)} %get-tuple-element.115.refs_5_), channel_id=1, source_target_pairs={{0,1},{1,0},{2,3},{3,2},{4,5},{5,4},{6,7},{7,6},{8,9},{9,8},{10,11... | collective-permute-start | bytes 393224 | tf_op jit(solution)/shard_map/ppermute | solution.py:111
  50.2 4.3 %collective-permute-start.15 = (f32[4,24,256]{2,1,0:T(8,128)S(1)}, f32[4,24,256]{2,1,0:T(8,128)S(1)}, u32[]{:S(2)}, u32[]{:S(2)}) collective-permute-start(f32[4,24,256]{2,1,0:T(8,128)S(1)} %get-tuple-element.123), channel_id=1, source_target_pairs={{0,1},{1,0},{8,9},{9,8},{16,17},{17,16},{24,25},{25,24},{2,3},{3,2... | collective-permute-start | bytes 294920 | tf_op jit(solution)/shard_map/ppermute | solution.py:107
  50.3 5.6 %collective-permute-start.13 = (f32[4,24,256]{2,1,0:T(8,128)S(1)}, f32[4,24,256]{2,1,0:T(8,128)S(1)}, u32[]{:S(2)}, u32[]{:S(2)}) collective-permute-start(f32[4,24,256]{2,1,0:T(8,128)S(1)} %get-tuple-element.116), channel_id=1, source_target_pairs={{0,25},{1,8},{8,1},{9,16},{16,9},{17,24},{24,17},{25,0},{2,27},{3,... | collective-permute-start | bytes 294920 | tf_op jit(solution)/shard_map/ppermute | solution.py:107
  56.7 4.4 %collective-permute-start.16 = (f32[16,4,256]{2,1,0:T(4,128)S(1)}, f32[16,4,256]{2,1,0:T(4,128)S(1)}, u32[]{:S(2)}, u32[]{:S(2)}) collective-permute-start(f32[16,4,256]{2,1,0:T(4,128)S(1)} %get-tuple-element.125), channel_id=1, source_target_pairs={{0,2},{2,0},{4,6},{6,4},{1,3},{3,1},{5,7},{7,5},{8,10},{10,8},{12,... | collective-permute-start | bytes 196616 | tf_op jit(solution)/shard_map/ppermute | solution.py:101
  58.8 2.4 %collective-permute-start.17 = (f32[16,4,256]{2,1,0:T(4,128)S(1)}, f32[16,4,256]{2,1,0:T(4,128)S(1)}, u32[]{:S(2)}, u32[]{:S(2)}) collective-permute-start(f32[16,4,256]{2,1,0:T(4,128)S(1)} %get-tuple-element.126), channel_id=1, source_target_pairs={{0,1},{1,0},{2,4},{3,5},{4,2},{5,3},{6,7},{7,6},{8,9},{9,8},{10,12... | collective-permute-start | bytes 196616 | tf_op jit(solution)/shard_map/ppermute | solution.py:101
  58.8 4.0 %collective-permute-start.19 = (f32[16,16,128]{2,1,0:T(8,128)S(1)}, f32[16,16,128]{2,1,0:T(8,128)S(1)}, u32[]{:S(2)}, u32[]{:S(2)}) collective-permute-start(f32[16,16,128]{2,1,0:T(8,128)S(1)} %get-tuple-element.128.refs_7_), channel_id=1, source_target_pairs={{0,1},{1,0},{2,3},{3,2},{4,5},{5,4},{6,7},{7,6},{8,9},{9,8},{10,11... | collective-permute-start | bytes 393224 | tf_op jit(solution)/shard_map/ppermute | solution.py:111
  61.2 4.5 %collective-permute-start.20 = (f32[4,24,256]{2,1,0:T(8,128)S(1)}, f32[4,24,256]{2,1,0:T(8,128)S(1)}, u32[]{:S(2)}, u32[]{:S(2)}) collective-permute-start(f32[4,24,256]{2,1,0:T(8,128)S(1)} %get-tuple-element.136), channel_id=1, source_target_pairs={{0,1},{1,0},{8,9},{9,8},{16,17},{17,16},{24,25},{25,24},{2,3},{3,2... | collective-permute-start | bytes 294920 | tf_op jit(solution)/shard_map/ppermute | solution.py:107
  61.3 5.3 %collective-permute-start.18 = (f32[4,24,256]{2,1,0:T(8,128)S(1)}, f32[4,24,256]{2,1,0:T(8,128)S(1)}, u32[]{:S(2)}, u32[]{:S(2)}) collective-permute-start(f32[4,24,256]{2,1,0:T(8,128)S(1)} %get-tuple-element.129), channel_id=1, source_target_pairs={{0,25},{1,8},{8,1},{9,16},{16,9},{17,24},{24,17},{25,0},{2,27},{3,... | collective-permute-start | bytes 294920 | tf_op jit(solution)/shard_map/ppermute | solution.py:107
  67.7 1.4 %collective-permute-start.21 = (f32[17,16,128]{2,1,0:T(8,128)S(1)}, f32[17,16,128]{2,1,0:T(8,128)S(1)}, u32[]{:S(2)}, u32[]{:S(2)}) collective-permute-start(f32[17,16,128]{2,1,0:T(8,128)S(1)} %get-tuple-element.137), channel_id=1, source_target_pairs={{0,1},{1,0},{2,3},{3,2},{4,5},{5,4},{6,7},{7,6},{8,9},{9,8},{10,11... | collective-permute-start | bytes 417800 | tf_op jit(solution)/shard_map/ppermute | solution.py:111
  69.1 3.8 %collective-permute-start.22 = (f32[2,16,128]{2,1,0:T(8,128)S(1)}, f32[2,16,128]{2,1,0:T(8,128)S(1)}, u32[]{:S(2)}, u32[]{:S(2)}) collective-permute-start(f32[2,16,128]{2,1,0:T(8,128)S(1)} %pad_maximum_fusion), channel_id=1, source_target_pairs={{0,24},{8,0},{16,8},{24,16},{1,25},{9,1},{17,9},{25,17},{2,26},{10... | collective-permute-start | bytes 49160 | tf_op jit(solution)/shard_map/ppermute | solution.py:678
  70.8 3.7 %collective-permute-start.23 = (f32[2,16,128]{2,1,0:T(8,128)S(1)}, f32[2,16,128]{2,1,0:T(8,128)S(1)}, u32[]{:S(2)}, u32[]{:S(2)}) collective-permute-start(f32[2,16,128]{2,1,0:T(8,128)S(1)} %pad_maximum_fusion), channel_id=1, source_target_pairs={{0,16},{8,24},{16,0},{24,8},{1,17},{9,25},{17,1},{25,9},{2,18},{10... | collective-permute-start | bytes 49160 | tf_op jit(solution)/shard_map/ppermute | solution.py:678
  71.9 4.6 %collective-permute-start.24 = (f32[2,16,128]{2,1,0:T(8,128)S(1)}, f32[2,16,128]{2,1,0:T(8,128)S(1)}, u32[]{:S(2)}, u32[]{:S(2)}) collective-permute-start(f32[2,16,128]{2,1,0:T(8,128)S(1)} %pad_maximum_fusion), channel_id=1, source_target_pairs={{0,8},{8,16},{16,24},{24,0},{1,9},{9,17},{17,25},{25,1},{2,10},{10... | collective-permute-start | bytes 49160 | tf_op jit(solution)/shard_map/ppermute | solution.py:678
  76.6 5.6 %collective-permute-start.25 = (f32[2,16,128]{2,1,0:T(8,128)S(1)}, f32[2,16,128]{2,1,0:T(8,128)S(1)}, u32[]{:S(2)}, u32[]{:S(2)}) collective-permute-start(f32[2,16,128]{2,1,0:T(8,128)S(1)} %pad_maximum_fusion.1), channel_id=1, source_target_pairs={{0,6},{2,0},{4,2},{6,4},{1,7},{3,1},{5,3},{7,5},{8,14},{10,8},{12,... | collective-permute-start | bytes 49160 | tf_op jit(solution)/shard_map/ppermute | solution.py:678
  79.5 4.6 %collective-permute-start.26 = (f32[2,16,128]{2,1,0:T(8,128)S(1)}, f32[2,16,128]{2,1,0:T(8,128)S(1)}, u32[]{:S(2)}, u32[]{:S(2)}) collective-permute-start(f32[2,16,128]{2,1,0:T(8,128)S(1)} %pad_maximum_fusion.1), channel_id=1, source_target_pairs={{0,4},{2,6},{4,0},{6,2},{1,5},{3,7},{5,1},{7,3},{8,12},{10,14},{12... | collective-permute-start | bytes 49160 | tf_op jit(solution)/shard_map/ppermute | solution.py:678
  80.2 5.5 %collective-permute-start.27 = (f32[2,16,128]{2,1,0:T(8,128)S(1)}, f32[2,16,128]{2,1,0:T(8,128)S(1)}, u32[]{:S(2)}, u32[]{:S(2)}) collective-permute-start(f32[2,16,128]{2,1,0:T(8,128)S(1)} %pad_maximum_fusion.1), channel_id=1, source_target_pairs={{0,2},{2,4},{4,6},{6,0},{1,3},{3,5},{5,7},{7,1},{8,10},{10,12},{12... | collective-permute-start | bytes 49160 | tf_op jit(solution)/shard_map/ppermute | solution.py:678

commit v9 on v8

--- a/solution.py
+++ b/solution.py
@@ -118,8 +118,20 @@
     return eta
 
 
-def gather_kernel(n, *refs):
-    forces, etas = refs[:n], refs[n : 2 * n]
+def eta_kernel(n, table, after, *refs):
+    slices, eta = refs[:n], refs[n]
+    rows = slices[0].shape[0]
+    for j in range(n):
+        base = lax.rem(lax.axis_index("gz") + j, n) * rows
+
+        def one(r, j=j, base=base):
+            eta[base + r] = lookup(slices[j][r], table)
+
+        rows_loop(0, rows, one, 4)
+
+
+def gather_kernel(n, table, *refs):
+    forces, phases = refs[:n], refs[n : 2 * n]
     full, send_a, send_b = refs[2 * n :]
     core = lax.axis_index("gz")
     odd = Place().odd_y
@@ -129,8 +141,8 @@
     for c in range(fields):
 
         def one(r, c=c):
-            parts = [q[c, r] for q in forces] if c < 3 else [q[r] for q in etas]
-            row = join_received(parts, core)
+            row = join_received([q[c, r] for q in forces] if c < 3 else [q[r] for q in phases], core)
+            row = row if c < 3 else lookup(row, table)
             full[c, r] = row
             send_a[c * rows + r] = jnp.where(odd, row[:h], row[ys - h :])
             send_b[c * rows + r] = jnp.where(odd, row[ys - h :], row[:h])
@@ -142,31 +154,65 @@
         send_b[fields * rows + r // 4, r % 4 : r % 4 + 1, :] = line
 
 
-def edge_list(h):
+def edge_list():
     tiles = []
     for c in range(4):
-        for k in range(h):
-            if c in (1, 2) and k == 0:
-                continue
-            for q in range(2 if c == 0 and k == 0 else 3):
-                tiles.append((c, k, q))
+        far = 1 if c in (1, 2) else 0
+        tiles += [(c, k, q) for k in range(far, HALO) for q in range(2)]
+        tiles += [(c, 3, 2), ("pack", c, 2, 1)] if c < 3 else [(c, 3, 2), (c, 2, 2), ("pack", c, 1, 0)]
     return tiles + [(3, -1, 0), (3, -1, 1)]
+
+
+def face_list():
+    return [(0, k, q) for k in range(HALO) for q in range(2)] + [(0, 3, 2), ("pack", 0, 2, 1)]
+
+
+def put_tile(send, t, tile, row, halo):
+    h = HALO
+    if tile[0] == "pack":
+        _, c, j, k = tile
+        (up, low), (up_k, low_k) = halo(c, j), halo(c, k)
+        send[t, 0:2, :] = up[0:2]
+        send[t, 2:3, :] = low_k[h - 1 :]
+        send[t, 3:4, :] = up_k[0:1]
+        send[t, 4:6, :] = low[0:2]
+        send[t, 6:8, :] = low[h - 2 :]
+    elif tile[2] < 2:
+        send[t] = row(tile[0], tile[1])[8 * tile[2] : 8 * tile[2] + 8]
+    else:
+        up, low = halo(tile[0], tile[1])
+        send[t, :h, :] = up
+        send[t, h:, :] = low
+
+
+def take_tile(tile, value, ys, target):
+    if tile[0] == "pack":
+        _, c, j, k = tile
+        ref, index = target(c, j)
+        ref[(*index, slice(ys, ys + 8), slice(None))] = value
+        ref, index = target(c, k)
+        ref[(*index, slice(ys, ys + 1), slice(None))] = value[3:4]
+        ref[(*index, slice(ys + 7, ys + 8), slice(None))] = value[2:3]
+    else:
+        ref, index = target(tile[0], tile[1])
+        ref[(*index, slice(8 * tile[2], 8 * tile[2] + 8), slice(None))] = value
 
 
 def force_edges_kernel(full, ya, yb, send_a, send_b):
     place = Place()
-    odd_x = place.odd
     _, rows, ys, _ = full.shape
     h = HALO
-    for send, first in ((send_a, odd_x), (send_b, jnp.logical_not(odd_x))):
-        for t, (c, k, q) in enumerate(edge_list(h)):
-            r = jnp.where(first, h - 1 - k, rows - h + k)
-            if q < 2:
-                send[t] = full[c, r, 8 * q : 8 * q + 8, :]
-            else:
-                a, b = ya[c * rows + r], yb[c * rows + r]
-                send[t, :h, :] = place.up(a, b)
-                send[t, h:, :] = place.low(a, b)
+    for send, first in ((send_a, place.odd), (send_b, jnp.logical_not(place.odd))):
+
+        def at(k, first=first):
+            return jnp.where(first, h - 1 - k, rows - h + k)
+
+        def halo(c, k, at=at):
+            a, b = ya[c * rows + at(k)], yb[c * rows + at(k)]
+            return place.up(a, b), place.low(a, b)
+
+        for t, tile in enumerate(edge_list()):
+            put_tile(send, t, tile, lambda c, k, at=at: full[c, at(k)], halo)
 
 
 def edges_kernel(p, ya, yb, *rest):
@@ -175,9 +221,16 @@
     rows = p.shape[0]
     h = HALO
     for send, first in ((send_a, place.odd), (send_b, jnp.logical_not(place.odd))):
-        start = jnp.where(first, 0, rows - h)
-        for k in range(h):
-            set_row(send, (k,), p[start + k], ya[start + k], yb[start + k], place)
+
+        def at(k, first=first):
+            return jnp.where(first, h - 1 - k, rows - h + k)
+
+        def halo(c, k, at=at):
+            a, b = ya[at(k)], yb[at(k)]
+            return place.up(a, b), place.low(a, b)
+
+        for t, tile in enumerate(face_list()):
+            put_tile(send, t, tile, lambda c, k, at=at: p[at(k)], halo)
 
 
 class Rows:
@@ -413,17 +466,20 @@
         low = side == "low"
         blank = jnp.zeros((slots, lanes), F32)
         for k in range(h):
-            line[k if low else h + rows + k] = jnp.zeros((1, lanes), F32)
-        for c in range(3):
-            force[c, 0 if low else total - 1] = blank
-        if low:
-            eta[0] = blank
-        for t, (c, k, q) in enumerate(edge_list(h)):
-            where = slice(8 * q, 8 * q + 8)
+            line[k if low else h + rows + k] = jnp.ones((1, lanes), F32)
+            for c in range(3):
+                force[c, k if low else total - 1 - k] = blank
+        for k in range(-1 if low else 0, h):
+            eta[1 + k if low else total - k] = blank + 1.0
+
+        def target(c, k):
             if c < 3:
-                force[c, k if low else total - 1 - k, where, :] = xs[t]
-            elif low or k >= 0:
-                eta[1 + k if low else total - k, where, :] = xs[t]
+                return force, (c, k if low else total - 1 - k)
+            return eta, (1 + k if low else total - k,)
+
+        for t, tile in enumerate(edge_list()):
+            if low or tile[0] == "pack" or tile[1] >= 0:
+                take_tile(tile, xs[t], ys, target)
         for r in todo:
             after = eta[min(r + 2, total)]
             coefs(r, eta[r + 1], eta[r], after, line[r], lambda c: force[c, r], kx, ky, kz, w, b)
@@ -508,18 +564,22 @@
             p_out, send_a, send_b, *refs = refs
         scratch = refs
     p, b, *buffers = scratch
-    rows = p_in.shape[0]
-    h = HALO
+    rows, ys, _ = p_in.shape
+    h = HALO
+    total = rows + 2 * h
     place = Place()
-    ranges, inner = spans(h, h + rows - 1, rows + 2 * h)
+    ranges, inner = spans(h, h + rows - 1, total)
 
     def body(side):
         low = side == "low"
+        blank = jnp.zeros(p.shape[1:], F32)
         for k in range(h):
-            row = xs[k]
+            p[k if low else total - 1 - k] = blank
+        for t, tile in enumerate(face_list()):
+            value = xs[t]
             if not near:
-                row = jnp.where(place.below_x if low else place.above_x, row, 0.0)
-            p[k if low else h + rows + k] = row
+                value = jnp.where(place.below_x if low else place.above_x, value, 0.0)
+            take_tile(tile, value, ys, lambda c, k: (p, (k if low else total - 1 - k,)))
         ps = Rows(p0, p, h, h + rows)
         for r in outside(ranges[0], inner[0], side):
             grads(ps, w, b, r)
@@ -695,14 +755,11 @@
     chain = nx * nz
 
     core = lax.axis_index("gz")
-    eta = lookup(phase, table)
-    forces, etas = [], []
-    for j in range(nz):
-        start = lax.rem(core + j, nz) * rows
-        forces.append(lax.dynamic_slice_in_dim(force, start, rows, 1))
-        etas.append(lax.dynamic_slice_in_dim(eta, start, rows, 0))
+    starts = [lax.rem(core + j, nz) * rows for j in range(nz)]
+    forces = [lax.dynamic_slice_in_dim(force, start, rows, 1) for start in starts]
+    slices = [lax.dynamic_slice_in_dim(phase, start, rows, 0) for start in starts]
     forces = forces[:1] + [core_shift(forces[j], nz, j) for j in range(1, nz)]
-    etas = etas[:1] + [core_shift(etas[j], nz, j) for j in range(1, nz)]
+    phases = slices[:1] + [core_shift(slices[j], nz, j) for j in range(1, nz)]
     full, ya, yb = call(
         functools.partial(gather_kernel, nz),
         [
@@ -710,11 +767,12 @@
             sds(4 * rows + rows // 4, h, zs),
             sds(4 * rows + rows // 4, h, zs),
         ],
-        (*forces, *etas),
+        (table, *forces, *phases),
+        [SMEM] + [VMEM] * (2 * nz),
         name="gather",
     )
     ya, yb = exchange_y(ya, yb, ny, nz)
-    edge = sds(len(edge_list(h)), 8, zs)
+    edge = sds(len(edge_list()), 8, zs)
     xa, xb = call(force_edges_kernel, [edge, edge], (full, ya, yb), name="force_edges")
     xa, xb = exchange_x(xa, xb, chain)
 
@@ -760,6 +818,13 @@
         name="join",
     )
     vs, ps, moments = [list(outs[:nz])], [outs[nz]], []
+    eta = call(
+        functools.partial(eta_kernel, nz),
+        sds(*phase.shape),
+        (table, outs[nz + 1], *slices),
+        [SMEM] + [VMEM] * (nz + 1),
+        name="eta",
+    )
     ya, yb = outs[nz + 1 : nz + 3]
     placed = []
     for step in range(1, ITERS + 1):
@@ -778,7 +843,7 @@
             )[0]
         )
         ya, yb = exchange_y(ya, yb, ny, nz)
-        edge = sds(h, slots, zs)
+        edge = sds(len(face_list()), 8, zs)
         xa, xb = call(edges_kernel, [edge, edge], (p, ya, yb, moments[-1]), name="edges")
         xa, xb = exchange_x(xa, xb, chain)
         early = call(

time: 88.1 us -> 80.7 us (0.916)
  other arithmetic: 5.29 us -> 0.08 us
  local copies, waits for them, and re-layouts: 2.87 us -> 1.24 us
  Pallas kernels: 24.8 us -> 26.3 us
  starting transfers between devices: 29.7 us -> 28.6 us
  waiting for transfers between devices: 24.1 us -> 23.2 us
    select_n x1 -> x0, other arithmetic: 5.21 us -> none  [lookup(): eta = jnp.where(ids == level, table[level], eta)]
    slice x1 -> x0, local copies, waits for them, and re-layouts: 1.62 us -> none  [lookup(): eta = jnp.where(ids == level, table[level], eta)]
    pallas_call x22 -> x23, Pallas kernels: 24.8 us -> 26.3 us  [call(): pl.pallas_call(kernel, out_shape=outs, in_specs=specs or [VMEM] * len(ins...]
  transfers between devices with their start and end apart: 28 -> 28, of which waited for: 13 -> 14; matrix products, arithmetic and copies ran while one was open for 8% -> 0% of each run, Pallas kernels for 20% -> 23%
where the time goes in v9:
time: 80.7 us; the launch traced here: 80.6 us
  starting transfers between devices  28.6 us (35%)
  Pallas kernels  26.3 us (33%)
  waiting for transfers between devices  23.2 us (29%)
  local copies, waits for them, and re-layouts  1.24 us (2%)
  between operations  1.12 us (1%)
    pallas_call x23, Pallas kernels, call(): pl.pallas_call(kernel, out_shape=outs, in_specs=specs or [VMEM] * len(ins...  26.3 us
    ppermute x8, waiting for transfers between devices, exchange_y(): return (lax.ppermute(a, 'gy', even), lax.ppermute(b, ('gy', 'gz'), odd))  11.9 us
    ppermute x8, starting transfers between devices, exchange_y(): return (lax.ppermute(a, 'gy', even), lax.ppermute(b, ('gy', 'gz'), odd))  10.1 us
    ppermute x6, starting transfers between devices, sum_along(): terms.append(lax.ppermute(pair, axis, moves))  8.59 us
    ppermute x4, starting transfers between devices, exchange_x(): lax.ppermute(b, ('gx', 'gz'), odd)  7.36 us
    ppermute x6, waiting for transfers between devices, sum_along(): terms.append(lax.ppermute(pair, axis, moves))  6.63 us
    ppermute x6, waiting for transfers between devices, core_shift(): return lax.ppermute(value, 'gz', [(i, (i + j) % n) for i in range(n)])  2.77 us
    ppermute x6, starting transfers between devices, core_shift(): return lax.ppermute(value, 'gz', [(i, (i + j) % n) for i in range(n)])  2.25 us
  transfers between devices with their start and end apart: 28, of which 14 were waited for; matrix products, arithmetic and copies ran while one was open for 0% of the time, Pallas kernels for 23%

profile of v9, /device:TPU:0, one launch (start us, length us, event | category | flops | bytes accessed | tf_op | source)
XLA Modules:
  0.0 80.6 jit_solution(18418572318883474627)
XLA Ops:
  0.7 1.2 %constant_dynamic-slice_fusion.2 = (f32[3,16,16,128]{3,2,1,0:T(8,128)S(1)}, f32[3,16,16,128]{3,2,1,0:T(8,128)S(1)}) fusion(f32[3,32,16,128]{3,2,1,0:T(8,128)} %param.4, s32[]{:T(128)S(6)} %select_n.161, s32[]{:T(128)S(6)} %select_n.160), kind=kLoop, calls=%fused_computation.33 | loop fusion | bytes 1572872 | tf_op jit(solution)/shard_map/dynamic_slice | solution.py:759
  2.6 1.4 %collective-permute-done.1.refs_3_ = s32[16,16,128]{2,1,0:T(8,128)S(1)} collective-permute-done((s32[16,16,128]{2,1,0:T(8,128)S(1)}, s32[16,16,128]{2,1,0:T(8,128)S(1)}, u32[]{:S(2)}, u32[]{:S(2)}) %collective-permute-start.1) | collective-permute-done | bytes 131104 | tf_op jit(solution)/shard_map/ppermute | solution.py:111
  4.9 3.0 %collective-permute-start.2 = (f32[68,4,256]{2,1,0:T(4,128)S(1)}, f32[68,4,256]{2,1,0:T(4,128)S(1)}, u32[]{:S(2)}, u32[]{:S(2)}) collective-permute-start(f32[68,4,256]{2,1,0:T(4,128)S(1)} %get-tuple-element.72), channel_id=1, source_target_pairs={{0,2},{2,0},{4,6},{6,4},{1,3},{3,1},{5,7},{7,5},{8,10},{10,8},{12,... | collective-permute-start | bytes 835592 | tf_op jit(solution)/shard_map/ppermute | solution.py:101
  7.9 7.0 %collective-permute-done.2.ya.refs_1_ = f32[68,4,256]{2,1,0:T(4,128)S(1)} collective-permute-done((f32[68,4,256]{2,1,0:T(4,128)S(1)}, f32[68,4,256]{2,1,0:T(4,128)S(1)}, u32[]{:S(2)}, u32[]{:S(2)}) %collective-permute-start.2) | collective-permute-done | bytes 278560 | tf_op jit(solution)/shard_map/ppermute | solution.py:101
  15.0 2.7 %collective-permute-start.4 = (f32[39,8,256]{2,1,0:T(8,128)S(1)}, f32[39,8,256]{2,1,0:T(8,128)S(1)}, u32[]{:S(2)}, u32[]{:S(2)}) collective-permute-start(f32[39,8,256]{2,1,0:T(8,128)S(1)} %get-tuple-element.74), channel_id=1, source_target_pairs={{0,25},{1,8},{8,1},{9,16},{16,9},{17,24},{24,17},{25,0},{2,27},{3,... | collective-permute-start | bytes 958472 | tf_op jit(solution)/shard_map/ppermute | solution.py:107
  17.7 4.8 %first_inner.1 = (f32[24,24,256]{2,1,0:T(8,128)S(1)}, f32[24,24,256]{2,1,0:T(8,128)S(1)}, f32[24,24,256]{2,1,0:T(8,128)S(1)}, f32[3,24,24,256]{3,2,1,0:T(8,128)S...) custom-call(f32[4,16,16,256]{3,2,1,0:T(8,128)S(1)} %get-tuple-elemen, ...), custom_call_target="tpu_custom_call" | custom-call | flops 40000000 | bytes 1048576 | tf_op jit(solution)/shard_map/first_inner/pallas_call | solution.py:26
  22.6 1.7 %first_near.1 = (f32[24,24,256]{2,1,0:T(8,128)S(1)}, f32[24,24,256]{2,1,0:T(8,128)S(1)}, f32[24,24,256]{2,1,0:T(8,128)S(1)}, f32[3,24,24,256]{3,2,1,0:T(8,128)S(1)}, f32[16,24,256]{2,1,0:T(8,128)S(1)}) custom-call(f32[4,16,16,256]{3,2,1,0:T(8,128)S(1)} %get-tuple-element.71.full.refs_0_.refs_3_, f32[68,4,256]{2,1,0:T(4,128)S(1)} %collective-permute-done.2.ya.refs_1_, ...), custom_call_target="tpu_custom_call" | custom-call | flops 20000000 | bytes 1048576 | tf_op jit(solution)/shard_map/first_near/pallas_call | solution.py:26
  25.0 1.9 %first.1 = (f32[16,16,128]{2,1,0:T(8,128)S(1)}, f32[16,16,128]{2,1,0:T(8,128)S(1)}, f32[16,16,256]{2,1,0:T(8,128)S(1)}, f32[16,4,256]{2,1,0:T(4,128)S(1)}, f32[1...) custom-call(f32[4,16,16,256]{3,2,1,0:T(8,128)S(1)} %get-tuple-elemen, ...), custom_call_target="tpu_custom_call" | custom-call | flops 20000000 | bytes 1048576 | tf_op jit(solution)/shard_map/first/pallas_call | solution.py:26
  26.9 3.1 %collective-permute-start.6 = (f32[16,4,256]{2,1,0:T(4,128)S(1)}, f32[16,4,256]{2,1,0:T(4,128)S(1)}, u32[]{:S(2)}, u32[]{:S(2)}) collective-permute-start(f32[16,4,256]{2,1,0:T(4,128)S(1)} %get-tuple-element.87.after), channel_id=1, source_target_pairs={{0,2},{2,0},{4,6},{6,4},{1,3},{3,1},{5,7},{7,5},{8,10},{10,8},{12,... | collective-permute-start | bytes 196616 | tf_op jit(solution)/shard_map/ppermute | solution.py:101
  30.6 1.6 %collective-permute-done.6.ya = f32[16,4,256]{2,1,0:T(4,128)S(1)} collective-permute-done((f32[16,4,256]{2,1,0:T(4,128)S(1)}, f32[16,4,256]{2,1,0:T(4,128)S(1)}, u32[]{:S(2)}, u32[]{:S(2)}) %collective-permute-start.6) | collective-permute-done | bytes 65568 | tf_op jit(solution)/shard_map/ppermute | solution.py:101
  32.3 1.9 %collective-permute-start.8 = (f32[10,8,256]{2,1,0:T(8,128)S(1)}, f32[10,8,256]{2,1,0:T(8,128)S(1)}, u32[]{:S(2)}, u32[]{:S(2)}) collective-permute-start(f32[10,8,256]{2,1,0:T(8,128)S(1)} %get-tuple-element.91), channel_id=1, source_target_pairs={{0,25},{1,8},{8,1},{9,16},{16,9},{17,24},{24,17},{25,0},{2,27},{3,... | collective-permute-start | bytes 245768 | tf_op jit(solution)/shard_map/ppermute | solution.py:107
  34.5 2.7 %next_inner.3 = (f32[24,24,256]{2,1,0:T(8,128)S(1)}, f32[3,24,24,256]{3,2,1,0:T(8,128)S(1)}, f32[3,24,24,256]{3,2,1,0:T(8,128)S(1)}, f32[3,24,24,256]{3,2,1,0:T(...) custom-call(f32[16,16,256]{2,1,0:T(8,128)S(1)} %get-tuple-element.86.refs_0_.p.p_in.refs_1_, ...), custom_call_target="tpu_custom_call" | custom-call | flops 40000000 | bytes 1048576 | tf_op jit(solution)/shard_map/next_inner/pallas_call | solution.py:26
  38.1 1.0 %next.3 = (f32[16,16,128]{2,1,0:T(8,128)S(1)}, f32[16,16,128]{2,1,0:T(8,128)S(1)}, f32[16,16,256]{2,1,0:T(8,128)S(1)}, f32[16,4,256]{2,1,0:T(4,128)S(1)}, f32[16,4,256]{2,1,0:T(4,128)S(1)}) custom-call(f32[16,16,256]{2,1,0:T(8,128)S(1)} %get-tuple-element.86.refs_0_.p.p_in.refs_1_, f32[10,8,256]{2,1,0:T(8,128)S(1)} %collective-permute-done.8.xs, ...), custom_call_target="tpu_custom_call" | custom-call | flops 10000000 | bytes 1048576 | tf_op jit(solution)/shard_map/next/pallas_call | solution.py:26
  39.2 2.0 %collective-permute-start.11 = (f32[16,4,256]{2,1,0:T(4,128)S(1)}, f32[16,4,256]{2,1,0:T(4,128)S(1)}, u32[]{:S(2)}, u32[]{:S(2)}) collective-permute-start(f32[16,4,256]{2,1,0:T(4,128)S(1)} %get-tuple-element.112), channel_id=1, source_target_pairs={{0,2},{2,0},{4,6},{6,4},{1,3},{3,1},{5,7},{7,5},{8,10},{10,8},{12,... | collective-permute-start | bytes 196616 | tf_op jit(solution)/shard_map/ppermute | solution.py:101
  41.8 1.7 %collective-permute-done.11.ya = f32[16,4,256]{2,1,0:T(4,128)S(1)} collective-permute-done((f32[16,4,256]{2,1,0:T(4,128)S(1)}, f32[16,4,256]{2,1,0:T(4,128)S(1)}, u32[]{:S(2)}, u32[]{:S(2)}) %collective-permute-start.11) | collective-permute-done | bytes 65568 | tf_op jit(solution)/shard_map/ppermute | solution.py:101
  43.6 1.7 %collective-permute-start.13 = (f32[10,8,256]{2,1,0:T(8,128)S(1)}, f32[10,8,256]{2,1,0:T(8,128)S(1)}, u32[]{:S(2)}, u32[]{:S(2)}) collective-permute-start(f32[10,8,256]{2,1,0:T(8,128)S(1)} %get-tuple-element.116), channel_id=1, source_target_pairs={{0,25},{1,8},{8,1},{9,16},{16,9},{17,24},{24,17},{25,0},{2,27},{3,... | collective-permute-start | bytes 245768 | tf_op jit(solution)/shard_map/ppermute | solution.py:107
  45.3 2.5 %next_inner.4 = (f32[24,24,256]{2,1,0:T(8,128)S(1)}, f32[3,24,24,256]{3,2,1,0:T(8,128)S(1)}, f32[3,24,24,256]{3,2,1,0:T(8,128)S(1)}, f32[3,24,24,256]{3,2,1,0:T(...) custom-call(f32[16,16,256]{2,1,0:T(8,128)S(1)} %get-tuple-element.111.refs_0_.p.p_in.refs_1_, ...), custom_call_target="tpu_custom_call" | custom-call | flops 40000000 | bytes 1048576 | tf_op jit(solution)/shard_map/next_inner/pallas_call | solution.py:26
  50.0 2.0 %collective-permute-start.16 = (f32[16,4,256]{2,1,0:T(4,128)S(1)}, f32[16,4,256]{2,1,0:T(4,128)S(1)}, u32[]{:S(2)}, u32[]{:S(2)}) collective-permute-start(f32[16,4,256]{2,1,0:T(4,128)S(1)} %get-tuple-element.125), channel_id=1, source_target_pairs={{0,2},{2,0},{4,6},{6,4},{1,3},{3,1},{5,7},{7,5},{8,10},{10,8},{12,... | collective-permute-start | bytes 196616 | tf_op jit(solution)/shard_map/ppermute | solution.py:101
  52.7 1.6 %collective-permute-done.16.ya = f32[16,4,256]{2,1,0:T(4,128)S(1)} collective-permute-done((f32[16,4,256]{2,1,0:T(4,128)S(1)}, f32[16,4,256]{2,1,0:T(4,128)S(1)}, u32[]{:S(2)}, u32[]{:S(2)}) %collective-permute-start.16) | collective-permute-done | bytes 65568 | tf_op jit(solution)/shard_map/ppermute | solution.py:101
  54.5 1.1 %collective-permute-start.18 = (f32[10,8,256]{2,1,0:T(8,128)S(1)}, f32[10,8,256]{2,1,0:T(8,128)S(1)}, u32[]{:S(2)}, u32[]{:S(2)}) collective-permute-start(f32[10,8,256]{2,1,0:T(8,128)S(1)} %get-tuple-element.129), channel_id=1, source_target_pairs={{0,25},{1,8},{8,1},{9,16},{16,9},{17,24},{24,17},{25,0},{2,27},{3,... | collective-permute-start | bytes 245768 | tf_op jit(solution)/shard_map/ppermute | solution.py:107
  55.6 2.8 %next_inner.5 = (f32[24,24,256]{2,1,0:T(8,128)S(1)}, f32[3,24,24,256]{3,2,1,0:T(8,128)S(1)}, f32[3,24,24,256]{3,2,1,0:T(8,128)S(1)}, f32[3,24,24,256]{3,2,1,0:T(...) custom-call(f32[16,16,256]{2,1,0:T(8,128)S(1)} %get-tuple-element.124.refs_0_.p.p_in, ...), custom_call_target="tpu_custom_call" | custom-call | flops 40000000 | bytes 1048576 | tf_op jit(solution)/shard_map/next_inner/pallas_call | solution.py:26
  58.4 1.1 %next_near.5.refs_5_ = f32[16,24,256]{2,1,0:T(8,128)S(1)} custom-call(f32[16,16,256]{2,1,0:T(8,128)S(1)} %get-tuple-element.124.refs_0_.p.p_in, f32[10,8,256]{2,1,0:T(8,128)S(1)} %collective-permute-done.20.xs, f32[24,24,256]{2,1,0:T(8,128)S(1)} %get-tuple-element.100.kx, f32[24,24,256]{2,1,0:T(8,128)S(1)} %get-tuple-element.101.ky, ...), custom_call_target="tpu_custom_call" | custom-call | flops 10000000 | bytes 1048576 | tf_op jit(solution)/shard_map/next_near/pallas_call | solution.py:26
  61.0 1.3 %collective-permute-done.21.refs_7_ = f32[17,16,128]{2,1,0:T(8,128)S(1)} collective-permute-done((f32[17,16,128]{2,1,0:T(8,128)S(1)}, f32[17,16,128]{2,1,0:T(8,128)S(1)}, u32[]{:S(2)}, u32[]{:S(2)}) %collective-permute-start.21) | collective-permute-done | bytes 139296 | tf_op jit(solution)/shard_map/ppermute | solution.py:111
  62.4 1.2 %collective-permute-start.22 = (f32[2,16,128]{2,1,0:T(8,128)S(1)}, f32[2,16,128]{2,1,0:T(8,128)S(1)}, u32[]{:S(2)}, u32[]{:S(2)}) collective-permute-start(f32[2,16,128]{2,1,0:T(8,128)S(1)} %pad_maximum_fusion), channel_id=1, source_target_pairs={{0,24},{8,0},{16,8},{24,16},{1,25},{9,1},{17,9},{25,17},{2,26},{10... | collective-permute-start | bytes 49160 | tf_op jit(solution)/shard_map/ppermute | solution.py:738
  63.5 1.0 %collective-permute-start.23 = (f32[2,16,128]{2,1,0:T(8,128)S(1)}, f32[2,16,128]{2,1,0:T(8,128)S(1)}, u32[]{:S(2)}, u32[]{:S(2)}) collective-permute-start(f32[2,16,128]{2,1,0:T(8,128)S(1)} %pad_maximum_fusion), channel_id=1, source_target_pairs={{0,16},{8,24},{16,0},{24,8},{1,17},{9,25},{17,1},{25,9},{2,18},{10... | collective-permute-start | bytes 49160 | tf_op jit(solution)/shard_map/ppermute | solution.py:738
  66.2 1.1 %collective-permute-done.23 = f32[2,16,128]{2,1,0:T(8,128)S(1)} collective-permute-done((f32[2,16,128]{2,1,0:T(8,128)S(1)}, f32[2,16,128]{2,1,0:T(8,128)S(1)}, u32[]{:S(2)}, u32[]{:S(2)}) %collective-permute-start.23) | collective-permute-done | bytes 16416 | tf_op jit(solution)/shard_map/ppermute | solution.py:738
  67.3 1.9 %collective-permute-done.24 = f32[2,16,128]{2,1,0:T(8,128)S(1)} collective-permute-done((f32[2,16,128]{2,1,0:T(8,128)S(1)}, f32[2,16,128]{2,1,0:T(8,128)S(1)}, u32[]{:S(2)}, u32[]{:S(2)}) %collective-permute-start.24) | collective-permute-done | bytes 16416 | tf_op jit(solution)/shard_map/ppermute | solution.py:738
  69.2 2.9 %collective-permute-start.25 = (f32[2,16,128]{2,1,0:T(8,128)S(1)}, f32[2,16,128]{2,1,0:T(8,128)S(1)}, u32[]{:S(2)}, u32[]{:S(2)}) collective-permute-start(f32[2,16,128]{2,1,0:T(8,128)S(1)} %pad_maximum_fusion.1), channel_id=1, source_target_pairs={{0,6},{2,0},{4,2},{6,4},{1,7},{3,1},{5,3},{7,5},{8,14},{10,8},{12,... | collective-permute-start | bytes 49160 | tf_op jit(solution)/shard_map/ppermute | solution.py:738
  72.9 1.9 %collective-permute-start.27 = (f32[2,16,128]{2,1,0:T(8,128)S(1)}, f32[2,16,128]{2,1,0:T(8,128)S(1)}, u32[]{:S(2)}, u32[]{:S(2)}) collective-permute-start(f32[2,16,128]{2,1,0:T(8,128)S(1)} %pad_maximum_fusion.1), channel_id=1, source_target_pairs={{0,2},{2,4},{4,6},{6,0},{1,3},{3,5},{5,7},{7,1},{8,10},{10,12},{12... | collective-permute-start | bytes 49160 | tf_op jit(solution)/shard_map/ppermute | solution.py:738
  75.5 1.2 %collective-permute-done.26 = f32[2,16,128]{2,1,0:T(8,128)S(1)} collective-permute-done((f32[2,16,128]{2,1,0:T(8,128)S(1)}, f32[2,16,128]{2,1,0:T(8,128)S(1)}, u32[]{:S(2)}, u32[]{:S(2)}) %collective-permute-start.26) | collective-permute-done | bytes 16416 | tf_op jit(solution)/shard_map/ppermute | solution.py:738
  76.8 1.6 %collective-permute-done.27 = f32[2,16,128]{2,1,0:T(8,128)S(1)} collective-permute-done((f32[2,16,128]{2,1,0:T(8,128)S(1)}, f32[2,16,128]{2,1,0:T(8,128)S(1)}, u32[]{:S(2)}, u32[]{:S(2)}) %collective-permute-start.27) | collective-permute-done | bytes 16416 | tf_op jit(solution)/shard_map/ppermute | solution.py:738
  78.4 2.0 %last.1 = (f32[32,16,128]{2,1,0:T(8,128)}, f32[32,16,128]{2,1,0:T(8,128)}, f32[3]{0:T(128)}) custom-call(f32[2,16,128]{2,1,0:T(8,128)S(1)} %pad_maximum_fusion.2.sums, f32[32,16,128]{2,1,0:T(8,128)S(1)} %eta.1, f32[16,16,128]{2,1,0:T(8,128)S(1)} %get-tuple-element.89.refs_1_.refs_2_.refs_0_, f32[16,16,128]{2,1,0:T(8,128)S(1)} %collective-permute-done.9.rest_0_.refs_1_, ...), custom_call_target="tpu_custom_call" | custom-call | flops 1000000 | bytes 1048576 | tf_op jit(solution)/shard_map/last/pallas_call | solution.py:26
  (65 shorter events, 12.7 us)
Async XLA Ops:
  0.6 1.8 %copy-start.2 = (s32[32,16,128]{2,1,0:T(8,128)S(1)}, s32[32,16,128]{2,1,0:T(8,128)}, u32[]{:S(2)}) copy-start(s32[32,16,128]{2,1,0:T(8,128)} %param.5) | copy-start | bytes 786436
  0.6 3.4 %copy-start.1 = (f32[8]{0:T(128)S(1)}, f32[8]{0:T(128)}, u32[]{:S(2)}) copy-start(f32[8]{0:T(128)} %table.3) | copy-start | bytes 100
  1.9 15.9 %copy-start = (s32[6]{0:T(128)S(1)}, s32[6]{0:T(128)}, u32[]{:S(2)}) copy-start(s32[6]{0:T(128)} %refs_4_.3) | copy-start | bytes 76
  1.9 2.1 %collective-permute-start = (f32[3,16,16,128]{3,2,1,0:T(8,128)S(1)}, f32[3,16,16,128]{3,2,1,0:T(8,128)S(1)}, u32[]{:S(2)}, u32[]{:S(2)}) collective-permute-start(f32[3,16,16,128]{3,2,1,0:T(8,128)S(1)} %get-tuple-element.145), channel_id=1, source_target_pairs={{0,1},{1,0},{2,3},{3,2},{4,5},{5,4},{6,7},{7,6},{8,9},{9,8},{10,11... | collective-permute-start | bytes 1179656 | tf_op jit(solution)/shard_map/ppermute | solution.py:111
  2.5 1.5 %collective-permute-start.1 = (s32[16,16,128]{2,1,0:T(8,128)S(1)}, s32[16,16,128]{2,1,0:T(8,128)S(1)}, u32[]{:S(2)}, u32[]{:S(2)}) collective-permute-start(s32[16,16,128]{2,1,0:T(8,128)S(1)} %get-tuple-element.147.refs_1_), channel_id=1, source_target_pairs={{0,1},{1,0},{2,3},{3,2},{4,5},{5,4},{6,7},{7,6},{8,9},{9,8},{10,11... | collective-permute-start | bytes 393224 | tf_op jit(solution)/shard_map/ppermute | solution.py:111
  4.9 10.0 %collective-permute-start.2 = (f32[68,4,256]{2,1,0:T(4,128)S(1)}, f32[68,4,256]{2,1,0:T(4,128)S(1)}, u32[]{:S(2)}, u32[]{:S(2)}) collective-permute-start(f32[68,4,256]{2,1,0:T(4,128)S(1)} %get-tuple-element.72), channel_id=1, source_target_pairs={{0,2},{2,0},{4,6},{6,4},{1,3},{3,1},{5,7},{7,5},{8,10},{10,8},{12,... | collective-permute-start | bytes 835592 | tf_op jit(solution)/shard_map/ppermute | solution.py:101
  7.9 7.0 %collective-permute-start.3 = (f32[68,4,256]{2,1,0:T(4,128)S(1)}, f32[68,4,256]{2,1,0:T(4,128)S(1)}, u32[]{:S(2)}, u32[]{:S(2)}) collective-permute-start(f32[68,4,256]{2,1,0:T(4,128)S(1)} %get-tuple-element.73), channel_id=1, source_target_pairs={{0,1},{1,0},{2,4},{3,5},{4,2},{5,3},{6,7},{7,6},{8,9},{9,8},{10,12... | collective-permute-start | bytes 835592 | tf_op jit(solution)/shard_map/ppermute | solution.py:101
  15.0 7.6 %collective-permute-start.5 = (f32[39,8,256]{2,1,0:T(8,128)S(1)}, f32[39,8,256]{2,1,0:T(8,128)S(1)}, u32[]{:S(2)}, u32[]{:S(2)}) collective-permute-start(f32[39,8,256]{2,1,0:T(8,128)S(1)} %get-tuple-element.84), channel_id=1, source_target_pairs={{0,1},{1,0},{8,9},{9,8},{16,17},{17,16},{24,25},{25,24},{2,3},{3,2... | collective-permute-start | bytes 958472 | tf_op jit(solution)/shard_map/ppermute | solution.py:107
  15.0 10.0 %collective-permute-start.4 = (f32[39,8,256]{2,1,0:T(8,128)S(1)}, f32[39,8,256]{2,1,0:T(8,128)S(1)}, u32[]{:S(2)}, u32[]{:S(2)}) collective-permute-start(f32[39,8,256]{2,1,0:T(8,128)S(1)} %get-tuple-element.74), channel_id=1, source_target_pairs={{0,25},{1,8},{8,1},{9,16},{16,9},{17,24},{24,17},{25,0},{2,27},{3,... | collective-permute-start | bytes 958472 | tf_op jit(solution)/shard_map/ppermute | solution.py:107
  26.9 5.3 %collective-permute-start.6 = (f32[16,4,256]{2,1,0:T(4,128)S(1)}, f32[16,4,256]{2,1,0:T(4,128)S(1)}, u32[]{:S(2)}, u32[]{:S(2)}) collective-permute-start(f32[16,4,256]{2,1,0:T(4,128)S(1)} %get-tuple-element.87.after), channel_id=1, source_target_pairs={{0,2},{2,0},{4,6},{6,4},{1,3},{3,1},{5,7},{7,5},{8,10},{10,8},{12,... | collective-permute-start | bytes 196616 | tf_op jit(solution)/shard_map/ppermute | solution.py:101
  30.0 2.2 %collective-permute-start.7 = (f32[16,4,256]{2,1,0:T(4,128)S(1)}, f32[16,4,256]{2,1,0:T(4,128)S(1)}, u32[]{:S(2)}, u32[]{:S(2)}) collective-permute-start(f32[16,4,256]{2,1,0:T(4,128)S(1)} %get-tuple-element.88), channel_id=1, source_target_pairs={{0,1},{1,0},{2,4},{3,5},{4,2},{5,3},{6,7},{7,6},{8,9},{9,8},{10,12... | collective-permute-start | bytes 196616 | tf_op jit(solution)/shard_map/ppermute | solution.py:101
  30.0 4.5 %collective-permute-start.9 = (f32[16,16,128]{2,1,0:T(8,128)S(1)}, f32[16,16,128]{2,1,0:T(8,128)S(1)}, u32[]{:S(2)}, u32[]{:S(2)}) collective-permute-start(f32[16,16,128]{2,1,0:T(8,128)S(1)} %get-tuple-element.90.refs_2_.refs_3_), channel_id=1, source_target_pairs={{0,1},{1,0},{2,3},{3,2},{4,5},{5,4},{6,7},{7,6},{8,9},{9,8},{10,11... | collective-permute-start | bytes 393224 | tf_op jit(solution)/shard_map/ppermute | solution.py:111
  32.3 5.0 %collective-permute-start.10 = (f32[10,8,256]{2,1,0:T(8,128)S(1)}, f32[10,8,256]{2,1,0:T(8,128)S(1)}, u32[]{:S(2)}, u32[]{:S(2)}) collective-permute-start(f32[10,8,256]{2,1,0:T(8,128)S(1)} %get-tuple-element.110), channel_id=1, source_target_pairs={{0,1},{1,0},{8,9},{9,8},{16,17},{17,16},{24,25},{25,24},{2,3},{3,2... | collective-permute-start | bytes 245768 | tf_op jit(solution)/shard_map/ppermute | solution.py:107
  32.3 5.8 %collective-permute-start.8 = (f32[10,8,256]{2,1,0:T(8,128)S(1)}, f32[10,8,256]{2,1,0:T(8,128)S(1)}, u32[]{:S(2)}, u32[]{:S(2)}) collective-permute-start(f32[10,8,256]{2,1,0:T(8,128)S(1)} %get-tuple-element.91), channel_id=1, source_target_pairs={{0,25},{1,8},{8,1},{9,16},{16,9},{17,24},{24,17},{25,0},{2,27},{3,... | collective-permute-start | bytes 245768 | tf_op jit(solution)/shard_map/ppermute | solution.py:107
  39.2 4.3 %collective-permute-start.11 = (f32[16,4,256]{2,1,0:T(4,128)S(1)}, f32[16,4,256]{2,1,0:T(4,128)S(1)}, u32[]{:S(2)}, u32[]{:S(2)}) collective-permute-start(f32[16,4,256]{2,1,0:T(4,128)S(1)} %get-tuple-element.112), channel_id=1, source_target_pairs={{0,2},{2,0},{4,6},{6,4},{1,3},{3,1},{5,7},{7,5},{8,10},{10,8},{12,... | collective-permute-start | bytes 196616 | tf_op jit(solution)/shard_map/ppermute | solution.py:101
  41.2 2.3 %collective-permute-start.12 = (f32[16,4,256]{2,1,0:T(4,128)S(1)}, f32[16,4,256]{2,1,0:T(4,128)S(1)}, u32[]{:S(2)}, u32[]{:S(2)}) collective-permute-start(f32[16,4,256]{2,1,0:T(4,128)S(1)} %get-tuple-element.113), channel_id=1, source_target_pairs={{0,1},{1,0},{2,4},{3,5},{4,2},{5,3},{6,7},{7,6},{8,9},{9,8},{10,12... | collective-permute-start | bytes 196616 | tf_op jit(solution)/shard_map/ppermute | solution.py:101
  41.2 4.1 %collective-permute-start.14 = (f32[16,16,128]{2,1,0:T(8,128)S(1)}, f32[16,16,128]{2,1,0:T(8,128)S(1)}, u32[]{:S(2)}, u32[]{:S(2)}) collective-permute-start(f32[16,16,128]{2,1,0:T(8,128)S(1)} %get-tuple-element.115.refs_5_), channel_id=1, source_target_pairs={{0,1},{1,0},{2,3},{3,2},{4,5},{5,4},{6,7},{7,6},{8,9},{9,8},{10,11... | collective-permute-start | bytes 393224 | tf_op jit(solution)/shard_map/ppermute | solution.py:111
  43.6 4.3 %collective-permute-start.15 = (f32[10,8,256]{2,1,0:T(8,128)S(1)}, f32[10,8,256]{2,1,0:T(8,128)S(1)}, u32[]{:S(2)}, u32[]{:S(2)}) collective-permute-start(f32[10,8,256]{2,1,0:T(8,128)S(1)} %get-tuple-element.123), channel_id=1, source_target_pairs={{0,1},{1,0},{8,9},{9,8},{16,17},{17,16},{24,25},{25,24},{2,3},{3,2... | collective-permute-start | bytes 245768 | tf_op jit(solution)/shard_map/ppermute | solution.py:107
  43.6 5.6 %collective-permute-start.13 = (f32[10,8,256]{2,1,0:T(8,128)S(1)}, f32[10,8,256]{2,1,0:T(8,128)S(1)}, u32[]{:S(2)}, u32[]{:S(2)}) collective-permute-start(f32[10,8,256]{2,1,0:T(8,128)S(1)} %get-tuple-element.116), channel_id=1, source_target_pairs={{0,25},{1,8},{8,1},{9,16},{16,9},{17,24},{24,17},{25,0},{2,27},{3,... | collective-permute-start | bytes 245768 | tf_op jit(solution)/shard_map/ppermute | solution.py:107
  50.0 4.3 %collective-permute-start.16 = (f32[16,4,256]{2,1,0:T(4,128)S(1)}, f32[16,4,256]{2,1,0:T(4,128)S(1)}, u32[]{:S(2)}, u32[]{:S(2)}) collective-permute-start(f32[16,4,256]{2,1,0:T(4,128)S(1)} %get-tuple-element.125), channel_id=1, source_target_pairs={{0,2},{2,0},{4,6},{6,4},{1,3},{3,1},{5,7},{7,5},{8,10},{10,8},{12,... | collective-permute-start | bytes 196616 | tf_op jit(solution)/shard_map/ppermute | solution.py:101
  52.1 2.3 %collective-permute-start.17 = (f32[16,4,256]{2,1,0:T(4,128)S(1)}, f32[16,4,256]{2,1,0:T(4,128)S(1)}, u32[]{:S(2)}, u32[]{:S(2)}) collective-permute-start(f32[16,4,256]{2,1,0:T(4,128)S(1)} %get-tuple-element.126), channel_id=1, source_target_pairs={{0,1},{1,0},{2,4},{3,5},{4,2},{5,3},{6,7},{7,6},{8,9},{9,8},{10,12... | collective-permute-start | bytes 196616 | tf_op jit(solution)/shard_map/ppermute | solution.py:101
  52.1 3.5 %collective-permute-start.19 = (f32[16,16,128]{2,1,0:T(8,128)S(1)}, f32[16,16,128]{2,1,0:T(8,128)S(1)}, u32[]{:S(2)}, u32[]{:S(2)}) collective-permute-start(f32[16,16,128]{2,1,0:T(8,128)S(1)} %get-tuple-element.128.refs_7_), channel_id=1, source_target_pairs={{0,1},{1,0},{2,3},{3,2},{4,5},{5,4},{6,7},{7,6},{8,9},{9,8},{10,11... | collective-permute-start | bytes 393224 | tf_op jit(solution)/shard_map/ppermute | solution.py:111
  54.4 4.0 %collective-permute-start.20 = (f32[10,8,256]{2,1,0:T(8,128)S(1)}, f32[10,8,256]{2,1,0:T(8,128)S(1)}, u32[]{:S(2)}, u32[]{:S(2)}) collective-permute-start(f32[10,8,256]{2,1,0:T(8,128)S(1)} %get-tuple-element.136), channel_id=1, source_target_pairs={{0,1},{1,0},{8,9},{9,8},{16,17},{17,16},{24,25},{25,24},{2,3},{3,2... | collective-permute-start | bytes 245768 | tf_op jit(solution)/shard_map/ppermute | solution.py:107
  54.5 5.6 %collective-permute-start.18 = (f32[10,8,256]{2,1,0:T(8,128)S(1)}, f32[10,8,256]{2,1,0:T(8,128)S(1)}, u32[]{:S(2)}, u32[]{:S(2)}) collective-permute-start(f32[10,8,256]{2,1,0:T(8,128)S(1)} %get-tuple-element.129), channel_id=1, source_target_pairs={{0,25},{1,8},{8,1},{9,16},{16,9},{17,24},{24,17},{25,0},{2,27},{3,... | collective-permute-start | bytes 245768 | tf_op jit(solution)/shard_map/ppermute | solution.py:107
  60.9 1.4 %collective-permute-start.21 = (f32[17,16,128]{2,1,0:T(8,128)S(1)}, f32[17,16,128]{2,1,0:T(8,128)S(1)}, u32[]{:S(2)}, u32[]{:S(2)}) collective-permute-start(f32[17,16,128]{2,1,0:T(8,128)S(1)} %get-tuple-element.137), channel_id=1, source_target_pairs={{0,1},{1,0},{2,3},{3,2},{4,5},{5,4},{6,7},{7,6},{8,9},{9,8},{10,11... | collective-permute-start | bytes 417800 | tf_op jit(solution)/shard_map/ppermute | solution.py:111
  62.4 3.8 %collective-permute-start.22 = (f32[2,16,128]{2,1,0:T(8,128)S(1)}, f32[2,16,128]{2,1,0:T(8,128)S(1)}, u32[]{:S(2)}, u32[]{:S(2)}) collective-permute-start(f32[2,16,128]{2,1,0:T(8,128)S(1)} %pad_maximum_fusion), channel_id=1, source_target_pairs={{0,24},{8,0},{16,8},{24,16},{1,25},{9,1},{17,9},{25,17},{2,26},{10... | collective-permute-start | bytes 49160 | tf_op jit(solution)/shard_map/ppermute | solution.py:738
  63.5 3.7 %collective-permute-start.23 = (f32[2,16,128]{2,1,0:T(8,128)S(1)}, f32[2,16,128]{2,1,0:T(8,128)S(1)}, u32[]{:S(2)}, u32[]{:S(2)}) collective-permute-start(f32[2,16,128]{2,1,0:T(8,128)S(1)} %pad_maximum_fusion), channel_id=1, source_target_pairs={{0,16},{8,24},{16,0},{24,8},{1,17},{9,25},{17,1},{25,9},{2,18},{10... | collective-permute-start | bytes 49160 | tf_op jit(solution)/shard_map/ppermute | solution.py:738
  64.5 4.6 %collective-permute-start.24 = (f32[2,16,128]{2,1,0:T(8,128)S(1)}, f32[2,16,128]{2,1,0:T(8,128)S(1)}, u32[]{:S(2)}, u32[]{:S(2)}) collective-permute-start(f32[2,16,128]{2,1,0:T(8,128)S(1)} %pad_maximum_fusion), channel_id=1, source_target_pairs={{0,8},{8,16},{16,24},{24,0},{1,9},{9,17},{17,25},{25,1},{2,10},{10... | collective-permute-start | bytes 49160 | tf_op jit(solution)/shard_map/ppermute | solution.py:738
  69.2 6.3 %collective-permute-start.25 = (f32[2,16,128]{2,1,0:T(8,128)S(1)}, f32[2,16,128]{2,1,0:T(8,128)S(1)}, u32[]{:S(2)}, u32[]{:S(2)}) collective-permute-start(f32[2,16,128]{2,1,0:T(8,128)S(1)} %pad_maximum_fusion.1), channel_id=1, source_target_pairs={{0,6},{2,0},{4,2},{6,4},{1,7},{3,1},{5,3},{7,5},{8,14},{10,8},{12,... | collective-permute-start | bytes 49160 | tf_op jit(solution)/shard_map/ppermute | solution.py:738
  72.1 4.6 %collective-permute-start.26 = (f32[2,16,128]{2,1,0:T(8,128)S(1)}, f32[2,16,128]{2,1,0:T(8,128)S(1)}, u32[]{:S(2)}, u32[]{:S(2)}) collective-permute-start(f32[2,16,128]{2,1,0:T(8,128)S(1)} %pad_maximum_fusion.1), channel_id=1, source_target_pairs={{0,4},{2,6},{4,0},{6,2},{1,5},{3,7},{5,1},{7,3},{8,12},{10,14},{12... | collective-permute-start | bytes 49160 | tf_op jit(solution)/shard_map/ppermute | solution.py:738
  72.9 5.5 %collective-permute-start.27 = (f32[2,16,128]{2,1,0:T(8,128)S(1)}, f32[2,16,128]{2,1,0:T(8,128)S(1)}, u32[]{:S(2)}, u32[]{:S(2)}) collective-permute-start(f32[2,16,128]{2,1,0:T(8,128)S(1)} %pad_maximum_fusion.1), channel_id=1, source_target_pairs={{0,2},{2,4},{4,6},{6,0},{1,3},{3,5},{5,7},{7,1},{8,10},{10,12},{12... | collective-permute-start | bytes 49160 | tf_op jit(solution)/shard_map/ppermute | solution.py:738

commit v10 on v9

--- a/solution.py
+++ b/solution.py
@@ -7,6 +7,7 @@
 from jax.experimental.pallas import tpu as pltpu
 from jax.sharding import PartitionSpec as P
 
+
 ITERS = 3
 SWEEPS = 4
 OMEGA = 0.8
@@ -22,7 +23,7 @@
     return jax.ShapeDtypeStruct(shape, F32)
 
 
-def call(kernel, outs, ins, specs=None, scratch=(), flops=10**6, name=None, out_specs=None):
+def call(kernel, outs, ins, specs=None, scratch=(), flops=10**6, out_specs=None):
     return pl.pallas_call(
         kernel,
         out_shape=outs,
@@ -31,7 +32,6 @@
         scratch_shapes=list(scratch),
         compiler_params=pltpu.CompilerParams(vmem_limit_bytes=24 * 2**20),
         cost_estimate=pl.CostEstimate(flops=flops, bytes_accessed=2**20, transcendentals=0),
-        name=name,
     )(*ins)
 
 
@@ -104,7 +104,9 @@
 def exchange_x(a, b, n):
     even = [(i, i ^ 1) for i in range(n)]
     odd = [(i, (i + (1 if i % 2 else -1)) % n) for i in range(n)]
-    return lax.ppermute(a, ("gx", "gz"), even), lax.ppermute(b, ("gx", "gz"), odd)
+    b = lax.ppermute(b, ("gx", "gz"), odd)
+    a = lax.ppermute(a, ("gx", "gz"), even)
+    return a, b
 
 
 def core_shift(value, n, j):
@@ -147,7 +149,7 @@
             send_a[c * rows + r] = jnp.where(odd, row[:h], row[ys - h :])
             send_b[c * rows + r] = jnp.where(odd, row[ys - h :], row[:h])
 
-        rows_loop(0, rows, one, 4)
+        rows_loop(0, rows, one, 16 if c == 3 else 4)
     for r in range(rows):
         line = full[3, r, ys - h - 1 : ys - h, :]
         send_a[fields * rows + r // 4, r % 4 : r % 4 + 1, :] = line
@@ -200,7 +202,7 @@
 
 def force_edges_kernel(full, ya, yb, send_a, send_b):
     place = Place()
-    _, rows, ys, _ = full.shape
+    _, rows, _, _ = full.shape
     h = HALO
     for send, first in ((send_a, place.odd), (send_b, jnp.logical_not(place.odd))):
 
@@ -215,22 +217,22 @@
             put_tile(send, t, tile, lambda c, k, at=at: full[c, at(k)], halo)
 
 
-def edges_kernel(p, ya, yb, *rest):
-    send_a, send_b = rest[-2:]
+def edges_kernel(near, p, ya, yb, *rest):
+    send = rest[-1]
     place = Place()
+    first = place.odd if near else jnp.logical_not(place.odd)
     rows = p.shape[0]
     h = HALO
-    for send, first in ((send_a, place.odd), (send_b, jnp.logical_not(place.odd))):
-
-        def at(k, first=first):
-            return jnp.where(first, h - 1 - k, rows - h + k)
-
-        def halo(c, k, at=at):
-            a, b = ya[at(k)], yb[at(k)]
-            return place.up(a, b), place.low(a, b)
-
-        for t, tile in enumerate(face_list()):
-            put_tile(send, t, tile, lambda c, k, at=at: p[at(k)], halo)
+
+    def at(k):
+        return jnp.where(first, h - 1 - k, rows - h + k)
+
+    def halo(c, k):
+        a, b = ya[at(k)], yb[at(k)]
+        return place.up(a, b), place.low(a, b)
+
+    for t, tile in enumerate(face_list()):
+        put_tile(send, t, tile, lambda c, k: p[at(k)], halo)
 
 
 class Rows:
@@ -769,11 +771,10 @@
         ],
         (table, *forces, *phases),
         [SMEM] + [VMEM] * (2 * nz),
-        name="gather",
     )
     ya, yb = exchange_y(ya, yb, ny, nz)
     edge = sds(len(edge_list()), 8, zs)
-    xa, xb = call(force_edges_kernel, [edge, edge], (full, ya, yb), name="force_edges")
+    xa, xb = call(force_edges_kernel, [edge, edge], (full, ya, yb))
     xa, xb = exchange_x(xa, xb, chain)
 
     v_shape = [sds(rows, ys, lanes)] * nz
@@ -789,7 +790,6 @@
         [VMEM] * 3 + [SMEM],
         [field, pltpu.VMEM((total, slots, zs), F32), line],
         heavy,
-        "first_inner",
     )
     scratch = [field, pltpu.VMEM((total + 1, slots, zs), F32), line] + [field] * SWEEPS
     result = sds(rows, slots, zs)
@@ -800,7 +800,6 @@
         [VMEM] * 4 + [SMEM] + [VMEM] * len(early),
         scratch,
         heavy // 2,
-        "first_near",
     )
     outs = call(
         functools.partial(first_side, nz, sizes, False),
@@ -809,13 +808,11 @@
         [VMEM] * 4 + [SMEM] + [VMEM] * (len(early) + 1),
         scratch,
         heavy // 2,
-        "first",
     )
     coefs = call(
         functools.partial(join_kernel, total, rows),
         [scalar] * 3 + [vector],
         (*early[:4], *near[:4], *outs[nz + 3 :]),
-        name="join",
     )
     vs, ps, moments = [list(outs[:nz])], [outs[nz]], []
     eta = call(
@@ -823,7 +820,6 @@
         sds(*phase.shape),
         (table, outs[nz + 1], *slices),
         [SMEM] + [VMEM] * (nz + 1),
-        name="eta",
     )
     ya, yb = outs[nz + 1 : nz + 3]
     placed = []
@@ -839,12 +835,14 @@
                 (p, *ps[:-1][-1:], *[q for v in vs for q in v]),
                 None,
                 [pltpu.VMEM((count, ys, zs), F32)],
-                name="moments",
             )[0]
         )
         ya, yb = exchange_y(ya, yb, ny, nz)
         edge = sds(len(face_list()), 8, zs)
-        xa, xb = call(edges_kernel, [edge, edge], (p, ya, yb, moments[-1]), name="edges")
+        far_edges = functools.partial(edges_kernel, False)
+        xb = call(far_edges, edge, (p, ya, yb, moments[-1]))
+        near_edges = functools.partial(edges_kernel, True)
+        xa = call(near_edges, edge, (p, ya, yb, xb))
         xa, xb = exchange_x(xa, xb, chain)
         early = call(
             functools.partial(next_inner, nz - 1),
@@ -853,7 +851,6 @@
             None,
             (),
             heavy,
-            "next_inner",
         )
         scratch = [pltpu.VMEM((total, slots, zs), F32)] + [field] * SWEEPS
         near = call(
@@ -863,7 +860,6 @@
             None,
             scratch,
             heavy // 4,
-            "next_near",
         )
         joint = v_shape[:-1] + [sds(rows + 1, ys, lanes)]
         outs = call(
@@ -873,7 +869,6 @@
             None,
             scratch + ([pltpu.VMEM((ys, zs), F32)] if last else []),
             heavy // 4,
-            "next",
         )
         vs.append(list(outs[:nz]))
         if not last:
@@ -893,7 +888,6 @@
         functools.partial(last_kernel, nz, cells),
         [sds(*phase.shape), sds(*phase.shape), sds(ITERS)],
         (pair, eta, *[q for v in placed for q in v]),
-        name="last",
         out_specs=[VMEM, VMEM, SMEM],
     )
     return pressure, residual, norms

time: 80.7 us -> 80.8 us (level)
    pallas_call x23 -> x26, Pallas kernels: 26.3 us -> 26.4 us  [call(): pl.pallas_call(kernel, out_shape=outs, in_specs=specs or [VMEM] * len(ins...]
where the time goes in v10:
time: 80.8 us; the launch traced here: 80.6 us
  starting transfers between devices  28.6 us (35%)
  Pallas kernels  26.4 us (33%)
  waiting for transfers between devices  23.2 us (29%)
  local copies, waits for them, and re-layouts  1.24 us (2%)
  between operations  1.14 us (1%)
    pallas_call x26, Pallas kernels, call(): pl.pallas_call(kernel, out_shape=outs, in_specs=specs or [VMEM] * len(ins...  26.4 us
    ppermute x8, waiting for transfers between devices, exchange_y(): return (lax.ppermute(a, 'gy', even), lax.ppermute(b, ('gy', 'gz'), odd))  11.9 us
    ppermute x8, starting transfers between devices, exchange_y(): return (lax.ppermute(a, 'gy', even), lax.ppermute(b, ('gy', 'gz'), odd))  10.1 us
    ppermute x6, starting transfers between devices, sum_along(): terms.append(lax.ppermute(pair, axis, moves))  8.57 us
    ppermute x4, starting transfers between devices, exchange_x(): b = lax.ppermute(b, ('gx', 'gz'), odd)  7.36 us
    ppermute x6, waiting for transfers between devices, sum_along(): terms.append(lax.ppermute(pair, axis, moves))  6.63 us
    ppermute x6, waiting for transfers between devices, core_shift(): return lax.ppermute(value, 'gz', [(i, (i + j) % n) for i in range(n)])  2.77 us
    ppermute x6, starting transfers between devices, core_shift(): return lax.ppermute(value, 'gz', [(i, (i + j) % n) for i in range(n)])  2.25 us
  transfers between devices with their start and end apart: 28, of which 14 were waited for; matrix products, arithmetic and copies ran while one was open for 0% of the time, Pallas kernels for 23%

profile of v10, /device:TPU:0, one launch (start us, length us, event | category | flops | bytes accessed | tf_op | source)
XLA Modules:
  0.0 80.6 jit_solution(10443957661498357857)
XLA Ops:
  0.7 1.2 %constant_dynamic-slice_fusion.2 = (f32[3,16,16,128]{3,2,1,0:T(8,128)S(1)}, f32[3,16,16,128]{3,2,1,0:T(8,128)S(1)}) fusion(f32[3,32,16,128]{3,2,1,0:T(8,128)} %param.4, s32[]{:T(128)S(6)} %select_n.161, s32[]{:T(128)S(6)} %select_n.160), kind=kLoop, calls=%fused_computation.33 | loop fusion | bytes 1572872 | tf_op jit(solution)/shard_map/dynamic_slice | solution.py:761
  2.6 1.4 %collective-permute-done.1.refs_3_ = s32[16,16,128]{2,1,0:T(8,128)S(1)} collective-permute-done((s32[16,16,128]{2,1,0:T(8,128)S(1)}, s32[16,16,128]{2,1,0:T(8,128)S(1)}, u32[]{:S(2)}, u32[]{:S(2)}) %collective-permute-start.1) | collective-permute-done | bytes 131104 | tf_op jit(solution)/shard_map/ppermute | solution.py:113
  4.9 3.0 %collective-permute-start.2 = (f32[68,4,256]{2,1,0:T(4,128)S(1)}, f32[68,4,256]{2,1,0:T(4,128)S(1)}, u32[]{:S(2)}, u32[]{:S(2)}) collective-permute-start(f32[68,4,256]{2,1,0:T(4,128)S(1)} %get-tuple-element.66), channel_id=1, source_target_pairs={{0,2},{2,0},{4,6},{6,4},{1,3},{3,1},{5,7},{7,5},{8,10},{10,8},{12,... | collective-permute-start | bytes 835592 | tf_op jit(solution)/shard_map/ppermute | solution.py:101
  7.9 7.0 %collective-permute-done.2.ya.refs_1_ = f32[68,4,256]{2,1,0:T(4,128)S(1)} collective-permute-done((f32[68,4,256]{2,1,0:T(4,128)S(1)}, f32[68,4,256]{2,1,0:T(4,128)S(1)}, u32[]{:S(2)}, u32[]{:S(2)}) %collective-permute-start.2) | collective-permute-done | bytes 278560 | tf_op jit(solution)/shard_map/ppermute | solution.py:101
  15.0 2.7 %collective-permute-start.4 = (f32[39,8,256]{2,1,0:T(8,128)S(1)}, f32[39,8,256]{2,1,0:T(8,128)S(1)}, u32[]{:S(2)}, u32[]{:S(2)}) collective-permute-start(f32[39,8,256]{2,1,0:T(8,128)S(1)} %get-tuple-element.68), channel_id=1, source_target_pairs={{0,25},{1,8},{8,1},{9,16},{16,9},{17,24},{24,17},{25,0},{2,27},{3,... | collective-permute-start | bytes 958472 | tf_op jit(solution)/shard_map/ppermute | solution.py:107
  17.7 4.8 %shard_map.69 = (f32[24,24,256]{2,1,0:T(8,128)S(1)}, f32[24,24,256]{2,1,0:T(8,128)S(1)}, f32[24,24,256]{2,1,0:T(8,128)S(1)}, f32[3,24,24,256]{3,2,1,0:T(8,128)S(...) custom-call(f32[4,16,16,256]{3,2,1,0:T(8,128)S(1)} %get-tuple-elemen, ...), custom_call_target="tpu_custom_call" | custom-call | flops 40000000 | bytes 1048576 | tf_op jit(solution)/shard_map/pallas_call | solution.py:27
  22.5 1.7 %shard_map.70 = (f32[24,24,256]{2,1,0:T(8,128)S(1)}, f32[24,24,256]{2,1,0:T(8,128)S(1)}, f32[24,24,256]{2,1,0:T(8,128)S(1)}, f32[3,24,24,256]{3,2,1,0:T(8,128)S(1)}, f32[16,24,256]{2,1,0:T(8,128)S(1)}) custom-call(f32[4,16,16,256]{3,2,1,0:T(8,128)S(1)} %get-tuple-element.65.full.refs_0_.refs_3_, f32[68,4,256]{2,1,0:T(4,128)S(1)} %collective-permute-done.2.ya.refs_1_, ...), custom_call_target="tpu_custom_call" | custom-call | flops 20000000 | bytes 1048576 | tf_op jit(solution)/shard_map/pallas_call | solution.py:27
  25.0 1.9 %shard_map.71 = (f32[16,16,128]{2,1,0:T(8,128)S(1)}, f32[16,16,128]{2,1,0:T(8,128)S(1)}, f32[16,16,256]{2,1,0:T(8,128)S(1)}, f32[16,4,256]{2,1,0:T(4,128)S(1)}, ...) custom-call(f32[4,16,16,256]{3,2,1,0:T(8,128)S(1)} %get-tuple-elemen, ...), custom_call_target="tpu_custom_call" | custom-call | flops 20000000 | bytes 1048576 | tf_op jit(solution)/shard_map/pallas_call | solution.py:27
  26.9 3.1 %collective-permute-start.6 = (f32[16,4,256]{2,1,0:T(4,128)S(1)}, f32[16,4,256]{2,1,0:T(4,128)S(1)}, u32[]{:S(2)}, u32[]{:S(2)}) collective-permute-start(f32[16,4,256]{2,1,0:T(4,128)S(1)} %get-tuple-element.81.after), channel_id=1, source_target_pairs={{0,2},{2,0},{4,6},{6,4},{1,3},{3,1},{5,7},{7,5},{8,10},{10,8},{12,... | collective-permute-start | bytes 196616 | tf_op jit(solution)/shard_map/ppermute | solution.py:101
  30.6 1.6 %collective-permute-done.6.ya = f32[16,4,256]{2,1,0:T(4,128)S(1)} collective-permute-done((f32[16,4,256]{2,1,0:T(4,128)S(1)}, f32[16,4,256]{2,1,0:T(4,128)S(1)}, u32[]{:S(2)}, u32[]{:S(2)}) %collective-permute-start.6) | collective-permute-done | bytes 65568 | tf_op jit(solution)/shard_map/ppermute | solution.py:101
  32.3 1.9 %collective-permute-start.8 = (f32[10,8,256]{2,1,0:T(8,128)S(1)}, f32[10,8,256]{2,1,0:T(8,128)S(1)}, u32[]{:S(2)}, u32[]{:S(2)}) collective-permute-start(f32[10,8,256]{2,1,0:T(8,128)S(1)} %shard_map.73.rest_0_), channel_id=1, source_target_pairs={{0,25},{1,8},{8,1},{9,16},{16,9},{17,24},{24,17},{25,0},{2,27},{3,... | collective-permute-start | bytes 245768 | tf_op jit(solution)/shard_map/ppermute | solution.py:107
  34.5 2.7 %shard_map.75 = (f32[24,24,256]{2,1,0:T(8,128)S(1)}, f32[3,24,24,256]{3,2,1,0:T(8,128)S(1)}, f32[3,24,24,256]{3,2,1,0:T(8,128)S(1)}, f32[3,24,24,256]{3,2,1,0:T(...) custom-call(f32[16,16,256]{2,1,0:T(8,128)S(1)} %get-tuple-element.80.refs_0_.p.p_in.refs_1_, ...), custom_call_target="tpu_custom_call" | custom-call | flops 40000000 | bytes 1048576 | tf_op jit(solution)/shard_map/pallas_call | solution.py:27
  38.1 1.0 %shard_map.78 = (f32[16,16,128]{2,1,0:T(8,128)S(1)}, f32[16,16,128]{2,1,0:T(8,128)S(1)}, f32[16,16,256]{2,1,0:T(8,128)S(1)}, f32[16,4,256]{2,1,0:T(4,128)S(1)}, f32[16,4,256]{2,1,0:T(4,128)S(1)}) custom-call(f32[16,16,256]{2,1,0:T(8,128)S(1)} %get-tuple-element.80.refs_0_.p.p_in.refs_1_, f32[10,8,256]{2,1,0:T(8,128)S(1)} %collective-permute-done.8.xs, ...), custom_call_target="tpu_custom_call" | custom-call | flops 10000000 | bytes 1048576 | tf_op jit(solution)/shard_map/pallas_call | solution.py:27
  39.2 2.0 %collective-permute-start.11 = (f32[16,4,256]{2,1,0:T(4,128)S(1)}, f32[16,4,256]{2,1,0:T(4,128)S(1)}, u32[]{:S(2)}, u32[]{:S(2)}) collective-permute-start(f32[16,4,256]{2,1,0:T(4,128)S(1)} %get-tuple-element.104), channel_id=1, source_target_pairs={{0,2},{2,0},{4,6},{6,4},{1,3},{3,1},{5,7},{7,5},{8,10},{10,8},{12,... | collective-permute-start | bytes 196616 | tf_op jit(solution)/shard_map/ppermute | solution.py:101
  41.8 1.7 %collective-permute-done.11.ya = f32[16,4,256]{2,1,0:T(4,128)S(1)} collective-permute-done((f32[16,4,256]{2,1,0:T(4,128)S(1)}, f32[16,4,256]{2,1,0:T(4,128)S(1)}, u32[]{:S(2)}, u32[]{:S(2)}) %collective-permute-start.11) | collective-permute-done | bytes 65568 | tf_op jit(solution)/shard_map/ppermute | solution.py:101
  43.7 1.7 %collective-permute-start.13 = (f32[10,8,256]{2,1,0:T(8,128)S(1)}, f32[10,8,256]{2,1,0:T(8,128)S(1)}, u32[]{:S(2)}, u32[]{:S(2)}) collective-permute-start(f32[10,8,256]{2,1,0:T(8,128)S(1)} %shard_map.80.rest_0_), channel_id=1, source_target_pairs={{0,25},{1,8},{8,1},{9,16},{16,9},{17,24},{24,17},{25,0},{2,27},{3,... | collective-permute-start | bytes 245768 | tf_op jit(solution)/shard_map/ppermute | solution.py:107
  45.3 2.5 %shard_map.81 = (f32[24,24,256]{2,1,0:T(8,128)S(1)}, f32[3,24,24,256]{3,2,1,0:T(8,128)S(1)}, f32[3,24,24,256]{3,2,1,0:T(8,128)S(1)}, f32[3,24,24,256]{3,2,1,0:T(...) custom-call(f32[16,16,256]{2,1,0:T(8,128)S(1)} %get-tuple-element.103.refs_0_.p.p_in.refs_1_, ...), custom_call_target="tpu_custom_call" | custom-call | flops 40000000 | bytes 1048576 | tf_op jit(solution)/shard_map/pallas_call | solution.py:27
  50.1 2.0 %collective-permute-start.16 = (f32[16,4,256]{2,1,0:T(4,128)S(1)}, f32[16,4,256]{2,1,0:T(4,128)S(1)}, u32[]{:S(2)}, u32[]{:S(2)}) collective-permute-start(f32[16,4,256]{2,1,0:T(4,128)S(1)} %get-tuple-element.115), channel_id=1, source_target_pairs={{0,2},{2,0},{4,6},{6,4},{1,3},{3,1},{5,7},{7,5},{8,10},{10,8},{12,... | collective-permute-start | bytes 196616 | tf_op jit(solution)/shard_map/ppermute | solution.py:101
  52.8 1.7 %collective-permute-done.16.ya = f32[16,4,256]{2,1,0:T(4,128)S(1)} collective-permute-done((f32[16,4,256]{2,1,0:T(4,128)S(1)}, f32[16,4,256]{2,1,0:T(4,128)S(1)}, u32[]{:S(2)}, u32[]{:S(2)}) %collective-permute-start.16) | collective-permute-done | bytes 65568 | tf_op jit(solution)/shard_map/ppermute | solution.py:101
  54.6 1.1 %collective-permute-start.18 = (f32[10,8,256]{2,1,0:T(8,128)S(1)}, f32[10,8,256]{2,1,0:T(8,128)S(1)}, u32[]{:S(2)}, u32[]{:S(2)}) collective-permute-start(f32[10,8,256]{2,1,0:T(8,128)S(1)} %shard_map.86.rest_0_), channel_id=1, source_target_pairs={{0,25},{1,8},{8,1},{9,16},{16,9},{17,24},{24,17},{25,0},{2,27},{3,... | collective-permute-start | bytes 245768 | tf_op jit(solution)/shard_map/ppermute | solution.py:107
  55.6 2.8 %shard_map.87 = (f32[24,24,256]{2,1,0:T(8,128)S(1)}, f32[3,24,24,256]{3,2,1,0:T(8,128)S(1)}, f32[3,24,24,256]{3,2,1,0:T(8,128)S(1)}, f32[3,24,24,256]{3,2,1,0:T(...) custom-call(f32[16,16,256]{2,1,0:T(8,128)S(1)} %get-tuple-element.114.refs_0_.p.p_in, ...), custom_call_target="tpu_custom_call" | custom-call | flops 40000000 | bytes 1048576 | tf_op jit(solution)/shard_map/pallas_call | solution.py:27
  58.5 1.1 %shard_map.89.refs_5_ = f32[16,24,256]{2,1,0:T(8,128)S(1)} custom-call(f32[16,16,256]{2,1,0:T(8,128)S(1)} %get-tuple-element.114.refs_0_.p.p_in, f32[10,8,256]{2,1,0:T(8,128)S(1)} %collective-permute-done.20.xs, f32[24,24,256]{2,1,0:T(8,128)S(1)} %get-tuple-element.93.kx, f32[24,24,256]{2,1,0:T(8,128)S(1)} %get-tuple-element.94.ky, ...), custom_call_target="tpu_custom_call" | custom-call | flops 10000000 | bytes 1048576 | tf_op jit(solution)/shard_map/pallas_call | solution.py:27
  61.1 1.3 %collective-permute-done.21.refs_7_ = f32[17,16,128]{2,1,0:T(8,128)S(1)} collective-permute-done((f32[17,16,128]{2,1,0:T(8,128)S(1)}, f32[17,16,128]{2,1,0:T(8,128)S(1)}, u32[]{:S(2)}, u32[]{:S(2)}) %collective-permute-start.21) | collective-permute-done | bytes 139296 | tf_op jit(solution)/shard_map/ppermute | solution.py:113
  62.4 1.2 %collective-permute-start.22 = (f32[2,16,128]{2,1,0:T(8,128)S(1)}, f32[2,16,128]{2,1,0:T(8,128)S(1)}, u32[]{:S(2)}, u32[]{:S(2)}) collective-permute-start(f32[2,16,128]{2,1,0:T(8,128)S(1)} %pad_maximum_fusion), channel_id=1, source_target_pairs={{0,24},{8,0},{16,8},{24,16},{1,25},{9,1},{17,9},{25,17},{2,26},{10... | collective-permute-start | bytes 49160 | tf_op jit(solution)/shard_map/ppermute | solution.py:740
  63.6 1.0 %collective-permute-start.23 = (f32[2,16,128]{2,1,0:T(8,128)S(1)}, f32[2,16,128]{2,1,0:T(8,128)S(1)}, u32[]{:S(2)}, u32[]{:S(2)}) collective-permute-start(f32[2,16,128]{2,1,0:T(8,128)S(1)} %pad_maximum_fusion), channel_id=1, source_target_pairs={{0,16},{8,24},{16,0},{24,8},{1,17},{9,25},{17,1},{25,9},{2,18},{10... | collective-permute-start | bytes 49160 | tf_op jit(solution)/shard_map/ppermute | solution.py:740
  66.2 1.1 %collective-permute-done.23 = f32[2,16,128]{2,1,0:T(8,128)S(1)} collective-permute-done((f32[2,16,128]{2,1,0:T(8,128)S(1)}, f32[2,16,128]{2,1,0:T(8,128)S(1)}, u32[]{:S(2)}, u32[]{:S(2)}) %collective-permute-start.23) | collective-permute-done | bytes 16416 | tf_op jit(solution)/shard_map/ppermute | solution.py:740
  67.4 1.9 %collective-permute-done.24 = f32[2,16,128]{2,1,0:T(8,128)S(1)} collective-permute-done((f32[2,16,128]{2,1,0:T(8,128)S(1)}, f32[2,16,128]{2,1,0:T(8,128)S(1)}, u32[]{:S(2)}, u32[]{:S(2)}) %collective-permute-start.24) | collective-permute-done | bytes 16416 | tf_op jit(solution)/shard_map/ppermute | solution.py:740
  69.3 2.9 %collective-permute-start.25 = (f32[2,16,128]{2,1,0:T(8,128)S(1)}, f32[2,16,128]{2,1,0:T(8,128)S(1)}, u32[]{:S(2)}, u32[]{:S(2)}) collective-permute-start(f32[2,16,128]{2,1,0:T(8,128)S(1)} %pad_maximum_fusion.1), channel_id=1, source_target_pairs={{0,6},{2,0},{4,2},{6,4},{1,7},{3,1},{5,3},{7,5},{8,14},{10,8},{12,... | collective-permute-start | bytes 49160 | tf_op jit(solution)/shard_map/ppermute | solution.py:740
  72.9 1.9 %collective-permute-start.27 = (f32[2,16,128]{2,1,0:T(8,128)S(1)}, f32[2,16,128]{2,1,0:T(8,128)S(1)}, u32[]{:S(2)}, u32[]{:S(2)}) collective-permute-start(f32[2,16,128]{2,1,0:T(8,128)S(1)} %pad_maximum_fusion.1), channel_id=1, source_target_pairs={{0,2},{2,4},{4,6},{6,0},{1,3},{3,5},{5,7},{7,1},{8,10},{10,12},{12... | collective-permute-start | bytes 49160 | tf_op jit(solution)/shard_map/ppermute | solution.py:740
  75.6 1.2 %collective-permute-done.26 = f32[2,16,128]{2,1,0:T(8,128)S(1)} collective-permute-done((f32[2,16,128]{2,1,0:T(8,128)S(1)}, f32[2,16,128]{2,1,0:T(8,128)S(1)}, u32[]{:S(2)}, u32[]{:S(2)}) %collective-permute-start.26) | collective-permute-done | bytes 16416 | tf_op jit(solution)/shard_map/ppermute | solution.py:740
  76.8 1.6 %collective-permute-done.27 = f32[2,16,128]{2,1,0:T(8,128)S(1)} collective-permute-done((f32[2,16,128]{2,1,0:T(8,128)S(1)}, f32[2,16,128]{2,1,0:T(8,128)S(1)}, u32[]{:S(2)}, u32[]{:S(2)}) %collective-permute-start.27) | collective-permute-done | bytes 16416 | tf_op jit(solution)/shard_map/ppermute | solution.py:740
  78.5 2.0 %shard_map.92 = (f32[32,16,128]{2,1,0:T(8,128)}, f32[32,16,128]{2,1,0:T(8,128)}, f32[3]{0:T(128)}) custom-call(f32[2,16,128]{2,1,0:T(8,128)S(1)} %pad_maximum_fusion.2.sums, f32[32,16,128]{2,1,0:T(8,128)S(1)} %shard_map.91.eta, f32[16,16,128]{2,1,0:T(8,128)S(1)} %get-tuple-element.83.refs_1_.refs_2_.refs_0_, ...), custom_call_target="tpu_custom_call" | custom-call | flops 1000000 | bytes 1048576 | tf_op jit(solution)/shard_map/pallas_call | solution.py:27
  (68 shorter events, 12.8 us)
Async XLA Ops:
  0.6 1.8 %copy-start.2 = (s32[32,16,128]{2,1,0:T(8,128)S(1)}, s32[32,16,128]{2,1,0:T(8,128)}, u32[]{:S(2)}) copy-start(s32[32,16,128]{2,1,0:T(8,128)} %param.5) | copy-start | bytes 786436
  0.6 3.4 %copy-start.1 = (f32[8]{0:T(128)S(1)}, f32[8]{0:T(128)}, u32[]{:S(2)}) copy-start(f32[8]{0:T(128)} %table.3) | copy-start | bytes 100
  1.9 15.8 %copy-start = (s32[6]{0:T(128)S(1)}, s32[6]{0:T(128)}, u32[]{:S(2)}) copy-start(s32[6]{0:T(128)} %refs_4_.3) | copy-start | bytes 76
  1.9 2.1 %collective-permute-start = (f32[3,16,16,128]{3,2,1,0:T(8,128)S(1)}, f32[3,16,16,128]{3,2,1,0:T(8,128)S(1)}, u32[]{:S(2)}, u32[]{:S(2)}) collective-permute-start(f32[3,16,16,128]{3,2,1,0:T(8,128)S(1)} %get-tuple-element.133), channel_id=1, source_target_pairs={{0,1},{1,0},{2,3},{3,2},{4,5},{5,4},{6,7},{7,6},{8,9},{9,8},{10,11... | collective-permute-start | bytes 1179656 | tf_op jit(solution)/shard_map/ppermute | solution.py:113
  2.5 1.5 %collective-permute-start.1 = (s32[16,16,128]{2,1,0:T(8,128)S(1)}, s32[16,16,128]{2,1,0:T(8,128)S(1)}, u32[]{:S(2)}, u32[]{:S(2)}) collective-permute-start(s32[16,16,128]{2,1,0:T(8,128)S(1)} %get-tuple-element.135.refs_1_), channel_id=1, source_target_pairs={{0,1},{1,0},{2,3},{3,2},{4,5},{5,4},{6,7},{7,6},{8,9},{9,8},{10,11... | collective-permute-start | bytes 393224 | tf_op jit(solution)/shard_map/ppermute | solution.py:113
  4.9 10.0 %collective-permute-start.2 = (f32[68,4,256]{2,1,0:T(4,128)S(1)}, f32[68,4,256]{2,1,0:T(4,128)S(1)}, u32[]{:S(2)}, u32[]{:S(2)}) collective-permute-start(f32[68,4,256]{2,1,0:T(4,128)S(1)} %get-tuple-element.66), channel_id=1, source_target_pairs={{0,2},{2,0},{4,6},{6,4},{1,3},{3,1},{5,7},{7,5},{8,10},{10,8},{12,... | collective-permute-start | bytes 835592 | tf_op jit(solution)/shard_map/ppermute | solution.py:101
  7.9 7.0 %collective-permute-start.3 = (f32[68,4,256]{2,1,0:T(4,128)S(1)}, f32[68,4,256]{2,1,0:T(4,128)S(1)}, u32[]{:S(2)}, u32[]{:S(2)}) collective-permute-start(f32[68,4,256]{2,1,0:T(4,128)S(1)} %get-tuple-element.67), channel_id=1, source_target_pairs={{0,1},{1,0},{2,4},{3,5},{4,2},{5,3},{6,7},{7,6},{8,9},{9,8},{10,12... | collective-permute-start | bytes 835592 | tf_op jit(solution)/shard_map/ppermute | solution.py:101
  14.9 7.6 %collective-permute-start.5 = (f32[39,8,256]{2,1,0:T(8,128)S(1)}, f32[39,8,256]{2,1,0:T(8,128)S(1)}, u32[]{:S(2)}, u32[]{:S(2)}) collective-permute-start(f32[39,8,256]{2,1,0:T(8,128)S(1)} %get-tuple-element.78), channel_id=1, source_target_pairs={{0,1},{1,0},{8,9},{9,8},{16,17},{17,16},{24,25},{25,24},{2,3},{3,2... | collective-permute-start | bytes 958472 | tf_op jit(solution)/shard_map/ppermute | solution.py:108
  15.0 10.0 %collective-permute-start.4 = (f32[39,8,256]{2,1,0:T(8,128)S(1)}, f32[39,8,256]{2,1,0:T(8,128)S(1)}, u32[]{:S(2)}, u32[]{:S(2)}) collective-permute-start(f32[39,8,256]{2,1,0:T(8,128)S(1)} %get-tuple-element.68), channel_id=1, source_target_pairs={{0,25},{1,8},{8,1},{9,16},{16,9},{17,24},{24,17},{25,0},{2,27},{3,... | collective-permute-start | bytes 958472 | tf_op jit(solution)/shard_map/ppermute | solution.py:107
  26.9 5.3 %collective-permute-start.6 = (f32[16,4,256]{2,1,0:T(4,128)S(1)}, f32[16,4,256]{2,1,0:T(4,128)S(1)}, u32[]{:S(2)}, u32[]{:S(2)}) collective-permute-start(f32[16,4,256]{2,1,0:T(4,128)S(1)} %get-tuple-element.81.after), channel_id=1, source_target_pairs={{0,2},{2,0},{4,6},{6,4},{1,3},{3,1},{5,7},{7,5},{8,10},{10,8},{12,... | collective-permute-start | bytes 196616 | tf_op jit(solution)/shard_map/ppermute | solution.py:101
  30.0 2.2 %collective-permute-start.7 = (f32[16,4,256]{2,1,0:T(4,128)S(1)}, f32[16,4,256]{2,1,0:T(4,128)S(1)}, u32[]{:S(2)}, u32[]{:S(2)}) collective-permute-start(f32[16,4,256]{2,1,0:T(4,128)S(1)} %get-tuple-element.82), channel_id=1, source_target_pairs={{0,1},{1,0},{2,4},{3,5},{4,2},{5,3},{6,7},{7,6},{8,9},{9,8},{10,12... | collective-permute-start | bytes 196616 | tf_op jit(solution)/shard_map/ppermute | solution.py:101
  30.0 4.6 %collective-permute-start.9 = (f32[16,16,128]{2,1,0:T(8,128)S(1)}, f32[16,16,128]{2,1,0:T(8,128)S(1)}, u32[]{:S(2)}, u32[]{:S(2)}) collective-permute-start(f32[16,16,128]{2,1,0:T(8,128)S(1)} %get-tuple-element.84.refs_2_.refs_3_), channel_id=1, source_target_pairs={{0,1},{1,0},{2,3},{3,2},{4,5},{5,4},{6,7},{7,6},{8,9},{9,8},{10,11... | collective-permute-start | bytes 393224 | tf_op jit(solution)/shard_map/ppermute | solution.py:113
  32.3 5.0 %collective-permute-start.10 = (f32[10,8,256]{2,1,0:T(8,128)S(1)}, f32[10,8,256]{2,1,0:T(8,128)S(1)}, u32[]{:S(2)}, u32[]{:S(2)}) collective-permute-start(f32[10,8,256]{2,1,0:T(8,128)S(1)} %shard_map.76), channel_id=1, source_target_pairs={{0,1},{1,0},{8,9},{9,8},{16,17},{17,16},{24,25},{25,24},{2,3},{3,2... | collective-permute-start | bytes 245768 | tf_op jit(solution)/shard_map/ppermute | solution.py:108
  32.3 5.8 %collective-permute-start.8 = (f32[10,8,256]{2,1,0:T(8,128)S(1)}, f32[10,8,256]{2,1,0:T(8,128)S(1)}, u32[]{:S(2)}, u32[]{:S(2)}) collective-permute-start(f32[10,8,256]{2,1,0:T(8,128)S(1)} %shard_map.73.rest_0_), channel_id=1, source_target_pairs={{0,25},{1,8},{8,1},{9,16},{16,9},{17,24},{24,17},{25,0},{2,27},{3,... | collective-permute-start | bytes 245768 | tf_op jit(solution)/shard_map/ppermute | solution.py:107
  39.2 4.3 %collective-permute-start.11 = (f32[16,4,256]{2,1,0:T(4,128)S(1)}, f32[16,4,256]{2,1,0:T(4,128)S(1)}, u32[]{:S(2)}, u32[]{:S(2)}) collective-permute-start(f32[16,4,256]{2,1,0:T(4,128)S(1)} %get-tuple-element.104), channel_id=1, source_target_pairs={{0,2},{2,0},{4,6},{6,4},{1,3},{3,1},{5,7},{7,5},{8,10},{10,8},{12,... | collective-permute-start | bytes 196616 | tf_op jit(solution)/shard_map/ppermute | solution.py:101
  41.2 2.3 %collective-permute-start.12 = (f32[16,4,256]{2,1,0:T(4,128)S(1)}, f32[16,4,256]{2,1,0:T(4,128)S(1)}, u32[]{:S(2)}, u32[]{:S(2)}) collective-permute-start(f32[16,4,256]{2,1,0:T(4,128)S(1)} %get-tuple-element.105), channel_id=1, source_target_pairs={{0,1},{1,0},{2,4},{3,5},{4,2},{5,3},{6,7},{7,6},{8,9},{9,8},{10,12... | collective-permute-start | bytes 196616 | tf_op jit(solution)/shard_map/ppermute | solution.py:101
  41.2 4.1 %collective-permute-start.14 = (f32[16,16,128]{2,1,0:T(8,128)S(1)}, f32[16,16,128]{2,1,0:T(8,128)S(1)}, u32[]{:S(2)}, u32[]{:S(2)}) collective-permute-start(f32[16,16,128]{2,1,0:T(8,128)S(1)} %get-tuple-element.107.refs_5_), channel_id=1, source_target_pairs={{0,1},{1,0},{2,3},{3,2},{4,5},{5,4},{6,7},{7,6},{8,9},{9,8},{10,11... | collective-permute-start | bytes 393224 | tf_op jit(solution)/shard_map/ppermute | solution.py:113
  43.6 4.3 %collective-permute-start.15 = (f32[10,8,256]{2,1,0:T(8,128)S(1)}, f32[10,8,256]{2,1,0:T(8,128)S(1)}, u32[]{:S(2)}, u32[]{:S(2)}) collective-permute-start(f32[10,8,256]{2,1,0:T(8,128)S(1)} %shard_map.82), channel_id=1, source_target_pairs={{0,1},{1,0},{8,9},{9,8},{16,17},{17,16},{24,25},{25,24},{2,3},{3,2... | collective-permute-start | bytes 245768 | tf_op jit(solution)/shard_map/ppermute | solution.py:108
  43.7 5.6 %collective-permute-start.13 = (f32[10,8,256]{2,1,0:T(8,128)S(1)}, f32[10,8,256]{2,1,0:T(8,128)S(1)}, u32[]{:S(2)}, u32[]{:S(2)}) collective-permute-start(f32[10,8,256]{2,1,0:T(8,128)S(1)} %shard_map.80.rest_0_), channel_id=1, source_target_pairs={{0,25},{1,8},{8,1},{9,16},{16,9},{17,24},{24,17},{25,0},{2,27},{3,... | collective-permute-start | bytes 245768 | tf_op jit(solution)/shard_map/ppermute | solution.py:107
  50.1 4.3 %collective-permute-start.16 = (f32[16,4,256]{2,1,0:T(4,128)S(1)}, f32[16,4,256]{2,1,0:T(4,128)S(1)}, u32[]{:S(2)}, u32[]{:S(2)}) collective-permute-start(f32[16,4,256]{2,1,0:T(4,128)S(1)} %get-tuple-element.115), channel_id=1, source_target_pairs={{0,2},{2,0},{4,6},{6,4},{1,3},{3,1},{5,7},{7,5},{8,10},{10,8},{12,... | collective-permute-start | bytes 196616 | tf_op jit(solution)/shard_map/ppermute | solution.py:101
  52.1 2.3 %collective-permute-start.17 = (f32[16,4,256]{2,1,0:T(4,128)S(1)}, f32[16,4,256]{2,1,0:T(4,128)S(1)}, u32[]{:S(2)}, u32[]{:S(2)}) collective-permute-start(f32[16,4,256]{2,1,0:T(4,128)S(1)} %get-tuple-element.116), channel_id=1, source_target_pairs={{0,1},{1,0},{2,4},{3,5},{4,2},{5,3},{6,7},{7,6},{8,9},{9,8},{10,12... | collective-permute-start | bytes 196616 | tf_op jit(solution)/shard_map/ppermute | solution.py:101
  52.1 3.5 %collective-permute-start.19 = (f32[16,16,128]{2,1,0:T(8,128)S(1)}, f32[16,16,128]{2,1,0:T(8,128)S(1)}, u32[]{:S(2)}, u32[]{:S(2)}) collective-permute-start(f32[16,16,128]{2,1,0:T(8,128)S(1)} %get-tuple-element.118.refs_7_), channel_id=1, source_target_pairs={{0,1},{1,0},{2,3},{3,2},{4,5},{5,4},{6,7},{7,6},{8,9},{9,8},{10,11... | collective-permute-start | bytes 393224 | tf_op jit(solution)/shard_map/ppermute | solution.py:113
  54.5 4.0 %collective-permute-start.20 = (f32[10,8,256]{2,1,0:T(8,128)S(1)}, f32[10,8,256]{2,1,0:T(8,128)S(1)}, u32[]{:S(2)}, u32[]{:S(2)}) collective-permute-start(f32[10,8,256]{2,1,0:T(8,128)S(1)} %shard_map.88), channel_id=1, source_target_pairs={{0,1},{1,0},{8,9},{9,8},{16,17},{17,16},{24,25},{25,24},{2,3},{3,2... | collective-permute-start | bytes 245768 | tf_op jit(solution)/shard_map/ppermute | solution.py:108
  54.6 5.6 %collective-permute-start.18 = (f32[10,8,256]{2,1,0:T(8,128)S(1)}, f32[10,8,256]{2,1,0:T(8,128)S(1)}, u32[]{:S(2)}, u32[]{:S(2)}) collective-permute-start(f32[10,8,256]{2,1,0:T(8,128)S(1)} %shard_map.86.rest_0_), channel_id=1, source_target_pairs={{0,25},{1,8},{8,1},{9,16},{16,9},{17,24},{24,17},{25,0},{2,27},{3,... | collective-permute-start | bytes 245768 | tf_op jit(solution)/shard_map/ppermute | solution.py:107
  61.0 1.4 %collective-permute-start.21 = (f32[17,16,128]{2,1,0:T(8,128)S(1)}, f32[17,16,128]{2,1,0:T(8,128)S(1)}, u32[]{:S(2)}, u32[]{:S(2)}) collective-permute-start(f32[17,16,128]{2,1,0:T(8,128)S(1)} %get-tuple-element.125), channel_id=1, source_target_pairs={{0,1},{1,0},{2,3},{3,2},{4,5},{5,4},{6,7},{7,6},{8,9},{9,8},{10,11... | collective-permute-start | bytes 417800 | tf_op jit(solution)/shard_map/ppermute | solution.py:113
  62.4 3.8 %collective-permute-start.22 = (f32[2,16,128]{2,1,0:T(8,128)S(1)}, f32[2,16,128]{2,1,0:T(8,128)S(1)}, u32[]{:S(2)}, u32[]{:S(2)}) collective-permute-start(f32[2,16,128]{2,1,0:T(8,128)S(1)} %pad_maximum_fusion), channel_id=1, source_target_pairs={{0,24},{8,0},{16,8},{24,16},{1,25},{9,1},{17,9},{25,17},{2,26},{10... | collective-permute-start | bytes 49160 | tf_op jit(solution)/shard_map/ppermute | solution.py:740
  63.6 3.7 %collective-permute-start.23 = (f32[2,16,128]{2,1,0:T(8,128)S(1)}, f32[2,16,128]{2,1,0:T(8,128)S(1)}, u32[]{:S(2)}, u32[]{:S(2)}) collective-permute-start(f32[2,16,128]{2,1,0:T(8,128)S(1)} %pad_maximum_fusion), channel_id=1, source_target_pairs={{0,16},{8,24},{16,0},{24,8},{1,17},{9,25},{17,1},{25,9},{2,18},{10... | collective-permute-start | bytes 49160 | tf_op jit(solution)/shard_map/ppermute | solution.py:740
  64.6 4.6 %collective-permute-start.24 = (f32[2,16,128]{2,1,0:T(8,128)S(1)}, f32[2,16,128]{2,1,0:T(8,128)S(1)}, u32[]{:S(2)}, u32[]{:S(2)}) collective-permute-start(f32[2,16,128]{2,1,0:T(8,128)S(1)} %pad_maximum_fusion), channel_id=1, source_target_pairs={{0,8},{8,16},{16,24},{24,0},{1,9},{9,17},{17,25},{25,1},{2,10},{10... | collective-permute-start | bytes 49160 | tf_op jit(solution)/shard_map/ppermute | solution.py:740
  69.3 6.3 %collective-permute-start.25 = (f32[2,16,128]{2,1,0:T(8,128)S(1)}, f32[2,16,128]{2,1,0:T(8,128)S(1)}, u32[]{:S(2)}, u32[]{:S(2)}) collective-permute-start(f32[2,16,128]{2,1,0:T(8,128)S(1)} %pad_maximum_fusion.1), channel_id=1, source_target_pairs={{0,6},{2,0},{4,2},{6,4},{1,7},{3,1},{5,3},{7,5},{8,14},{10,8},{12,... | collective-permute-start | bytes 49160 | tf_op jit(solution)/shard_map/ppermute | solution.py:740
  72.2 4.6 %collective-permute-start.26 = (f32[2,16,128]{2,1,0:T(8,128)S(1)}, f32[2,16,128]{2,1,0:T(8,128)S(1)}, u32[]{:S(2)}, u32[]{:S(2)}) collective-permute-start(f32[2,16,128]{2,1,0:T(8,128)S(1)} %pad_maximum_fusion.1), channel_id=1, source_target_pairs={{0,4},{2,6},{4,0},{6,2},{1,5},{3,7},{5,1},{7,3},{8,12},{10,14},{12... | collective-permute-start | bytes 49160 | tf_op jit(solution)/shard_map/ppermute | solution.py:740
  72.9 5.5 %collective-permute-start.27 = (f32[2,16,128]{2,1,0:T(8,128)S(1)}, f32[2,16,128]{2,1,0:T(8,128)S(1)}, u32[]{:S(2)}, u32[]{:S(2)}) collective-permute-start(f32[2,16,128]{2,1,0:T(8,128)S(1)} %pad_maximum_fusion.1), channel_id=1, source_target_pairs={{0,2},{2,4},{4,6},{6,0},{1,3},{3,5},{5,7},{7,1},{8,10},{10,12},{12... | collective-permute-start | bytes 49160 | tf_op jit(solution)/shard_map/ppermute | solution.py:740

commit v11 on v10

--- a/solution.py
+++ b/solution.py
@@ -116,7 +116,7 @@
 def lookup(ids, table):
     eta = jnp.zeros(ids.shape, F32)
     for level in range(table.shape[0]):
-        eta = jnp.where(ids == level, table[level], eta)
+        eta = jnp.where(ids == level, table[level : level + 1, : ids.shape[1]], eta)
     return eta
 
 
@@ -284,7 +284,7 @@
 def emit_early(emit, near_side, full, inner, out_inner, out_near):
     for r in outside(full[SWEEPS], inner[SWEEPS], near_side):
         emit(r - HALO, out_near[r - HALO])
-    rows_loop(inner[SWEEPS][0] - HALO, inner[SWEEPS][1] - HALO, lambda r: emit(r, out_inner[r]), 4)
+    rows_loop(inner[SWEEPS][0] - HALO, inner[SWEEPS][1] - HALO, lambda r: emit(r, out_inner[r]), 16)
 
 
 def inner_solve(b, levels, out, inner, w, kx, ky, kz, step):
@@ -381,7 +381,7 @@
     in_y = (at_y >= 0) & (at_y < sizes[1])
     y_up, y_low = at_y + 1 < sizes[1], at_y >= 1
     z_up, z_low = at_z + 1 < sizes[2], at_z >= 1
-    wall = [jnp.where(flags[k] == 0, 1.0, 0.0).astype(F32) for k in range(6)]
+    wall = [flags[k : k + 1, :] for k in range(6)]
 
     def coefs(r, mid, before, after, line, force_at, kx, ky, kz, w, b):
         at_x = place * rows - h + r
@@ -722,7 +722,7 @@
             pressure[base + r] = eta[base + r] * (p0 * x0 + p1 * x1 + p2 * x2)
             residual[base + r] = (x0 + r1 * x1) + (r2 * x2 + r3 * x3)
 
-        rows_loop(0, rows, one_row, 4)
+        rows_loop(0, rows, one_row, 16)
 
 
 def add_pairs(a, b):
@@ -756,6 +756,8 @@
     cells = float(sizes[0] * sizes[1] * sizes[2])
     chain = nx * nz
 
+    table = jnp.broadcast_to(table[:, None], (table.shape[0], zs))
+    flags = jnp.broadcast_to(jnp.where(flags == 0, 1.0, 0.0).astype(F32)[:, None], (6, zs))
     core = lax.axis_index("gz")
     starts = [lax.rem(core + j, nz) * rows for j in range(nz)]
     forces = [lax.dynamic_slice_in_dim(force, start, rows, 1) for start in starts]
@@ -770,7 +772,6 @@
             sds(4 * rows + rows // 4, h, zs),
         ],
         (table, *forces, *phases),
-        [SMEM] + [VMEM] * (2 * nz),
     )
     ya, yb = exchange_y(ya, yb, ny, nz)
     edge = sds(len(edge_list()), 8, zs)
@@ -787,7 +788,7 @@
         functools.partial(first_inner, sizes),
         [scalar] * 3 + [vector] * (1 + SWEEPS) + [sds(rows, slots, zs)],
         (full, ya, yb, flags),
-        [VMEM] * 3 + [SMEM],
+        None,
         [field, pltpu.VMEM((total, slots, zs), F32), line],
         heavy,
     )
@@ -797,7 +798,7 @@
         functools.partial(first_side, nz, sizes, True),
         [scalar] * 3 + [vector, result],
         (full, ya, yb, xa, flags, *early),
-        [VMEM] * 4 + [SMEM] + [VMEM] * len(early),
+        None,
         scratch,
         heavy // 2,
     )
@@ -805,7 +806,7 @@
         functools.partial(first_side, nz, sizes, False),
         v_shape + sent + [scalar] * 3 + [vector],
         (full, ya, yb, xb, flags, *early, near[-1]),
-        [VMEM] * 4 + [SMEM] + [VMEM] * (len(early) + 1),
+        None,
         scratch,
         heavy // 2,
     )
@@ -815,12 +816,7 @@
         (*early[:4], *near[:4], *outs[nz + 3 :]),
     )
     vs, ps, moments = [list(outs[:nz])], [outs[nz]], []
-    eta = call(
-        functools.partial(eta_kernel, nz),
-        sds(*phase.shape),
-        (table, outs[nz + 1], *slices),
-        [SMEM] + [VMEM] * (nz + 1),
-    )
+    eta = call(functools.partial(eta_kernel, nz), sds(*phase.shape), (table, outs[nz + 1], *slices))
     ya, yb = outs[nz + 1 : nz + 3]
     placed = []
     for step in range(1, ITERS + 1):

time: 80.8 us -> 79.4 us (0.983)
  Pallas kernels: 26.4 us -> 22.8 us
  waiting for transfers between devices: 23.2 us -> 24.4 us
  starting transfers between devices: 28.6 us -> 29.5 us
    pallas_call x26, Pallas kernels: 26.4 us -> 22.8 us  [call(): pl.pallas_call(kernel, out_shape=outs, in_specs=specs or [VMEM] * len(ins...]
  transfers between devices with their start and end apart: 28 -> 28, of which waited for: 14 -> 13; matrix products, arithmetic and copies ran while one was open for 0% -> 0% of each run, Pallas kernels for 23% -> 21%
where the time goes in v11:
time: 79.4 us; the launch traced here: 79.3 us
  starting transfers between devices  29.5 us (37%)
  waiting for transfers between devices  24.4 us (31%)
  Pallas kernels  22.8 us (29%)
  local copies, waits for them, and re-layouts  1.41 us (2%)
  between operations  1.16 us (1%)
    pallas_call x26, Pallas kernels, call(): pl.pallas_call(kernel, out_shape=outs, in_specs=specs or [VMEM] * len(ins...  22.8 us
    ppermute x8, waiting for transfers between devices, exchange_y(): return (lax.ppermute(a, 'gy', even), lax.ppermute(b, ('gy', 'gz'), odd))  12 us
    ppermute x8, starting transfers between devices, exchange_y(): return (lax.ppermute(a, 'gy', even), lax.ppermute(b, ('gy', 'gz'), odd))  10.1 us
    ppermute x6, starting transfers between devices, sum_along(): terms.append(lax.ppermute(pair, axis, moves))  8.97 us
    ppermute x4, starting transfers between devices, exchange_x(): b = lax.ppermute(b, ('gx', 'gz'), odd)  7.88 us
    ppermute x6, waiting for transfers between devices, sum_along(): terms.append(lax.ppermute(pair, axis, moves))  7.3 us
    ppermute x6, waiting for transfers between devices, core_shift(): return lax.ppermute(value, 'gz', [(i, (i + j) % n) for i in range(n)])  2.77 us
    ppermute x4, waiting for transfers between devices, exchange_x(): b = lax.ppermute(b, ('gx', 'gz'), odd)  2.27 us
  transfers between devices with their start and end apart: 28, of which 13 were waited for; matrix products, arithmetic and copies ran while one was open for 0% of the time, Pallas kernels for 21%

profile of v11, /device:TPU:0, one launch (start us, length us, event | category | flops | bytes accessed | tf_op | source)
XLA Modules:
  0.0 79.3 jit_solution(3553593016103218372)
XLA Ops:
  0.7 1.2 %constant_dynamic-slice_fusion.2 = (f32[3,16,16,128]{3,2,1,0:T(8,128)S(1)}, f32[3,16,16,128]{3,2,1,0:T(8,128)S(1)}) fusion(f32[3,32,16,128]{3,2,1,0:T(8,128)} %param.4, s32[]{:T(128)S(6)} %select_n.165, s32[]{:T(128)S(6)} %select_n.164), kind=kLoop, calls=%fused_computation.34 | loop fusion | bytes 1572872 | tf_op jit(solution)/shard_map/dynamic_slice | solution.py:763
  2.6 1.4 %collective-permute-done.1.refs_3_ = s32[16,16,128]{2,1,0:T(8,128)S(1)} collective-permute-done((s32[16,16,128]{2,1,0:T(8,128)S(1)}, s32[16,16,128]{2,1,0:T(8,128)S(1)}, u32[]{:S(2)}, u32[]{:S(2)}) %collective-permute-start.1) | collective-permute-done | bytes 131104 | tf_op jit(solution)/shard_map/ppermute | solution.py:113
  4.4 3.0 %collective-permute-start.2 = (f32[68,4,256]{2,1,0:T(4,128)S(1)}, f32[68,4,256]{2,1,0:T(4,128)S(1)}, u32[]{:S(2)}, u32[]{:S(2)}) collective-permute-start(f32[68,4,256]{2,1,0:T(4,128)S(1)} %get-tuple-element.66), channel_id=1, source_target_pairs={{0,2},{2,0},{4,6},{6,4},{1,3},{3,1},{5,7},{7,5},{8,10},{10,8},{12,... | collective-permute-start | bytes 835592 | tf_op jit(solution)/shard_map/ppermute | solution.py:101
  7.4 7.0 %collective-permute-done.2.ya.refs_1_ = f32[68,4,256]{2,1,0:T(4,128)S(1)} collective-permute-done((f32[68,4,256]{2,1,0:T(4,128)S(1)}, f32[68,4,256]{2,1,0:T(4,128)S(1)}, u32[]{:S(2)}, u32[]{:S(2)}) %collective-permute-start.2) | collective-permute-done | bytes 278560 | tf_op jit(solution)/shard_map/ppermute | solution.py:101
  14.5 2.7 %collective-permute-start.4 = (f32[39,8,256]{2,1,0:T(8,128)S(1)}, f32[39,8,256]{2,1,0:T(8,128)S(1)}, u32[]{:S(2)}, u32[]{:S(2)}) collective-permute-start(f32[39,8,256]{2,1,0:T(8,128)S(1)} %get-tuple-element.68), channel_id=1, source_target_pairs={{0,25},{1,8},{8,1},{9,16},{16,9},{17,24},{24,17},{25,0},{2,27},{3,... | collective-permute-start | bytes 958472 | tf_op jit(solution)/shard_map/ppermute | solution.py:107
  17.3 4.2 %shard_map.69 = (f32[24,24,256]{2,1,0:T(8,128)S(1)}, f32[24,24,256]{2,1,0:T(8,128)S(1)}, f32[24,24,256]{2,1,0:T(8,128)S(1)}, f32[3,24,24,256]{3,2,1,0:T(8,128)S(...) custom-call(f32[4,16,16,256]{3,2,1,0:T(8,128)S(1)} %get-tuple-elemen, ...), custom_call_target="tpu_custom_call" | custom-call | flops 40000000 | bytes 1048576 | tf_op jit(solution)/shard_map/pallas_call | solution.py:27
  21.5 1.1 %shard_map.70 = (f32[24,24,256]{2,1,0:T(8,128)S(1)}, f32[24,24,256]{2,1,0:T(8,128)S(1)}, f32[24,24,256]{2,1,0:T(8,128)S(1)}, f32[3,24,24,256]{3,2,1,0:T(8,128)S(1)}, f32[16,24,256]{2,1,0:T(8,128)S(1)}) custom-call(f32[4,16,16,256]{3,2,1,0:T(8,128)S(1)} %get-tuple-element.65.full.refs_0_.refs_3_, f32[68,4,256]{2,1,0:T(4,128)S(1)} %collective-permute-done.2.ya.refs_1_, ...), custom_call_target="tpu_custom_call" | custom-call | flops 20000000 | bytes 1048576 | tf_op jit(solution)/shard_map/pallas_call | solution.py:27
  22.6 1.9 %collective-permute-done.4.refs_3_ = f32[39,8,256]{2,1,0:T(8,128)S(1)} collective-permute-done((f32[39,8,256]{2,1,0:T(8,128)S(1)}, f32[39,8,256]{2,1,0:T(8,128)S(1)}, u32[]{:S(2)}, u32[]{:S(2)}) %collective-permute-start.4) | collective-permute-done | bytes 319520 | tf_op jit(solution)/shard_map/ppermute | solution.py:107
  24.5 1.3 %shard_map.71 = (f32[16,16,128]{2,1,0:T(8,128)S(1)}, f32[16,16,128]{2,1,0:T(8,128)S(1)}, f32[16,16,256]{2,1,0:T(8,128)S(1)}, f32[16,4,256]{2,1,0:T(4,128)S(1)}, ...) custom-call(f32[4,16,16,256]{3,2,1,0:T(8,128)S(1)} %get-tuple-elemen, ...), custom_call_target="tpu_custom_call" | custom-call | flops 20000000 | bytes 1048576 | tf_op jit(solution)/shard_map/pallas_call | solution.py:27
  25.8 3.1 %collective-permute-start.6 = (f32[16,4,256]{2,1,0:T(4,128)S(1)}, f32[16,4,256]{2,1,0:T(4,128)S(1)}, u32[]{:S(2)}, u32[]{:S(2)}) collective-permute-start(f32[16,4,256]{2,1,0:T(4,128)S(1)} %get-tuple-element.81.after), channel_id=1, source_target_pairs={{0,2},{2,0},{4,6},{6,4},{1,3},{3,1},{5,7},{7,5},{8,10},{10,8},{12,... | collective-permute-start | bytes 196616 | tf_op jit(solution)/shard_map/ppermute | solution.py:101
  29.5 1.6 %collective-permute-done.6.ya = f32[16,4,256]{2,1,0:T(4,128)S(1)} collective-permute-done((f32[16,4,256]{2,1,0:T(4,128)S(1)}, f32[16,4,256]{2,1,0:T(4,128)S(1)}, u32[]{:S(2)}, u32[]{:S(2)}) %collective-permute-start.6) | collective-permute-done | bytes 65568 | tf_op jit(solution)/shard_map/ppermute | solution.py:101
  31.3 1.9 %collective-permute-start.8 = (f32[10,8,256]{2,1,0:T(8,128)S(1)}, f32[10,8,256]{2,1,0:T(8,128)S(1)}, u32[]{:S(2)}, u32[]{:S(2)}) collective-permute-start(f32[10,8,256]{2,1,0:T(8,128)S(1)} %shard_map.73.rest_0_), channel_id=1, source_target_pairs={{0,25},{1,8},{8,1},{9,16},{16,9},{17,24},{24,17},{25,0},{2,27},{3,... | collective-permute-start | bytes 245768 | tf_op jit(solution)/shard_map/ppermute | solution.py:107
  33.5 2.5 %shard_map.75 = (f32[24,24,256]{2,1,0:T(8,128)S(1)}, f32[3,24,24,256]{3,2,1,0:T(8,128)S(1)}, f32[3,24,24,256]{3,2,1,0:T(8,128)S(1)}, f32[3,24,24,256]{3,2,1,0:T(...) custom-call(f32[16,16,256]{2,1,0:T(8,128)S(1)} %get-tuple-element.80.refs_0_.p.p_in.refs_1_, ...), custom_call_target="tpu_custom_call" | custom-call | flops 40000000 | bytes 1048576 | tf_op jit(solution)/shard_map/pallas_call | solution.py:27
  37.8 2.0 %collective-permute-start.11 = (f32[16,4,256]{2,1,0:T(4,128)S(1)}, f32[16,4,256]{2,1,0:T(4,128)S(1)}, u32[]{:S(2)}, u32[]{:S(2)}) collective-permute-start(f32[16,4,256]{2,1,0:T(4,128)S(1)} %get-tuple-element.104), channel_id=1, source_target_pairs={{0,2},{2,0},{4,6},{6,4},{1,3},{3,1},{5,7},{7,5},{8,10},{10,8},{12,... | collective-permute-start | bytes 196616 | tf_op jit(solution)/shard_map/ppermute | solution.py:101
  40.4 1.7 %collective-permute-done.11.ya = f32[16,4,256]{2,1,0:T(4,128)S(1)} collective-permute-done((f32[16,4,256]{2,1,0:T(4,128)S(1)}, f32[16,4,256]{2,1,0:T(4,128)S(1)}, u32[]{:S(2)}, u32[]{:S(2)}) %collective-permute-start.11) | collective-permute-done | bytes 65568 | tf_op jit(solution)/shard_map/ppermute | solution.py:101
  42.2 1.7 %collective-permute-start.13 = (f32[10,8,256]{2,1,0:T(8,128)S(1)}, f32[10,8,256]{2,1,0:T(8,128)S(1)}, u32[]{:S(2)}, u32[]{:S(2)}) collective-permute-start(f32[10,8,256]{2,1,0:T(8,128)S(1)} %shard_map.80.rest_0_), channel_id=1, source_target_pairs={{0,25},{1,8},{8,1},{9,16},{16,9},{17,24},{24,17},{25,0},{2,27},{3,... | collective-permute-start | bytes 245768 | tf_op jit(solution)/shard_map/ppermute | solution.py:107
  43.9 2.5 %shard_map.81 = (f32[24,24,256]{2,1,0:T(8,128)S(1)}, f32[3,24,24,256]{3,2,1,0:T(8,128)S(1)}, f32[3,24,24,256]{3,2,1,0:T(8,128)S(1)}, f32[3,24,24,256]{3,2,1,0:T(...) custom-call(f32[16,16,256]{2,1,0:T(8,128)S(1)} %get-tuple-element.103.refs_0_.p.p_in.refs_1_, ...), custom_call_target="tpu_custom_call" | custom-call | flops 40000000 | bytes 1048576 | tf_op jit(solution)/shard_map/pallas_call | solution.py:27
  48.3 2.0 %collective-permute-start.16 = (f32[16,4,256]{2,1,0:T(4,128)S(1)}, f32[16,4,256]{2,1,0:T(4,128)S(1)}, u32[]{:S(2)}, u32[]{:S(2)}) collective-permute-start(f32[16,4,256]{2,1,0:T(4,128)S(1)} %get-tuple-element.115), channel_id=1, source_target_pairs={{0,2},{2,0},{4,6},{6,4},{1,3},{3,1},{5,7},{7,5},{8,10},{10,8},{12,... | collective-permute-start | bytes 196616 | tf_op jit(solution)/shard_map/ppermute | solution.py:101
  51.0 1.7 %collective-permute-done.16.ya = f32[16,4,256]{2,1,0:T(4,128)S(1)} collective-permute-done((f32[16,4,256]{2,1,0:T(4,128)S(1)}, f32[16,4,256]{2,1,0:T(4,128)S(1)}, u32[]{:S(2)}, u32[]{:S(2)}) %collective-permute-start.16) | collective-permute-done | bytes 65568 | tf_op jit(solution)/shard_map/ppermute | solution.py:101
  52.9 1.6 %collective-permute-start.18 = (f32[10,8,256]{2,1,0:T(8,128)S(1)}, f32[10,8,256]{2,1,0:T(8,128)S(1)}, u32[]{:S(2)}, u32[]{:S(2)}) collective-permute-start(f32[10,8,256]{2,1,0:T(8,128)S(1)} %shard_map.86.rest_0_), channel_id=1, source_target_pairs={{0,25},{1,8},{8,1},{9,16},{16,9},{17,24},{24,17},{25,0},{2,27},{3,... | collective-permute-start | bytes 245768 | tf_op jit(solution)/shard_map/ppermute | solution.py:107
  54.5 2.8 %shard_map.87 = (f32[24,24,256]{2,1,0:T(8,128)S(1)}, f32[3,24,24,256]{3,2,1,0:T(8,128)S(1)}, f32[3,24,24,256]{3,2,1,0:T(8,128)S(1)}, f32[3,24,24,256]{3,2,1,0:T(...) custom-call(f32[16,16,256]{2,1,0:T(8,128)S(1)} %get-tuple-element.114.refs_0_.p.p_in, ...), custom_call_target="tpu_custom_call" | custom-call | flops 40000000 | bytes 1048576 | tf_op jit(solution)/shard_map/pallas_call | solution.py:27
  57.3 1.1 %shard_map.89.refs_5_ = f32[16,24,256]{2,1,0:T(8,128)S(1)} custom-call(f32[16,16,256]{2,1,0:T(8,128)S(1)} %get-tuple-element.114.refs_0_.p.p_in, f32[10,8,256]{2,1,0:T(8,128)S(1)} %collective-permute-done.20.xs, f32[24,24,256]{2,1,0:T(8,128)S(1)} %get-tuple-element.93.kx, f32[24,24,256]{2,1,0:T(8,128)S(1)} %get-tuple-element.94.ky, ...), custom_call_target="tpu_custom_call" | custom-call | flops 10000000 | bytes 1048576 | tf_op jit(solution)/shard_map/pallas_call | solution.py:27
  59.3 1.3 %collective-permute-done.21.refs_7_ = f32[17,16,128]{2,1,0:T(8,128)S(1)} collective-permute-done((f32[17,16,128]{2,1,0:T(8,128)S(1)}, f32[17,16,128]{2,1,0:T(8,128)S(1)}, u32[]{:S(2)}, u32[]{:S(2)}) %collective-permute-start.21) | collective-permute-done | bytes 139296 | tf_op jit(solution)/shard_map/ppermute | solution.py:113
  60.7 1.5 %collective-permute-start.22 = (f32[2,16,128]{2,1,0:T(8,128)S(1)}, f32[2,16,128]{2,1,0:T(8,128)S(1)}, u32[]{:S(2)}, u32[]{:S(2)}) collective-permute-start(f32[2,16,128]{2,1,0:T(8,128)S(1)} %pad_maximum_fusion), channel_id=1, source_target_pairs={{0,24},{8,0},{16,8},{24,16},{1,25},{9,1},{17,9},{25,17},{2,26},{10... | collective-permute-start | bytes 49160 | tf_op jit(solution)/shard_map/ppermute | solution.py:740
  62.2 1.2 %collective-permute-start.23 = (f32[2,16,128]{2,1,0:T(8,128)S(1)}, f32[2,16,128]{2,1,0:T(8,128)S(1)}, u32[]{:S(2)}, u32[]{:S(2)}) collective-permute-start(f32[2,16,128]{2,1,0:T(8,128)S(1)} %pad_maximum_fusion), channel_id=1, source_target_pairs={{0,16},{8,24},{16,0},{24,8},{1,17},{9,25},{17,1},{25,9},{2,18},{10... | collective-permute-start | bytes 49160 | tf_op jit(solution)/shard_map/ppermute | solution.py:740
  64.5 1.5 %collective-permute-done.23 = f32[2,16,128]{2,1,0:T(8,128)S(1)} collective-permute-done((f32[2,16,128]{2,1,0:T(8,128)S(1)}, f32[2,16,128]{2,1,0:T(8,128)S(1)}, u32[]{:S(2)}, u32[]{:S(2)}) %collective-permute-start.23) | collective-permute-done | bytes 16416 | tf_op jit(solution)/shard_map/ppermute | solution.py:740
  65.9 2.1 %collective-permute-done.24 = f32[2,16,128]{2,1,0:T(8,128)S(1)} collective-permute-done((f32[2,16,128]{2,1,0:T(8,128)S(1)}, f32[2,16,128]{2,1,0:T(8,128)S(1)}, u32[]{:S(2)}, u32[]{:S(2)}) %collective-permute-start.24) | collective-permute-done | bytes 16416 | tf_op jit(solution)/shard_map/ppermute | solution.py:740
  68.0 2.9 %collective-permute-start.25 = (f32[2,16,128]{2,1,0:T(8,128)S(1)}, f32[2,16,128]{2,1,0:T(8,128)S(1)}, u32[]{:S(2)}, u32[]{:S(2)}) collective-permute-start(f32[2,16,128]{2,1,0:T(8,128)S(1)} %pad_maximum_fusion.1), channel_id=1, source_target_pairs={{0,6},{2,0},{4,2},{6,4},{1,7},{3,1},{5,3},{7,5},{8,14},{10,8},{12,... | collective-permute-start | bytes 49160 | tf_op jit(solution)/shard_map/ppermute | solution.py:740
  71.7 1.9 %collective-permute-start.27 = (f32[2,16,128]{2,1,0:T(8,128)S(1)}, f32[2,16,128]{2,1,0:T(8,128)S(1)}, u32[]{:S(2)}, u32[]{:S(2)}) collective-permute-start(f32[2,16,128]{2,1,0:T(8,128)S(1)} %pad_maximum_fusion.1), channel_id=1, source_target_pairs={{0,2},{2,4},{4,6},{6,0},{1,3},{3,5},{5,7},{7,1},{8,10},{10,12},{12... | collective-permute-start | bytes 49160 | tf_op jit(solution)/shard_map/ppermute | solution.py:740
  73.8 1.8 %collective-permute-done.26 = f32[2,16,128]{2,1,0:T(8,128)S(1)} collective-permute-done((f32[2,16,128]{2,1,0:T(8,128)S(1)}, f32[2,16,128]{2,1,0:T(8,128)S(1)}, u32[]{:S(2)}, u32[]{:S(2)}) %collective-permute-start.26) | collective-permute-done | bytes 16416 | tf_op jit(solution)/shard_map/ppermute | solution.py:740
  75.6 1.6 %collective-permute-done.27 = f32[2,16,128]{2,1,0:T(8,128)S(1)} collective-permute-done((f32[2,16,128]{2,1,0:T(8,128)S(1)}, f32[2,16,128]{2,1,0:T(8,128)S(1)}, u32[]{:S(2)}, u32[]{:S(2)}) %collective-permute-start.27) | collective-permute-done | bytes 16416 | tf_op jit(solution)/shard_map/ppermute | solution.py:740
  77.2 1.9 %shard_map.92 = (f32[32,16,128]{2,1,0:T(8,128)}, f32[32,16,128]{2,1,0:T(8,128)}, f32[3]{0:T(128)}) custom-call(f32[2,16,128]{2,1,0:T(8,128)S(1)} %pad_maximum_fusion.2.sums, f32[32,16,128]{2,1,0:T(8,128)S(1)} %shard_map.91.eta, f32[16,16,128]{2,1,0:T(8,128)S(1)} %get-tuple-element.83.refs_1_.refs_2_.refs_0_, ...), custom_call_target="tpu_custom_call" | custom-call | flops 1000000 | bytes 1048576 | tf_op jit(solution)/shard_map/pallas_call | solution.py:27
  (71 shorter events, 10.6 us)
Async XLA Ops:
  0.6 1.8 %copy-start = (s32[32,16,128]{2,1,0:T(8,128)S(1)}, s32[32,16,128]{2,1,0:T(8,128)}, u32[]{:S(2)}) copy-start(s32[32,16,128]{2,1,0:T(8,128)} %param.5) | copy-start | bytes 786436
  0.6 3.4 %copy-start.1 = (f32[8]{0:T(128)S(1)}, f32[8]{0:T(128)}, u32[]{:S(2)}) copy-start(f32[8]{0:T(128)} %param.6) | copy-start | bytes 100
  1.9 15.3 %copy-start.2 = (s32[6]{0:T(128)S(1)}, s32[6]{0:T(128)}, u32[]{:S(2)}) copy-start(s32[6]{0:T(128)} %param.7) | copy-start | bytes 76
  1.9 2.1 %collective-permute-start = (f32[3,16,16,128]{3,2,1,0:T(8,128)S(1)}, f32[3,16,16,128]{3,2,1,0:T(8,128)S(1)}, u32[]{:S(2)}, u32[]{:S(2)}) collective-permute-start(f32[3,16,16,128]{3,2,1,0:T(8,128)S(1)} %get-tuple-element.133), channel_id=1, source_target_pairs={{0,1},{1,0},{2,3},{3,2},{4,5},{5,4},{6,7},{7,6},{8,9},{9,8},{10,11... | collective-permute-start | bytes 1179656 | tf_op jit(solution)/shard_map/ppermute | solution.py:113
  2.5 1.5 %collective-permute-start.1 = (s32[16,16,128]{2,1,0:T(8,128)S(1)}, s32[16,16,128]{2,1,0:T(8,128)S(1)}, u32[]{:S(2)}, u32[]{:S(2)}) collective-permute-start(s32[16,16,128]{2,1,0:T(8,128)S(1)} %get-tuple-element.135.refs_1_), channel_id=1, source_target_pairs={{0,1},{1,0},{2,3},{3,2},{4,5},{5,4},{6,7},{7,6},{8,9},{9,8},{10,11... | collective-permute-start | bytes 393224 | tf_op jit(solution)/shard_map/ppermute | solution.py:113
  4.4 10.0 %collective-permute-start.2 = (f32[68,4,256]{2,1,0:T(4,128)S(1)}, f32[68,4,256]{2,1,0:T(4,128)S(1)}, u32[]{:S(2)}, u32[]{:S(2)}) collective-permute-start(f32[68,4,256]{2,1,0:T(4,128)S(1)} %get-tuple-element.66), channel_id=1, source_target_pairs={{0,2},{2,0},{4,6},{6,4},{1,3},{3,1},{5,7},{7,5},{8,10},{10,8},{12,... | collective-permute-start | bytes 835592 | tf_op jit(solution)/shard_map/ppermute | solution.py:101
  7.4 7.0 %collective-permute-start.3 = (f32[68,4,256]{2,1,0:T(4,128)S(1)}, f32[68,4,256]{2,1,0:T(4,128)S(1)}, u32[]{:S(2)}, u32[]{:S(2)}) collective-permute-start(f32[68,4,256]{2,1,0:T(4,128)S(1)} %get-tuple-element.67), channel_id=1, source_target_pairs={{0,1},{1,0},{2,4},{3,5},{4,2},{5,3},{6,7},{7,6},{8,9},{9,8},{10,12... | collective-permute-start | bytes 835592 | tf_op jit(solution)/shard_map/ppermute | solution.py:101
  14.4 7.0 %collective-permute-start.5 = (f32[39,8,256]{2,1,0:T(8,128)S(1)}, f32[39,8,256]{2,1,0:T(8,128)S(1)}, u32[]{:S(2)}, u32[]{:S(2)}) collective-permute-start(f32[39,8,256]{2,1,0:T(8,128)S(1)} %get-tuple-element.78), channel_id=1, source_target_pairs={{0,1},{1,0},{8,9},{9,8},{16,17},{17,16},{24,25},{25,24},{2,3},{3,2... | collective-permute-start | bytes 958472 | tf_op jit(solution)/shard_map/ppermute | solution.py:108
  14.5 10.0 %collective-permute-start.4 = (f32[39,8,256]{2,1,0:T(8,128)S(1)}, f32[39,8,256]{2,1,0:T(8,128)S(1)}, u32[]{:S(2)}, u32[]{:S(2)}) collective-permute-start(f32[39,8,256]{2,1,0:T(8,128)S(1)} %get-tuple-element.68), channel_id=1, source_target_pairs={{0,25},{1,8},{8,1},{9,16},{16,9},{17,24},{24,17},{25,0},{2,27},{3,... | collective-permute-start | bytes 958472 | tf_op jit(solution)/shard_map/ppermute | solution.py:107
  25.8 5.3 %collective-permute-start.6 = (f32[16,4,256]{2,1,0:T(4,128)S(1)}, f32[16,4,256]{2,1,0:T(4,128)S(1)}, u32[]{:S(2)}, u32[]{:S(2)}) collective-permute-start(f32[16,4,256]{2,1,0:T(4,128)S(1)} %get-tuple-element.81.after), channel_id=1, source_target_pairs={{0,2},{2,0},{4,6},{6,4},{1,3},{3,1},{5,7},{7,5},{8,10},{10,8},{12,... | collective-permute-start | bytes 196616 | tf_op jit(solution)/shard_map/ppermute | solution.py:101
  28.9 2.2 %collective-permute-start.7 = (f32[16,4,256]{2,1,0:T(4,128)S(1)}, f32[16,4,256]{2,1,0:T(4,128)S(1)}, u32[]{:S(2)}, u32[]{:S(2)}) collective-permute-start(f32[16,4,256]{2,1,0:T(4,128)S(1)} %get-tuple-element.82), channel_id=1, source_target_pairs={{0,1},{1,0},{2,4},{3,5},{4,2},{5,3},{6,7},{7,6},{8,9},{9,8},{10,12... | collective-permute-start | bytes 196616 | tf_op jit(solution)/shard_map/ppermute | solution.py:101
  28.9 4.6 %collective-permute-start.9 = (f32[16,16,128]{2,1,0:T(8,128)S(1)}, f32[16,16,128]{2,1,0:T(8,128)S(1)}, u32[]{:S(2)}, u32[]{:S(2)}) collective-permute-start(f32[16,16,128]{2,1,0:T(8,128)S(1)} %get-tuple-element.84.refs_2_.refs_3_), channel_id=1, source_target_pairs={{0,1},{1,0},{2,3},{3,2},{4,5},{5,4},{6,7},{7,6},{8,9},{9,8},{10,11... | collective-permute-start | bytes 393224 | tf_op jit(solution)/shard_map/ppermute | solution.py:113
  31.2 4.8 %collective-permute-start.10 = (f32[10,8,256]{2,1,0:T(8,128)S(1)}, f32[10,8,256]{2,1,0:T(8,128)S(1)}, u32[]{:S(2)}, u32[]{:S(2)}) collective-permute-start(f32[10,8,256]{2,1,0:T(8,128)S(1)} %shard_map.76), channel_id=1, source_target_pairs={{0,1},{1,0},{8,9},{9,8},{16,17},{17,16},{24,25},{25,24},{2,3},{3,2... | collective-permute-start | bytes 245768 | tf_op jit(solution)/shard_map/ppermute | solution.py:108
  31.3 5.5 %collective-permute-start.8 = (f32[10,8,256]{2,1,0:T(8,128)S(1)}, f32[10,8,256]{2,1,0:T(8,128)S(1)}, u32[]{:S(2)}, u32[]{:S(2)}) collective-permute-start(f32[10,8,256]{2,1,0:T(8,128)S(1)} %shard_map.73.rest_0_), channel_id=1, source_target_pairs={{0,25},{1,8},{8,1},{9,16},{16,9},{17,24},{24,17},{25,0},{2,27},{3,... | collective-permute-start | bytes 245768 | tf_op jit(solution)/shard_map/ppermute | solution.py:107
  37.8 4.3 %collective-permute-start.11 = (f32[16,4,256]{2,1,0:T(4,128)S(1)}, f32[16,4,256]{2,1,0:T(4,128)S(1)}, u32[]{:S(2)}, u32[]{:S(2)}) collective-permute-start(f32[16,4,256]{2,1,0:T(4,128)S(1)} %get-tuple-element.104), channel_id=1, source_target_pairs={{0,2},{2,0},{4,6},{6,4},{1,3},{3,1},{5,7},{7,5},{8,10},{10,8},{12,... | collective-permute-start | bytes 196616 | tf_op jit(solution)/shard_map/ppermute | solution.py:101
  39.8 2.3 %collective-permute-start.12 = (f32[16,4,256]{2,1,0:T(4,128)S(1)}, f32[16,4,256]{2,1,0:T(4,128)S(1)}, u32[]{:S(2)}, u32[]{:S(2)}) collective-permute-start(f32[16,4,256]{2,1,0:T(4,128)S(1)} %get-tuple-element.105), channel_id=1, source_target_pairs={{0,1},{1,0},{2,4},{3,5},{4,2},{5,3},{6,7},{7,6},{8,9},{9,8},{10,12... | collective-permute-start | bytes 196616 | tf_op jit(solution)/shard_map/ppermute | solution.py:101
  39.8 4.1 %collective-permute-start.14 = (f32[16,16,128]{2,1,0:T(8,128)S(1)}, f32[16,16,128]{2,1,0:T(8,128)S(1)}, u32[]{:S(2)}, u32[]{:S(2)}) collective-permute-start(f32[16,16,128]{2,1,0:T(8,128)S(1)} %get-tuple-element.107.refs_5_), channel_id=1, source_target_pairs={{0,1},{1,0},{2,3},{3,2},{4,5},{5,4},{6,7},{7,6},{8,9},{9,8},{10,11... | collective-permute-start | bytes 393224 | tf_op jit(solution)/shard_map/ppermute | solution.py:113
  42.2 4.2 %collective-permute-start.15 = (f32[10,8,256]{2,1,0:T(8,128)S(1)}, f32[10,8,256]{2,1,0:T(8,128)S(1)}, u32[]{:S(2)}, u32[]{:S(2)}) collective-permute-start(f32[10,8,256]{2,1,0:T(8,128)S(1)} %shard_map.82), channel_id=1, source_target_pairs={{0,1},{1,0},{8,9},{9,8},{16,17},{17,16},{24,25},{25,24},{2,3},{3,2... | collective-permute-start | bytes 245768 | tf_op jit(solution)/shard_map/ppermute | solution.py:108
  42.2 5.3 %collective-permute-start.13 = (f32[10,8,256]{2,1,0:T(8,128)S(1)}, f32[10,8,256]{2,1,0:T(8,128)S(1)}, u32[]{:S(2)}, u32[]{:S(2)}) collective-permute-start(f32[10,8,256]{2,1,0:T(8,128)S(1)} %shard_map.80.rest_0_), channel_id=1, source_target_pairs={{0,25},{1,8},{8,1},{9,16},{16,9},{17,24},{24,17},{25,0},{2,27},{3,... | collective-permute-start | bytes 245768 | tf_op jit(solution)/shard_map/ppermute | solution.py:107
  48.3 4.4 %collective-permute-start.16 = (f32[16,4,256]{2,1,0:T(4,128)S(1)}, f32[16,4,256]{2,1,0:T(4,128)S(1)}, u32[]{:S(2)}, u32[]{:S(2)}) collective-permute-start(f32[16,4,256]{2,1,0:T(4,128)S(1)} %get-tuple-element.115), channel_id=1, source_target_pairs={{0,2},{2,0},{4,6},{6,4},{1,3},{3,1},{5,7},{7,5},{8,10},{10,8},{12,... | collective-permute-start | bytes 196616 | tf_op jit(solution)/shard_map/ppermute | solution.py:101
  50.4 2.4 %collective-permute-start.17 = (f32[16,4,256]{2,1,0:T(4,128)S(1)}, f32[16,4,256]{2,1,0:T(4,128)S(1)}, u32[]{:S(2)}, u32[]{:S(2)}) collective-permute-start(f32[16,4,256]{2,1,0:T(4,128)S(1)} %get-tuple-element.116), channel_id=1, source_target_pairs={{0,1},{1,0},{2,4},{3,5},{4,2},{5,3},{6,7},{7,6},{8,9},{9,8},{10,12... | collective-permute-start | bytes 196616 | tf_op jit(solution)/shard_map/ppermute | solution.py:101
  50.4 4.1 %collective-permute-start.19 = (f32[16,16,128]{2,1,0:T(8,128)S(1)}, f32[16,16,128]{2,1,0:T(8,128)S(1)}, u32[]{:S(2)}, u32[]{:S(2)}) collective-permute-start(f32[16,16,128]{2,1,0:T(8,128)S(1)} %get-tuple-element.118.refs_7_), channel_id=1, source_target_pairs={{0,1},{1,0},{2,3},{3,2},{4,5},{5,4},{6,7},{7,6},{8,9},{9,8},{10,11... | collective-permute-start | bytes 393224 | tf_op jit(solution)/shard_map/ppermute | solution.py:113
  52.8 4.5 %collective-permute-start.20 = (f32[10,8,256]{2,1,0:T(8,128)S(1)}, f32[10,8,256]{2,1,0:T(8,128)S(1)}, u32[]{:S(2)}, u32[]{:S(2)}) collective-permute-start(f32[10,8,256]{2,1,0:T(8,128)S(1)} %shard_map.88), channel_id=1, source_target_pairs={{0,1},{1,0},{8,9},{9,8},{16,17},{17,16},{24,25},{25,24},{2,3},{3,2... | collective-permute-start | bytes 245768 | tf_op jit(solution)/shard_map/ppermute | solution.py:108
  52.9 5.5 %collective-permute-start.18 = (f32[10,8,256]{2,1,0:T(8,128)S(1)}, f32[10,8,256]{2,1,0:T(8,128)S(1)}, u32[]{:S(2)}, u32[]{:S(2)}) collective-permute-start(f32[10,8,256]{2,1,0:T(8,128)S(1)} %shard_map.86.rest_0_), channel_id=1, source_target_pairs={{0,25},{1,8},{8,1},{9,16},{16,9},{17,24},{24,17},{25,0},{2,27},{3,... | collective-permute-start | bytes 245768 | tf_op jit(solution)/shard_map/ppermute | solution.py:107
  59.3 1.4 %collective-permute-start.21 = (f32[17,16,128]{2,1,0:T(8,128)S(1)}, f32[17,16,128]{2,1,0:T(8,128)S(1)}, u32[]{:S(2)}, u32[]{:S(2)}) collective-permute-start(f32[17,16,128]{2,1,0:T(8,128)S(1)} %get-tuple-element.125), channel_id=1, source_target_pairs={{0,1},{1,0},{2,3},{3,2},{4,5},{5,4},{6,7},{7,6},{8,9},{9,8},{10,11... | collective-permute-start | bytes 417800 | tf_op jit(solution)/shard_map/ppermute | solution.py:113
  60.7 3.8 %collective-permute-start.22 = (f32[2,16,128]{2,1,0:T(8,128)S(1)}, f32[2,16,128]{2,1,0:T(8,128)S(1)}, u32[]{:S(2)}, u32[]{:S(2)}) collective-permute-start(f32[2,16,128]{2,1,0:T(8,128)S(1)} %pad_maximum_fusion), channel_id=1, source_target_pairs={{0,24},{8,0},{16,8},{24,16},{1,25},{9,1},{17,9},{25,17},{2,26},{10... | collective-permute-start | bytes 49160 | tf_op jit(solution)/shard_map/ppermute | solution.py:740
  62.2 3.7 %collective-permute-start.23 = (f32[2,16,128]{2,1,0:T(8,128)S(1)}, f32[2,16,128]{2,1,0:T(8,128)S(1)}, u32[]{:S(2)}, u32[]{:S(2)}) collective-permute-start(f32[2,16,128]{2,1,0:T(8,128)S(1)} %pad_maximum_fusion), channel_id=1, source_target_pairs={{0,16},{8,24},{16,0},{24,8},{1,17},{9,25},{17,1},{25,9},{2,18},{10... | collective-permute-start | bytes 49160 | tf_op jit(solution)/shard_map/ppermute | solution.py:740
  63.4 4.6 %collective-permute-start.24 = (f32[2,16,128]{2,1,0:T(8,128)S(1)}, f32[2,16,128]{2,1,0:T(8,128)S(1)}, u32[]{:S(2)}, u32[]{:S(2)}) collective-permute-start(f32[2,16,128]{2,1,0:T(8,128)S(1)} %pad_maximum_fusion), channel_id=1, source_target_pairs={{0,8},{8,16},{16,24},{24,0},{1,9},{9,17},{17,25},{25,1},{2,10},{10... | collective-permute-start | bytes 49160 | tf_op jit(solution)/shard_map/ppermute | solution.py:740
  68.0 5.7 %collective-permute-start.25 = (f32[2,16,128]{2,1,0:T(8,128)S(1)}, f32[2,16,128]{2,1,0:T(8,128)S(1)}, u32[]{:S(2)}, u32[]{:S(2)}) collective-permute-start(f32[2,16,128]{2,1,0:T(8,128)S(1)} %pad_maximum_fusion.1), channel_id=1, source_target_pairs={{0,6},{2,0},{4,2},{6,4},{1,7},{3,1},{5,3},{7,5},{8,14},{10,8},{12,... | collective-permute-start | bytes 49160 | tf_op jit(solution)/shard_map/ppermute | solution.py:740
  70.9 4.6 %collective-permute-start.26 = (f32[2,16,128]{2,1,0:T(8,128)S(1)}, f32[2,16,128]{2,1,0:T(8,128)S(1)}, u32[]{:S(2)}, u32[]{:S(2)}) collective-permute-start(f32[2,16,128]{2,1,0:T(8,128)S(1)} %pad_maximum_fusion.1), channel_id=1, source_target_pairs={{0,4},{2,6},{4,0},{6,2},{1,5},{3,7},{5,1},{7,3},{8,12},{10,14},{12... | collective-permute-start | bytes 49160 | tf_op jit(solution)/shard_map/ppermute | solution.py:740
  71.7 5.5 %collective-permute-start.27 = (f32[2,16,128]{2,1,0:T(8,128)S(1)}, f32[2,16,128]{2,1,0:T(8,128)S(1)}, u32[]{:S(2)}, u32[]{:S(2)}) collective-permute-start(f32[2,16,128]{2,1,0:T(8,128)S(1)} %pad_maximum_fusion.1), channel_id=1, source_target_pairs={{0,2},{2,4},{4,6},{6,0},{1,3},{3,5},{5,7},{7,1},{8,10},{10,12},{12... | collective-permute-start | bytes 49160 | tf_op jit(solution)/shard_map/ppermute | solution.py:740
